TPU v7x, 8 devices: a whole 2x2x1 slice. The times are simulated.
8 devices in a mesh: dp: 1 (over z), tp: 2 (over y), ep: 4 (over x, core).
Axes of the slice: x: 2, y: 2, z: 1, core: 2. Of those that a mesh axis runs over, the one named last changes fastest.
Arguments:
- tokens: bfloat16 [8192, 768], P(('dp', 'ep'))
- grad_out: bfloat16 [8192, 768], P(('dp', 'ep'))
- w_router: bfloat16 [768, 8], replicated
- w_in: bfloat16 [8, 768, 3072], P('ep', None, 'tp')
- w_out: bfloat16 [8, 3072, 768], P('ep', 'tp')
- expert_ids: int32 [8192], P(('dp', 'ep'))
Outputs:
- output 1: bfloat16 [8192, 768], P(('dp', 'ep'))
- output 2: bfloat16 [8192, 768], P(('dp', 'ep'))
- output 3: float32 [8, 768, 3072], P(('dp', 'ep'), None, 'tp')
- output 4: float32 [8, 3072, 768], P(('dp', 'ep'), 'tp')
- output 5: float32 [768, 8], P('dp')
All inputs are finite; a program needn't handle non-finite values.
Results may differ from a plain program's by a relative error of at most 0.00617232.
Values are sent between devices in bfloat16 or wider.
A program may use at most 1 GiB of HBM per device.

v0:
```python
import jax
import jax.numpy as jnp
from jax import lax
from jax.experimental import pallas as pl
from jax.experimental.pallas import tpu as pltpu
from jax.sharding import PartitionSpec as P


GELU_C = 0.7978845608028654
GELU_K = 0.044715
BF16 = jnp.bfloat16
F32 = jnp.float32
VMEM_LIMIT = 56 * 2**20
INFO_ROWS = 16


def nn(a, b):
    return jnp.dot(a, b, preferred_element_type=F32)


def nt(a, b):
    return lax.dot_general(a, b, (((1,), (1,)), ((), ())), preferred_element_type=F32)


def tn(a, b):
    return lax.dot_general(a, b, (((0,), (0,)), ((), ())), preferred_element_type=F32)


def gelu_and_slope(a):
    sq = a * a
    th = jnp.tanh(a * (GELU_C + (GELU_C * GELU_K) * sq))
    up = 1.0 + th
    act = (0.5 * a) * up
    return act, 0.5 * up + act * (1.0 - th) * (GELU_C + (3.0 * GELU_C * GELU_K) * sq)


def hidden_grads(x, dy, wi, wo):
    a = nn(x, wi)
    dh = nt(dy, wo)
    act, slope = gelu_and_slope(a)
    return act.astype(BF16), (dh * slope).astype(BF16)


def params(dims):
    return pltpu.CompilerParams(dimension_semantics=("arbitrary",) * dims, vmem_limit_bytes=VMEM_LIMIT)


def cost(flops, mib):
    return pl.CostEstimate(flops=int(flops), bytes_accessed=int(mib * 2**20), transcendentals=0)


def shape(dims, dtype=BF16):
    return jax.ShapeDtypeStruct(dims, dtype)


def whole(dims):
    return pl.BlockSpec(dims, lambda *_: (0,) * len(dims))


def route(ids_row, tokens, wg_t, capacity, cap):
    n_experts = wg_t.shape[0]
    n_tok = tokens.shape[0]
    step = 256

    def body(ids_ref, x_ref, wg_ref, info_ref):
        ids = ids_ref[...]
        logits = nt(wg_ref[...], x_ref[...])
        raised = jnp.exp(logits - jnp.max(logits, axis=0, keepdims=True))
        prob = raised / jnp.sum(raised, axis=0, keepdims=True)
        hot = ids == lax.broadcasted_iota(jnp.int32, (n_experts, n_tok), 0)
        hot_f = jnp.where(hot, 1.0, 0.0)
        upper = lax.broadcasted_iota(jnp.int32, (step, step), 0) <= lax.broadcasted_iota(jnp.int32, (step, step), 1)
        upper = jnp.where(upper, 1.0, 0.0).astype(BF16)
        carry = jnp.zeros((n_experts, 1), F32)
        for b in range(n_tok // step):
            cols = slice(b * step, (b + 1) * step)
            seen = nn(hot_f[:, cols].astype(BF16), upper) + carry
            carry = seen[:, step - 1 : step]
            pos = jnp.sum(seen * hot_f[:, cols], axis=0, keepdims=True) - 1.0
            slot = ids[:, cols].astype(F32) * cap + pos
            info_ref[0:1, cols] = jnp.where(pos < capacity, slot, -1.0)
        info_ref[1:2, :] = jnp.sum(hot_f * prob, axis=0, keepdims=True)
        info_ref[2:3, :] = ids.astype(F32)
        info_ref[3:8, :] = jnp.zeros((5, n_tok), F32)
        info_ref[8:16, :] = prob

    return pl.pallas_call(
        body,
        grid=(1,),
        in_specs=[whole(ids_row.shape), whole(tokens.shape), whole(wg_t.shape)],
        out_specs=whole((INFO_ROWS, n_tok)),
        out_shape=shape((INFO_ROWS, n_tok), F32),
        compiler_params=params(1),
        cost_estimate=cost(2e9, 3),
        name="route",
    )(ids_row, tokens, wg_t)


def dispatch(meta, info, tokens, grad_out, groups, cap):
    n_tok, d_model = tokens.shape
    count = len(groups)

    def body(meta_ref, info_ref, x_ref, gy_ref, *outs):
        g = pl.program_id(0)
        first, flip = groups[0]
        for p in range(1, count):
            first = jnp.where(g == p, groups[p][0], first)
            flip = jnp.where(g == p, groups[p][1], flip)
        k = jnp.bitwise_xor(meta_ref[0], flip)
        row = lax.broadcasted_iota(jnp.int32, (2 * cap, 1), 0)
        low = row < cap
        base_a = (jnp.bitwise_xor(meta_ref[1], first) * 2 + k) * cap
        base_b = (jnp.bitwise_xor(meta_ref[1], first + 1) * 2 + k) * cap - cap
        codes = (row + jnp.where(low, base_a, base_b)).astype(F32)
        hit = info_ref[0:1, :] == codes
        pick = jnp.where(hit, 1.0, 0.0).astype(BF16)
        row_gate = jnp.sum(jnp.where(hit, info_ref[1:2, :], 0.0), axis=1, keepdims=True)
        x = nn(pick, x_ref[...]).astype(BF16)
        dy = (row_gate * nn(pick, gy_ref[...])).astype(BF16)
        for p in range(count):

            @pl.when(g == p)
            def _():
                outs[2 * p][0] = x[:cap]
                outs[2 * p][1] = dy[:cap]
                outs[2 * p + 1][0] = x[cap:]
                outs[2 * p + 1][1] = dy[cap:]

    return pl.pallas_call(
        body,
        grid_spec=pltpu.PrefetchScalarGridSpec(
            num_scalar_prefetch=1,
            grid=(count,),
            in_specs=[whole(info.shape), whole(tokens.shape), whole(tokens.shape)],
            out_specs=[whole((2, cap, d_model))] * (2 * count),
        ),
        out_shape=[shape((2, cap, d_model))] * (2 * count),
        compiler_params=params(1),
        cost_estimate=cost(8 * count * cap * n_tok * d_model, 8 + 4 * count),
        name="dispatch",
    )(meta, info, tokens, grad_out)


def own_half(meta, pair_a, pair_b, w_in, w_out, chunk, group, so_far):
    _, d_model, width = w_in.shape
    cap = pair_a.shape[1]
    rows = 2 * cap

    def body(meta_ref, pa, pb, wi, wo, *refs):
        h_ref, da_ref, y_ref, s_ref, x_ref, dy_ref = refs[-6:]
        c = pl.program_id(0)

        @pl.when(c == 0)
        def _():
            x_ref[:cap] = pa[0]
            x_ref[cap:] = pb[0]
            dy_ref[:cap] = pa[1]
            dy_ref[cap:] = pb[1]

        h, da = hidden_grads(x_ref[...], dy_ref[...], wi[0], wo[0])
        h_ref[...] = h
        da_ref[...] = da
        y = nn(h, wo[0])
        s = nt(da, wi[0])

        @pl.when(c == 0)
        def _():
            y_ref[...] = y
            s_ref[...] = s

        @pl.when(c > 0)
        def _():
            y_ref[...] += y
            s_ref[...] += s

    hid = pl.BlockSpec((rows, chunk), lambda c, m: (group, c))
    full = pl.BlockSpec((rows, d_model), lambda c, m: (group, 0))
    return pl.pallas_call(
        body,
        grid_spec=pltpu.PrefetchScalarGridSpec(
            num_scalar_prefetch=1,
            grid=(width // chunk,),
            in_specs=[
                whole(pair_a.shape),
                whole(pair_a.shape),
                pl.BlockSpec((1, d_model, chunk), lambda c, m: (m[0], 0, c)),
                pl.BlockSpec((1, chunk, d_model), lambda c, m: (m[0], c, 0)),
            ]
            + [pl.BlockSpec(memory_space=pl.ANY)] * len(so_far),
            out_specs=[hid, hid] + [full] * 4,
        ),
        out_shape=[shape((2 * rows, width))] * 2
        + [shape((2 * rows, d_model), F32)] * 2
        + [shape((2 * rows, d_model))] * 2,
        input_output_aliases={5 + i: i for i in range(len(so_far))},
        compiler_params=params(1),
        cost_estimate=cost(8 * rows * width * d_model, 20),
        name="own_half",
    )(meta, pair_a, pair_b, w_in, w_out, *so_far)


def far_half(x, dy, wi, wo, y_in, s_in, chunk, group):
    rows, d_model = x.shape
    width = wi.shape[1]
    steps = width // chunk
    if group is not None:
        rows //= 2
    half = rows // 2

    def body(x_ref, dy_ref, wi_ref, wo_ref, y0, s0, *outs):
        c = pl.program_id(0)
        h, da = hidden_grads(x_ref[...], dy_ref[...], wi_ref[...], wo_ref[...])
        y = nn(h, wo_ref[...])
        s = nt(da, wi_ref[...])
        if group is not None:
            for p in range(2):
                part = slice(p * half, (p + 1) * half)
                outs[p][...] = (y0[part] + y[part]).astype(BF16)
                outs[2 + p][...] = (s0[part] + s[part]).astype(BF16)
            return

        @pl.when(c == 0)
        def _():
            outs[0][...] = y0[...] + y
            outs[1][...] = s0[...] + s

        @pl.when(c > 0)
        def _():
            outs[0][...] += y
            outs[1][...] += s

    full = pl.BlockSpec((rows, d_model), lambda c: (group or 0, 0))
    if group is not None:
        out_specs, out_shape = [whole((half, d_model))] * 4, [shape((half, d_model))] * 4
    else:
        out_specs, out_shape = [full] * 2, [shape((rows, d_model), F32)] * 2
    return pl.pallas_call(
        body,
        grid=(steps,),
        in_specs=[
            full,
            full,
            pl.BlockSpec((d_model, chunk), lambda c: (0, c)),
            pl.BlockSpec((chunk, d_model), lambda c: (c, 0)),
            full,
            full,
        ],
        out_specs=out_specs,
        out_shape=out_shape,
        compiler_params=params(1),
        cost_estimate=cost(8 * rows * width * d_model, 10),
        name="far_half",
    )(x, dy, wi, wo, y_in, s_in)


def finished_grads(meta, x, dy, h, da, n_local, chunk):
    rows, d_model = x.shape
    width = h.shape[1]

    def body(meta_ref, x_ref, dy_ref, h_ref, da_ref, gi, go):
        gi[0] = tn(x_ref[...], da_ref[...])
        go[0] = tn(h_ref[...], dy_ref[...])

    hid = pl.BlockSpec((rows, chunk), lambda c, m: (0, c))
    return pl.pallas_call(
        body,
        grid_spec=pltpu.PrefetchScalarGridSpec(
            num_scalar_prefetch=1,
            grid=(width // chunk,),
            in_specs=[whole((rows, d_model))] * 2 + [hid] * 2,
            out_specs=[
                pl.BlockSpec((1, d_model, chunk), lambda c, m: (m[0], 0, c)),
                pl.BlockSpec((1, chunk, d_model), lambda c, m: (m[0], c, 0)),
            ],
        ),
        out_shape=[shape((n_local, d_model, width), F32), shape((n_local, width, d_model), F32)],
        compiler_params=params(1),
        cost_estimate=cost(4 * rows * width * d_model, 25),
        name="finished_grads",
    )(meta, x, dy, h, da)


def other_grads(meta, pairs, w_in, w_out, grad_w_in, grad_w_out, chunk):
    _, d_model, width = w_in.shape
    cap = pairs[0].shape[1]
    rows = len(pairs) * cap

    def body(meta_ref, *refs):
        parts = refs[: len(pairs)]
        wi, wo, _, _, gi, go, x, dy = refs[len(pairs) :]

        @pl.when(pl.program_id(0) == 0)
        def _():
            for p, part in enumerate(parts):
                x[p * cap : (p + 1) * cap, :] = part[0]
                dy[p * cap : (p + 1) * cap, :] = part[1]

        h, da = hidden_grads(x[...], dy[...], wi[0], wo[0])
        gi[0] = tn(x[...], da)
        go[0] = tn(h, dy[...])

    def other(m):
        return 1 - m[0]

    any_spec = pl.BlockSpec(memory_space=pl.ANY)
    wi_spec = pl.BlockSpec((1, d_model, chunk), lambda c, m: (other(m), 0, c))
    wo_spec = pl.BlockSpec((1, chunk, d_model), lambda c, m: (other(m), c, 0))
    return pl.pallas_call(
        body,
        grid_spec=pltpu.PrefetchScalarGridSpec(
            num_scalar_prefetch=1,
            grid=(width // chunk,),
            in_specs=[whole(pairs[0].shape)] * len(pairs) + [wi_spec, wo_spec, any_spec, any_spec],
            out_specs=[wi_spec, wo_spec],
            scratch_shapes=[pltpu.VMEM((rows, d_model), BF16)] * 2,
        ),
        out_shape=[shape(grad_w_in.shape, F32), shape(grad_w_out.shape, F32)],
        input_output_aliases={len(pairs) + 3: 0, len(pairs) + 4: 1},
        compiler_params=params(1),
        cost_estimate=cost(8 * rows * width * d_model, 25),
        name="other_grads",
    )(meta, *pairs, w_in, w_out, grad_w_in, grad_w_out)


def stack_rows(parts, all_rows):
    @pl.when(pl.program_id(0) == 0)
    def _():
        cap = parts[0].shape[0]
        for p, part in enumerate(parts):
            all_rows[p * cap : (p + 1) * cap, :] = part[...]


def piece_pick(meta_ref, info_v, pieces, cap):
    lane = lax.broadcasted_iota(jnp.int32, (1, cap * len(pieces)), 1)
    codes = lane
    for p, (d, k) in enumerate(pieces):
        owner = jnp.bitwise_xor(meta_ref[1], d) * 2 + jnp.bitwise_xor(meta_ref[0], k)
        codes = jnp.where(lane >= p * cap, lane + (owner - p) * cap, codes)
    return jnp.where(info_v[:, 0:1] == codes.astype(F32), 1.0, 0.0).astype(BF16)


def combine_y(meta, pieces, info, tokens, grad_out, block):
    n_tok, d_model = tokens.shape
    keys, rows = list(pieces), list(pieces.values())
    cap = rows[0].shape[0]
    n_experts = INFO_ROWS - 8

    def body(meta_ref, *refs):
        parts = refs[: len(keys)]
        info_ref, x_ref, gy_ref, out_ref, dlog_ref, dwg_ref, all_rows = refs[len(keys) :]
        stack_rows(parts, all_rows)
        info_v = info_ref[...].T
        y = nn(piece_pick(meta_ref, info_v, keys, cap), all_rows[...])
        gate = info_v[:, 1:2]
        prob = info_v[:, 8:16]
        hot = info_v[:, 2:3] == lax.broadcasted_iota(jnp.int32, prob.shape, 1).astype(F32)
        out_ref[...] = (gate * y).astype(BF16)
        d_gate = jnp.sum(gy_ref[...].astype(F32) * y, axis=1, keepdims=True)
        dlog = (d_gate * prob * (jnp.where(hot, 1.0, 0.0) - gate)).astype(BF16)
        dlog_ref[...] = dlog
        dwg = tn(dlog, x_ref[...])

        @pl.when(pl.program_id(0) == 0)
        def _():
            dwg_ref[...] = dwg

        @pl.when(pl.program_id(0) > 0)
        def _():
            dwg_ref[...] += dwg

    tok = pl.BlockSpec((block, d_model), lambda b, m: (b, 0))
    return pl.pallas_call(
        body,
        grid_spec=pltpu.PrefetchScalarGridSpec(
            num_scalar_prefetch=1,
            grid=(n_tok // block,),
            in_specs=[whole((cap, d_model))] * len(keys)
            + [pl.BlockSpec((INFO_ROWS, block), lambda b, m: (0, b)), tok, tok],
            out_specs=[tok, pl.BlockSpec((block, n_experts), lambda b, m: (b, 0)), whole((n_experts, d_model))],
            scratch_shapes=[pltpu.VMEM((cap * len(keys), d_model), BF16)],
        ),
        out_shape=[shape((n_tok, d_model)), shape((n_tok, n_experts)), shape((n_experts, d_model), F32)],
        compiler_params=params(1),
        cost_estimate=cost(2 * n_tok * cap * len(keys) * d_model, 16),
        name="combine_y",
    )(meta, *rows, info, tokens, grad_out)


def combine_s(meta, pieces, info, extra, block):
    n_tok = info.shape[1]
    keys, rows = list(pieces), list(pieces.values())
    cap, d_model = rows[0].shape

    def body(meta_ref, *refs):
        parts = refs[: len(keys)]
        info_ref, *mid, out_ref, all_rows = refs[len(keys) :]
        stack_rows(parts, all_rows)
        s = nn(piece_pick(meta_ref, info_ref[...].T, keys, cap), all_rows[...])
        if extra:
            so_far, dlog_ref, wg_ref = mid
            s = s + so_far[...].astype(F32) + nn(dlog_ref[...], wg_ref[...])
        out_ref[...] = s.astype(BF16)

    tok = pl.BlockSpec((block, d_model), lambda b, m: (b, 0))
    extra_specs = []
    if extra:
        extra_specs = [tok, pl.BlockSpec((block, extra[1].shape[1]), lambda b, m: (b, 0)), whole(extra[2].shape)]
    return pl.pallas_call(
        body,
        grid_spec=pltpu.PrefetchScalarGridSpec(
            num_scalar_prefetch=1,
            grid=(n_tok // block,),
            in_specs=[whole((cap, d_model))] * len(keys)
            + [pl.BlockSpec((INFO_ROWS, block), lambda b, m: (0, b))]
            + extra_specs,
            out_specs=tok,
            scratch_shapes=[pltpu.VMEM((cap * len(keys), d_model), BF16)],
        ),
        out_shape=shape((n_tok, d_model)),
        compiler_params=params(1),
        cost_estimate=cost(2 * n_tok * cap * len(keys) * d_model, 10),
        name="combine_s",
    )(meta, *rows, info, *extra)


def solution(mesh):
    ep_size = mesh.shape["ep"]
    row_spec = P(("dp", "ep"), None)

    def to_ep(v, d):
        return lax.ppermute(v, "ep", [(i, i ^ d) for i in range(ep_size)])

    def to_twin(v):
        return lax.ppermute(v, "tp", [(0, 1), (1, 0)])

    def block(tokens, grad_out, w_router, w_in, w_out, expert_ids):
        n_tok, d_model = tokens.shape
        n_experts = w_router.shape[1]
        width = w_in.shape[2]
        capacity = (6 * n_tok + 5 * n_experts - 1) // (5 * n_experts)
        cap = (capacity + 15) // 16 * 16
        chunk = width // 3
        tp, ep = lax.axis_index("tp"), lax.axis_index("ep")
        meta = jnp.where(jnp.arange(2) == 0, tp, ep).astype(jnp.int32)

        far_w = {}
        for stage, lo, hi in (("a", 0, 4), ("b", 4, 5), ("c", 5, 6)):
            lo, size = lo * width // 6, (hi - lo) * width // 6
            part_in = lax.dynamic_slice(w_in, (1 - tp, 0, lo), (1, d_model, size))[0]
            part_out = lax.dynamic_slice(w_out, (1 - tp, lo, 0), (1, size, d_model))[0]
            far_w[stage] = to_twin(part_in), to_twin(part_out)

        info = route(expert_ids[None, :], tokens, w_router.T, capacity, cap)

        f2, f3 = dispatch(meta, info, tokens, grad_out, ((2, 0),), cap)
        f2, f3 = to_ep(f2, 2), to_ep(f3, 3)
        f0, f1, g2, g3, g0, g1 = dispatch(meta, info, tokens, grad_out, ((0, 0), (2, 1), (0, 1)), cap)
        f1 = to_ep(f1, 1)
        g2, g3 = to_ep(g2, 2), to_ep(g3, 3)
        g1 = to_ep(g1, 1)

        part = own_half(meta, f0, f1, w_in, w_out, chunk, 0, ())
        h, da, y, s, x, dy = own_half(meta, f2, f3, w_in, w_out, chunk, 1, part)
        y, s = far_half(x, dy, *far_w["a"], y, s, chunk, None)
        y, s = far_half(x, dy, *far_w["b"], y, s, width // 6, None)
        y0, y1, s0, s1 = far_half(x, dy, *far_w["c"], y, s, width // 6, 0)
        y2, y3, s2, s3 = far_half(x, dy, *far_w["c"], y, s, width // 6, 1)

        y1, s1 = to_ep(y1, 1), to_ep(s1, 1)
        y2, y3 = to_ep(y2, 2), to_ep(y3, 3)
        s2, s3 = to_ep(s2, 2), to_ep(s3, 3)
        y_mine, s_mine = [y0, y1, y2, y3], [s0, s1, s2, s3]
        y_twin = [to_twin(v) for v in y_mine]
        s_twin = [to_twin(v) for v in s_mine]

        grads = finished_grads(meta, x, dy, h, da, w_in.shape[0], chunk)
        grad_w_in, grad_w_out = other_grads(meta, (g0, g1, g2, g3), w_in, w_out, *grads, chunk)

        y_all = {(d, k): v for k, side in enumerate((y_mine, y_twin)) for d, v in enumerate(side)}
        s_all = {(d, k): v for k, side in enumerate((s_mine, s_twin)) for d, v in enumerate(side)}
        s_late = {key: s_all.pop(key) for key in ((2, 1), (3, 1))}
        moe_out, dlog, dwg = combine_y(meta, y_all, info, tokens, grad_out, n_tok // 8)
        dwg = dwg + to_ep(dwg, 1)
        dwg = dwg + to_ep(dwg, 2)
        so_far = combine_s(meta, s_all, info, (), n_tok // 8)
        grad_tokens = combine_s(meta, s_late, info, (so_far, dlog, w_router.T), n_tok // 8)
        return moe_out, grad_tokens, grad_w_in, grad_w_out, dwg.T

    in_specs = (row_spec, row_spec, P(None, None), P("ep", None, "tp"), P("ep", "tp", None), P(("dp", "ep")))
    out_specs = (row_spec, row_spec, P(("dp", "ep"), None, "tp"), P(("dp", "ep"), "tp", None), P("dp", None))
    return jax.shard_map(block, mesh=mesh, in_specs=in_specs, out_specs=out_specs, check_vma=False)
```

profile of v0, /device:TPU:0, one launch (start us, length us, event | category | flops | bytes accessed | tf_op | source)
XLA Modules:
  0.0 270.9 jit_solution(2257009426981629388)
XLA Ops:
  0.6 0.6 compare_select_fusion.meta_ref
  1.2 4.0 %route.1.info_ref.refs_8_.refs_6_.refs_2_ = f32[16,2048]{1,0:T(8,128)} custom-call(s32[1,2048]{1,0:T(1,128)} %bitcast.18, bf16[2048,768]{1,0:T(8,128)(2,1)} %refs_9_.1, bf16[8,768]{1,0:T(8,128)(2,1)} %bitcast.16), custom_call_target="tpu_custom_call" | custom-call | flops 2000000000 | bytes 3145728 | tf_op jit(solution)/shard_map/route/pallas_call | solution.py:87
  5.2 19.6 %dispatch.3 = (bf16[2,320,768]{2,1,0:T(8,128)(2,1)}, bf16[2,320,768]{2,1,0:T(8,128)(2,1)}, bf16[2,320,768]{2,1,0:T(8,128)(2,1)}, bf16[2,320,768]{2,1,0:T(8,128)(...) custom-call(s32[2]{0:T(128)} %compare_select_fusion.meta_ref, ...), custom_call_target="tpu_custom_call" | custom-call | flops 12079595520 | bytes 20971520 | tf_op jit(solution)/shard_map/dispatch/pallas_call | solution.py:129
  24.8 0.8 collective-permute-start.2
  25.7 1.5 dynamic-slice_bitcast_fusion.1
  27.2 2.5 collective-permute-start.7
  29.7 1.5 dynamic-slice_bitcast_fusion
  31.2 0.0 collective-permute-start.8
  31.3 9.0 %dispatch.2 = (bf16[2,320,768]{2,1,0:T(8,128)(2,1)}, bf16[2,320,768]{2,1,0:T(8,128)(2,1)}) custom-call(s32[2]{0:T(128)} %compare_select_fusion.meta_ref, f32[16,2048]{1,0:T(8,128)} %route.1.info_ref.refs_8_.refs_6_.refs_2_, bf16[2048,768]{1,0:T(8,128)(2,1)} %refs_9_.1, bf16[2048,768]{1,0:T(8,128)(2,1)} %refs_10_.1), custom_call_target="tpu_custom_call" | custom-call | flops 4026531840 | bytes 12582912 | tf_op jit(solution)/shard_map/dispatch/pallas_call | solution.py:129
  40.3 2.0 collective-permute-start
  42.3 1.2 dynamic-slice_bitcast_fusion.3
  43.5 1.2 dynamic-slice_bitcast_fusion.2
  44.7 0.0 collective-permute-done.2.pb
  44.7 1.5 collective-permute-start.5
  46.2 14.0 %own_half.2 = (bf16[1280,1536]{1,0:T(8,128)(2,1)}, bf16[1280,1536]{1,0:T(8,128)(2,1)}, f32[1280,768]{1,0:T(8,128)}, f32[1280,768]{1,0:T(8,128)}, bf16[1280,768]{1,0:T(8,128)(2,1)}, /*index=5*/bf16[1280,768]{1,0:T(8,128)(2,1)}) custom-call(s32[2]{0:T(128)} %compare_select_fusion.meta_ref, bf16[2,320,768]{2,1,0:T(8,128)(2,1)} %get-tuple-element.46.pa, ...), custom_call_target="tpu_custom_call" | custom-call | flops 6039797760 | bytes 20971520 | tf_op jit(solution)/shard_map/own_half/pallas_call | solution.py:178
  60.2 4.9 %collective-permute-done.pa = bf16[2,320,768]{2,1,0:T(8,128)(2,1)S(1)} collective-permute-done((bf16[2,320,768]{2,1,0:T(8,128)(2,1)}, bf16[2,320,768]{2,1,0:T(8,128)(2,1)S(1)}, u32[]{:S(2)}, u32[]{:S(2)}) %collective-permute-start) | collective-permute-done | bytes 983072 | tf_op jit(solution)/shard_map/ppermute | solution.py:431
  65.2 2.0 collective-permute-start.6
  67.2 17.6 %collective-permute-done.1.pb = bf16[2,320,768]{2,1,0:T(8,128)(2,1)S(1)} collective-permute-done((bf16[2,320,768]{2,1,0:T(8,128)(2,1)}, bf16[2,320,768]{2,1,0:T(8,128)(2,1)S(1)}, u32[]{:S(2)}, u32[]{:S(2)}) %collective-permute-start.1) | collective-permute-done | bytes 983072 | tf_op jit(solution)/shard_map/ppermute | solution.py:431
  84.8 1.5 collective-permute-start.3
  86.3 14.2 %own_half.3 = (bf16[1280,1536]{1,0:T(8,128)(2,1)}, bf16[1280,1536]{1,0:T(8,128)(2,1)}, f32[1280,768]{1,0:T(8,128)}, f32[1280,768]{1,0:T(8,128)}, bf16[1280,768]{1,0:T(8,128)(2,1)}, /*index=5*/bf16[1280,768]{1,0:T(8,128)(2,1)}) custom-call(s32[2]{0:T(128)} %compare_select_fusion.meta_ref, ...), custom_call_target="tpu_custom_call", output_to_operand_aliasing={{0}: (5, {}), {1}: (6, {}), {2}: (7, {}), {3}: (8, {}), {4}... | custom-call | flops 6039797760 | bytes 20971520 | tf_op jit(solution)/shard_map/own_half/pallas_call | solution.py:178
  100.5 6.6 %collective-permute-done.5.wi_ref = bf16[768,256]{1,0:T(8,128)(2,1)S(1)} collective-permute-done((bf16[768,256]{1,0:T(8,128)(2,1)S(1)}, bf16[768,256]{1,0:T(8,128)(2,1)S(1)}, u32[]{:S(2)}, u32[]{:S(2)}) %collective-permute-start.5) | collective-permute-done | bytes 393248 | tf_op jit(solution)/shard_map/ppermute | solution.py:434
  107.1 2.0 collective-permute-start.4
  109.1 6.4 %collective-permute-done.6.wo_ref = bf16[256,768]{1,0:T(8,128)(2,1)S(1)} collective-permute-done((bf16[256,768]{1,0:T(8,128)(2,1)S(1)}, bf16[256,768]{1,0:T(8,128)(2,1)S(1)}, u32[]{:S(2)}, u32[]{:S(2)}) %collective-permute-start.6) | collective-permute-done | bytes 393248 | tf_op jit(solution)/shard_map/ppermute | solution.py:434
  115.5 0.0 collective-permute-start.23
  115.5 0.0 collective-permute-done.7.wi_ref
  115.6 2.0 collective-permute-start.24
  117.6 0.1 collective-permute-start.25
  117.7 18.7 %far_half.4 = (f32[1280,768]{1,0:T(8,128)}, f32[1280,768]{1,0:T(8,128)}) custom-call(bf16[1280,768]{1,0:T(8,128)(2,1)} %get-tuple-element.54.x_ref, bf16[1280,768]{1,0:T(8,128)(2,1)} %get-tuple-element.55.dy_ref, bf16[768,1024]{1,0:T(8,128)(2,1)} %collective-permute-done.7.wi_ref, bf16[1024,768]{1,0:T(8,128)(2,1)} %collective-permute-done.8.wo_ref, ...), custom_call_target="tpu_custom_call" | custom-call | flops 8053063680 | bytes 10485760 | tf_op jit(solution)/shard_map/far_half/pallas_call | solution.py:237
  136.4 10.2 %far_half.5 = (f32[1280,768]{1,0:T(8,128)}, f32[1280,768]{1,0:T(8,128)}) custom-call(bf16[1280,768]{1,0:T(8,128)(2,1)} %get-tuple-element.54.x_ref, bf16[1280,768]{1,0:T(8,128)(2,1)} %get-tuple-element.55.dy_ref, bf16[768,256]{1,0:T(8,128)(2,1)} %copy-done.6, bf16[256,768]{1,0:T(8,128)(2,1)} %copy-done.7, f32[1280,768]{1,0:T(8,128)} %get-tuple-element.58.y0, ...), custom_call_target="tpu_custom_call" | custom-call | flops 2013265920 | bytes 10485760 | tf_op jit(solution)/shard_map/far_half/pallas_call | solution.py:237
  146.6 0.0 collective-permute-done.4.wo_ref
  146.6 0.8 copy-done
  147.4 0.2 copy-done.1
  147.5 5.4 %far_half.7 = (bf16[320,768]{1,0:T(8,128)(2,1)}, bf16[320,768]{1,0:T(8,128)(2,1)}, bf16[320,768]{1,0:T(8,128)(2,1)}, bf16[320,768]{1,0:T(8,128)(2,1)}) custom-call(bf16[1280,768]{1,0:T(8,128)(2,1)} %get-tuple-element.54.x_ref, bf16[1280,768]{1,0:T(8,128)(2,1)} %get-tuple-element.55.dy_ref, bf16[768,256]{1,0:T(8,128)(2,1)} %copy-done, ...), custom_call_target="tpu_custom_call" | custom-call | flops 1006632960 | bytes 10485760 | tf_op jit(solution)/shard_map/far_half/pallas_call | solution.py:237
  152.9 1.7 collective-permute-start.10
  154.7 5.6 %far_half.6 = (bf16[320,768]{1,0:T(8,128)(2,1)}, bf16[320,768]{1,0:T(8,128)(2,1)}, bf16[320,768]{1,0:T(8,128)(2,1)}, bf16[320,768]{1,0:T(8,128)(2,1)}) custom-call(bf16[1280,768]{1,0:T(8,128)(2,1)} %get-tuple-element.54.x_ref, bf16[1280,768]{1,0:T(8,128)(2,1)} %get-tuple-element.55.dy_ref, bf16[768,256]{1,0:T(8,128)(2,1)} %copy-done, ...), custom_call_target="tpu_custom_call" | custom-call | flops 1006632960 | bytes 10485760 | tf_op jit(solution)/shard_map/far_half/pallas_call | solution.py:237
  160.3 0.4 collective-permute-start.9
  160.7 1.8 collective-permute-start.12
  162.4 1.5 collective-permute-start.16
  163.9 11.8 %finished_grads.1 = (f32[2,768,1536]{2,1,0:T(8,128)}, f32[2,1536,768]{2,1,0:T(8,128)}) custom-call(s32[2]{0:T(128)} %compare_select_fusion.meta_ref, bf16[1280,768]{1,0:T(8,128)(2,1)} %get-tuple-element.54.x_ref, bf16[1280,768]{1,0:T(8,128)(2,1)} %get-tuple-element.55.dy_ref, bf16[1280,1536]{1,0:T(8,128)(2,1)} %get-tuple-element.76.h_ref, ...), custom_call_target="tpu_custom_call" | custom-call | flops 6039797760 | bytes 26214400 | tf_op jit(solution)/shard_map/finished_grads/pallas_call | solution.py:265
  175.7 0.0 collective-permute-start.18
  175.8 6.4 %collective-permute-done.11.refs_3_ = bf16[320,768]{1,0:T(8,128)(2,1)S(1)} collective-permute-done((bf16[320,768]{1,0:T(8,128)(2,1)}, bf16[320,768]{1,0:T(8,128)(2,1)S(1)}, u32[]{:S(2)}, u32[]{:S(2)}) %collective-permute-start.11) | collective-permute-done | bytes 491552 | tf_op jit(solution)/shard_map/ppermute | solution.py:431
  182.2 0.2 collective-permute-start.20
  182.4 2.0 collective-permute-start.14
  184.4 0.0 collective-permute-start.15
  184.4 8.6 %collective-permute-done.16.refs_2_ = bf16[320,768]{1,0:T(8,128)(2,1)S(1)} collective-permute-done((bf16[320,768]{1,0:T(8,128)(2,1)S(1)}, bf16[320,768]{1,0:T(8,128)(2,1)S(1)}, u32[]{:S(2)}, u32[]{:S(2)}) %collective-permute-start.16) | collective-permute-done | bytes 491552 | tf_op jit(solution)/shard_map/ppermute | solution.py:431
  193.1 2.0 collective-permute-start.13
  195.1 19.5 %other_grads.1 = (f32[2,768,1536]{2,1,0:T(8,128)}, f32[2,1536,768]{2,1,0:T(8,128)}) custom-call(s32[2]{0:T(128)} %compare_select_fusion.meta_ref, bf16[2,320,768]{2,1,0:T(8,128)(2,1)} %get-tuple-element.72.refs_0_, bf16[2,320,768]{2,1,0:T(8,128)(2,1)} %copy-done.9, bf16[2,320,768]{2,1,0:T(8,128)(2,1)} %copy-done.10, ...), custom_call_target="tpu_custom_call", output_to_operand_aliasing={{0}: (7, {}), {1}: (8, {})} | custom-call | flops 12079595520 | bytes 26214400 | tf_op jit(solution)/shard_map/other_grads/pallas_call | solution.py:308
  214.7 0.0 collective-permute-start.21
  214.7 2.0 collective-permute-start.22
  216.7 0.1 collective-permute-start.17
  216.8 2.0 collective-permute-start.19
  218.8 0.8 copy-done.25
  219.6 18.6 %combine_y.1 = (bf16[2048,768]{1,0:T(8,128)(2,1)}, bf16[2048,8]{1,0:T(8,128)(2,1)}, f32[8,768]{1,0:T(8,128)}) custom-call(s32[2]{0:T(128)} %compare_select_fusion.meta_ref, bf16[320,768]{1,0:T(8,128)(2,1)} %get-tuple-element.62.refs_0_, bf16[320,768]{1,0:T(8,128)(2,1)} %copy-done.17, bf16[320,768]{1,0:T(8,128)(2,1)} %copy-done.13, ...), custom_call_target="tpu_custom_call" | custom-call | flops 8053063680 | bytes 16777216 | tf_op jit(solution)/shard_map/combine_y/pallas_call | solution.py:372
  238.2 0.0 copy-start.8
  238.2 0.0 collective-permute-start.26
  238.2 0.0 copy-start.26
  238.2 1.1 collective-permute-done.22.refs_5_
  239.3 0.8 copy-done.27
  240.1 13.0 %combine_s.2.refs_3_ = bf16[2048,768]{1,0:T(8,128)(2,1)} custom-call(s32[2]{0:T(128)} %compare_select_fusion.meta_ref, bf16[320,768]{1,0:T(8,128)(2,1)} %get-tuple-element.69.refs_0_, bf16[320,768]{1,0:T(8,128)(2,1)} %copy-done.21, bf16[320,768]{1,0:T(8,128)(2,1)} %copy-done.15, bf16[320,768]{1,0:T(8,128)(2,1)} %copy-done.16, bf16[320,768]{1,0:T(8,128)(2,1)} %copy-done.26, ...), custom_call_target="tpu_custom_call" | custom-call | flops 6039797760 | bytes 10485760 | tf_op jit(solution)/shard_map/combine_s/pallas_call | solution.py:408
  253.1 1.5 collective-permute-start.27
  254.6 4.4 %collective-permute-done.19.refs_1_ = bf16[320,768]{1,0:T(8,128)(2,1)S(1)} collective-permute-done((bf16[320,768]{1,0:T(8,128)(2,1)S(1)}, bf16[320,768]{1,0:T(8,128)(2,1)S(1)}, u32[]{:S(2)}, u32[]{:S(2)}) %collective-permute-start.19) | collective-permute-done | bytes 491552 | tf_op jit(solution)/shard_map/ppermute | solution.py:434
  259.0 0.8 copy-done.5
  259.8 10.4 %combine_s.3 = bf16[2048,768]{1,0:T(8,128)(2,1)} custom-call(s32[2]{0:T(128)} %compare_select_fusion.meta_ref, bf16[320,768]{1,0:T(8,128)(2,1)} %copy-done.4, bf16[320,768]{1,0:T(8,128)(2,1)} %copy-done.5, f32[16,2048]{1,0:T(8,128)} %route.1.info_ref.refs_8_.refs_6_.refs_2_, bf16[2048,768]{1,0:T(8,128)(2,1)} %combine_s.2.refs_3_, ...), custom_call_target="tpu_custom_call" | custom-call | flops 2013265920 | bytes 10485760 | tf_op jit(solution)/shard_map/combine_s/pallas_call | solution.py:408
  270.3 0.6 add_bitcast_fusion
  (69 shorter events, 0.1 us)
Async XLA Ops:
  24.8 19.8 %collective-permute-start.2 = (bf16[2,320,768]{2,1,0:T(8,128)(2,1)}, bf16[2,320,768]{2,1,0:T(8,128)(2,1)}, u32[]{:S(2)}, u32[]{:S(2)}) collective-permute-start(bf16[2,320,768]{2,1,0:T(8,128)(2,1)} %get-tuple-element.47), channel_id=1, source_target_pairs={{0,1},{1,0},{2,3},{3,2},{4,5},{5,4},{6,7},{7,6}} | collective-permute-start | bytes 2949128 | tf_op jit(solution)/shard_map/ppermute | solution.py:431
  27.2 88.3 %collective-permute-start.7 = (bf16[768,1024]{1,0:T(8,128)(2,1)S(1)}, bf16[768,1024]{1,0:T(8,128)(2,1)}, u32[]{:S(2)}, u32[]{:S(2)}) collective-permute-start(bf16[768,1024]{1,0:T(8,128)(2,1)S(1)} %dynamic-slice_bitcast_fusion.1), channel_id=1, source_target_pairs={{0,4},{4,0},{1,5},{5,1},{2,6},{6,2},{3,7},{7,3}} | collective-permute-start | bytes 4718600 | tf_op jit(solution)/shard_map/ppermute | solution.py:434
  31.2 86.3 %collective-permute-start.8 = (bf16[1024,768]{1,0:T(8,128)(2,1)S(1)}, bf16[1024,768]{1,0:T(8,128)(2,1)}, u32[]{:S(2)}, u32[]{:S(2)}) collective-permute-start(bf16[1024,768]{1,0:T(8,128)(2,1)S(1)} %dynamic-slice_bitcast_fusion), channel_id=1, source_target_pairs={{0,4},{4,0},{1,5},{5,1},{2,6},{6,2},{3,7},{7,3}} | collective-permute-start | bytes 4718600 | tf_op jit(solution)/shard_map/ppermute | solution.py:434
  40.3 24.8 %collective-permute-start = (bf16[2,320,768]{2,1,0:T(8,128)(2,1)}, bf16[2,320,768]{2,1,0:T(8,128)(2,1)S(1)}, u32[]{:S(2)}, u32[]{:S(2)}) collective-permute-start(bf16[2,320,768]{2,1,0:T(8,128)(2,1)} %get-tuple-element.44), channel_id=1, source_target_pairs={{0,2},{1,3},{2,0},{3,1},{4,6},{5,7},{6,4},{7,5}} | collective-permute-start | bytes 2949128 | tf_op jit(solution)/shard_map/ppermute | solution.py:431
  42.3 42.5 %collective-permute-start.1 = (bf16[2,320,768]{2,1,0:T(8,128)(2,1)}, bf16[2,320,768]{2,1,0:T(8,128)(2,1)S(1)}, u32[]{:S(2)}, u32[]{:S(2)}) collective-permute-start(bf16[2,320,768]{2,1,0:T(8,128)(2,1)} %get-tuple-element.45), channel_id=1, source_target_pairs={{0,3},{1,2},{2,1},{3,0},{4,7},{5,6},{6,5},{7,4}} | collective-permute-start | bytes 2949128 | tf_op jit(solution)/shard_map/ppermute | solution.py:431
  44.7 62.4 %collective-permute-start.5 = (bf16[768,256]{1,0:T(8,128)(2,1)S(1)}, bf16[768,256]{1,0:T(8,128)(2,1)S(1)}, u32[]{:S(2)}, u32[]{:S(2)}) collective-permute-start(bf16[768,256]{1,0:T(8,128)(2,1)S(1)} %get-tuple-element.85), channel_id=1, source_target_pairs={{0,4},{4,0},{1,5},{5,1},{2,6},{6,2},{3,7},{7,3}} | collective-permute-start | bytes 1179656 | tf_op jit(solution)/shard_map/ppermute | solution.py:434
  65.2 21.2 %copy-start.2 = (bf16[2,320,768]{2,1,0:T(8,128)(2,1)}, bf16[2,320,768]{2,1,0:T(8,128)(2,1)S(1)}, u32[]{:S(2)}) copy-start(bf16[2,320,768]{2,1,0:T(8,128)(2,1)S(1)} %collective-permute-done.pa) | copy-start | bytes 2949124
  65.2 50.4 %collective-permute-start.6 = (bf16[256,768]{1,0:T(8,128)(2,1)S(1)}, bf16[256,768]{1,0:T(8,128)(2,1)S(1)}, u32[]{:S(2)}, u32[]{:S(2)}) collective-permute-start(bf16[256,768]{1,0:T(8,128)(2,1)S(1)} %get-tuple-element.83), channel_id=1, source_target_pairs={{0,4},{4,0},{1,5},{5,1},{2,6},{6,2},{3,7},{7,3}} | collective-permute-start | bytes 1179656 | tf_op jit(solution)/shard_map/ppermute | solution.py:434
  84.8 1.5 copy-start.3
  84.8 61.8 %collective-permute-start.3 = (bf16[768,256]{1,0:T(8,128)(2,1)S(1)}, bf16[768,256]{1,0:T(8,128)(2,1)S(1)}, u32[]{:S(2)}, u32[]{:S(2)}) collective-permute-start(bf16[768,256]{1,0:T(8,128)(2,1)S(1)} %get-tuple-element.86), channel_id=1, source_target_pairs={{0,4},{4,0},{1,5},{5,1},{2,6},{6,2},{3,7},{7,3}} | collective-permute-start | bytes 1179656 | tf_op jit(solution)/shard_map/ppermute | solution.py:434
  107.1 29.3 %copy-start.6 = (bf16[768,256]{1,0:T(8,128)(2,1)}, bf16[768,256]{1,0:T(8,128)(2,1)S(1)}, u32[]{:S(2)}) copy-start(bf16[768,256]{1,0:T(8,128)(2,1)S(1)} %collective-permute-done.5.wi_ref) | copy-start | bytes 1179652
  107.1 39.5 %collective-permute-start.4 = (bf16[256,768]{1,0:T(8,128)(2,1)S(1)}, bf16[256,768]{1,0:T(8,128)(2,1)S(1)}, u32[]{:S(2)}, u32[]{:S(2)}) collective-permute-start(bf16[256,768]{1,0:T(8,128)(2,1)S(1)} %get-tuple-element.84), channel_id=1, source_target_pairs={{0,4},{4,0},{1,5},{5,1},{2,6},{6,2},{3,7},{7,3}} | collective-permute-start | bytes 1179656 | tf_op jit(solution)/shard_map/ppermute | solution.py:434
  115.5 20.8 %copy-start.7 = (bf16[256,768]{1,0:T(8,128)(2,1)}, bf16[256,768]{1,0:T(8,128)(2,1)S(1)}, u32[]{:S(2)}) copy-start(bf16[256,768]{1,0:T(8,128)(2,1)S(1)} %collective-permute-done.6.wo_ref) | copy-start | bytes 1179652
  115.5 44.7 %collective-permute-start.23 = (bf16[2,320,768]{2,1,0:T(8,128)(2,1)}, bf16[2,320,768]{2,1,0:T(8,128)(2,1)S(1)}, u32[]{:S(2)}, u32[]{:S(2)}) collective-permute-start(bf16[2,320,768]{2,1,0:T(8,128)(2,1)} %get-tuple-element.73), channel_id=1, source_target_pairs={{0,1},{1,0},{2,3},{3,2},{4,5},{5,4},{6,7},{7,6}} | collective-permute-start | bytes 2949128 | tf_op jit(solution)/shard_map/ppermute | solution.py:431
  115.6 45.1 %collective-permute-start.24 = (bf16[2,320,768]{2,1,0:T(8,128)(2,1)}, bf16[2,320,768]{2,1,0:T(8,128)(2,1)S(1)}, u32[]{:S(2)}, u32[]{:S(2)}) collective-permute-start(bf16[2,320,768]{2,1,0:T(8,128)(2,1)} %get-tuple-element.74), channel_id=1, source_target_pairs={{0,2},{1,3},{2,0},{3,1},{4,6},{5,7},{6,4},{7,5}} | collective-permute-start | bytes 2949128 | tf_op jit(solution)/shard_map/ppermute | solution.py:431
  117.6 44.8 %collective-permute-start.25 = (bf16[2,320,768]{2,1,0:T(8,128)(2,1)}, bf16[2,320,768]{2,1,0:T(8,128)(2,1)S(1)}, u32[]{:S(2)}, u32[]{:S(2)}) collective-permute-start(bf16[2,320,768]{2,1,0:T(8,128)(2,1)} %get-tuple-element.75), channel_id=1, source_target_pairs={{0,3},{1,2},{2,1},{3,0},{4,7},{5,6},{6,5},{7,4}} | collective-permute-start | bytes 2949128 | tf_op jit(solution)/shard_map/ppermute | solution.py:431
  146.6 0.8 copy-start
  146.6 0.9 copy-start.1
  152.9 22.8 %collective-permute-start.10 = (bf16[320,768]{1,0:T(8,128)(2,1)}, bf16[320,768]{1,0:T(8,128)(2,1)S(1)}, u32[]{:S(2)}, u32[]{:S(2)}) collective-permute-start(bf16[320,768]{1,0:T(8,128)(2,1)} %get-tuple-element.64), channel_id=1, source_target_pairs={{0,2},{1,3},{2,0},{3,1},{4,6},{5,7},{6,4},{7,5}} | collective-permute-start | bytes 1474568 | tf_op jit(solution)/shard_map/ppermute | solution.py:431
  154.7 7.8 %copy-start.22 = (bf16[320,768]{1,0:T(8,128)(2,1)S(1)}, bf16[320,768]{1,0:T(8,128)(2,1)}, u32[]{:S(2)}) copy-start(bf16[320,768]{1,0:T(8,128)(2,1)} %get-tuple-element.67) | copy-start | bytes 1474564
  154.7 27.5 %collective-permute-start.11 = (bf16[320,768]{1,0:T(8,128)(2,1)}, bf16[320,768]{1,0:T(8,128)(2,1)S(1)}, u32[]{:S(2)}, u32[]{:S(2)}) collective-permute-start(bf16[320,768]{1,0:T(8,128)(2,1)} %get-tuple-element.65), channel_id=1, source_target_pairs={{0,3},{1,2},{2,1},{3,0},{4,7},{5,6},{6,5},{7,4}} | collective-permute-start | bytes 1474568 | tf_op jit(solution)/shard_map/ppermute | solution.py:431
  160.2 15.4 %copy-start.9 = (bf16[2,320,768]{2,1,0:T(8,128)(2,1)}, bf16[2,320,768]{2,1,0:T(8,128)(2,1)S(1)}, u32[]{:S(2)}) copy-start(bf16[2,320,768]{2,1,0:T(8,128)(2,1)S(1)} %collective-permute-done.23.refs_1_) | copy-start | bytes 2949124
  160.3 22.1 %collective-permute-start.9 = (bf16[320,768]{1,0:T(8,128)(2,1)}, bf16[320,768]{1,0:T(8,128)(2,1)S(1)}, u32[]{:S(2)}, u32[]{:S(2)}) collective-permute-start(bf16[320,768]{1,0:T(8,128)(2,1)} %get-tuple-element.63), channel_id=1, source_target_pairs={{0,1},{1,0},{2,3},{3,2},{4,5},{5,4},{6,7},{7,6}} | collective-permute-start | bytes 1474568 | tf_op jit(solution)/shard_map/ppermute | solution.py:431
  160.7 15.0 %copy-start.10 = (bf16[2,320,768]{2,1,0:T(8,128)(2,1)}, bf16[2,320,768]{2,1,0:T(8,128)(2,1)S(1)}, u32[]{:S(2)}) copy-start(bf16[2,320,768]{2,1,0:T(8,128)(2,1)S(1)} %collective-permute-done.24.refs_2_) | copy-start | bytes 2949124
  160.7 23.7 %collective-permute-start.12 = (bf16[320,768]{1,0:T(8,128)(2,1)}, bf16[320,768]{1,0:T(8,128)(2,1)S(1)}, u32[]{:S(2)}, u32[]{:S(2)}) collective-permute-start(bf16[320,768]{1,0:T(8,128)(2,1)} %get-tuple-element.62.refs_0_), channel_id=1, source_target_pairs={{0,4},{4,0},{1,5},{5,1},{2,6},{6,2},{3,7},{7,3}} | collective-permute-start | bytes 1474568 | tf_op jit(solution)/shard_map/ppermute | solution.py:434
  162.4 13.3 %copy-start.11 = (bf16[2,320,768]{2,1,0:T(8,128)(2,1)}, bf16[2,320,768]{2,1,0:T(8,128)(2,1)S(1)}, u32[]{:S(2)}) copy-start(bf16[2,320,768]{2,1,0:T(8,128)(2,1)S(1)} %collective-permute-done.25.refs_3_) | copy-start | bytes 2949124
  162.4 30.7 %collective-permute-start.16 = (bf16[320,768]{1,0:T(8,128)(2,1)S(1)}, bf16[320,768]{1,0:T(8,128)(2,1)S(1)}, u32[]{:S(2)}, u32[]{:S(2)}) collective-permute-start(bf16[320,768]{1,0:T(8,128)(2,1)S(1)} %copy-done.22), channel_id=1, source_target_pairs={{0,2},{1,3},{2,0},{3,1},{4,6},{5,7},{6,4},{7,5}} | collective-permute-start | bytes 1474568 | tf_op jit(solution)/shard_map/ppermute | solution.py:431
  163.9 11.8 %copy-start.19 = (bf16[320,768]{1,0:T(8,128)(2,1)S(1)}, bf16[320,768]{1,0:T(8,128)(2,1)}, u32[]{:S(2)}) copy-start(bf16[320,768]{1,0:T(8,128)(2,1)} %get-tuple-element.68) | copy-start | bytes 1474564
  163.9 18.2 %copy-start.20 = (bf16[320,768]{1,0:T(8,128)(2,1)S(1)}, bf16[320,768]{1,0:T(8,128)(2,1)}, u32[]{:S(2)}) copy-start(bf16[320,768]{1,0:T(8,128)(2,1)} %get-tuple-element.70) | copy-start | bytes 1474564
  175.7 38.9 %copy-start.13 = (bf16[320,768]{1,0:T(8,128)(2,1)}, bf16[320,768]{1,0:T(8,128)(2,1)S(1)}, u32[]{:S(2)}) copy-start(bf16[320,768]{1,0:T(8,128)(2,1)S(1)} %collective-permute-done.10.refs_2_) | copy-start | bytes 1474564
  175.7 38.9 %collective-permute-start.18 = (bf16[320,768]{1,0:T(8,128)(2,1)S(1)}, bf16[320,768]{1,0:T(8,128)(2,1)S(1)}, u32[]{:S(2)}, u32[]{:S(2)}) collective-permute-start(bf16[320,768]{1,0:T(8,128)(2,1)S(1)} %copy-done.19), channel_id=1, source_target_pairs={{0,3},{1,2},{2,1},{3,0},{4,7},{5,6},{6,5},{7,4}} | collective-permute-start | bytes 1474568 | tf_op jit(solution)/shard_map/ppermute | solution.py:431
  182.2 32.4 %copy-start.14 = (bf16[320,768]{1,0:T(8,128)(2,1)}, bf16[320,768]{1,0:T(8,128)(2,1)S(1)}, u32[]{:S(2)}) copy-start(bf16[320,768]{1,0:T(8,128)(2,1)S(1)} %collective-permute-done.11.refs_3_) | copy-start | bytes 1474564
  182.2 32.5 %collective-permute-start.20 = (bf16[320,768]{1,0:T(8,128)(2,1)S(1)}, bf16[320,768]{1,0:T(8,128)(2,1)S(1)}, u32[]{:S(2)}, u32[]{:S(2)}) collective-permute-start(bf16[320,768]{1,0:T(8,128)(2,1)S(1)} %copy-done.20), channel_id=1, source_target_pairs={{0,1},{1,0},{2,3},{3,2},{4,5},{5,4},{6,7},{7,6}} | collective-permute-start | bytes 1474568 | tf_op jit(solution)/shard_map/ppermute | solution.py:431
  182.4 32.2 %copy-start.17 = (bf16[320,768]{1,0:T(8,128)(2,1)}, bf16[320,768]{1,0:T(8,128)(2,1)S(1)}, u32[]{:S(2)}) copy-start(bf16[320,768]{1,0:T(8,128)(2,1)S(1)} %collective-permute-done.9.refs_1_) | copy-start | bytes 1474564
  182.4 34.3 %collective-permute-start.14 = (bf16[320,768]{1,0:T(8,128)(2,1)S(1)}, bf16[320,768]{1,0:T(8,128)(2,1)S(1)}, u32[]{:S(2)}, u32[]{:S(2)}) collective-permute-start(bf16[320,768]{1,0:T(8,128)(2,1)S(1)} %collective-permute-done.10.refs_2_), channel_id=1, source_target_pairs={{0,4},{4,0},{1,5},{5,1},{2,6},{6,2},{3,7},{7,3}} | collective-permute-start | bytes 1474568 | tf_op jit(solution)/shard_map/ppermute | solution.py:434
  184.4 30.2 %copy-start.18 = (bf16[320,768]{1,0:T(8,128)(2,1)}, bf16[320,768]{1,0:T(8,128)(2,1)S(1)}, u32[]{:S(2)}) copy-start(bf16[320,768]{1,0:T(8,128)(2,1)S(1)} %collective-permute-done.12.refs_4_) | copy-start | bytes 1474564
  184.4 32.4 %collective-permute-start.15 = (bf16[320,768]{1,0:T(8,128)(2,1)S(1)}, bf16[320,768]{1,0:T(8,128)(2,1)S(1)}, u32[]{:S(2)}, u32[]{:S(2)}) collective-permute-start(bf16[320,768]{1,0:T(8,128)(2,1)S(1)} %collective-permute-done.11.refs_3_), channel_id=1, source_target_pairs={{0,4},{4,0},{1,5},{5,1},{2,6},{6,2},{3,7},{7,3}} | collective-permute-start | bytes 1474568 | tf_op jit(solution)/shard_map/ppermute | solution.py:434
  193.1 23.6 %copy-start.15 = (bf16[320,768]{1,0:T(8,128)(2,1)}, bf16[320,768]{1,0:T(8,128)(2,1)S(1)}, u32[]{:S(2)}) copy-start(bf16[320,768]{1,0:T(8,128)(2,1)S(1)} %collective-permute-done.16.refs_2_) | copy-start | bytes 1474564
  193.1 25.7 %collective-permute-start.13 = (bf16[320,768]{1,0:T(8,128)(2,1)S(1)}, bf16[320,768]{1,0:T(8,128)(2,1)S(1)}, u32[]{:S(2)}, u32[]{:S(2)}) collective-permute-start(bf16[320,768]{1,0:T(8,128)(2,1)S(1)} %collective-permute-done.9.refs_1_), channel_id=1, source_target_pairs={{0,4},{4,0},{1,5},{5,1},{2,6},{6,2},{3,7},{7,3}} | collective-permute-start | bytes 1474568 | tf_op jit(solution)/shard_map/ppermute | solution.py:434
  195.1 19.5 %copy-start.12 = (bf16[320,768]{1,0:T(8,128)(2,1)S(1)}, bf16[320,768]{1,0:T(8,128)(2,1)}, u32[]{:S(2)}) copy-start(bf16[320,768]{1,0:T(8,128)(2,1)} %get-tuple-element.69.refs_0_) | copy-start | bytes 1474564
  214.6 23.5 %copy-start.16 = (bf16[320,768]{1,0:T(8,128)(2,1)}, bf16[320,768]{1,0:T(8,128)(2,1)S(1)}, u32[]{:S(2)}) copy-start(bf16[320,768]{1,0:T(8,128)(2,1)S(1)} %collective-permute-done.18.refs_3_) | copy-start | bytes 1474564
  214.7 23.6 %collective-permute-start.21 = (bf16[320,768]{1,0:T(8,128)(2,1)S(1)}, bf16[320,768]{1,0:T(8,128)(2,1)S(1)}, u32[]{:S(2)}, u32[]{:S(2)}) collective-permute-start(bf16[320,768]{1,0:T(8,128)(2,1)S(1)} %copy-done.12), channel_id=1, source_target_pairs={{0,4},{4,0},{1,5},{5,1},{2,6},{6,2},{3,7},{7,3}} | collective-permute-start | bytes 1474568 | tf_op jit(solution)/shard_map/ppermute | solution.py:434
  214.7 23.5 %copy-start.21 = (bf16[320,768]{1,0:T(8,128)(2,1)}, bf16[320,768]{1,0:T(8,128)(2,1)S(1)}, u32[]{:S(2)}) copy-start(bf16[320,768]{1,0:T(8,128)(2,1)S(1)} %collective-permute-done.20.refs_1_) | copy-start | bytes 1474564
  214.7 24.6 %collective-permute-start.22 = (bf16[320,768]{1,0:T(8,128)(2,1)S(1)}, bf16[320,768]{1,0:T(8,128)(2,1)S(1)}, u32[]{:S(2)}, u32[]{:S(2)}) collective-permute-start(bf16[320,768]{1,0:T(8,128)(2,1)S(1)} %collective-permute-done.20.refs_1_), channel_id=1, source_target_pairs={{0,4},{4,0},{1,5},{5,1},{2,6},{6,2},{3,7},{7,3}} | collective-permute-start | bytes 1474568 | tf_op jit(solution)/shard_map/ppermute | solution.py:434
  216.7 2.1 copy-start.23
  216.7 37.9 %collective-permute-start.17 = (bf16[320,768]{1,0:T(8,128)(2,1)S(1)}, bf16[320,768]{1,0:T(8,128)(2,1)S(1)}, u32[]{:S(2)}, u32[]{:S(2)}) collective-permute-start(bf16[320,768]{1,0:T(8,128)(2,1)S(1)} %collective-permute-done.16.refs_2_), channel_id=1, source_target_pairs={{0,4},{4,0},{1,5},{5,1},{2,6},{6,2},{3,7},{7,3}} | collective-permute-start | bytes 1474568 | tf_op jit(solution)/shard_map/ppermute | solution.py:434
  216.8 2.0 copy-start.24
  216.8 42.2 %collective-permute-start.19 = (bf16[320,768]{1,0:T(8,128)(2,1)S(1)}, bf16[320,768]{1,0:T(8,128)(2,1)S(1)}, u32[]{:S(2)}, u32[]{:S(2)}) collective-permute-start(bf16[320,768]{1,0:T(8,128)(2,1)S(1)} %collective-permute-done.18.refs_3_), channel_id=1, source_target_pairs={{0,4},{4,0},{1,5},{5,1},{2,6},{6,2},{3,7},{7,3}} | collective-permute-start | bytes 1474568 | tf_op jit(solution)/shard_map/ppermute | solution.py:434
  218.8 0.8 copy-start.25
  238.2 14.9 %copy-start.8 = (f32[8,768]{1,0:T(8,128)S(1)}, f32[8,768]{1,0:T(8,128)}, u32[]{:S(2)}) copy-start(f32[8,768]{1,0:T(8,128)} %get-tuple-element.82) | copy-start | bytes 73732
  238.2 14.9 %collective-permute-start.26 = (f32[8,768]{1,0:T(8,128)}, f32[8,768]{1,0:T(8,128)S(1)}, u32[]{:S(2)}, u32[]{:S(2)}) collective-permute-start(f32[8,768]{1,0:T(8,128)} %get-tuple-element.82), channel_id=1, source_target_pairs={{0,1},{1,0},{2,3},{3,2},{4,5},{5,4},{6,7},{7,6}} | collective-permute-start | bytes 73736 | tf_op jit(solution)/shard_map/ppermute | solution.py:431
  238.2 1.1 copy-start.26
  239.3 0.8 copy-start.27
  253.1 17.1 %collective-permute-start.27 = (f32[8,768]{1,0:T(8,128)S(1)}, f32[8,768]{1,0:T(8,128)S(1)}, u32[]{:S(2)}, u32[]{:S(2)}) collective-permute-start(f32[8,768]{1,0:T(8,128)S(1)} %add.16), channel_id=1, source_target_pairs={{0,2},{1,3},{2,0},{3,1},{4,6},{5,7},{6,4},{7,5}} | collective-permute-start | bytes 73736 | tf_op jit(solution)/shard_map/ppermute | solution.py:431
  254.6 4.4 %copy-start.4 = (bf16[320,768]{1,0:T(8,128)(2,1)}, bf16[320,768]{1,0:T(8,128)(2,1)S(1)}, u32[]{:S(2)}) copy-start(bf16[320,768]{1,0:T(8,128)(2,1)S(1)} %collective-permute-done.17.refs_0_) | copy-start | bytes 1474564
  259.0 0.8 copy-start.5
where the time goes:
time: 271 us
  Pallas kernels  174 us (64%)
  waiting for transfers between devices  56.1 us (21%)
  starting transfers between devices  29.9 us (11%)
  local copies, waits for them, and re-layouts  8.77 us (3%)
    pallas_call x4, Pallas kernels, far_half(): pl.pallas_call(body, grid=(steps,), in_specs=[full, full, pl.BlockSpec((d...  39.9 us
    ppermute x14, waiting for transfers between devices, to_ep(): return lax.ppermute(v, 'ep', [(i, i ^ d) for i in range(ep_size)])  37.6 us
    pallas_call x2, Pallas kernels, dispatch(): pl.pallas_call(body, grid_spec=pltpu.PrefetchScalarGridSpec(num_scalar_pr...  28.6 us
    pallas_call x2, Pallas kernels, own_half(): pl.pallas_call(body, grid_spec=pltpu.PrefetchScalarGridSpec(num_scalar_pr...  28.2 us
    pallas_call x2, Pallas kernels, combine_s(): pl.pallas_call(body, grid_spec=pltpu.PrefetchScalarGridSpec(num_scalar_pr...  23.4 us
    ppermute x14, starting transfers between devices, to_twin(): return lax.ppermute(v, 'tp', [(0, 1), (1, 0)])  19.6 us
    pallas_call x1, Pallas kernels, other_grads(): pl.pallas_call(body, grid_spec=pltpu.PrefetchScalarGridSpec(num_scalar_pr...  19.5 us
    pallas_call x1, Pallas kernels, combine_y(): pl.pallas_call(body, grid_spec=pltpu.PrefetchScalarGridSpec(num_scalar_pr...  18.6 us
  transfers between devices with their start and end apart: 28, of which 8 were waited for; matrix products, arithmetic and copies ran while one was open for 2% of the time, Pallas kernels for 56%

commit v1 on v0

--- a/solution.py
+++ b/solution.py
@@ -322,14 +322,6 @@
     )(meta, *pairs, w_in, w_out, grad_w_in, grad_w_out)
 
 
-def stack_rows(parts, all_rows):
-    @pl.when(pl.program_id(0) == 0)
-    def _():
-        cap = parts[0].shape[0]
-        for p, part in enumerate(parts):
-            all_rows[p * cap : (p + 1) * cap, :] = part[...]
-
-
 def piece_pick(meta_ref, info_v, pieces, cap):
     lane = lax.broadcasted_iota(jnp.int32, (1, cap * len(pieces)), 1)
     codes = lane
@@ -339,49 +331,81 @@
     return jnp.where(info_v[:, 0:1] == codes.astype(F32), 1.0, 0.0).astype(BF16)
 
 
+def start_all(copies):
+    for copy in copies:
+        copy.start()
+
+
+def wait_all(copies):
+    for copy in copies:
+        copy.wait()
+
+
 def combine_y(meta, pieces, info, tokens, grad_out, block):
     n_tok, d_model = tokens.shape
     keys, rows = list(pieces), list(pieces.values())
-    cap = rows[0].shape[0]
+    count, cap = len(keys), rows[0].shape[0]
     n_experts = INFO_ROWS - 8
+    blocks = n_tok // block
 
     def body(meta_ref, *refs):
-        parts = refs[: len(keys)]
-        info_ref, x_ref, gy_ref, out_ref, dlog_ref, dwg_ref, all_rows = refs[len(keys) :]
-        stack_rows(parts, all_rows)
-        info_v = info_ref[...].T
-        y = nn(piece_pick(meta_ref, info_v, keys, cap), all_rows[...])
-        gate = info_v[:, 1:2]
-        prob = info_v[:, 8:16]
-        hot = info_v[:, 2:3] == lax.broadcasted_iota(jnp.int32, prob.shape, 1).astype(F32)
-        out_ref[...] = (gate * y).astype(BF16)
-        d_gate = jnp.sum(gy_ref[...].astype(F32) * y, axis=1, keepdims=True)
-        dlog = (d_gate * prob * (jnp.where(hot, 1.0, 0.0) - gate)).astype(BF16)
-        dlog_ref[...] = dlog
-        dwg = tn(dlog, x_ref[...])
-
-        @pl.when(pl.program_id(0) == 0)
-        def _():
-            dwg_ref[...] = dwg
-
-        @pl.when(pl.program_id(0) > 0)
-        def _():
-            dwg_ref[...] += dwg
-
-    tok = pl.BlockSpec((block, d_model), lambda b, m: (b, 0))
+        parts = refs[:count]
+        info_ref, x_hbm, gy_hbm, out_hbm, dlog_ref, dwg_ref, all_rows, x, gy, out, row_sem, x_sem, gy_sem, out_sem = refs[count:]
+
+        def tok(b):
+            return pl.ds(pl.multiple_of(b * block, block), block)
+
+        def row_copy(p):
+            return pltpu.make_async_copy(parts[p], all_rows.at[pl.ds(p * cap, cap)], row_sem.at[p])
+
+        def in_copies(b):
+            return (
+                pltpu.make_async_copy(gy_hbm.at[tok(b)], gy.at[tok(b)], gy_sem.at[b]),
+                pltpu.make_async_copy(x_hbm.at[tok(b)], x.at[tok(b)], x_sem.at[b]),
+            )
+
+        def out_copy(b):
+            return pltpu.make_async_copy(out.at[tok(b)], out_hbm.at[tok(b)], out_sem.at[b])
+
+        start_all([row_copy(p) for p in range(count)])
+        for b in range(blocks):
+            start_all(in_copies(b))
+        dwg_ref[...] = jnp.zeros_like(dwg_ref)
+        wait_all([row_copy(p) for p in range(count)])
+
+        @pl.loop(0, blocks)
+        def _(b):
+            info_v = info_ref[:, tok(b)].T
+            y = nn(piece_pick(meta_ref, info_v, keys, cap), all_rows[...])
+            gate = info_v[:, 1:2]
+            prob = info_v[:, 8:16]
+            hot = info_v[:, 2:3] == lax.broadcasted_iota(jnp.int32, prob.shape, 1).astype(F32)
+            out[tok(b), :] = (gate * y).astype(BF16)
+            wait_all(in_copies(b))
+            out_copy(b).start()
+            d_gate = jnp.sum(gy[tok(b), :].astype(F32) * y, axis=1, keepdims=True)
+            dlog = d_gate * prob * (jnp.where(hot, 1.0, 0.0) - gate)
+            dlog_ref[:, tok(b)] = dlog.T
+            dwg_ref[...] += tn(dlog.astype(BF16), x[tok(b), :])
+
+        wait_all([out_copy(b) for b in range(blocks)])
+
+    any_spec = pl.BlockSpec(memory_space=pl.ANY)
     return pl.pallas_call(
         body,
         grid_spec=pltpu.PrefetchScalarGridSpec(
             num_scalar_prefetch=1,
-            grid=(n_tok // block,),
-            in_specs=[whole((cap, d_model))] * len(keys)
-            + [pl.BlockSpec((INFO_ROWS, block), lambda b, m: (0, b)), tok, tok],
-            out_specs=[tok, pl.BlockSpec((block, n_experts), lambda b, m: (b, 0)), whole((n_experts, d_model))],
-            scratch_shapes=[pltpu.VMEM((cap * len(keys), d_model), BF16)],
+            grid=(1,),
+            in_specs=[any_spec] * count + [whole((INFO_ROWS, n_tok)), any_spec, any_spec],
+            out_specs=[any_spec, whole((n_experts, n_tok)), whole((n_experts, d_model))],
+            scratch_shapes=[pltpu.VMEM((cap * count, d_model), BF16)]
+            + [pltpu.VMEM((n_tok, d_model), BF16)] * 3
+            + [pltpu.SemaphoreType.DMA((count,))]
+            + [pltpu.SemaphoreType.DMA((blocks,))] * 3,
         ),
-        out_shape=[shape((n_tok, d_model)), shape((n_tok, n_experts)), shape((n_experts, d_model), F32)],
-        compiler_params=params(1),
-        cost_estimate=cost(2 * n_tok * cap * len(keys) * d_model, 16),
+        out_shape=[shape((n_tok, d_model)), shape((n_experts, n_tok), F32), shape((n_experts, d_model), F32)],
+        compiler_params=params(1),
+        cost_estimate=cost(2 * n_tok * cap * count * d_model, 16),
         name="combine_y",
     )(meta, *rows, info, tokens, grad_out)
 
@@ -389,36 +413,64 @@
 def combine_s(meta, pieces, info, extra, block):
     n_tok = info.shape[1]
     keys, rows = list(pieces), list(pieces.values())
+    count = len(keys)
     cap, d_model = rows[0].shape
+    blocks = n_tok // block
 
     def body(meta_ref, *refs):
-        parts = refs[: len(keys)]
-        info_ref, *mid, out_ref, all_rows = refs[len(keys) :]
-        stack_rows(parts, all_rows)
-        s = nn(piece_pick(meta_ref, info_ref[...].T, keys, cap), all_rows[...])
+        parts, refs = refs[:count], refs[count:]
         if extra:
-            so_far, dlog_ref, wg_ref = mid
-            s = s + so_far[...].astype(F32) + nn(dlog_ref[...], wg_ref[...])
-        out_ref[...] = s.astype(BF16)
-
-    tok = pl.BlockSpec((block, d_model), lambda b, m: (b, 0))
-    extra_specs = []
+            info_ref, dlog_ref, wg_ref, so_hbm, out_hbm, all_rows, out, row_sem, out_sem, so_far, so_sem = refs
+        else:
+            info_ref, out_hbm, all_rows, out, row_sem, out_sem = refs
+
+        def tok(b):
+            return pl.ds(pl.multiple_of(b * block, block), block)
+
+        def row_copy(p):
+            return pltpu.make_async_copy(parts[p], all_rows.at[pl.ds(p * cap, cap)], row_sem.at[p])
+
+        def so_copy(b):
+            return pltpu.make_async_copy(so_hbm.at[tok(b)], so_far.at[tok(b)], so_sem.at[b])
+
+        def out_copy(b):
+            return pltpu.make_async_copy(out.at[tok(b)], out_hbm.at[tok(b)], out_sem.at[b])
+
+        start_all([row_copy(p) for p in range(count)])
+        if extra:
+            start_all([so_copy(b) for b in range(blocks)])
+        wait_all([row_copy(p) for p in range(count)])
+
+        @pl.loop(0, blocks)
+        def _(b):
+            s = nn(piece_pick(meta_ref, info_ref[:, tok(b)].T, keys, cap), all_rows[...])
+            if extra:
+                dlog = dlog_ref[:, tok(b)].T.astype(BF16)
+                s = s + nn(dlog, wg_ref[...])
+                so_copy(b).wait()
+                s = s + so_far[tok(b), :].astype(F32)
+            out[tok(b), :] = s.astype(BF16)
+            out_copy(b).start()
+
+        wait_all([out_copy(b) for b in range(blocks)])
+
+    any_spec = pl.BlockSpec(memory_space=pl.ANY)
+    scratch = [pltpu.VMEM((cap * count, d_model), BF16), pltpu.VMEM((n_tok, d_model), BF16)]
+    scratch += [pltpu.SemaphoreType.DMA((count,)), pltpu.SemaphoreType.DMA((blocks,))]
+    in_specs = [any_spec] * count + [whole((INFO_ROWS, n_tok))]
     if extra:
-        extra_specs = [tok, pl.BlockSpec((block, extra[1].shape[1]), lambda b, m: (b, 0)), whole(extra[2].shape)]
+        so_far, dlog_t, wg_t = extra
+        in_specs += [whole(dlog_t.shape), whole(wg_t.shape), any_spec]
+        extra = (dlog_t, wg_t, so_far)
+        scratch += [pltpu.VMEM((n_tok, d_model), BF16), pltpu.SemaphoreType.DMA((blocks,))]
     return pl.pallas_call(
         body,
         grid_spec=pltpu.PrefetchScalarGridSpec(
-            num_scalar_prefetch=1,
-            grid=(n_tok // block,),
-            in_specs=[whole((cap, d_model))] * len(keys)
-            + [pl.BlockSpec((INFO_ROWS, block), lambda b, m: (0, b))]
-            + extra_specs,
-            out_specs=tok,
-            scratch_shapes=[pltpu.VMEM((cap * len(keys), d_model), BF16)],
+            num_scalar_prefetch=1, grid=(1,), in_specs=in_specs, out_specs=any_spec, scratch_shapes=scratch
         ),
         out_shape=shape((n_tok, d_model)),
         compiler_params=params(1),
-        cost_estimate=cost(2 * n_tok * cap * len(keys) * d_model, 10),
+        cost_estimate=cost(2 * n_tok * cap * count * d_model, 10),
         name="combine_s",
     )(meta, *rows, info, *extra)
 
@@ -444,8 +496,8 @@
         meta = jnp.where(jnp.arange(2) == 0, tp, ep).astype(jnp.int32)
 
         far_w = {}
-        for stage, lo, hi in (("a", 0, 4), ("b", 4, 5), ("c", 5, 6)):
-            lo, size = lo * width // 6, (hi - lo) * width // 6
+        for stage, lo, hi in (("a", 0, 2), ("b", 2, 3)):
+            lo, size = lo * chunk, (hi - lo) * chunk
             part_in = lax.dynamic_slice(w_in, (1 - tp, 0, lo), (1, d_model, size))[0]
             part_out = lax.dynamic_slice(w_out, (1 - tp, lo, 0), (1, size, d_model))[0]
             far_w[stage] = to_twin(part_in), to_twin(part_out)
@@ -462,9 +514,8 @@
         part = own_half(meta, f0, f1, w_in, w_out, chunk, 0, ())
         h, da, y, s, x, dy = own_half(meta, f2, f3, w_in, w_out, chunk, 1, part)
         y, s = far_half(x, dy, *far_w["a"], y, s, chunk, None)
-        y, s = far_half(x, dy, *far_w["b"], y, s, width // 6, None)
-        y0, y1, s0, s1 = far_half(x, dy, *far_w["c"], y, s, width // 6, 0)
-        y2, y3, s2, s3 = far_half(x, dy, *far_w["c"], y, s, width // 6, 1)
+        y0, y1, s0, s1 = far_half(x, dy, *far_w["b"], y, s, chunk, 0)
+        y2, y3, s2, s3 = far_half(x, dy, *far_w["b"], y, s, chunk, 1)
 
         y1, s1 = to_ep(y1, 1), to_ep(s1, 1)
         y2, y3 = to_ep(y2, 2), to_ep(y3, 3)
@@ -479,11 +530,11 @@
         y_all = {(d, k): v for k, side in enumerate((y_mine, y_twin)) for d, v in enumerate(side)}
         s_all = {(d, k): v for k, side in enumerate((s_mine, s_twin)) for d, v in enumerate(side)}
         s_late = {key: s_all.pop(key) for key in ((2, 1), (3, 1))}
-        moe_out, dlog, dwg = combine_y(meta, y_all, info, tokens, grad_out, n_tok // 8)
+        moe_out, dlog, dwg = combine_y(meta, y_all, info, tokens, grad_out, n_tok // 4)
         dwg = dwg + to_ep(dwg, 1)
         dwg = dwg + to_ep(dwg, 2)
-        so_far = combine_s(meta, s_all, info, (), n_tok // 8)
-        grad_tokens = combine_s(meta, s_late, info, (so_far, dlog, w_router.T), n_tok // 8)
+        so_far = combine_s(meta, s_all, info, (), n_tok // 4)
+        grad_tokens = combine_s(meta, s_late, info, (so_far, dlog, w_router.T), n_tok // 4)
         return moe_out, grad_tokens, grad_w_in, grad_w_out, dwg.T
 
     in_specs = (row_spec, row_spec, P(None, None), P("ep", None, "tp"), P("ep", "tp", None), P(("dp", "ep")))

time: 271 us -> 255 us (0.941)
  Pallas kernels: 174 us -> 165 us
  waiting for transfers between devices: 56.1 us -> 50.8 us
  starting transfers between devices: 29.9 us -> 26.9 us
    pallas_call x4 -> x3, Pallas kernels: 39.9 us -> 31.7 us  [far_half(): pl.pallas_call(body, grid=(steps,), in_specs=[full, full, pl.BlockSpec((d...]
    ppermute x14 -> x12, starting transfers between devices: 19.6 us -> 15.6 us  [to_twin(): return lax.ppermute(v, 'tp', [(0, 1), (1, 0)])]
    ppermute x14, waiting for transfers between devices: 37.6 us -> 34.7 us  [to_ep(): return lax.ppermute(v, 'ep', [(i, i ^ d) for i in range(ep_size)])]
    ppermute x14 -> x12, waiting for transfers between devices: 18.5 us -> 16.1 us  [to_twin(): return lax.ppermute(v, 'tp', [(0, 1), (1, 0)])]
  transfers between devices with their start and end apart: 28 -> 26, of which waited for: 8 -> 6; matrix products, arithmetic and copies ran while one was open for 2% -> 2% of each run, Pallas kernels for 56% -> 56%
where the time goes in v1:
time: 255 us
  Pallas kernels  165 us (65%)
  waiting for transfers between devices  50.8 us (20%)
  starting transfers between devices  26.9 us (11%)
  local copies, waits for them, and re-layouts  9.51 us (4%)
    ppermute x14, waiting for transfers between devices, to_ep(): return lax.ppermute(v, 'ep', [(i, i ^ d) for i in range(ep_size)])  34.7 us
    pallas_call x3, Pallas kernels, far_half(): pl.pallas_call(body, grid=(steps,), in_specs=[full, full, pl.BlockSpec((d...  31.7 us
    pallas_call x2, Pallas kernels, dispatch(): pl.pallas_call(body, grid_spec=pltpu.PrefetchScalarGridSpec(num_scalar_pr...  28.7 us
    pallas_call x2, Pallas kernels, own_half(): pl.pallas_call(body, grid_spec=pltpu.PrefetchScalarGridSpec(num_scalar_pr...  28.2 us
    pallas_call x2, Pallas kernels, combine_s(): pl.pallas_call(body, grid_spec=pltpu.PrefetchScalarGridSpec(num_scalar_pr...  22 us
    pallas_call x1, Pallas kernels, combine_y(): pl.pallas_call(body, grid_spec=pltpu.PrefetchScalarGridSpec(num_scalar_pr...  19.7 us
    pallas_call x1, Pallas kernels, other_grads(): pl.pallas_call(body, grid_spec=pltpu.PrefetchScalarGridSpec(num_scalar_pr...  19.2 us
    ppermute x12, waiting for transfers between devices, to_twin(): return lax.ppermute(v, 'tp', [(0, 1), (1, 0)])  16.1 us
  transfers between devices with their start and end apart: 26, of which 6 were waited for; matrix products, arithmetic and copies ran while one was open for 2% of the time, Pallas kernels for 56%

profile of v1, /device:TPU:0, one launch (start us, length us, event | category | flops | bytes accessed | tf_op | source)
XLA Modules:
  0.0 254.6 jit_solution(7671934970279520085)
XLA Ops:
  0.6 0.6 compare_select_fusion.meta_ref
  1.2 4.0 %route.1.info_ref.refs_8_.refs_6_.refs_2_ = f32[16,2048]{1,0:T(8,128)} custom-call(s32[1,2048]{1,0:T(1,128)} %bitcast.14, bf16[2048,768]{1,0:T(8,128)(2,1)} %refs_9_.1, bf16[8,768]{1,0:T(8,128)(2,1)} %bitcast.12), custom_call_target="tpu_custom_call" | custom-call | flops 2000000000 | bytes 3145728 | tf_op jit(solution)/shard_map/route/pallas_call | solution.py:87
  5.2 19.6 %dispatch.3 = (bf16[2,320,768]{2,1,0:T(8,128)(2,1)}, bf16[2,320,768]{2,1,0:T(8,128)(2,1)}, bf16[2,320,768]{2,1,0:T(8,128)(2,1)}, bf16[2,320,768]{2,1,0:T(8,128)(...) custom-call(s32[2]{0:T(128)} %compare_select_fusion.meta_ref, ...), custom_call_target="tpu_custom_call" | custom-call | flops 12079595520 | bytes 20971520 | tf_op jit(solution)/shard_map/dispatch/pallas_call | solution.py:129
  24.9 0.8 collective-permute-start.2
  25.7 1.5 dynamic-slice_bitcast_fusion.1
  27.2 2.5 collective-permute-start.5
  29.8 1.5 dynamic-slice_bitcast_fusion
  31.3 0.0 collective-permute-start.6
  31.3 9.0 %dispatch.2 = (bf16[2,320,768]{2,1,0:T(8,128)(2,1)}, bf16[2,320,768]{2,1,0:T(8,128)(2,1)}) custom-call(s32[2]{0:T(128)} %compare_select_fusion.meta_ref, f32[16,2048]{1,0:T(8,128)} %route.1.info_ref.refs_8_.refs_6_.refs_2_, bf16[2048,768]{1,0:T(8,128)(2,1)} %refs_9_.1, bf16[2048,768]{1,0:T(8,128)(2,1)} %refs_10_.1), custom_call_target="tpu_custom_call" | custom-call | flops 4026531840 | bytes 12582912 | tf_op jit(solution)/shard_map/dispatch/pallas_call | solution.py:129
  40.3 2.0 collective-permute-start
  42.3 1.2 dynamic-slice_bitcast_fusion.3
  43.5 1.2 dynamic-slice_bitcast_fusion.2
  44.7 1.5 collective-permute-start.3
  46.2 14.0 %own_half.2 = (bf16[1280,1536]{1,0:T(8,128)(2,1)}, bf16[1280,1536]{1,0:T(8,128)(2,1)}, f32[1280,768]{1,0:T(8,128)}, f32[1280,768]{1,0:T(8,128)}, bf16[1280,768]{1,0:T(8,128)(2,1)}, /*index=5*/bf16[1280,768]{1,0:T(8,128)(2,1)}) custom-call(s32[2]{0:T(128)} %compare_select_fusion.meta_ref, bf16[2,320,768]{2,1,0:T(8,128)(2,1)} %get-tuple-element.44.pa, ...), custom_call_target="tpu_custom_call" | custom-call | flops 6039797760 | bytes 20971520 | tf_op jit(solution)/shard_map/own_half/pallas_call | solution.py:178
  60.2 4.9 %collective-permute-done.pa = bf16[2,320,768]{2,1,0:T(8,128)(2,1)S(1)} collective-permute-done((bf16[2,320,768]{2,1,0:T(8,128)(2,1)}, bf16[2,320,768]{2,1,0:T(8,128)(2,1)S(1)}, u32[]{:S(2)}, u32[]{:S(2)}) %collective-permute-start) | collective-permute-done | bytes 983072 | tf_op jit(solution)/shard_map/ppermute | solution.py:483
  65.2 2.0 collective-permute-start.4
  67.2 17.6 %collective-permute-done.1.pb = bf16[2,320,768]{2,1,0:T(8,128)(2,1)S(1)} collective-permute-done((bf16[2,320,768]{2,1,0:T(8,128)(2,1)}, bf16[2,320,768]{2,1,0:T(8,128)(2,1)S(1)}, u32[]{:S(2)}, u32[]{:S(2)}) %collective-permute-start.1) | collective-permute-done | bytes 983072 | tf_op jit(solution)/shard_map/ppermute | solution.py:483
  84.8 0.9 collective-permute-start.21
  85.7 0.1 copy-done.3
  85.8 14.2 %own_half.3 = (bf16[1280,1536]{1,0:T(8,128)(2,1)}, bf16[1280,1536]{1,0:T(8,128)(2,1)}, f32[1280,768]{1,0:T(8,128)}, f32[1280,768]{1,0:T(8,128)}, bf16[1280,768]{1,0:T(8,128)(2,1)}, /*index=5*/bf16[1280,768]{1,0:T(8,128)(2,1)}) custom-call(s32[2]{0:T(128)} %compare_select_fusion.meta_ref, ...), custom_call_target="tpu_custom_call", output_to_operand_aliasing={{0}: (5, {}), {1}: (6, {}), {2}: (7, {}), {3}: (8, {}), {4}... | custom-call | flops 6039797760 | bytes 20971520 | tf_op jit(solution)/shard_map/own_half/pallas_call | solution.py:178
  100.0 1.7 collective-permute-start.22
  101.6 0.0 collective-permute-done.6.wo_ref
  101.7 0.6 collective-permute-start.23
  102.3 18.8 %far_half.3 = (f32[1280,768]{1,0:T(8,128)}, f32[1280,768]{1,0:T(8,128)}) custom-call(bf16[1280,768]{1,0:T(8,128)(2,1)} %get-tuple-element.52.x_ref, bf16[1280,768]{1,0:T(8,128)(2,1)} %get-tuple-element.53.dy_ref, bf16[768,1024]{1,0:T(8,128)(2,1)} %collective-permute-done.5.wi_ref, bf16[1024,768]{1,0:T(8,128)(2,1)} %collective-permute-done.6.wo_ref, ...), custom_call_target="tpu_custom_call" | custom-call | flops 8053063680 | bytes 10485760 | tf_op jit(solution)/shard_map/far_half/pallas_call | solution.py:237
  121.1 0.0 collective-permute-done.3.wi_ref
  121.1 11.2 %collective-permute-done.4.wo_ref = bf16[512,768]{1,0:T(8,128)(2,1)S(1)} collective-permute-done((bf16[512,768]{1,0:T(8,128)(2,1)S(1)}, bf16[512,768]{1,0:T(8,128)(2,1)S(1)}, u32[]{:S(2)}, u32[]{:S(2)}) %collective-permute-start.4) | collective-permute-done | bytes 786464 | tf_op jit(solution)/shard_map/ppermute | solution.py:486
  132.3 0.9 copy-done.1
  133.1 6.4 %far_half.5 = (bf16[320,768]{1,0:T(8,128)(2,1)}, bf16[320,768]{1,0:T(8,128)(2,1)}, bf16[320,768]{1,0:T(8,128)(2,1)}, bf16[320,768]{1,0:T(8,128)(2,1)}) custom-call(bf16[1280,768]{1,0:T(8,128)(2,1)} %get-tuple-element.52.x_ref, bf16[1280,768]{1,0:T(8,128)(2,1)} %get-tuple-element.53.dy_ref, bf16[768,512]{1,0:T(8,128)(2,1)} %copy-done, ...), custom_call_target="tpu_custom_call" | custom-call | flops 2013265920 | bytes 10485760 | tf_op jit(solution)/shard_map/far_half/pallas_call | solution.py:237
  139.6 1.7 collective-permute-start.8
  141.3 0.0 collective-permute-start.9
  141.3 6.4 %far_half.4 = (bf16[320,768]{1,0:T(8,128)(2,1)}, bf16[320,768]{1,0:T(8,128)(2,1)}, bf16[320,768]{1,0:T(8,128)(2,1)}, bf16[320,768]{1,0:T(8,128)(2,1)}) custom-call(bf16[1280,768]{1,0:T(8,128)(2,1)} %get-tuple-element.52.x_ref, bf16[1280,768]{1,0:T(8,128)(2,1)} %get-tuple-element.53.dy_ref, bf16[768,512]{1,0:T(8,128)(2,1)} %copy-done, ...), custom_call_target="tpu_custom_call" | custom-call | flops 2013265920 | bytes 10485760 | tf_op jit(solution)/shard_map/far_half/pallas_call | solution.py:237
  147.7 0.0 collective-permute-done.21.refs_1_
  147.7 0.4 collective-permute-start.7
  148.1 1.7 collective-permute-start.10
  149.8 0.0 collective-permute-done.23.refs_3_
  149.9 1.5 collective-permute-start.14
  151.4 11.8 %finished_grads.1 = (f32[2,768,1536]{2,1,0:T(8,128)}, f32[2,1536,768]{2,1,0:T(8,128)}) custom-call(s32[2]{0:T(128)} %compare_select_fusion.meta_ref, bf16[1280,768]{1,0:T(8,128)(2,1)} %get-tuple-element.52.x_ref, bf16[1280,768]{1,0:T(8,128)(2,1)} %get-tuple-element.53.dy_ref, bf16[1280,1536]{1,0:T(8,128)(2,1)} %get-tuple-element.72.h_ref, ...), custom_call_target="tpu_custom_call" | custom-call | flops 6039797760 | bytes 26214400 | tf_op jit(solution)/shard_map/finished_grads/pallas_call | solution.py:265
  163.1 0.0 collective-permute-done.8.refs_2_
  163.2 0.0 collective-permute-start.16
  163.2 3.6 %collective-permute-done.9.refs_3_ = bf16[320,768]{1,0:T(8,128)(2,1)S(1)} collective-permute-done((bf16[320,768]{1,0:T(8,128)(2,1)}, bf16[320,768]{1,0:T(8,128)(2,1)S(1)}, u32[]{:S(2)}, u32[]{:S(2)}) %collective-permute-start.9) | collective-permute-done | bytes 491552 | tf_op jit(solution)/shard_map/ppermute | solution.py:483
  166.8 0.1 collective-permute-start.18
  167.0 1.8 collective-permute-start.12
  168.7 0.2 collective-permute-start.13
  169.0 8.5 %collective-permute-done.14.refs_2_ = bf16[320,768]{1,0:T(8,128)(2,1)S(1)} collective-permute-done((bf16[320,768]{1,0:T(8,128)(2,1)S(1)}, bf16[320,768]{1,0:T(8,128)(2,1)S(1)}, u32[]{:S(2)}, u32[]{:S(2)}) %collective-permute-start.14) | collective-permute-done | bytes 491552 | tf_op jit(solution)/shard_map/ppermute | solution.py:483
  177.5 1.7 collective-permute-start.11
  179.2 19.2 %other_grads.1 = (f32[2,768,1536]{2,1,0:T(8,128)}, f32[2,1536,768]{2,1,0:T(8,128)}) custom-call(s32[2]{0:T(128)} %compare_select_fusion.meta_ref, bf16[2,320,768]{2,1,0:T(8,128)(2,1)} %get-tuple-element.68.refs_0_, bf16[2,320,768]{2,1,0:T(8,128)(2,1)} %collective-permute-done.21.refs_1_, ...), custom_call_target="tpu_custom_call", output_to_operand_aliasing={{0}: (7, {}), {1}: (8, {})} | custom-call | flops 12079595520 | bytes 26214400 | tf_op jit(solution)/shard_map/other_grads/pallas_call | solution.py:308
  198.4 0.0 collective-permute-done.16.refs_3_
  198.5 0.4 collective-permute-start.19
  198.9 1.7 collective-permute-start.20
  200.5 0.4 collective-permute-start.15
  200.9 1.7 collective-permute-start.17
  202.6 0.8 copy-done.22
  203.4 19.7 %combine_y.1 = (bf16[2048,768]{1,0:T(8,128)(2,1)}, f32[8,2048]{1,0:T(8,128)}, f32[8,768]{1,0:T(8,128)}) custom-call(s32[2]{0:T(128)} %compare_select_fusion.meta_ref, bf16[320,768]{1,0:T(8,128)(2,1)} %get-tuple-element.58.refs_0_, bf16[320,768]{1,0:T(8,128)(2,1)} %copy-done.14, bf16[320,768]{1,0:T(8,128)(2,1)} %copy-done.10, bf16[320,768]{1,0:T(8,128)(2,1)} %copy-done.11, ...), custom_call_target="tpu_custom_call" | custom-call | flops 8053063680 | bytes 16777216 | tf_op jit(solution)/shard_map/combine_y/pallas_call | solution.py:394
  223.1 0.0 copy-start.6
  223.1 0.0 collective-permute-start.24
  223.2 0.0 copy-start.23
  223.2 0.8 copy-done.23
  224.0 0.8 copy-done.24
  224.8 12.5 %combine_s.2.refs_5_ = bf16[2048,768]{1,0:T(8,128)(2,1)} custom-call(s32[2]{0:T(128)} %compare_select_fusion.meta_ref, bf16[320,768]{1,0:T(8,128)(2,1)} %get-tuple-element.66.refs_0_, bf16[320,768]{1,0:T(8,128)(2,1)} %copy-done.18, bf16[320,768]{1,0:T(8,128)(2,1)} %copy-done.12, bf16[320,768]{1,0:T(8,128)(2,1)} %copy-done.13, bf16[320,768]{1,0:T(8,128)(2,1)} %copy-done.23, ...), custom_call_target="tpu_custom_call" | custom-call | flops 6039797760 | bytes 10485760 | tf_op jit(solution)/shard_map/combine_s/pallas_call | solution.py:466
  237.3 1.5 collective-permute-start.25
  238.8 4.9 %collective-permute-done.17.refs_1_ = bf16[320,768]{1,0:T(8,128)(2,1)S(1)} collective-permute-done((bf16[320,768]{1,0:T(8,128)(2,1)S(1)}, bf16[320,768]{1,0:T(8,128)(2,1)S(1)}, u32[]{:S(2)}, u32[]{:S(2)}) %collective-permute-start.17) | collective-permute-done | bytes 491552 | tf_op jit(solution)/shard_map/ppermute | solution.py:486
  243.7 0.8 copy-done.5
  244.5 9.5 %combine_s.3 = bf16[2048,768]{1,0:T(8,128)(2,1)} custom-call(s32[2]{0:T(128)} %compare_select_fusion.meta_ref, bf16[320,768]{1,0:T(8,128)(2,1)} %copy-done.4, bf16[320,768]{1,0:T(8,128)(2,1)} %copy-done.5, f32[16,2048]{1,0:T(8,128)} %route.1.info_ref.refs_8_.refs_6_.refs_2_, f32[8,2048]{1,0:T(8,128)} %get-tuple-element.65.refs_3_, bf16[8,768]{1,0:T(8,128)(2,1)} %bitcast.13, ...), custom_call_target="tpu_custom_call" | custom-call | flops 2013265920 | bytes 10485760 | tf_op jit(solution)/shard_map/combine_s/pallas_call | solution.py:466
  254.0 0.6 add_bitcast_fusion
  (58 shorter events, 0.1 us)
Async XLA Ops:
  24.9 19.8 %collective-permute-start.2 = (bf16[2,320,768]{2,1,0:T(8,128)(2,1)}, bf16[2,320,768]{2,1,0:T(8,128)(2,1)}, u32[]{:S(2)}, u32[]{:S(2)}) collective-permute-start(bf16[2,320,768]{2,1,0:T(8,128)(2,1)} %get-tuple-element.45), channel_id=1, source_target_pairs={{0,1},{1,0},{2,3},{3,2},{4,5},{5,4},{6,7},{7,6}} | collective-permute-start | bytes 2949128 | tf_op jit(solution)/shard_map/ppermute | solution.py:483
  27.2 72.7 %collective-permute-start.5 = (bf16[768,1024]{1,0:T(8,128)(2,1)S(1)}, bf16[768,1024]{1,0:T(8,128)(2,1)}, u32[]{:S(2)}, u32[]{:S(2)}) collective-permute-start(bf16[768,1024]{1,0:T(8,128)(2,1)S(1)} %dynamic-slice_bitcast_fusion.1), channel_id=1, source_target_pairs={{0,4},{4,0},{1,5},{5,1},{2,6},{6,2},{3,7},{7,3}} | collective-permute-start | bytes 4718600 | tf_op jit(solution)/shard_map/ppermute | solution.py:486
  31.3 70.4 %collective-permute-start.6 = (bf16[1024,768]{1,0:T(8,128)(2,1)S(1)}, bf16[1024,768]{1,0:T(8,128)(2,1)}, u32[]{:S(2)}, u32[]{:S(2)}) collective-permute-start(bf16[1024,768]{1,0:T(8,128)(2,1)S(1)} %dynamic-slice_bitcast_fusion), channel_id=1, source_target_pairs={{0,4},{4,0},{1,5},{5,1},{2,6},{6,2},{3,7},{7,3}} | collective-permute-start | bytes 4718600 | tf_op jit(solution)/shard_map/ppermute | solution.py:486
  40.3 24.8 %collective-permute-start = (bf16[2,320,768]{2,1,0:T(8,128)(2,1)}, bf16[2,320,768]{2,1,0:T(8,128)(2,1)S(1)}, u32[]{:S(2)}, u32[]{:S(2)}) collective-permute-start(bf16[2,320,768]{2,1,0:T(8,128)(2,1)} %get-tuple-element.42), channel_id=1, source_target_pairs={{0,2},{1,3},{2,0},{3,1},{4,6},{5,7},{6,4},{7,5}} | collective-permute-start | bytes 2949128 | tf_op jit(solution)/shard_map/ppermute | solution.py:483
  42.3 42.5 %collective-permute-start.1 = (bf16[2,320,768]{2,1,0:T(8,128)(2,1)}, bf16[2,320,768]{2,1,0:T(8,128)(2,1)S(1)}, u32[]{:S(2)}, u32[]{:S(2)}) collective-permute-start(bf16[2,320,768]{2,1,0:T(8,128)(2,1)} %get-tuple-element.43), channel_id=1, source_target_pairs={{0,3},{1,2},{2,1},{3,0},{4,7},{5,6},{6,5},{7,4}} | collective-permute-start | bytes 2949128 | tf_op jit(solution)/shard_map/ppermute | solution.py:483
  44.7 76.4 %collective-permute-start.3 = (bf16[768,512]{1,0:T(8,128)(2,1)S(1)}, bf16[768,512]{1,0:T(8,128)(2,1)S(1)}, u32[]{:S(2)}, u32[]{:S(2)}) collective-permute-start(bf16[768,512]{1,0:T(8,128)(2,1)S(1)} %dynamic-slice_bitcast_fusion.3), channel_id=1, source_target_pairs={{0,4},{4,0},{1,5},{5,1},{2,6},{6,2},{3,7},{7,3}} | collective-permute-start | bytes 2359304 | tf_op jit(solution)/shard_map/ppermute | solution.py:486
  65.2 20.6 %copy-start.2 = (bf16[2,320,768]{2,1,0:T(8,128)(2,1)}, bf16[2,320,768]{2,1,0:T(8,128)(2,1)S(1)}, u32[]{:S(2)}) copy-start(bf16[2,320,768]{2,1,0:T(8,128)(2,1)S(1)} %collective-permute-done.pa) | copy-start | bytes 2949124
  65.2 67.1 %collective-permute-start.4 = (bf16[512,768]{1,0:T(8,128)(2,1)S(1)}, bf16[512,768]{1,0:T(8,128)(2,1)S(1)}, u32[]{:S(2)}, u32[]{:S(2)}) collective-permute-start(bf16[512,768]{1,0:T(8,128)(2,1)S(1)} %dynamic-slice_bitcast_fusion.2), channel_id=1, source_target_pairs={{0,4},{4,0},{1,5},{5,1},{2,6},{6,2},{3,7},{7,3}} | collective-permute-start | bytes 2359304 | tf_op jit(solution)/shard_map/ppermute | solution.py:486
  84.8 1.0 copy-start.3
  84.8 62.9 %collective-permute-start.21 = (bf16[2,320,768]{2,1,0:T(8,128)(2,1)}, bf16[2,320,768]{2,1,0:T(8,128)(2,1)}, u32[]{:S(2)}, u32[]{:S(2)}) collective-permute-start(bf16[2,320,768]{2,1,0:T(8,128)(2,1)} %get-tuple-element.69), channel_id=1, source_target_pairs={{0,1},{1,0},{2,3},{3,2},{4,5},{5,4},{6,7},{7,6}} | collective-permute-start | bytes 2949128 | tf_op jit(solution)/shard_map/ppermute | solution.py:483
  100.0 48.1 %collective-permute-start.22 = (bf16[2,320,768]{2,1,0:T(8,128)(2,1)}, bf16[2,320,768]{2,1,0:T(8,128)(2,1)S(1)}, u32[]{:S(2)}, u32[]{:S(2)}) collective-permute-start(bf16[2,320,768]{2,1,0:T(8,128)(2,1)} %get-tuple-element.70), channel_id=1, source_target_pairs={{0,2},{1,3},{2,0},{3,1},{4,6},{5,7},{6,4},{7,5}} | collective-permute-start | bytes 2949128 | tf_op jit(solution)/shard_map/ppermute | solution.py:483
  101.7 48.2 %collective-permute-start.23 = (bf16[2,320,768]{2,1,0:T(8,128)(2,1)}, bf16[2,320,768]{2,1,0:T(8,128)(2,1)S(1)}, u32[]{:S(2)}, u32[]{:S(2)}) collective-permute-start(bf16[2,320,768]{2,1,0:T(8,128)(2,1)} %get-tuple-element.71), channel_id=1, source_target_pairs={{0,3},{1,2},{2,1},{3,0},{4,7},{5,6},{6,5},{7,4}} | collective-permute-start | bytes 2949128 | tf_op jit(solution)/shard_map/ppermute | solution.py:483
  121.1 11.2 %copy-start = (bf16[768,512]{1,0:T(8,128)(2,1)}, bf16[768,512]{1,0:T(8,128)(2,1)S(1)}, u32[]{:S(2)}) copy-start(bf16[768,512]{1,0:T(8,128)(2,1)S(1)} %collective-permute-done.3.wi_ref) | copy-start | bytes 2359300
  132.2 0.9 copy-start.1
  139.6 23.6 %collective-permute-start.8 = (bf16[320,768]{1,0:T(8,128)(2,1)}, bf16[320,768]{1,0:T(8,128)(2,1)S(1)}, u32[]{:S(2)}, u32[]{:S(2)}) collective-permute-start(bf16[320,768]{1,0:T(8,128)(2,1)} %get-tuple-element.60), channel_id=1, source_target_pairs={{0,2},{1,3},{2,0},{3,1},{4,6},{5,7},{6,4},{7,5}} | collective-permute-start | bytes 1474568 | tf_op jit(solution)/shard_map/ppermute | solution.py:483
  141.3 8.6 %copy-start.19 = (bf16[320,768]{1,0:T(8,128)(2,1)S(1)}, bf16[320,768]{1,0:T(8,128)(2,1)}, u32[]{:S(2)}) copy-start(bf16[320,768]{1,0:T(8,128)(2,1)} %get-tuple-element.63) | copy-start | bytes 1474564
  141.3 25.6 %collective-permute-start.9 = (bf16[320,768]{1,0:T(8,128)(2,1)}, bf16[320,768]{1,0:T(8,128)(2,1)S(1)}, u32[]{:S(2)}, u32[]{:S(2)}) collective-permute-start(bf16[320,768]{1,0:T(8,128)(2,1)} %get-tuple-element.61), channel_id=1, source_target_pairs={{0,3},{1,2},{2,1},{3,0},{4,7},{5,6},{6,5},{7,4}} | collective-permute-start | bytes 1474568 | tf_op jit(solution)/shard_map/ppermute | solution.py:483
  147.7 19.2 %collective-permute-start.7 = (bf16[320,768]{1,0:T(8,128)(2,1)}, bf16[320,768]{1,0:T(8,128)(2,1)S(1)}, u32[]{:S(2)}, u32[]{:S(2)}) collective-permute-start(bf16[320,768]{1,0:T(8,128)(2,1)} %get-tuple-element.59), channel_id=1, source_target_pairs={{0,1},{1,0},{2,3},{3,2},{4,5},{5,4},{6,7},{7,6}} | collective-permute-start | bytes 1474568 | tf_op jit(solution)/shard_map/ppermute | solution.py:483
  148.1 15.0 %copy-start.7 = (bf16[2,320,768]{2,1,0:T(8,128)(2,1)}, bf16[2,320,768]{2,1,0:T(8,128)(2,1)S(1)}, u32[]{:S(2)}) copy-start(bf16[2,320,768]{2,1,0:T(8,128)(2,1)S(1)} %collective-permute-done.22.refs_2_) | copy-start | bytes 2949124
  148.1 20.6 %collective-permute-start.10 = (bf16[320,768]{1,0:T(8,128)(2,1)}, bf16[320,768]{1,0:T(8,128)(2,1)S(1)}, u32[]{:S(2)}, u32[]{:S(2)}) collective-permute-start(bf16[320,768]{1,0:T(8,128)(2,1)} %get-tuple-element.58.refs_0_), channel_id=1, source_target_pairs={{0,4},{4,0},{1,5},{5,1},{2,6},{6,2},{3,7},{7,3}} | collective-permute-start | bytes 1474568 | tf_op jit(solution)/shard_map/ppermute | solution.py:486
  149.8 13.3 %copy-start.8 = (bf16[2,320,768]{2,1,0:T(8,128)(2,1)}, bf16[2,320,768]{2,1,0:T(8,128)(2,1)S(1)}, u32[]{:S(2)}) copy-start(bf16[2,320,768]{2,1,0:T(8,128)(2,1)S(1)} %collective-permute-done.23.refs_3_) | copy-start | bytes 2949124
  149.9 27.7 %collective-permute-start.14 = (bf16[320,768]{1,0:T(8,128)(2,1)S(1)}, bf16[320,768]{1,0:T(8,128)(2,1)S(1)}, u32[]{:S(2)}, u32[]{:S(2)}) collective-permute-start(bf16[320,768]{1,0:T(8,128)(2,1)S(1)} %copy-done.19), channel_id=1, source_target_pairs={{0,2},{1,3},{2,0},{3,1},{4,6},{5,7},{6,4},{7,5}} | collective-permute-start | bytes 1474568 | tf_op jit(solution)/shard_map/ppermute | solution.py:483
  151.4 11.8 %copy-start.16 = (bf16[320,768]{1,0:T(8,128)(2,1)S(1)}, bf16[320,768]{1,0:T(8,128)(2,1)}, u32[]{:S(2)}) copy-start(bf16[320,768]{1,0:T(8,128)(2,1)} %get-tuple-element.64) | copy-start | bytes 1474564
  151.4 15.5 %copy-start.17 = (bf16[320,768]{1,0:T(8,128)(2,1)S(1)}, bf16[320,768]{1,0:T(8,128)(2,1)}, u32[]{:S(2)}) copy-start(bf16[320,768]{1,0:T(8,128)(2,1)} %get-tuple-element.67) | copy-start | bytes 1474564
  163.1 35.3 %copy-start.10 = (bf16[320,768]{1,0:T(8,128)(2,1)}, bf16[320,768]{1,0:T(8,128)(2,1)S(1)}, u32[]{:S(2)}) copy-start(bf16[320,768]{1,0:T(8,128)(2,1)S(1)} %collective-permute-done.8.refs_2_) | copy-start | bytes 1474564
  163.2 35.3 %collective-permute-start.16 = (bf16[320,768]{1,0:T(8,128)(2,1)S(1)}, bf16[320,768]{1,0:T(8,128)(2,1)S(1)}, u32[]{:S(2)}, u32[]{:S(2)}) collective-permute-start(bf16[320,768]{1,0:T(8,128)(2,1)S(1)} %copy-done.16), channel_id=1, source_target_pairs={{0,3},{1,2},{2,1},{3,0},{4,7},{5,6},{6,5},{7,4}} | collective-permute-start | bytes 1474568 | tf_op jit(solution)/shard_map/ppermute | solution.py:483
  166.8 31.6 %copy-start.11 = (bf16[320,768]{1,0:T(8,128)(2,1)}, bf16[320,768]{1,0:T(8,128)(2,1)S(1)}, u32[]{:S(2)}) copy-start(bf16[320,768]{1,0:T(8,128)(2,1)S(1)} %collective-permute-done.9.refs_3_) | copy-start | bytes 1474564
  166.8 32.0 %collective-permute-start.18 = (bf16[320,768]{1,0:T(8,128)(2,1)S(1)}, bf16[320,768]{1,0:T(8,128)(2,1)S(1)}, u32[]{:S(2)}, u32[]{:S(2)}) collective-permute-start(bf16[320,768]{1,0:T(8,128)(2,1)S(1)} %copy-done.17), channel_id=1, source_target_pairs={{0,1},{1,0},{2,3},{3,2},{4,5},{5,4},{6,7},{7,6}} | collective-permute-start | bytes 1474568 | tf_op jit(solution)/shard_map/ppermute | solution.py:483
  166.9 31.5 %copy-start.14 = (bf16[320,768]{1,0:T(8,128)(2,1)}, bf16[320,768]{1,0:T(8,128)(2,1)S(1)}, u32[]{:S(2)}) copy-start(bf16[320,768]{1,0:T(8,128)(2,1)S(1)} %collective-permute-done.7.refs_1_) | copy-start | bytes 1474564
  167.0 33.6 %collective-permute-start.12 = (bf16[320,768]{1,0:T(8,128)(2,1)S(1)}, bf16[320,768]{1,0:T(8,128)(2,1)S(1)}, u32[]{:S(2)}, u32[]{:S(2)}) collective-permute-start(bf16[320,768]{1,0:T(8,128)(2,1)S(1)} %collective-permute-done.8.refs_2_), channel_id=1, source_target_pairs={{0,4},{4,0},{1,5},{5,1},{2,6},{6,2},{3,7},{7,3}} | collective-permute-start | bytes 1474568 | tf_op jit(solution)/shard_map/ppermute | solution.py:486
  168.7 29.7 %copy-start.15 = (bf16[320,768]{1,0:T(8,128)(2,1)}, bf16[320,768]{1,0:T(8,128)(2,1)S(1)}, u32[]{:S(2)}) copy-start(bf16[320,768]{1,0:T(8,128)(2,1)S(1)} %collective-permute-done.10.refs_4_) | copy-start | bytes 1474564
  168.7 32.2 %collective-permute-start.13 = (bf16[320,768]{1,0:T(8,128)(2,1)S(1)}, bf16[320,768]{1,0:T(8,128)(2,1)S(1)}, u32[]{:S(2)}, u32[]{:S(2)}) collective-permute-start(bf16[320,768]{1,0:T(8,128)(2,1)S(1)} %collective-permute-done.9.refs_3_), channel_id=1, source_target_pairs={{0,4},{4,0},{1,5},{5,1},{2,6},{6,2},{3,7},{7,3}} | collective-permute-start | bytes 1474568 | tf_op jit(solution)/shard_map/ppermute | solution.py:486
  177.5 23.0 %copy-start.12 = (bf16[320,768]{1,0:T(8,128)(2,1)}, bf16[320,768]{1,0:T(8,128)(2,1)S(1)}, u32[]{:S(2)}) copy-start(bf16[320,768]{1,0:T(8,128)(2,1)S(1)} %collective-permute-done.14.refs_2_) | copy-start | bytes 1474564
  177.5 25.1 %collective-permute-start.11 = (bf16[320,768]{1,0:T(8,128)(2,1)S(1)}, bf16[320,768]{1,0:T(8,128)(2,1)S(1)}, u32[]{:S(2)}, u32[]{:S(2)}) collective-permute-start(bf16[320,768]{1,0:T(8,128)(2,1)S(1)} %collective-permute-done.7.refs_1_), channel_id=1, source_target_pairs={{0,4},{4,0},{1,5},{5,1},{2,6},{6,2},{3,7},{7,3}} | collective-permute-start | bytes 1474568 | tf_op jit(solution)/shard_map/ppermute | solution.py:486
  179.2 19.3 %copy-start.9 = (bf16[320,768]{1,0:T(8,128)(2,1)S(1)}, bf16[320,768]{1,0:T(8,128)(2,1)}, u32[]{:S(2)}) copy-start(bf16[320,768]{1,0:T(8,128)(2,1)} %get-tuple-element.66.refs_0_) | copy-start | bytes 1474564
  198.5 24.6 %copy-start.13 = (bf16[320,768]{1,0:T(8,128)(2,1)}, bf16[320,768]{1,0:T(8,128)(2,1)S(1)}, u32[]{:S(2)}) copy-start(bf16[320,768]{1,0:T(8,128)(2,1)S(1)} %collective-permute-done.16.refs_3_) | copy-start | bytes 1474564
  198.5 24.7 %collective-permute-start.19 = (bf16[320,768]{1,0:T(8,128)(2,1)S(1)}, bf16[320,768]{1,0:T(8,128)(2,1)S(1)}, u32[]{:S(2)}, u32[]{:S(2)}) collective-permute-start(bf16[320,768]{1,0:T(8,128)(2,1)S(1)} %copy-done.9), channel_id=1, source_target_pairs={{0,4},{4,0},{1,5},{5,1},{2,6},{6,2},{3,7},{7,3}} | collective-permute-start | bytes 1474568 | tf_op jit(solution)/shard_map/ppermute | solution.py:486
  198.9 24.3 %copy-start.18 = (bf16[320,768]{1,0:T(8,128)(2,1)}, bf16[320,768]{1,0:T(8,128)(2,1)S(1)}, u32[]{:S(2)}) copy-start(bf16[320,768]{1,0:T(8,128)(2,1)S(1)} %collective-permute-done.18.refs_1_) | copy-start | bytes 1474564
  198.9 24.3 %collective-permute-start.20 = (bf16[320,768]{1,0:T(8,128)(2,1)S(1)}, bf16[320,768]{1,0:T(8,128)(2,1)S(1)}, u32[]{:S(2)}, u32[]{:S(2)}) collective-permute-start(bf16[320,768]{1,0:T(8,128)(2,1)S(1)} %collective-permute-done.18.refs_1_), channel_id=1, source_target_pairs={{0,4},{4,0},{1,5},{5,1},{2,6},{6,2},{3,7},{7,3}} | collective-permute-start | bytes 1474568 | tf_op jit(solution)/shard_map/ppermute | solution.py:486
  200.5 2.1 copy-start.20
  200.5 38.3 %collective-permute-start.15 = (bf16[320,768]{1,0:T(8,128)(2,1)S(1)}, bf16[320,768]{1,0:T(8,128)(2,1)S(1)}, u32[]{:S(2)}, u32[]{:S(2)}) collective-permute-start(bf16[320,768]{1,0:T(8,128)(2,1)S(1)} %collective-permute-done.14.refs_2_), channel_id=1, source_target_pairs={{0,4},{4,0},{1,5},{5,1},{2,6},{6,2},{3,7},{7,3}} | collective-permute-start | bytes 1474568 | tf_op jit(solution)/shard_map/ppermute | solution.py:486
  200.9 1.7 copy-start.21
  200.9 42.8 %collective-permute-start.17 = (bf16[320,768]{1,0:T(8,128)(2,1)S(1)}, bf16[320,768]{1,0:T(8,128)(2,1)S(1)}, u32[]{:S(2)}, u32[]{:S(2)}) collective-permute-start(bf16[320,768]{1,0:T(8,128)(2,1)S(1)} %collective-permute-done.16.refs_3_), channel_id=1, source_target_pairs={{0,4},{4,0},{1,5},{5,1},{2,6},{6,2},{3,7},{7,3}} | collective-permute-start | bytes 1474568 | tf_op jit(solution)/shard_map/ppermute | solution.py:486
  202.6 0.8 copy-start.22
  223.1 14.2 %copy-start.6 = (f32[8,768]{1,0:T(8,128)S(1)}, f32[8,768]{1,0:T(8,128)}, u32[]{:S(2)}) copy-start(f32[8,768]{1,0:T(8,128)} %get-tuple-element.78) | copy-start | bytes 73732
  223.1 14.1 %collective-permute-start.24 = (f32[8,768]{1,0:T(8,128)}, f32[8,768]{1,0:T(8,128)S(1)}, u32[]{:S(2)}, u32[]{:S(2)}) collective-permute-start(f32[8,768]{1,0:T(8,128)} %get-tuple-element.78), channel_id=1, source_target_pairs={{0,1},{1,0},{2,3},{3,2},{4,5},{5,4},{6,7},{7,6}} | collective-permute-start | bytes 73736 | tf_op jit(solution)/shard_map/ppermute | solution.py:483
  223.2 0.8 copy-start.23
  224.0 0.8 copy-start.24
  237.3 16.7 %collective-permute-start.25 = (f32[8,768]{1,0:T(8,128)S(1)}, f32[8,768]{1,0:T(8,128)S(1)}, u32[]{:S(2)}, u32[]{:S(2)}) collective-permute-start(f32[8,768]{1,0:T(8,128)S(1)} %add.14), channel_id=1, source_target_pairs={{0,2},{1,3},{2,0},{3,1},{4,6},{5,7},{6,4},{7,5}} | collective-permute-start | bytes 73736 | tf_op jit(solution)/shard_map/ppermute | solution.py:483
  238.8 4.9 %copy-start.4 = (bf16[320,768]{1,0:T(8,128)(2,1)}, bf16[320,768]{1,0:T(8,128)(2,1)S(1)}, u32[]{:S(2)}) copy-start(bf16[320,768]{1,0:T(8,128)(2,1)S(1)} %collective-permute-done.15.refs_0_) | copy-start | bytes 1474564
  243.7 0.8 copy-start.5

commit v2 on v0

--- a/solution.py
+++ b/solution.py
@@ -444,8 +444,8 @@
         meta = jnp.where(jnp.arange(2) == 0, tp, ep).astype(jnp.int32)
 
         far_w = {}
-        for stage, lo, hi in (("a", 0, 4), ("b", 4, 5), ("c", 5, 6)):
-            lo, size = lo * width // 6, (hi - lo) * width // 6
+        for stage, lo, hi in (("a", 0, 2), ("b", 2, 3)):
+            lo, size = lo * chunk, (hi - lo) * chunk
             part_in = lax.dynamic_slice(w_in, (1 - tp, 0, lo), (1, d_model, size))[0]
             part_out = lax.dynamic_slice(w_out, (1 - tp, lo, 0), (1, size, d_model))[0]
             far_w[stage] = to_twin(part_in), to_twin(part_out)
@@ -462,9 +462,8 @@
         part = own_half(meta, f0, f1, w_in, w_out, chunk, 0, ())
         h, da, y, s, x, dy = own_half(meta, f2, f3, w_in, w_out, chunk, 1, part)
         y, s = far_half(x, dy, *far_w["a"], y, s, chunk, None)
-        y, s = far_half(x, dy, *far_w["b"], y, s, width // 6, None)
-        y0, y1, s0, s1 = far_half(x, dy, *far_w["c"], y, s, width // 6, 0)
-        y2, y3, s2, s3 = far_half(x, dy, *far_w["c"], y, s, width // 6, 1)
+        y0, y1, s0, s1 = far_half(x, dy, *far_w["b"], y, s, chunk, 0)
+        y2, y3, s2, s3 = far_half(x, dy, *far_w["b"], y, s, chunk, 1)
 
         y1, s1 = to_ep(y1, 1), to_ep(s1, 1)
         y2, y3 = to_ep(y2, 2), to_ep(y3, 3)
@@ -479,11 +478,11 @@
         y_all = {(d, k): v for k, side in enumerate((y_mine, y_twin)) for d, v in enumerate(side)}
         s_all = {(d, k): v for k, side in enumerate((s_mine, s_twin)) for d, v in enumerate(side)}
         s_late = {key: s_all.pop(key) for key in ((2, 1), (3, 1))}
-        moe_out, dlog, dwg = combine_y(meta, y_all, info, tokens, grad_out, n_tok // 8)
+        moe_out, dlog, dwg = combine_y(meta, y_all, info, tokens, grad_out, n_tok // 4)
         dwg = dwg + to_ep(dwg, 1)
         dwg = dwg + to_ep(dwg, 2)
-        so_far = combine_s(meta, s_all, info, (), n_tok // 8)
-        grad_tokens = combine_s(meta, s_late, info, (so_far, dlog, w_router.T), n_tok // 8)
+        so_far = combine_s(meta, s_all, info, (), n_tok // 4)
+        grad_tokens = combine_s(meta, s_late, info, (so_far, dlog, w_router.T), n_tok // 4)
         return moe_out, grad_tokens, grad_w_in, grad_w_out, dwg.T
 
     in_specs = (row_spec, row_spec, P(None, None), P("ep", None, "tp"), P("ep", "tp", None), P(("dp", "ep")))

time: 271 us -> 254 us (0.937)
  Pallas kernels: 174 us -> 162 us
    pallas_call x4 -> x3, Pallas kernels: 39.9 us -> 31.7 us  [far_half(): pl.pallas_call(body, grid=(steps,), in_specs=[full, full, pl.BlockSpec((d...]
    ppermute x14 -> x12, starting transfers between devices: 19.6 us -> 15.6 us  [to_twin(): return lax.ppermute(v, 'tp', [(0, 1), (1, 0)])]
    pallas_call x2, Pallas kernels: 23.4 us -> 20.5 us  [combine_s(): pl.pallas_call(body, grid_spec=pltpu.PrefetchScalarGridSpec(num_scalar_pr...]
    ppermute x14, waiting for transfers between devices: 37.6 us -> 34.7 us  [to_ep(): return lax.ppermute(v, 'ep', [(i, i ^ d) for i in range(ep_size)])]
    ppermute x14 -> x12, waiting for transfers between devices: 18.5 us -> 19.3 us  [to_twin(): return lax.ppermute(v, 'tp', [(0, 1), (1, 0)])]
  transfers between devices with their start and end apart: 28 -> 26, of which waited for: 8 -> 7; matrix products, arithmetic and copies ran while one was open for 2% -> 2% of each run, Pallas kernels for 56% -> 54%
where the time goes in v2:
time: 254 us
  Pallas kernels  162 us (64%)
  waiting for transfers between devices  54 us (21%)
  starting transfers between devices  27.2 us (11%)
  local copies, waits for them, and re-layouts  8.77 us (3%)
    ppermute x14, waiting for transfers between devices, to_ep(): return lax.ppermute(v, 'ep', [(i, i ^ d) for i in range(ep_size)])  34.7 us
    pallas_call x3, Pallas kernels, far_half(): pl.pallas_call(body, grid=(steps,), in_specs=[full, full, pl.BlockSpec((d...  31.7 us
    pallas_call x2, Pallas kernels, dispatch(): pl.pallas_call(body, grid_spec=pltpu.PrefetchScalarGridSpec(num_scalar_pr...  28.7 us
    pallas_call x2, Pallas kernels, own_half(): pl.pallas_call(body, grid_spec=pltpu.PrefetchScalarGridSpec(num_scalar_pr...  28.2 us
    pallas_call x2, Pallas kernels, combine_s(): pl.pallas_call(body, grid_spec=pltpu.PrefetchScalarGridSpec(num_scalar_pr...  20.5 us
    ppermute x12, waiting for transfers between devices, to_twin(): return lax.ppermute(v, 'tp', [(0, 1), (1, 0)])  19.3 us
    pallas_call x1, Pallas kernels, other_grads(): pl.pallas_call(body, grid_spec=pltpu.PrefetchScalarGridSpec(num_scalar_pr...  19.2 us
    pallas_call x1, Pallas kernels, combine_y(): pl.pallas_call(body, grid_spec=pltpu.PrefetchScalarGridSpec(num_scalar_pr...  17.7 us
  transfers between devices with their start and end apart: 26, of which 7 were waited for; matrix products, arithmetic and copies ran while one was open for 2% of the time, Pallas kernels for 54%

profile of v2, /device:TPU:0, one launch (start us, length us, event | category | flops | bytes accessed | tf_op | source)
XLA Modules:
  0.0 253.8 jit_solution(13042492471867337101)
XLA Ops:
  0.6 0.6 compare_select_fusion.meta_ref
  1.2 4.0 %route.1.info_ref.refs_8_.refs_6_.refs_2_ = f32[16,2048]{1,0:T(8,128)} custom-call(s32[1,2048]{1,0:T(1,128)} %bitcast.14, bf16[2048,768]{1,0:T(8,128)(2,1)} %refs_9_.1, bf16[8,768]{1,0:T(8,128)(2,1)} %bitcast.12), custom_call_target="tpu_custom_call" | custom-call | flops 2000000000 | bytes 3145728 | tf_op jit(solution)/shard_map/route/pallas_call | solution.py:87
  5.2 19.6 %dispatch.3 = (bf16[2,320,768]{2,1,0:T(8,128)(2,1)}, bf16[2,320,768]{2,1,0:T(8,128)(2,1)}, bf16[2,320,768]{2,1,0:T(8,128)(2,1)}, bf16[2,320,768]{2,1,0:T(8,128)(...) custom-call(s32[2]{0:T(128)} %compare_select_fusion.meta_ref, ...), custom_call_target="tpu_custom_call" | custom-call | flops 12079595520 | bytes 20971520 | tf_op jit(solution)/shard_map/dispatch/pallas_call | solution.py:129
  24.9 0.8 collective-permute-start.2
  25.7 1.5 dynamic-slice_bitcast_fusion.1
  27.2 2.5 collective-permute-start.5
  29.8 1.5 dynamic-slice_bitcast_fusion
  31.3 0.0 collective-permute-start.6
  31.3 9.0 %dispatch.2 = (bf16[2,320,768]{2,1,0:T(8,128)(2,1)}, bf16[2,320,768]{2,1,0:T(8,128)(2,1)}) custom-call(s32[2]{0:T(128)} %compare_select_fusion.meta_ref, f32[16,2048]{1,0:T(8,128)} %route.1.info_ref.refs_8_.refs_6_.refs_2_, bf16[2048,768]{1,0:T(8,128)(2,1)} %refs_9_.1, bf16[2048,768]{1,0:T(8,128)(2,1)} %refs_10_.1), custom_call_target="tpu_custom_call" | custom-call | flops 4026531840 | bytes 12582912 | tf_op jit(solution)/shard_map/dispatch/pallas_call | solution.py:129
  40.3 2.0 collective-permute-start
  42.3 1.2 dynamic-slice_bitcast_fusion.3
  43.5 1.2 dynamic-slice_bitcast_fusion.2
  44.7 1.5 collective-permute-start.3
  46.2 14.0 %own_half.2 = (bf16[1280,1536]{1,0:T(8,128)(2,1)}, bf16[1280,1536]{1,0:T(8,128)(2,1)}, f32[1280,768]{1,0:T(8,128)}, f32[1280,768]{1,0:T(8,128)}, bf16[1280,768]{1,0:T(8,128)(2,1)}, /*index=5*/bf16[1280,768]{1,0:T(8,128)(2,1)}) custom-call(s32[2]{0:T(128)} %compare_select_fusion.meta_ref, bf16[2,320,768]{2,1,0:T(8,128)(2,1)} %get-tuple-element.44.pa, ...), custom_call_target="tpu_custom_call" | custom-call | flops 6039797760 | bytes 20971520 | tf_op jit(solution)/shard_map/own_half/pallas_call | solution.py:178
  60.2 4.9 %collective-permute-done.pa = bf16[2,320,768]{2,1,0:T(8,128)(2,1)S(1)} collective-permute-done((bf16[2,320,768]{2,1,0:T(8,128)(2,1)}, bf16[2,320,768]{2,1,0:T(8,128)(2,1)S(1)}, u32[]{:S(2)}, u32[]{:S(2)}) %collective-permute-start) | collective-permute-done | bytes 983072 | tf_op jit(solution)/shard_map/ppermute | solution.py:431
  65.2 2.0 collective-permute-start.4
  67.2 17.6 %collective-permute-done.1.pb = bf16[2,320,768]{2,1,0:T(8,128)(2,1)S(1)} collective-permute-done((bf16[2,320,768]{2,1,0:T(8,128)(2,1)}, bf16[2,320,768]{2,1,0:T(8,128)(2,1)S(1)}, u32[]{:S(2)}, u32[]{:S(2)}) %collective-permute-start.1) | collective-permute-done | bytes 983072 | tf_op jit(solution)/shard_map/ppermute | solution.py:431
  84.8 0.9 collective-permute-start.21
  85.7 0.1 copy-done.3
  85.8 14.2 %own_half.3 = (bf16[1280,1536]{1,0:T(8,128)(2,1)}, bf16[1280,1536]{1,0:T(8,128)(2,1)}, f32[1280,768]{1,0:T(8,128)}, f32[1280,768]{1,0:T(8,128)}, bf16[1280,768]{1,0:T(8,128)(2,1)}, /*index=5*/bf16[1280,768]{1,0:T(8,128)(2,1)}) custom-call(s32[2]{0:T(128)} %compare_select_fusion.meta_ref, ...), custom_call_target="tpu_custom_call", output_to_operand_aliasing={{0}: (5, {}), {1}: (6, {}), {2}: (7, {}), {3}: (8, {}), {4}... | custom-call | flops 6039797760 | bytes 20971520 | tf_op jit(solution)/shard_map/own_half/pallas_call | solution.py:178
  100.0 1.7 collective-permute-start.22
  101.6 0.0 collective-permute-done.6.wo_ref
  101.7 0.6 collective-permute-start.23
  102.3 18.8 %far_half.3 = (f32[1280,768]{1,0:T(8,128)}, f32[1280,768]{1,0:T(8,128)}) custom-call(bf16[1280,768]{1,0:T(8,128)(2,1)} %get-tuple-element.52.x_ref, bf16[1280,768]{1,0:T(8,128)(2,1)} %get-tuple-element.53.dy_ref, bf16[768,1024]{1,0:T(8,128)(2,1)} %collective-permute-done.5.wi_ref, bf16[1024,768]{1,0:T(8,128)(2,1)} %collective-permute-done.6.wo_ref, ...), custom_call_target="tpu_custom_call" | custom-call | flops 8053063680 | bytes 10485760 | tf_op jit(solution)/shard_map/far_half/pallas_call | solution.py:237
  121.1 0.0 collective-permute-done.3.wi_ref
  121.1 11.2 %collective-permute-done.4.wo_ref = bf16[512,768]{1,0:T(8,128)(2,1)S(1)} collective-permute-done((bf16[512,768]{1,0:T(8,128)(2,1)S(1)}, bf16[512,768]{1,0:T(8,128)(2,1)S(1)}, u32[]{:S(2)}, u32[]{:S(2)}) %collective-permute-start.4) | collective-permute-done | bytes 786464 | tf_op jit(solution)/shard_map/ppermute | solution.py:434
  132.3 0.9 copy-done.1
  133.1 6.4 %far_half.5 = (bf16[320,768]{1,0:T(8,128)(2,1)}, bf16[320,768]{1,0:T(8,128)(2,1)}, bf16[320,768]{1,0:T(8,128)(2,1)}, bf16[320,768]{1,0:T(8,128)(2,1)}) custom-call(bf16[1280,768]{1,0:T(8,128)(2,1)} %get-tuple-element.52.x_ref, bf16[1280,768]{1,0:T(8,128)(2,1)} %get-tuple-element.53.dy_ref, bf16[768,512]{1,0:T(8,128)(2,1)} %copy-done, ...), custom_call_target="tpu_custom_call" | custom-call | flops 2013265920 | bytes 10485760 | tf_op jit(solution)/shard_map/far_half/pallas_call | solution.py:237
  139.6 1.7 collective-permute-start.8
  141.3 0.0 collective-permute-start.9
  141.3 6.4 %far_half.4 = (bf16[320,768]{1,0:T(8,128)(2,1)}, bf16[320,768]{1,0:T(8,128)(2,1)}, bf16[320,768]{1,0:T(8,128)(2,1)}, bf16[320,768]{1,0:T(8,128)(2,1)}) custom-call(bf16[1280,768]{1,0:T(8,128)(2,1)} %get-tuple-element.52.x_ref, bf16[1280,768]{1,0:T(8,128)(2,1)} %get-tuple-element.53.dy_ref, bf16[768,512]{1,0:T(8,128)(2,1)} %copy-done, ...), custom_call_target="tpu_custom_call" | custom-call | flops 2013265920 | bytes 10485760 | tf_op jit(solution)/shard_map/far_half/pallas_call | solution.py:237
  147.7 0.0 collective-permute-done.21.refs_1_
  147.7 0.4 collective-permute-start.7
  148.1 1.7 collective-permute-start.10
  149.8 0.0 collective-permute-done.23.refs_3_
  149.9 1.5 collective-permute-start.14
  151.4 11.8 %finished_grads.1 = (f32[2,768,1536]{2,1,0:T(8,128)}, f32[2,1536,768]{2,1,0:T(8,128)}) custom-call(s32[2]{0:T(128)} %compare_select_fusion.meta_ref, bf16[1280,768]{1,0:T(8,128)(2,1)} %get-tuple-element.52.x_ref, bf16[1280,768]{1,0:T(8,128)(2,1)} %get-tuple-element.53.dy_ref, bf16[1280,1536]{1,0:T(8,128)(2,1)} %get-tuple-element.72.h_ref, ...), custom_call_target="tpu_custom_call" | custom-call | flops 6039797760 | bytes 26214400 | tf_op jit(solution)/shard_map/finished_grads/pallas_call | solution.py:265
  163.1 0.0 collective-permute-done.8.refs_2_
  163.2 0.0 collective-permute-start.16
  163.2 3.6 %collective-permute-done.9.refs_3_ = bf16[320,768]{1,0:T(8,128)(2,1)S(1)} collective-permute-done((bf16[320,768]{1,0:T(8,128)(2,1)}, bf16[320,768]{1,0:T(8,128)(2,1)S(1)}, u32[]{:S(2)}, u32[]{:S(2)}) %collective-permute-start.9) | collective-permute-done | bytes 491552 | tf_op jit(solution)/shard_map/ppermute | solution.py:431
  166.8 0.1 collective-permute-start.18
  167.0 1.8 collective-permute-start.12
  168.7 0.2 collective-permute-start.13
  169.0 8.5 %collective-permute-done.14.refs_2_ = bf16[320,768]{1,0:T(8,128)(2,1)S(1)} collective-permute-done((bf16[320,768]{1,0:T(8,128)(2,1)S(1)}, bf16[320,768]{1,0:T(8,128)(2,1)S(1)}, u32[]{:S(2)}, u32[]{:S(2)}) %collective-permute-start.14) | collective-permute-done | bytes 491552 | tf_op jit(solution)/shard_map/ppermute | solution.py:431
  177.5 1.7 collective-permute-start.11
  179.2 19.2 %other_grads.1 = (f32[2,768,1536]{2,1,0:T(8,128)}, f32[2,1536,768]{2,1,0:T(8,128)}) custom-call(s32[2]{0:T(128)} %compare_select_fusion.meta_ref, bf16[2,320,768]{2,1,0:T(8,128)(2,1)} %get-tuple-element.68.refs_0_, bf16[2,320,768]{2,1,0:T(8,128)(2,1)} %collective-permute-done.21.refs_1_, ...), custom_call_target="tpu_custom_call", output_to_operand_aliasing={{0}: (7, {}), {1}: (8, {})} | custom-call | flops 12079595520 | bytes 26214400 | tf_op jit(solution)/shard_map/other_grads/pallas_call | solution.py:308
  198.4 0.0 collective-permute-done.16.refs_3_
  198.5 0.4 collective-permute-start.19
  198.9 1.7 collective-permute-start.20
  200.5 0.4 collective-permute-start.15
  200.9 1.7 collective-permute-start.17
  202.6 0.8 copy-done.22
  203.4 17.7 %combine_y.1 = (bf16[2048,768]{1,0:T(8,128)(2,1)}, bf16[2048,8]{1,0:T(8,128)(2,1)}, f32[8,768]{1,0:T(8,128)}) custom-call(s32[2]{0:T(128)} %compare_select_fusion.meta_ref, bf16[320,768]{1,0:T(8,128)(2,1)} %get-tuple-element.58.refs_0_, bf16[320,768]{1,0:T(8,128)(2,1)} %copy-done.14, bf16[320,768]{1,0:T(8,128)(2,1)} %copy-done.10, ...), custom_call_target="tpu_custom_call" | custom-call | flops 8053063680 | bytes 16777216 | tf_op jit(solution)/shard_map/combine_y/pallas_call | solution.py:372
  221.1 0.0 copy-start.6
  221.1 0.0 collective-permute-start.24
  221.1 0.0 copy-start.23
  221.1 2.0 collective-permute-done.20.refs_5_
  223.2 0.8 copy-done.24
  224.0 11.9 %combine_s.2.refs_3_ = bf16[2048,768]{1,0:T(8,128)(2,1)} custom-call(s32[2]{0:T(128)} %compare_select_fusion.meta_ref, bf16[320,768]{1,0:T(8,128)(2,1)} %get-tuple-element.65.refs_0_, bf16[320,768]{1,0:T(8,128)(2,1)} %copy-done.18, bf16[320,768]{1,0:T(8,128)(2,1)} %copy-done.12, bf16[320,768]{1,0:T(8,128)(2,1)} %copy-done.13, bf16[320,768]{1,0:T(8,128)(2,1)} %copy-done.23, ...), custom_call_target="tpu_custom_call" | custom-call | flops 6039797760 | bytes 10485760 | tf_op jit(solution)/shard_map/combine_s/pallas_call | solution.py:408
  235.9 1.8 collective-permute-start.25
  237.7 6.1 %collective-permute-done.17.refs_1_ = bf16[320,768]{1,0:T(8,128)(2,1)S(1)} collective-permute-done((bf16[320,768]{1,0:T(8,128)(2,1)S(1)}, bf16[320,768]{1,0:T(8,128)(2,1)S(1)}, u32[]{:S(2)}, u32[]{:S(2)}) %collective-permute-start.17) | collective-permute-done | bytes 491552 | tf_op jit(solution)/shard_map/ppermute | solution.py:434
  243.7 0.8 copy-done.5
  244.5 8.7 %combine_s.3 = bf16[2048,768]{1,0:T(8,128)(2,1)} custom-call(s32[2]{0:T(128)} %compare_select_fusion.meta_ref, bf16[320,768]{1,0:T(8,128)(2,1)} %copy-done.4, bf16[320,768]{1,0:T(8,128)(2,1)} %copy-done.5, f32[16,2048]{1,0:T(8,128)} %route.1.info_ref.refs_8_.refs_6_.refs_2_, bf16[2048,768]{1,0:T(8,128)(2,1)} %combine_s.2.refs_3_, ...), custom_call_target="tpu_custom_call" | custom-call | flops 2013265920 | bytes 10485760 | tf_op jit(solution)/shard_map/combine_s/pallas_call | solution.py:408
  253.2 0.6 add_bitcast_fusion
  (58 shorter events, 0.1 us)
Async XLA Ops:
  24.9 19.8 %collective-permute-start.2 = (bf16[2,320,768]{2,1,0:T(8,128)(2,1)}, bf16[2,320,768]{2,1,0:T(8,128)(2,1)}, u32[]{:S(2)}, u32[]{:S(2)}) collective-permute-start(bf16[2,320,768]{2,1,0:T(8,128)(2,1)} %get-tuple-element.45), channel_id=1, source_target_pairs={{0,1},{1,0},{2,3},{3,2},{4,5},{5,4},{6,7},{7,6}} | collective-permute-start | bytes 2949128 | tf_op jit(solution)/shard_map/ppermute | solution.py:431
  27.2 72.7 %collective-permute-start.5 = (bf16[768,1024]{1,0:T(8,128)(2,1)S(1)}, bf16[768,1024]{1,0:T(8,128)(2,1)}, u32[]{:S(2)}, u32[]{:S(2)}) collective-permute-start(bf16[768,1024]{1,0:T(8,128)(2,1)S(1)} %dynamic-slice_bitcast_fusion.1), channel_id=1, source_target_pairs={{0,4},{4,0},{1,5},{5,1},{2,6},{6,2},{3,7},{7,3}} | collective-permute-start | bytes 4718600 | tf_op jit(solution)/shard_map/ppermute | solution.py:434
  31.3 70.4 %collective-permute-start.6 = (bf16[1024,768]{1,0:T(8,128)(2,1)S(1)}, bf16[1024,768]{1,0:T(8,128)(2,1)}, u32[]{:S(2)}, u32[]{:S(2)}) collective-permute-start(bf16[1024,768]{1,0:T(8,128)(2,1)S(1)} %dynamic-slice_bitcast_fusion), channel_id=1, source_target_pairs={{0,4},{4,0},{1,5},{5,1},{2,6},{6,2},{3,7},{7,3}} | collective-permute-start | bytes 4718600 | tf_op jit(solution)/shard_map/ppermute | solution.py:434
  40.3 24.8 %collective-permute-start = (bf16[2,320,768]{2,1,0:T(8,128)(2,1)}, bf16[2,320,768]{2,1,0:T(8,128)(2,1)S(1)}, u32[]{:S(2)}, u32[]{:S(2)}) collective-permute-start(bf16[2,320,768]{2,1,0:T(8,128)(2,1)} %get-tuple-element.42), channel_id=1, source_target_pairs={{0,2},{1,3},{2,0},{3,1},{4,6},{5,7},{6,4},{7,5}} | collective-permute-start | bytes 2949128 | tf_op jit(solution)/shard_map/ppermute | solution.py:431
  42.3 42.5 %collective-permute-start.1 = (bf16[2,320,768]{2,1,0:T(8,128)(2,1)}, bf16[2,320,768]{2,1,0:T(8,128)(2,1)S(1)}, u32[]{:S(2)}, u32[]{:S(2)}) collective-permute-start(bf16[2,320,768]{2,1,0:T(8,128)(2,1)} %get-tuple-element.43), channel_id=1, source_target_pairs={{0,3},{1,2},{2,1},{3,0},{4,7},{5,6},{6,5},{7,4}} | collective-permute-start | bytes 2949128 | tf_op jit(solution)/shard_map/ppermute | solution.py:431
  44.7 76.4 %collective-permute-start.3 = (bf16[768,512]{1,0:T(8,128)(2,1)S(1)}, bf16[768,512]{1,0:T(8,128)(2,1)S(1)}, u32[]{:S(2)}, u32[]{:S(2)}) collective-permute-start(bf16[768,512]{1,0:T(8,128)(2,1)S(1)} %dynamic-slice_bitcast_fusion.3), channel_id=1, source_target_pairs={{0,4},{4,0},{1,5},{5,1},{2,6},{6,2},{3,7},{7,3}} | collective-permute-start | bytes 2359304 | tf_op jit(solution)/shard_map/ppermute | solution.py:434
  65.2 20.6 %copy-start.2 = (bf16[2,320,768]{2,1,0:T(8,128)(2,1)}, bf16[2,320,768]{2,1,0:T(8,128)(2,1)S(1)}, u32[]{:S(2)}) copy-start(bf16[2,320,768]{2,1,0:T(8,128)(2,1)S(1)} %collective-permute-done.pa) | copy-start | bytes 2949124
  65.2 67.1 %collective-permute-start.4 = (bf16[512,768]{1,0:T(8,128)(2,1)S(1)}, bf16[512,768]{1,0:T(8,128)(2,1)S(1)}, u32[]{:S(2)}, u32[]{:S(2)}) collective-permute-start(bf16[512,768]{1,0:T(8,128)(2,1)S(1)} %dynamic-slice_bitcast_fusion.2), channel_id=1, source_target_pairs={{0,4},{4,0},{1,5},{5,1},{2,6},{6,2},{3,7},{7,3}} | collective-permute-start | bytes 2359304 | tf_op jit(solution)/shard_map/ppermute | solution.py:434
  84.8 1.0 copy-start.3
  84.8 62.9 %collective-permute-start.21 = (bf16[2,320,768]{2,1,0:T(8,128)(2,1)}, bf16[2,320,768]{2,1,0:T(8,128)(2,1)}, u32[]{:S(2)}, u32[]{:S(2)}) collective-permute-start(bf16[2,320,768]{2,1,0:T(8,128)(2,1)} %get-tuple-element.69), channel_id=1, source_target_pairs={{0,1},{1,0},{2,3},{3,2},{4,5},{5,4},{6,7},{7,6}} | collective-permute-start | bytes 2949128 | tf_op jit(solution)/shard_map/ppermute | solution.py:431
  100.0 48.1 %collective-permute-start.22 = (bf16[2,320,768]{2,1,0:T(8,128)(2,1)}, bf16[2,320,768]{2,1,0:T(8,128)(2,1)S(1)}, u32[]{:S(2)}, u32[]{:S(2)}) collective-permute-start(bf16[2,320,768]{2,1,0:T(8,128)(2,1)} %get-tuple-element.70), channel_id=1, source_target_pairs={{0,2},{1,3},{2,0},{3,1},{4,6},{5,7},{6,4},{7,5}} | collective-permute-start | bytes 2949128 | tf_op jit(solution)/shard_map/ppermute | solution.py:431
  101.7 48.2 %collective-permute-start.23 = (bf16[2,320,768]{2,1,0:T(8,128)(2,1)}, bf16[2,320,768]{2,1,0:T(8,128)(2,1)S(1)}, u32[]{:S(2)}, u32[]{:S(2)}) collective-permute-start(bf16[2,320,768]{2,1,0:T(8,128)(2,1)} %get-tuple-element.71), channel_id=1, source_target_pairs={{0,3},{1,2},{2,1},{3,0},{4,7},{5,6},{6,5},{7,4}} | collective-permute-start | bytes 2949128 | tf_op jit(solution)/shard_map/ppermute | solution.py:431
  121.1 11.2 %copy-start = (bf16[768,512]{1,0:T(8,128)(2,1)}, bf16[768,512]{1,0:T(8,128)(2,1)S(1)}, u32[]{:S(2)}) copy-start(bf16[768,512]{1,0:T(8,128)(2,1)S(1)} %collective-permute-done.3.wi_ref) | copy-start | bytes 2359300
  132.2 0.9 copy-start.1
  139.6 23.6 %collective-permute-start.8 = (bf16[320,768]{1,0:T(8,128)(2,1)}, bf16[320,768]{1,0:T(8,128)(2,1)S(1)}, u32[]{:S(2)}, u32[]{:S(2)}) collective-permute-start(bf16[320,768]{1,0:T(8,128)(2,1)} %get-tuple-element.60), channel_id=1, source_target_pairs={{0,2},{1,3},{2,0},{3,1},{4,6},{5,7},{6,4},{7,5}} | collective-permute-start | bytes 1474568 | tf_op jit(solution)/shard_map/ppermute | solution.py:431
  141.3 8.6 %copy-start.19 = (bf16[320,768]{1,0:T(8,128)(2,1)S(1)}, bf16[320,768]{1,0:T(8,128)(2,1)}, u32[]{:S(2)}) copy-start(bf16[320,768]{1,0:T(8,128)(2,1)} %get-tuple-element.63) | copy-start | bytes 1474564
  141.3 25.6 %collective-permute-start.9 = (bf16[320,768]{1,0:T(8,128)(2,1)}, bf16[320,768]{1,0:T(8,128)(2,1)S(1)}, u32[]{:S(2)}, u32[]{:S(2)}) collective-permute-start(bf16[320,768]{1,0:T(8,128)(2,1)} %get-tuple-element.61), channel_id=1, source_target_pairs={{0,3},{1,2},{2,1},{3,0},{4,7},{5,6},{6,5},{7,4}} | collective-permute-start | bytes 1474568 | tf_op jit(solution)/shard_map/ppermute | solution.py:431
  147.7 19.2 %collective-permute-start.7 = (bf16[320,768]{1,0:T(8,128)(2,1)}, bf16[320,768]{1,0:T(8,128)(2,1)S(1)}, u32[]{:S(2)}, u32[]{:S(2)}) collective-permute-start(bf16[320,768]{1,0:T(8,128)(2,1)} %get-tuple-element.59), channel_id=1, source_target_pairs={{0,1},{1,0},{2,3},{3,2},{4,5},{5,4},{6,7},{7,6}} | collective-permute-start | bytes 1474568 | tf_op jit(solution)/shard_map/ppermute | solution.py:431
  148.1 15.0 %copy-start.7 = (bf16[2,320,768]{2,1,0:T(8,128)(2,1)}, bf16[2,320,768]{2,1,0:T(8,128)(2,1)S(1)}, u32[]{:S(2)}) copy-start(bf16[2,320,768]{2,1,0:T(8,128)(2,1)S(1)} %collective-permute-done.22.refs_2_) | copy-start | bytes 2949124
  148.1 20.6 %collective-permute-start.10 = (bf16[320,768]{1,0:T(8,128)(2,1)}, bf16[320,768]{1,0:T(8,128)(2,1)S(1)}, u32[]{:S(2)}, u32[]{:S(2)}) collective-permute-start(bf16[320,768]{1,0:T(8,128)(2,1)} %get-tuple-element.58.refs_0_), channel_id=1, source_target_pairs={{0,4},{4,0},{1,5},{5,1},{2,6},{6,2},{3,7},{7,3}} | collective-permute-start | bytes 1474568 | tf_op jit(solution)/shard_map/ppermute | solution.py:434
  149.8 13.3 %copy-start.8 = (bf16[2,320,768]{2,1,0:T(8,128)(2,1)}, bf16[2,320,768]{2,1,0:T(8,128)(2,1)S(1)}, u32[]{:S(2)}) copy-start(bf16[2,320,768]{2,1,0:T(8,128)(2,1)S(1)} %collective-permute-done.23.refs_3_) | copy-start | bytes 2949124
  149.9 27.7 %collective-permute-start.14 = (bf16[320,768]{1,0:T(8,128)(2,1)S(1)}, bf16[320,768]{1,0:T(8,128)(2,1)S(1)}, u32[]{:S(2)}, u32[]{:S(2)}) collective-permute-start(bf16[320,768]{1,0:T(8,128)(2,1)S(1)} %copy-done.19), channel_id=1, source_target_pairs={{0,2},{1,3},{2,0},{3,1},{4,6},{5,7},{6,4},{7,5}} | collective-permute-start | bytes 1474568 | tf_op jit(solution)/shard_map/ppermute | solution.py:431
  151.4 11.8 %copy-start.16 = (bf16[320,768]{1,0:T(8,128)(2,1)S(1)}, bf16[320,768]{1,0:T(8,128)(2,1)}, u32[]{:S(2)}) copy-start(bf16[320,768]{1,0:T(8,128)(2,1)} %get-tuple-element.64) | copy-start | bytes 1474564
  151.4 15.5 %copy-start.17 = (bf16[320,768]{1,0:T(8,128)(2,1)S(1)}, bf16[320,768]{1,0:T(8,128)(2,1)}, u32[]{:S(2)}) copy-start(bf16[320,768]{1,0:T(8,128)(2,1)} %get-tuple-element.66) | copy-start | bytes 1474564
  163.1 35.3 %copy-start.10 = (bf16[320,768]{1,0:T(8,128)(2,1)}, bf16[320,768]{1,0:T(8,128)(2,1)S(1)}, u32[]{:S(2)}) copy-start(bf16[320,768]{1,0:T(8,128)(2,1)S(1)} %collective-permute-done.8.refs_2_) | copy-start | bytes 1474564
  163.2 35.3 %collective-permute-start.16 = (bf16[320,768]{1,0:T(8,128)(2,1)S(1)}, bf16[320,768]{1,0:T(8,128)(2,1)S(1)}, u32[]{:S(2)}, u32[]{:S(2)}) collective-permute-start(bf16[320,768]{1,0:T(8,128)(2,1)S(1)} %copy-done.16), channel_id=1, source_target_pairs={{0,3},{1,2},{2,1},{3,0},{4,7},{5,6},{6,5},{7,4}} | collective-permute-start | bytes 1474568 | tf_op jit(solution)/shard_map/ppermute | solution.py:431
  166.8 31.6 %copy-start.11 = (bf16[320,768]{1,0:T(8,128)(2,1)}, bf16[320,768]{1,0:T(8,128)(2,1)S(1)}, u32[]{:S(2)}) copy-start(bf16[320,768]{1,0:T(8,128)(2,1)S(1)} %collective-permute-done.9.refs_3_) | copy-start | bytes 1474564
  166.8 32.0 %collective-permute-start.18 = (bf16[320,768]{1,0:T(8,128)(2,1)S(1)}, bf16[320,768]{1,0:T(8,128)(2,1)S(1)}, u32[]{:S(2)}, u32[]{:S(2)}) collective-permute-start(bf16[320,768]{1,0:T(8,128)(2,1)S(1)} %copy-done.17), channel_id=1, source_target_pairs={{0,1},{1,0},{2,3},{3,2},{4,5},{5,4},{6,7},{7,6}} | collective-permute-start | bytes 1474568 | tf_op jit(solution)/shard_map/ppermute | solution.py:431
  166.9 31.5 %copy-start.14 = (bf16[320,768]{1,0:T(8,128)(2,1)}, bf16[320,768]{1,0:T(8,128)(2,1)S(1)}, u32[]{:S(2)}) copy-start(bf16[320,768]{1,0:T(8,128)(2,1)S(1)} %collective-permute-done.7.refs_1_) | copy-start | bytes 1474564
  167.0 33.6 %collective-permute-start.12 = (bf16[320,768]{1,0:T(8,128)(2,1)S(1)}, bf16[320,768]{1,0:T(8,128)(2,1)S(1)}, u32[]{:S(2)}, u32[]{:S(2)}) collective-permute-start(bf16[320,768]{1,0:T(8,128)(2,1)S(1)} %collective-permute-done.8.refs_2_), channel_id=1, source_target_pairs={{0,4},{4,0},{1,5},{5,1},{2,6},{6,2},{3,7},{7,3}} | collective-permute-start | bytes 1474568 | tf_op jit(solution)/shard_map/ppermute | solution.py:434
  168.7 29.7 %copy-start.15 = (bf16[320,768]{1,0:T(8,128)(2,1)}, bf16[320,768]{1,0:T(8,128)(2,1)S(1)}, u32[]{:S(2)}) copy-start(bf16[320,768]{1,0:T(8,128)(2,1)S(1)} %collective-permute-done.10.refs_4_) | copy-start | bytes 1474564
  168.7 32.2 %collective-permute-start.13 = (bf16[320,768]{1,0:T(8,128)(2,1)S(1)}, bf16[320,768]{1,0:T(8,128)(2,1)S(1)}, u32[]{:S(2)}, u32[]{:S(2)}) collective-permute-start(bf16[320,768]{1,0:T(8,128)(2,1)S(1)} %collective-permute-done.9.refs_3_), channel_id=1, source_target_pairs={{0,4},{4,0},{1,5},{5,1},{2,6},{6,2},{3,7},{7,3}} | collective-permute-start | bytes 1474568 | tf_op jit(solution)/shard_map/ppermute | solution.py:434
  177.5 23.0 %copy-start.12 = (bf16[320,768]{1,0:T(8,128)(2,1)}, bf16[320,768]{1,0:T(8,128)(2,1)S(1)}, u32[]{:S(2)}) copy-start(bf16[320,768]{1,0:T(8,128)(2,1)S(1)} %collective-permute-done.14.refs_2_) | copy-start | bytes 1474564
  177.5 25.1 %collective-permute-start.11 = (bf16[320,768]{1,0:T(8,128)(2,1)S(1)}, bf16[320,768]{1,0:T(8,128)(2,1)S(1)}, u32[]{:S(2)}, u32[]{:S(2)}) collective-permute-start(bf16[320,768]{1,0:T(8,128)(2,1)S(1)} %collective-permute-done.7.refs_1_), channel_id=1, source_target_pairs={{0,4},{4,0},{1,5},{5,1},{2,6},{6,2},{3,7},{7,3}} | collective-permute-start | bytes 1474568 | tf_op jit(solution)/shard_map/ppermute | solution.py:434
  179.2 19.3 %copy-start.9 = (bf16[320,768]{1,0:T(8,128)(2,1)S(1)}, bf16[320,768]{1,0:T(8,128)(2,1)}, u32[]{:S(2)}) copy-start(bf16[320,768]{1,0:T(8,128)(2,1)} %get-tuple-element.65.refs_0_) | copy-start | bytes 1474564
  198.5 22.6 %copy-start.13 = (bf16[320,768]{1,0:T(8,128)(2,1)}, bf16[320,768]{1,0:T(8,128)(2,1)S(1)}, u32[]{:S(2)}) copy-start(bf16[320,768]{1,0:T(8,128)(2,1)S(1)} %collective-permute-done.16.refs_3_) | copy-start | bytes 1474564
  198.5 22.6 %collective-permute-start.19 = (bf16[320,768]{1,0:T(8,128)(2,1)S(1)}, bf16[320,768]{1,0:T(8,128)(2,1)S(1)}, u32[]{:S(2)}, u32[]{:S(2)}) collective-permute-start(bf16[320,768]{1,0:T(8,128)(2,1)S(1)} %copy-done.9), channel_id=1, source_target_pairs={{0,4},{4,0},{1,5},{5,1},{2,6},{6,2},{3,7},{7,3}} | collective-permute-start | bytes 1474568 | tf_op jit(solution)/shard_map/ppermute | solution.py:434
  198.9 22.2 %copy-start.18 = (bf16[320,768]{1,0:T(8,128)(2,1)}, bf16[320,768]{1,0:T(8,128)(2,1)S(1)}, u32[]{:S(2)}) copy-start(bf16[320,768]{1,0:T(8,128)(2,1)S(1)} %collective-permute-done.18.refs_1_) | copy-start | bytes 1474564
  198.9 24.3 %collective-permute-start.20 = (bf16[320,768]{1,0:T(8,128)(2,1)S(1)}, bf16[320,768]{1,0:T(8,128)(2,1)S(1)}, u32[]{:S(2)}, u32[]{:S(2)}) collective-permute-start(bf16[320,768]{1,0:T(8,128)(2,1)S(1)} %collective-permute-done.18.refs_1_), channel_id=1, source_target_pairs={{0,4},{4,0},{1,5},{5,1},{2,6},{6,2},{3,7},{7,3}} | collective-permute-start | bytes 1474568 | tf_op jit(solution)/shard_map/ppermute | solution.py:434
  200.5 2.1 copy-start.20
  200.5 37.1 %collective-permute-start.15 = (bf16[320,768]{1,0:T(8,128)(2,1)S(1)}, bf16[320,768]{1,0:T(8,128)(2,1)S(1)}, u32[]{:S(2)}, u32[]{:S(2)}) collective-permute-start(bf16[320,768]{1,0:T(8,128)(2,1)S(1)} %collective-permute-done.14.refs_2_), channel_id=1, source_target_pairs={{0,4},{4,0},{1,5},{5,1},{2,6},{6,2},{3,7},{7,3}} | collective-permute-start | bytes 1474568 | tf_op jit(solution)/shard_map/ppermute | solution.py:434
  200.9 1.7 copy-start.21
  200.9 42.8 %collective-permute-start.17 = (bf16[320,768]{1,0:T(8,128)(2,1)S(1)}, bf16[320,768]{1,0:T(8,128)(2,1)S(1)}, u32[]{:S(2)}, u32[]{:S(2)}) collective-permute-start(bf16[320,768]{1,0:T(8,128)(2,1)S(1)} %collective-permute-done.16.refs_3_), channel_id=1, source_target_pairs={{0,4},{4,0},{1,5},{5,1},{2,6},{6,2},{3,7},{7,3}} | collective-permute-start | bytes 1474568 | tf_op jit(solution)/shard_map/ppermute | solution.py:434
  202.6 0.8 copy-start.22
  221.1 14.8 %copy-start.6 = (f32[8,768]{1,0:T(8,128)S(1)}, f32[8,768]{1,0:T(8,128)}, u32[]{:S(2)}) copy-start(f32[8,768]{1,0:T(8,128)} %get-tuple-element.78) | copy-start | bytes 73732
  221.1 14.8 %collective-permute-start.24 = (f32[8,768]{1,0:T(8,128)}, f32[8,768]{1,0:T(8,128)S(1)}, u32[]{:S(2)}, u32[]{:S(2)}) collective-permute-start(f32[8,768]{1,0:T(8,128)} %get-tuple-element.78), channel_id=1, source_target_pairs={{0,1},{1,0},{2,3},{3,2},{4,5},{5,4},{6,7},{7,6}} | collective-permute-start | bytes 73736 | tf_op jit(solution)/shard_map/ppermute | solution.py:431
  221.1 2.1 copy-start.23
  223.2 0.8 copy-start.24
  235.9 17.3 %collective-permute-start.25 = (f32[8,768]{1,0:T(8,128)S(1)}, f32[8,768]{1,0:T(8,128)S(1)}, u32[]{:S(2)}, u32[]{:S(2)}) collective-permute-start(f32[8,768]{1,0:T(8,128)S(1)} %add.14), channel_id=1, source_target_pairs={{0,2},{1,3},{2,0},{3,1},{4,6},{5,7},{6,4},{7,5}} | collective-permute-start | bytes 73736 | tf_op jit(solution)/shard_map/ppermute | solution.py:431
  237.6 6.1 %copy-start.4 = (bf16[320,768]{1,0:T(8,128)(2,1)}, bf16[320,768]{1,0:T(8,128)(2,1)S(1)}, u32[]{:S(2)}) copy-start(bf16[320,768]{1,0:T(8,128)(2,1)S(1)} %collective-permute-done.15.refs_0_) | copy-start | bytes 1474564
  243.7 0.8 copy-start.5

commit v3 on v2

--- a/solution.py
+++ b/solution.py
@@ -199,25 +199,25 @@
     )(meta, pair_a, pair_b, w_in, w_out, *so_far)
 
 
-def far_half(x, dy, wi, wo, y_in, s_in, chunk, group):
-    rows, d_model = x.shape
+def far_half(x, dy, wi, wo, y_in, s_in, chunk, group, joined):
+    d_model = x.shape[1]
+    rows = x.shape[0] // 2
+    cap = rows // 2
     width = wi.shape[1]
     steps = width // chunk
-    if group is not None:
-        rows //= 2
-    half = rows // 2
 
     def body(x_ref, dy_ref, wi_ref, wo_ref, y0, s0, *outs):
-        c = pl.program_id(0)
         h, da = hidden_grads(x_ref[...], dy_ref[...], wi_ref[...], wo_ref[...])
         y = nn(h, wo_ref[...])
         s = nt(da, wi_ref[...])
         if group is not None:
             for p in range(2):
-                part = slice(p * half, (p + 1) * half)
-                outs[p][...] = (y0[part] + y[part]).astype(BF16)
-                outs[2 + p][...] = (s0[part] + s[part]).astype(BF16)
+                part = slice(p * cap, (p + 1) * cap)
+                y_out, s_out = (outs[p].at[0], outs[p].at[1]) if joined else (outs[p], outs[2 + p])
+                y_out[...] = (y0[part] + y[part]).astype(BF16)
+                s_out[...] = (s0[part] + s[part]).astype(BF16)
             return
+        c = pl.program_id(1)
 
         @pl.when(c == 0)
         def _():
@@ -229,55 +229,61 @@
             outs[0][...] += y
             outs[1][...] += s
 
-    full = pl.BlockSpec((rows, d_model), lambda c: (group or 0, 0))
-    if group is not None:
-        out_specs, out_shape = [whole((half, d_model))] * 4, [shape((half, d_model))] * 4
+    if group is None:
+        grid = (2, steps)
+        full = pl.BlockSpec((rows, d_model), lambda g, c: (g, 0))
+        out_specs, out_shape = [full] * 2, [shape(x.shape, F32)] * 2
     else:
-        out_specs, out_shape = [full] * 2, [shape((rows, d_model), F32)] * 2
-    return pl.pallas_call(
-        body,
-        grid=(steps,),
+        grid = (1, steps)
+        full = pl.BlockSpec((rows, d_model), lambda g, c: (group, 0))
+        dims, count = ((2, cap, d_model), 2) if joined else ((cap, d_model), 4)
+        out_specs, out_shape = [whole(dims)] * count, [shape(dims)] * count
+    return pl.pallas_call(
+        body,
+        grid=grid,
         in_specs=[
             full,
             full,
-            pl.BlockSpec((d_model, chunk), lambda c: (0, c)),
-            pl.BlockSpec((chunk, d_model), lambda c: (c, 0)),
+            pl.BlockSpec((d_model, chunk), lambda g, c: (0, c)),
+            pl.BlockSpec((chunk, d_model), lambda g, c: (c, 0)),
             full,
             full,
         ],
         out_specs=out_specs,
         out_shape=out_shape,
-        compiler_params=params(1),
-        cost_estimate=cost(8 * rows * width * d_model, 10),
+        compiler_params=params(2),
+        cost_estimate=cost(8 * rows * grid[0] * width * d_model, 10),
         name="far_half",
     )(x, dy, wi, wo, y_in, s_in)
 
 
-def finished_grads(meta, x, dy, h, da, n_local, chunk):
+def finished_grads(meta, x, dy, h, da, n_local, chunk, lo, hi, so_far):
     rows, d_model = x.shape
     width = h.shape[1]
 
-    def body(meta_ref, x_ref, dy_ref, h_ref, da_ref, gi, go):
+    def body(meta_ref, x_ref, dy_ref, h_ref, da_ref, *refs):
+        gi, go = refs[-2:]
         gi[0] = tn(x_ref[...], da_ref[...])
         go[0] = tn(h_ref[...], dy_ref[...])
 
-    hid = pl.BlockSpec((rows, chunk), lambda c, m: (0, c))
+    hid = pl.BlockSpec((rows, chunk), lambda c, m: (0, c + lo))
     return pl.pallas_call(
         body,
         grid_spec=pltpu.PrefetchScalarGridSpec(
             num_scalar_prefetch=1,
-            grid=(width // chunk,),
-            in_specs=[whole((rows, d_model))] * 2 + [hid] * 2,
+            grid=(hi - lo,),
+            in_specs=[whole((rows, d_model))] * 2 + [hid] * 2 + [pl.BlockSpec(memory_space=pl.ANY)] * len(so_far),
             out_specs=[
-                pl.BlockSpec((1, d_model, chunk), lambda c, m: (m[0], 0, c)),
-                pl.BlockSpec((1, chunk, d_model), lambda c, m: (m[0], c, 0)),
+                pl.BlockSpec((1, d_model, chunk), lambda c, m: (m[0], 0, c + lo)),
+                pl.BlockSpec((1, chunk, d_model), lambda c, m: (m[0], c + lo, 0)),
             ],
         ),
         out_shape=[shape((n_local, d_model, width), F32), shape((n_local, width, d_model), F32)],
-        compiler_params=params(1),
-        cost_estimate=cost(4 * rows * width * d_model, 25),
+        input_output_aliases={5 + i: i for i in range(len(so_far))},
+        compiler_params=params(1),
+        cost_estimate=cost(4 * rows * (hi - lo) * chunk * d_model, 8 * (hi - lo)),
         name="finished_grads",
-    )(meta, x, dy, h, da)
+    )(meta, x, dy, h, da, *so_far)
 
 
 def other_grads(meta, pairs, w_in, w_out, grad_w_in, grad_w_out, chunk):
@@ -339,10 +345,23 @@
     return jnp.where(info_v[:, 0:1] == codes.astype(F32), 1.0, 0.0).astype(BF16)
 
 
+def piece_specs(rows):
+    specs, arrays = [], []
+    for piece in rows:
+        if isinstance(piece, tuple):
+            array, which = piece
+            specs.append(pl.BlockSpec((None,) + array.shape[1:], lambda *_, w=which: (w, 0, 0)))
+        else:
+            array = piece
+            specs.append(whole(array.shape))
+        arrays.append(array)
+    return specs, arrays, arrays[0].shape[-2]
+
+
 def combine_y(meta, pieces, info, tokens, grad_out, block):
     n_tok, d_model = tokens.shape
-    keys, rows = list(pieces), list(pieces.values())
-    cap = rows[0].shape[0]
+    keys = list(pieces)
+    specs, rows, cap = piece_specs(pieces.values())
     n_experts = INFO_ROWS - 8
 
     def body(meta_ref, *refs):
@@ -374,7 +393,7 @@
         grid_spec=pltpu.PrefetchScalarGridSpec(
             num_scalar_prefetch=1,
             grid=(n_tok // block,),
-            in_specs=[whole((cap, d_model))] * len(keys)
+            in_specs=specs
             + [pl.BlockSpec((INFO_ROWS, block), lambda b, m: (0, b)), tok, tok],
             out_specs=[tok, pl.BlockSpec((block, n_experts), lambda b, m: (b, 0)), whole((n_experts, d_model))],
             scratch_shapes=[pltpu.VMEM((cap * len(keys), d_model), BF16)],
@@ -388,8 +407,9 @@
 
 def combine_s(meta, pieces, info, extra, block):
     n_tok = info.shape[1]
-    keys, rows = list(pieces), list(pieces.values())
-    cap, d_model = rows[0].shape
+    keys = list(pieces)
+    specs, rows, cap = piece_specs(pieces.values())
+    d_model = rows[0].shape[-1]
 
     def body(meta_ref, *refs):
         parts = refs[: len(keys)]
@@ -410,7 +430,7 @@
         grid_spec=pltpu.PrefetchScalarGridSpec(
             num_scalar_prefetch=1,
             grid=(n_tok // block,),
-            in_specs=[whole((cap, d_model))] * len(keys)
+            in_specs=specs
             + [pl.BlockSpec((INFO_ROWS, block), lambda b, m: (0, b))]
             + extra_specs,
             out_specs=tok,
@@ -438,7 +458,7 @@
         n_experts = w_router.shape[1]
         width = w_in.shape[2]
         capacity = (6 * n_tok + 5 * n_experts - 1) // (5 * n_experts)
-        cap = (capacity + 15) // 16 * 16
+        cap = (capacity + 7) // 8 * 8
         chunk = width // 3
         tp, ep = lax.axis_index("tp"), lax.axis_index("ep")
         meta = jnp.where(jnp.arange(2) == 0, tp, ep).astype(jnp.int32)
@@ -461,18 +481,20 @@
 
         part = own_half(meta, f0, f1, w_in, w_out, chunk, 0, ())
         h, da, y, s, x, dy = own_half(meta, f2, f3, w_in, w_out, chunk, 1, part)
-        y, s = far_half(x, dy, *far_w["a"], y, s, chunk, None)
-        y0, y1, s0, s1 = far_half(x, dy, *far_w["b"], y, s, chunk, 0)
-        y2, y3, s2, s3 = far_half(x, dy, *far_w["b"], y, s, chunk, 1)
-
-        y1, s1 = to_ep(y1, 1), to_ep(s1, 1)
+        y, s = far_half(x, dy, *far_w["a"], y, s, chunk, None, False)
+        grads = finished_grads(meta, x, dy, h, da, w_in.shape[0], chunk, 0, 1, ())
+        ys0, ys1 = far_half(x, dy, *far_w["b"], y, s, chunk, 0, True)
+        y2, y3, s2, s3 = far_half(x, dy, *far_w["b"], y, s, chunk, 1, False)
+
+        ys1 = to_ep(ys1, 1)
         y2, y3 = to_ep(y2, 2), to_ep(y3, 3)
         s2, s3 = to_ep(s2, 2), to_ep(s3, 3)
-        y_mine, s_mine = [y0, y1, y2, y3], [s0, s1, s2, s3]
-        y_twin = [to_twin(v) for v in y_mine]
-        s_twin = [to_twin(v) for v in s_mine]
-
-        grads = finished_grads(meta, x, dy, h, da, w_in.shape[0], chunk)
+        twin0, twin1 = to_twin(ys0), to_twin(ys1)
+        y_mine, s_mine = [(ys0, 0), (ys1, 0), y2, y3], [(ys0, 1), (ys1, 1), s2, s3]
+        y_twin = [(twin0, 0), (twin1, 0), to_twin(y2), to_twin(y3)]
+        s_twin = [(twin0, 1), (twin1, 1), to_twin(s2), to_twin(s3)]
+
+        grads = finished_grads(meta, x, dy, h, da, w_in.shape[0], chunk, 1, 3, grads)
         grad_w_in, grad_w_out = other_grads(meta, (g0, g1, g2, g3), w_in, w_out, *grads, chunk)
 
         y_all = {(d, k): v for k, side in enumerate((y_mine, y_twin)) for d, v in enumerate(side)}
@@ -481,8 +503,8 @@
         moe_out, dlog, dwg = combine_y(meta, y_all, info, tokens, grad_out, n_tok // 4)
         dwg = dwg + to_ep(dwg, 1)
         dwg = dwg + to_ep(dwg, 2)
-        so_far = combine_s(meta, s_all, info, (), n_tok // 4)
-        grad_tokens = combine_s(meta, s_late, info, (so_far, dlog, w_router.T), n_tok // 4)
+        so_far = combine_s(meta, s_all, info, (), n_tok // 2)
+        grad_tokens = combine_s(meta, s_late, info, (so_far, dlog, w_router.T), n_tok // 2)
         return moe_out, grad_tokens, grad_w_in, grad_w_out, dwg.T
 
     in_specs = (row_spec, row_spec, P(None, None), P("ep", None, "tp"), P("ep", "tp", None), P(("dp", "ep")))

time: 254 us -> 273 us (1.075)
  waiting for transfers between devices: 54 us -> 75.9 us
    ppermute x12 -> x10, waiting for transfers between devices: 19.3 us -> 42.7 us  [to_twin(): return lax.ppermute(v, 'tp', [(0, 1), (1, 0)])]
    pallas_call x1 -> x2, Pallas kernels: 11.8 us -> 16.3 us  [finished_grads(): pl.pallas_call(body, grid_spec=pltpu.PrefetchScalarGridSpec(num_scalar_pr...]
    ppermute x12 -> x10, starting transfers between devices: 15.6 us -> 13.3 us  [to_twin(): return lax.ppermute(v, 'tp', [(0, 1), (1, 0)])]
    ppermute x14 -> x13, waiting for transfers between devices: 34.7 us -> 33.1 us  [to_ep(): return lax.ppermute(v, 'ep', [(i, i ^ d) for i in range(ep_size)])]
    ppermute x14 -> x13, starting transfers between devices: 11.5 us -> 11.3 us  [to_ep(): return lax.ppermute(v, 'ep', [(i, i ^ d) for i in range(ep_size)])]
  transfers between devices with their start and end apart: 26 -> 23, of which waited for: 7 -> 7; matrix products, arithmetic and copies ran while one was open for 2% -> 2% of each run, Pallas kernels for 54% -> 51%
where the time goes in v3:
time: 273 us; the launch traced here: 272 us
  Pallas kernels  162 us (59%)
  waiting for transfers between devices  75.9 us (28%)
  starting transfers between devices  24.6 us (9%)
  local copies, waits for them, and re-layouts  8.3 us (3%)
    ppermute x10, waiting for transfers between devices, to_twin(): return lax.ppermute(v, 'tp', [(0, 1), (1, 0)])  42.7 us
    ppermute x13, waiting for transfers between devices, to_ep(): return lax.ppermute(v, 'ep', [(i, i ^ d) for i in range(ep_size)])  33.1 us
    pallas_call x3, Pallas kernels, far_half(): pl.pallas_call(body, grid=grid, in_specs=[full, full, pl.BlockSpec((d_mod...  29.2 us
    pallas_call x2, Pallas kernels, dispatch(): pl.pallas_call(body, grid_spec=pltpu.PrefetchScalarGridSpec(num_scalar_pr...  28.2 us
    pallas_call x2, Pallas kernels, own_half(): pl.pallas_call(body, grid_spec=pltpu.PrefetchScalarGridSpec(num_scalar_pr...  27.6 us
    pallas_call x2, Pallas kernels, combine_s(): pl.pallas_call(body, grid_spec=pltpu.PrefetchScalarGridSpec(num_scalar_pr...  19.9 us
    pallas_call x1, Pallas kernels, other_grads(): pl.pallas_call(body, grid_spec=pltpu.PrefetchScalarGridSpec(num_scalar_pr...  19 us
    pallas_call x1, Pallas kernels, combine_y(): pl.pallas_call(body, grid_spec=pltpu.PrefetchScalarGridSpec(num_scalar_pr...  17.4 us
  transfers between devices with their start and end apart: 23, of which 7 were waited for; matrix products, arithmetic and copies ran while one was open for 2% of the time, Pallas kernels for 51%

profile of v3, /device:TPU:0, one launch (start us, length us, event | category | flops | bytes accessed | tf_op | source)
XLA Modules:
  0.0 272.3 jit_solution(13259390745890525535)
XLA Ops:
  0.6 0.6 compare_select_fusion.meta_ref
  1.2 4.0 %route.1.info_ref.refs_8_.refs_6_.refs_2_ = f32[16,2048]{1,0:T(8,128)} custom-call(s32[1,2048]{1,0:T(1,128)} %bitcast.14, bf16[2048,768]{1,0:T(8,128)(2,1)} %refs_9_.1, bf16[8,768]{1,0:T(8,128)(2,1)} %bitcast.12), custom_call_target="tpu_custom_call" | custom-call | flops 2000000000 | bytes 3145728 | tf_op jit(solution)/shard_map/route/pallas_call | solution.py:87
  5.2 19.3 %dispatch.3 = (bf16[2,312,768]{2,1,0:T(8,128)(2,1)}, bf16[2,312,768]{2,1,0:T(8,128)(2,1)}, bf16[2,312,768]{2,1,0:T(8,128)(2,1)}, bf16[2,312,768]{2,1,0:T(8,128)(...) custom-call(s32[2]{0:T(128)} %compare_select_fusion.meta_ref, ...), custom_call_target="tpu_custom_call" | custom-call | flops 11777605632 | bytes 20971520 | tf_op jit(solution)/shard_map/dispatch/pallas_call | solution.py:129
  24.5 0.9 collective-permute-start.2
  25.4 1.5 dynamic-slice_bitcast_fusion
  26.9 2.5 collective-permute-start.6
  29.4 1.5 dynamic-slice_bitcast_fusion.1
  30.9 0.0 collective-permute-start.5
  31.0 8.9 %dispatch.2 = (bf16[2,312,768]{2,1,0:T(8,128)(2,1)}, bf16[2,312,768]{2,1,0:T(8,128)(2,1)}) custom-call(s32[2]{0:T(128)} %compare_select_fusion.meta_ref, f32[16,2048]{1,0:T(8,128)} %route.1.info_ref.refs_8_.refs_6_.refs_2_, bf16[2048,768]{1,0:T(8,128)(2,1)} %refs_9_.1, bf16[2048,768]{1,0:T(8,128)(2,1)} %refs_10_.1), custom_call_target="tpu_custom_call" | custom-call | flops 3925868544 | bytes 12582912 | tf_op jit(solution)/shard_map/dispatch/pallas_call | solution.py:129
  39.9 2.0 collective-permute-start
  41.9 1.2 dynamic-slice_bitcast_fusion.3
  43.1 1.2 dynamic-slice_bitcast_fusion.2
  44.3 1.5 collective-permute-start.4
  45.8 13.8 %own_half.2 = (bf16[1248,1536]{1,0:T(8,128)(2,1)}, bf16[1248,1536]{1,0:T(8,128)(2,1)}, f32[1248,768]{1,0:T(8,128)}, f32[1248,768]{1,0:T(8,128)}, bf16[1248,768]{1,0:T(8,128)(2,1)}, /*index=5*/bf16[1248,768]{1,0:T(8,128)(2,1)}) custom-call(s32[2]{0:T(128)} %compare_select_fusion.meta_ref, bf16[2,312,768]{2,1,0:T(8,128)(2,1)} %get-tuple-element.44.pa, ...), custom_call_target="tpu_custom_call" | custom-call | flops 5888802816 | bytes 20971520 | tf_op jit(solution)/shard_map/own_half/pallas_call | solution.py:178
  59.6 4.6 %collective-permute-done.pa = bf16[2,312,768]{2,1,0:T(8,128)(2,1)S(1)} collective-permute-done((bf16[2,312,768]{2,1,0:T(8,128)(2,1)}, bf16[2,312,768]{2,1,0:T(8,128)(2,1)S(1)}, u32[]{:S(2)}, u32[]{:S(2)}) %collective-permute-start) | collective-permute-done | bytes 958496 | tf_op jit(solution)/shard_map/ppermute | solution.py:451
  64.2 2.0 collective-permute-start.3
  66.2 17.1 %collective-permute-done.1.pb = bf16[2,312,768]{2,1,0:T(8,128)(2,1)S(1)} collective-permute-done((bf16[2,312,768]{2,1,0:T(8,128)(2,1)}, bf16[2,312,768]{2,1,0:T(8,128)(2,1)S(1)}, u32[]{:S(2)}, u32[]{:S(2)}) %collective-permute-start.1) | collective-permute-done | bytes 958496 | tf_op jit(solution)/shard_map/ppermute | solution.py:451
  83.3 0.9 collective-permute-start.18
  84.2 0.1 copy-done.3
  84.3 13.8 %own_half.3 = (bf16[1248,1536]{1,0:T(8,128)(2,1)}, bf16[1248,1536]{1,0:T(8,128)(2,1)}, f32[1248,768]{1,0:T(8,128)}, f32[1248,768]{1,0:T(8,128)}, bf16[1248,768]{1,0:T(8,128)(2,1)}, /*index=5*/bf16[1248,768]{1,0:T(8,128)(2,1)}) custom-call(s32[2]{0:T(128)} %compare_select_fusion.meta_ref, ...), custom_call_target="tpu_custom_call", output_to_operand_aliasing={{0}: (5, {}), {1}: (6, {}), {2}: (7, {}), {3}: (8, {}), {4}... | custom-call | flops 5888802816 | bytes 20971520 | tf_op jit(solution)/shard_map/own_half/pallas_call | solution.py:178
  98.1 0.0 collective-permute-done.6.wo_ref
  98.1 1.6 collective-permute-start.19
  99.7 0.6 collective-permute-start.20
  100.4 16.2 %far_half.3 = (f32[1248,768]{1,0:T(8,128)}, f32[1248,768]{1,0:T(8,128)}) custom-call(bf16[1248,768]{1,0:T(8,128)(2,1)} %get-tuple-element.52.x_ref, bf16[1248,768]{1,0:T(8,128)(2,1)} %get-tuple-element.53.dy_ref, bf16[768,1024]{1,0:T(8,128)(2,1)} %collective-permute-done.5.wi_ref, bf16[1024,768]{1,0:T(8,128)(2,1)} %collective-permute-done.6.wo_ref, ...), custom_call_target="tpu_custom_call" | custom-call | flops 7851737088 | bytes 10485760 | tf_op jit(solution)/shard_map/far_half/pallas_call | solution.py:241
  116.6 0.0 copy-start
  116.6 15.2 %collective-permute-done.3.wi_ref = bf16[768,512]{1,0:T(8,128)(2,1)S(1)} collective-permute-done((bf16[768,512]{1,0:T(8,128)(2,1)S(1)}, bf16[768,512]{1,0:T(8,128)(2,1)S(1)}, u32[]{:S(2)}, u32[]{:S(2)}) %collective-permute-start.3) | collective-permute-done | bytes 786464 | tf_op jit(solution)/shard_map/ppermute | solution.py:454
  131.9 0.9 copy-done.1
  132.7 6.6 %far_half.4 = (bf16[2,312,768]{2,1,0:T(8,128)(2,1)}, bf16[2,312,768]{2,1,0:T(8,128)(2,1)}) custom-call(bf16[1248,768]{1,0:T(8,128)(2,1)} %get-tuple-element.52.x_ref, bf16[1248,768]{1,0:T(8,128)(2,1)} %get-tuple-element.53.dy_ref, bf16[768,512]{1,0:T(8,128)(2,1)} %copy-done.1, bf16[512,768]{1,0:T(8,128)(2,1)} %copy-done, f32[1248,768]{1,0:T(8,128)} %get-tuple-element.56.y0, ...), custom_call_target="tpu_custom_call" | custom-call | flops 1962934272 | bytes 10485760 | tf_op jit(solution)/shard_map/far_half/pallas_call | solution.py:241
  139.3 0.0 collective-permute-start.7
  139.3 6.3 %far_half.5 = (bf16[312,768]{1,0:T(8,128)(2,1)}, bf16[312,768]{1,0:T(8,128)(2,1)}, bf16[312,768]{1,0:T(8,128)(2,1)}, bf16[312,768]{1,0:T(8,128)(2,1)}) custom-call(bf16[1248,768]{1,0:T(8,128)(2,1)} %get-tuple-element.52.x_ref, bf16[1248,768]{1,0:T(8,128)(2,1)} %get-tuple-element.53.dy_ref, bf16[768,512]{1,0:T(8,128)(2,1)} %copy-done.1, ...), custom_call_target="tpu_custom_call" | custom-call | flops 1962934272 | bytes 10485760 | tf_op jit(solution)/shard_map/far_half/pallas_call | solution.py:241
  145.7 1.7 collective-permute-start.8
  147.4 0.0 collective-permute-done.18.refs_1_
  147.4 0.2 collective-permute-start.9
  147.5 0.0 collective-permute-done.19.refs_2_
  147.5 1.7 collective-permute-start.14
  149.2 6.9 %finished_grads.2 = (f32[2,768,1536]{2,1,0:T(8,128)}, f32[2,1536,768]{2,1,0:T(8,128)}) custom-call(s32[2]{0:T(128)} %compare_select_fusion.meta_ref, bf16[1248,768]{1,0:T(8,128)(2,1)} %get-tuple-element.52.x_ref, bf16[1248,768]{1,0:T(8,128)(2,1)} %get-tuple-element.53.dy_ref, bf16[1248,1536]{1,0:T(8,128)(2,1)} %get-tuple-element.70.h_ref, ...), custom_call_target="tpu_custom_call" | custom-call | flops 1962934272 | bytes 8388608 | tf_op jit(solution)/shard_map/finished_grads/pallas_call | solution.py:270
  156.1 9.4 %finished_grads.3 = (f32[2,768,1536]{2,1,0:T(8,128)}, f32[2,1536,768]{2,1,0:T(8,128)}) custom-call(s32[2]{0:T(128)} %compare_select_fusion.meta_ref, bf16[1248,768]{1,0:T(8,128)(2,1)} %get-tuple-element.52.x_ref, bf16[1248,768]{1,0:T(8,128)(2,1)} %get-tuple-element.53.dy_ref, ...), custom_call_target="tpu_custom_call", output_to_operand_aliasing={{0}: (5, {}), {1}: (6, {})} | custom-call | flops 3925868544 | bytes 16777216 | tf_op jit(solution)/shard_map/finished_grads/pallas_call | solution.py:270
  165.6 0.0 collective-permute-done.20.refs_3_
  165.6 0.0 collective-permute-start.16
  165.6 0.0 collective-permute-done.8.refs_2_
  165.7 1.6 collective-permute-start.10
  167.3 2.0 collective-permute-done.9.refs_3_
  169.3 1.5 collective-permute-start.12
  170.8 9.4 %collective-permute-done.14.refs_2_ = bf16[312,768]{1,0:T(8,128)(2,1)S(1)} collective-permute-done((bf16[312,768]{1,0:T(8,128)(2,1)}, bf16[312,768]{1,0:T(8,128)(2,1)S(1)}, u32[]{:S(2)}, u32[]{:S(2)}) %collective-permute-start.14) | collective-permute-done | bytes 479264 | tf_op jit(solution)/shard_map/ppermute | solution.py:451
  180.2 1.7 collective-permute-start.13
  182.0 0.3 collective-permute-start.11
  182.3 19.0 %other_grads.1 = (f32[2,768,1536]{2,1,0:T(8,128)}, f32[2,1536,768]{2,1,0:T(8,128)}) custom-call(s32[2]{0:T(128)} %compare_select_fusion.meta_ref, bf16[2,312,768]{2,1,0:T(8,128)(2,1)} %get-tuple-element.66.refs_0_, bf16[2,312,768]{2,1,0:T(8,128)(2,1)} %collective-permute-done.18.refs_1_, ...), custom_call_target="tpu_custom_call", output_to_operand_aliasing={{0}: (7, {}), {1}: (8, {})} | custom-call | flops 11777605632 | bytes 26214400 | tf_op jit(solution)/shard_map/other_grads/pallas_call | solution.py:314
  201.3 1.8 collective-permute-start.15
  203.1 0.0 collective-permute-done.10.refs_4_
  203.1 0.3 collective-permute-start.17
  203.4 0.0 collective-permute-done.12.refs_6_
  203.4 7.1 %collective-permute-done.13.refs_7_ = bf16[312,768]{1,0:T(8,128)(2,1)} collective-permute-done((bf16[312,768]{1,0:T(8,128)(2,1)S(1)}, bf16[312,768]{1,0:T(8,128)(2,1)}, u32[]{:S(2)}, u32[]{:S(2)}) %collective-permute-start.13) | collective-permute-done | bytes 479264 | tf_op jit(solution)/shard_map/ppermute | solution.py:454
  210.4 20.4 %collective-permute-done.11.refs_5_ = bf16[2,312,768]{2,1,0:T(8,128)(2,1)S(1)} collective-permute-done((bf16[2,312,768]{2,1,0:T(8,128)(2,1)S(1)}, bf16[2,312,768]{2,1,0:T(8,128)(2,1)S(1)}, u32[]{:S(2)}, u32[]{:S(2)}) %collective-permute-start.11) | collective-permute-done | bytes 958496 | tf_op jit(solution)/shard_map/ppermute | solution.py:454
  230.9 0.9 copy-done.12
  231.8 17.4 %combine_y.1 = (bf16[2048,768]{1,0:T(8,128)(2,1)}, bf16[2048,8]{1,0:T(8,128)(2,1)}, f32[8,768]{1,0:T(8,128)}) custom-call(s32[2]{0:T(128)} %compare_select_fusion.meta_ref, bf16[2,312,768]{2,1,0:T(8,128)(2,1)} %get-tuple-element.58.refs_0_, bf16[2,312,768]{2,1,0:T(8,128)(2,1)} %copy-done.8, bf16[312,768]{1,0:T(8,128)(2,1)} %copy-done.14, ...), custom_call_target="tpu_custom_call" | custom-call | flops 7851737088 | bytes 16777216 | tf_op jit(solution)/shard_map/combine_y/pallas_call | solution.py:391
  249.2 0.0 copy-start.6
  249.2 0.0 collective-permute-start.21
  249.2 11.4 %combine_s.2.refs_3_ = bf16[2048,768]{1,0:T(8,128)(2,1)} custom-call(s32[2]{0:T(128)} %compare_select_fusion.meta_ref, bf16[2,312,768]{2,1,0:T(8,128)(2,1)} %get-tuple-element.58.refs_0_, bf16[2,312,768]{2,1,0:T(8,128)(2,1)} %copy-done.8, bf16[312,768]{1,0:T(8,128)(2,1)} %copy-done.13, bf16[312,768]{1,0:T(8,128)(2,1)} %copy-done.16, ...), custom_call_target="tpu_custom_call" | custom-call | flops 5888802816 | bytes 10485760 | tf_op jit(solution)/shard_map/combine_s/pallas_call | solution.py:428
  260.6 0.0 collective-permute-done.21
  260.7 1.6 collective-permute-start.22
  262.3 0.8 copy-done.4
  263.1 0.2 copy-done.5
  263.3 8.5 %combine_s.3 = bf16[2048,768]{1,0:T(8,128)(2,1)} custom-call(s32[2]{0:T(128)} %compare_select_fusion.meta_ref, bf16[312,768]{1,0:T(8,128)(2,1)} %copy-done.4, bf16[312,768]{1,0:T(8,128)(2,1)} %copy-done.5, f32[16,2048]{1,0:T(8,128)} %route.1.info_ref.refs_8_.refs_6_.refs_2_, bf16[2048,768]{1,0:T(8,128)(2,1)} %combine_s.2.refs_3_, ...), custom_call_target="tpu_custom_call" | custom-call | flops 1962934272 | bytes 10485760 | tf_op jit(solution)/shard_map/combine_s/pallas_call | solution.py:428
  271.7 0.6 add_bitcast_fusion
  (39 shorter events, 0.1 us)
Async XLA Ops:
  24.5 19.8 %collective-permute-start.2 = (bf16[2,312,768]{2,1,0:T(8,128)(2,1)}, bf16[2,312,768]{2,1,0:T(8,128)(2,1)}, u32[]{:S(2)}, u32[]{:S(2)}) collective-permute-start(bf16[2,312,768]{2,1,0:T(8,128)(2,1)} %get-tuple-element.45), channel_id=1, source_target_pairs={{0,1},{1,0},{2,3},{3,2},{4,5},{5,4},{6,7},{7,6}} | collective-permute-start | bytes 2875400 | tf_op jit(solution)/shard_map/ppermute | solution.py:451
  26.9 71.2 %collective-permute-start.6 = (bf16[1024,768]{1,0:T(8,128)(2,1)S(1)}, bf16[1024,768]{1,0:T(8,128)(2,1)}, u32[]{:S(2)}, u32[]{:S(2)}) collective-permute-start(bf16[1024,768]{1,0:T(8,128)(2,1)S(1)} %dynamic-slice_bitcast_fusion), channel_id=1, source_target_pairs={{0,4},{4,0},{1,5},{5,1},{2,6},{6,2},{3,7},{7,3}} | collective-permute-start | bytes 4718600 | tf_op jit(solution)/shard_map/ppermute | solution.py:454
  30.9 68.8 %collective-permute-start.5 = (bf16[768,1024]{1,0:T(8,128)(2,1)S(1)}, bf16[768,1024]{1,0:T(8,128)(2,1)}, u32[]{:S(2)}, u32[]{:S(2)}) collective-permute-start(bf16[768,1024]{1,0:T(8,128)(2,1)S(1)} %dynamic-slice_bitcast_fusion.1), channel_id=1, source_target_pairs={{0,4},{4,0},{1,5},{5,1},{2,6},{6,2},{3,7},{7,3}} | collective-permute-start | bytes 4718600 | tf_op jit(solution)/shard_map/ppermute | solution.py:454
  39.9 24.3 %collective-permute-start = (bf16[2,312,768]{2,1,0:T(8,128)(2,1)}, bf16[2,312,768]{2,1,0:T(8,128)(2,1)S(1)}, u32[]{:S(2)}, u32[]{:S(2)}) collective-permute-start(bf16[2,312,768]{2,1,0:T(8,128)(2,1)} %get-tuple-element.42), channel_id=1, source_target_pairs={{0,2},{1,3},{2,0},{3,1},{4,6},{5,7},{6,4},{7,5}} | collective-permute-start | bytes 2875400 | tf_op jit(solution)/shard_map/ppermute | solution.py:451
  41.9 41.5 %collective-permute-start.1 = (bf16[2,312,768]{2,1,0:T(8,128)(2,1)}, bf16[2,312,768]{2,1,0:T(8,128)(2,1)S(1)}, u32[]{:S(2)}, u32[]{:S(2)}) collective-permute-start(bf16[2,312,768]{2,1,0:T(8,128)(2,1)} %get-tuple-element.43), channel_id=1, source_target_pairs={{0,3},{1,2},{2,1},{3,0},{4,7},{5,6},{6,5},{7,4}} | collective-permute-start | bytes 2875400 | tf_op jit(solution)/shard_map/ppermute | solution.py:451
  44.3 72.4 %collective-permute-start.4 = (bf16[512,768]{1,0:T(8,128)(2,1)S(1)}, bf16[512,768]{1,0:T(8,128)(2,1)S(1)}, u32[]{:S(2)}, u32[]{:S(2)}) collective-permute-start(bf16[512,768]{1,0:T(8,128)(2,1)S(1)} %dynamic-slice_bitcast_fusion.2), channel_id=1, source_target_pairs={{0,4},{4,0},{1,5},{5,1},{2,6},{6,2},{3,7},{7,3}} | collective-permute-start | bytes 2359304 | tf_op jit(solution)/shard_map/ppermute | solution.py:454
  64.2 20.0 %copy-start.2 = (bf16[2,312,768]{2,1,0:T(8,128)(2,1)}, bf16[2,312,768]{2,1,0:T(8,128)(2,1)S(1)}, u32[]{:S(2)}) copy-start(bf16[2,312,768]{2,1,0:T(8,128)(2,1)S(1)} %collective-permute-done.pa) | copy-start | bytes 2875396
  64.2 67.7 %collective-permute-start.3 = (bf16[768,512]{1,0:T(8,128)(2,1)S(1)}, bf16[768,512]{1,0:T(8,128)(2,1)S(1)}, u32[]{:S(2)}, u32[]{:S(2)}) collective-permute-start(bf16[768,512]{1,0:T(8,128)(2,1)S(1)} %dynamic-slice_bitcast_fusion.3), channel_id=1, source_target_pairs={{0,4},{4,0},{1,5},{5,1},{2,6},{6,2},{3,7},{7,3}} | collective-permute-start | bytes 2359304 | tf_op jit(solution)/shard_map/ppermute | solution.py:454
  83.3 1.0 copy-start.3
  83.3 64.0 %collective-permute-start.18 = (bf16[2,312,768]{2,1,0:T(8,128)(2,1)}, bf16[2,312,768]{2,1,0:T(8,128)(2,1)}, u32[]{:S(2)}, u32[]{:S(2)}) collective-permute-start(bf16[2,312,768]{2,1,0:T(8,128)(2,1)} %get-tuple-element.67), channel_id=1, source_target_pairs={{0,1},{1,0},{2,3},{3,2},{4,5},{5,4},{6,7},{7,6}} | collective-permute-start | bytes 2875400 | tf_op jit(solution)/shard_map/ppermute | solution.py:451
  98.1 49.4 %collective-permute-start.19 = (bf16[2,312,768]{2,1,0:T(8,128)(2,1)}, bf16[2,312,768]{2,1,0:T(8,128)(2,1)S(1)}, u32[]{:S(2)}, u32[]{:S(2)}) collective-permute-start(bf16[2,312,768]{2,1,0:T(8,128)(2,1)} %get-tuple-element.68), channel_id=1, source_target_pairs={{0,2},{1,3},{2,0},{3,1},{4,6},{5,7},{6,4},{7,5}} | collective-permute-start | bytes 2875400 | tf_op jit(solution)/shard_map/ppermute | solution.py:451
  99.7 65.8 %collective-permute-start.20 = (bf16[2,312,768]{2,1,0:T(8,128)(2,1)}, bf16[2,312,768]{2,1,0:T(8,128)(2,1)S(1)}, u32[]{:S(2)}, u32[]{:S(2)}) collective-permute-start(bf16[2,312,768]{2,1,0:T(8,128)(2,1)} %get-tuple-element.69), channel_id=1, source_target_pairs={{0,3},{1,2},{2,1},{3,0},{4,7},{5,6},{6,5},{7,4}} | collective-permute-start | bytes 2875400 | tf_op jit(solution)/shard_map/ppermute | solution.py:451
  116.6 15.2 %copy-start = (bf16[512,768]{1,0:T(8,128)(2,1)}, bf16[512,768]{1,0:T(8,128)(2,1)S(1)}, u32[]{:S(2)}) copy-start(bf16[512,768]{1,0:T(8,128)(2,1)S(1)} %collective-permute-done.4.wo_ref) | copy-start | bytes 2359300
  131.9 0.9 copy-start.1
  139.3 42.6 %collective-permute-start.7 = (bf16[2,312,768]{2,1,0:T(8,128)(2,1)}, bf16[2,312,768]{2,1,0:T(8,128)(2,1)S(1)}, u32[]{:S(2)}, u32[]{:S(2)}) collective-permute-start(bf16[2,312,768]{2,1,0:T(8,128)(2,1)} %get-tuple-element.59), channel_id=1, source_target_pairs={{0,1},{1,0},{2,3},{3,2},{4,5},{5,4},{6,7},{7,6}} | collective-permute-start | bytes 2875400 | tf_op jit(solution)/shard_map/ppermute | solution.py:451
  145.7 20.0 %collective-permute-start.8 = (bf16[312,768]{1,0:T(8,128)(2,1)}, bf16[312,768]{1,0:T(8,128)(2,1)S(1)}, u32[]{:S(2)}, u32[]{:S(2)}) collective-permute-start(bf16[312,768]{1,0:T(8,128)(2,1)} %get-tuple-element.60), channel_id=1, source_target_pairs={{0,2},{1,3},{2,0},{3,1},{4,6},{5,7},{6,4},{7,5}} | collective-permute-start | bytes 1437704 | tf_op jit(solution)/shard_map/ppermute | solution.py:451
  147.4 21.9 %collective-permute-start.9 = (bf16[312,768]{1,0:T(8,128)(2,1)}, bf16[312,768]{1,0:T(8,128)(2,1)S(1)}, u32[]{:S(2)}, u32[]{:S(2)}) collective-permute-start(bf16[312,768]{1,0:T(8,128)(2,1)} %get-tuple-element.61), channel_id=1, source_target_pairs={{0,3},{1,2},{2,1},{3,0},{4,7},{5,6},{6,5},{7,4}} | collective-permute-start | bytes 1437704 | tf_op jit(solution)/shard_map/ppermute | solution.py:451
  147.5 8.6 %copy-start.9 = (bf16[2,312,768]{2,1,0:T(8,128)(2,1)}, bf16[2,312,768]{2,1,0:T(8,128)(2,1)S(1)}, u32[]{:S(2)}) copy-start(bf16[2,312,768]{2,1,0:T(8,128)(2,1)S(1)} %collective-permute-done.19.refs_2_) | copy-start | bytes 2875396
  147.5 32.7 %collective-permute-start.14 = (bf16[312,768]{1,0:T(8,128)(2,1)}, bf16[312,768]{1,0:T(8,128)(2,1)S(1)}, u32[]{:S(2)}, u32[]{:S(2)}) collective-permute-start(bf16[312,768]{1,0:T(8,128)(2,1)} %get-tuple-element.63), channel_id=1, source_target_pairs={{0,2},{1,3},{2,0},{3,1},{4,6},{5,7},{6,4},{7,5}} | collective-permute-start | bytes 1437704 | tf_op jit(solution)/shard_map/ppermute | solution.py:451
  156.1 9.5 %copy-start.17 = (bf16[312,768]{1,0:T(8,128)(2,1)S(1)}, bf16[312,768]{1,0:T(8,128)(2,1)}, u32[]{:S(2)}) copy-start(bf16[312,768]{1,0:T(8,128)(2,1)} %get-tuple-element.64) | copy-start | bytes 1437700
  156.1 9.5 %copy-start.7 = (bf16[2,312,768]{2,1,0:T(8,128)(2,1)S(1)}, bf16[2,312,768]{2,1,0:T(8,128)(2,1)}, u32[]{:S(2)}) copy-start(bf16[2,312,768]{2,1,0:T(8,128)(2,1)} %get-tuple-element.58.refs_0_) | copy-start | bytes 2875396
  165.6 16.7 %copy-start.10 = (bf16[2,312,768]{2,1,0:T(8,128)(2,1)}, bf16[2,312,768]{2,1,0:T(8,128)(2,1)S(1)}, u32[]{:S(2)}) copy-start(bf16[2,312,768]{2,1,0:T(8,128)(2,1)S(1)} %collective-permute-done.20.refs_3_) | copy-start | bytes 2875396
  165.6 35.7 %collective-permute-start.16 = (bf16[312,768]{1,0:T(8,128)(2,1)S(1)}, bf16[312,768]{1,0:T(8,128)(2,1)S(1)}, u32[]{:S(2)}, u32[]{:S(2)}) collective-permute-start(bf16[312,768]{1,0:T(8,128)(2,1)S(1)} %copy-done.17), channel_id=1, source_target_pairs={{0,3},{1,2},{2,1},{3,0},{4,7},{5,6},{6,5},{7,4}} | collective-permute-start | bytes 1437704 | tf_op jit(solution)/shard_map/ppermute | solution.py:451
  165.6 35.6 %copy-start.14 = (bf16[312,768]{1,0:T(8,128)(2,1)}, bf16[312,768]{1,0:T(8,128)(2,1)S(1)}, u32[]{:S(2)}) copy-start(bf16[312,768]{1,0:T(8,128)(2,1)S(1)} %collective-permute-done.8.refs_2_) | copy-start | bytes 1437700
  165.7 37.4 %collective-permute-start.10 = (bf16[2,312,768]{2,1,0:T(8,128)(2,1)S(1)}, bf16[2,312,768]{2,1,0:T(8,128)(2,1)S(1)}, u32[]{:S(2)}, u32[]{:S(2)}) collective-permute-start(bf16[2,312,768]{2,1,0:T(8,128)(2,1)S(1)} %copy-done.7), channel_id=1, source_target_pairs={{0,4},{4,0},{1,5},{5,1},{2,6},{6,2},{3,7},{7,3}} | collective-permute-start | bytes 2875400 | tf_op jit(solution)/shard_map/ppermute | solution.py:454
  169.3 32.0 %copy-start.15 = (bf16[312,768]{1,0:T(8,128)(2,1)}, bf16[312,768]{1,0:T(8,128)(2,1)S(1)}, u32[]{:S(2)}) copy-start(bf16[312,768]{1,0:T(8,128)(2,1)S(1)} %collective-permute-done.9.refs_3_) | copy-start | bytes 1437700
  169.3 34.1 %collective-permute-start.12 = (bf16[312,768]{1,0:T(8,128)(2,1)S(1)}, bf16[312,768]{1,0:T(8,128)(2,1)}, u32[]{:S(2)}, u32[]{:S(2)}) collective-permute-start(bf16[312,768]{1,0:T(8,128)(2,1)S(1)} %collective-permute-done.8.refs_2_), channel_id=1, source_target_pairs={{0,4},{4,0},{1,5},{5,1},{2,6},{6,2},{3,7},{7,3}} | collective-permute-start | bytes 1437704 | tf_op jit(solution)/shard_map/ppermute | solution.py:454
  180.2 21.1 %copy-start.13 = (bf16[312,768]{1,0:T(8,128)(2,1)}, bf16[312,768]{1,0:T(8,128)(2,1)S(1)}, u32[]{:S(2)}) copy-start(bf16[312,768]{1,0:T(8,128)(2,1)S(1)} %collective-permute-done.14.refs_2_) | copy-start | bytes 1437700
  180.2 30.2 %collective-permute-start.13 = (bf16[312,768]{1,0:T(8,128)(2,1)S(1)}, bf16[312,768]{1,0:T(8,128)(2,1)}, u32[]{:S(2)}, u32[]{:S(2)}) collective-permute-start(bf16[312,768]{1,0:T(8,128)(2,1)S(1)} %collective-permute-done.9.refs_3_), channel_id=1, source_target_pairs={{0,4},{4,0},{1,5},{5,1},{2,6},{6,2},{3,7},{7,3}} | collective-permute-start | bytes 1437704 | tf_op jit(solution)/shard_map/ppermute | solution.py:454
  182.0 19.3 %copy-start.8 = (bf16[2,312,768]{2,1,0:T(8,128)(2,1)}, bf16[2,312,768]{2,1,0:T(8,128)(2,1)S(1)}, u32[]{:S(2)}) copy-start(bf16[2,312,768]{2,1,0:T(8,128)(2,1)S(1)} %collective-permute-done.7.refs_1_) | copy-start | bytes 2875396
  182.0 48.9 %collective-permute-start.11 = (bf16[2,312,768]{2,1,0:T(8,128)(2,1)S(1)}, bf16[2,312,768]{2,1,0:T(8,128)(2,1)S(1)}, u32[]{:S(2)}, u32[]{:S(2)}) collective-permute-start(bf16[2,312,768]{2,1,0:T(8,128)(2,1)S(1)} %collective-permute-done.7.refs_1_), channel_id=1, source_target_pairs={{0,4},{4,0},{1,5},{5,1},{2,6},{6,2},{3,7},{7,3}} | collective-permute-start | bytes 2875400 | tf_op jit(solution)/shard_map/ppermute | solution.py:454
  201.3 47.9 %copy-start.16 = (bf16[312,768]{1,0:T(8,128)(2,1)}, bf16[312,768]{1,0:T(8,128)(2,1)S(1)}, u32[]{:S(2)}) copy-start(bf16[312,768]{1,0:T(8,128)(2,1)S(1)} %collective-permute-done.16.refs_3_) | copy-start | bytes 1437700
  201.3 61.0 %collective-permute-start.15 = (bf16[312,768]{1,0:T(8,128)(2,1)S(1)}, bf16[312,768]{1,0:T(8,128)(2,1)S(1)}, u32[]{:S(2)}, u32[]{:S(2)}) collective-permute-start(bf16[312,768]{1,0:T(8,128)(2,1)S(1)} %collective-permute-done.14.refs_2_), channel_id=1, source_target_pairs={{0,4},{4,0},{1,5},{5,1},{2,6},{6,2},{3,7},{7,3}} | collective-permute-start | bytes 1437704 | tf_op jit(solution)/shard_map/ppermute | solution.py:454
  203.1 27.8 %copy-start.11 = (bf16[2,312,768]{2,1,0:T(8,128)(2,1)}, bf16[2,312,768]{2,1,0:T(8,128)(2,1)S(1)}, u32[]{:S(2)}) copy-start(bf16[2,312,768]{2,1,0:T(8,128)(2,1)S(1)} %collective-permute-done.10.refs_4_) | copy-start | bytes 2875396
  203.1 59.2 %collective-permute-start.17 = (bf16[312,768]{1,0:T(8,128)(2,1)S(1)}, bf16[312,768]{1,0:T(8,128)(2,1)S(1)}, u32[]{:S(2)}, u32[]{:S(2)}) collective-permute-start(bf16[312,768]{1,0:T(8,128)(2,1)S(1)} %collective-permute-done.16.refs_3_), channel_id=1, source_target_pairs={{0,4},{4,0},{1,5},{5,1},{2,6},{6,2},{3,7},{7,3}} | collective-permute-start | bytes 1437704 | tf_op jit(solution)/shard_map/ppermute | solution.py:454
  230.9 0.9 copy-start.12
  249.2 11.5 %copy-start.6 = (f32[8,768]{1,0:T(8,128)S(1)}, f32[8,768]{1,0:T(8,128)}, u32[]{:S(2)}) copy-start(f32[8,768]{1,0:T(8,128)} %get-tuple-element.78) | copy-start | bytes 73732
  249.2 11.4 %collective-permute-start.21 = (f32[8,768]{1,0:T(8,128)}, f32[8,768]{1,0:T(8,128)S(1)}, u32[]{:S(2)}, u32[]{:S(2)}) collective-permute-start(f32[8,768]{1,0:T(8,128)} %get-tuple-element.78), channel_id=1, source_target_pairs={{0,1},{1,0},{2,3},{3,2},{4,5},{5,4},{6,7},{7,6}} | collective-permute-start | bytes 73736 | tf_op jit(solution)/shard_map/ppermute | solution.py:451
  260.7 11.1 %collective-permute-start.22 = (f32[8,768]{1,0:T(8,128)S(1)}, f32[8,768]{1,0:T(8,128)S(1)}, u32[]{:S(2)}, u32[]{:S(2)}) collective-permute-start(f32[8,768]{1,0:T(8,128)S(1)} %add.14), channel_id=1, source_target_pairs={{0,2},{1,3},{2,0},{3,1},{4,6},{5,7},{6,4},{7,5}} | collective-permute-start | bytes 73736 | tf_op jit(solution)/shard_map/ppermute | solution.py:451
  262.3 0.8 copy-start.4
  262.3 1.0 copy-start.5

commit v4 on v3

--- a/solution.py
+++ b/solution.py
@@ -257,33 +257,31 @@
     )(x, dy, wi, wo, y_in, s_in)
 
 
-def finished_grads(meta, x, dy, h, da, n_local, chunk, lo, hi, so_far):
+def finished_grads(meta, x, dy, h, da, n_local, chunk):
     rows, d_model = x.shape
     width = h.shape[1]
 
-    def body(meta_ref, x_ref, dy_ref, h_ref, da_ref, *refs):
-        gi, go = refs[-2:]
+    def body(meta_ref, x_ref, dy_ref, h_ref, da_ref, gi, go):
         gi[0] = tn(x_ref[...], da_ref[...])
         go[0] = tn(h_ref[...], dy_ref[...])
 
-    hid = pl.BlockSpec((rows, chunk), lambda c, m: (0, c + lo))
+    hid = pl.BlockSpec((rows, chunk), lambda c, m: (0, c))
     return pl.pallas_call(
         body,
         grid_spec=pltpu.PrefetchScalarGridSpec(
             num_scalar_prefetch=1,
-            grid=(hi - lo,),
-            in_specs=[whole((rows, d_model))] * 2 + [hid] * 2 + [pl.BlockSpec(memory_space=pl.ANY)] * len(so_far),
+            grid=(width // chunk,),
+            in_specs=[whole((rows, d_model))] * 2 + [hid] * 2,
             out_specs=[
-                pl.BlockSpec((1, d_model, chunk), lambda c, m: (m[0], 0, c + lo)),
-                pl.BlockSpec((1, chunk, d_model), lambda c, m: (m[0], c + lo, 0)),
+                pl.BlockSpec((1, d_model, chunk), lambda c, m: (m[0], 0, c)),
+                pl.BlockSpec((1, chunk, d_model), lambda c, m: (m[0], c, 0)),
             ],
         ),
         out_shape=[shape((n_local, d_model, width), F32), shape((n_local, width, d_model), F32)],
-        input_output_aliases={5 + i: i for i in range(len(so_far))},
-        compiler_params=params(1),
-        cost_estimate=cost(4 * rows * (hi - lo) * chunk * d_model, 8 * (hi - lo)),
+        compiler_params=params(1),
+        cost_estimate=cost(4 * rows * width * d_model, 25),
         name="finished_grads",
-    )(meta, x, dy, h, da, *so_far)
+    )(meta, x, dy, h, da)
 
 
 def other_grads(meta, pairs, w_in, w_out, grad_w_in, grad_w_out, chunk):
@@ -482,7 +480,7 @@
         part = own_half(meta, f0, f1, w_in, w_out, chunk, 0, ())
         h, da, y, s, x, dy = own_half(meta, f2, f3, w_in, w_out, chunk, 1, part)
         y, s = far_half(x, dy, *far_w["a"], y, s, chunk, None, False)
-        grads = finished_grads(meta, x, dy, h, da, w_in.shape[0], chunk, 0, 1, ())
+        grads = finished_grads(meta, x, dy, h, da, w_in.shape[0], chunk)
         ys0, ys1 = far_half(x, dy, *far_w["b"], y, s, chunk, 0, True)
         y2, y3, s2, s3 = far_half(x, dy, *far_w["b"], y, s, chunk, 1, False)
 
@@ -494,13 +492,12 @@
         y_twin = [(twin0, 0), (twin1, 0), to_twin(y2), to_twin(y3)]
         s_twin = [(twin0, 1), (twin1, 1), to_twin(s2), to_twin(s3)]
 
-        grads = finished_grads(meta, x, dy, h, da, w_in.shape[0], chunk, 1, 3, grads)
         grad_w_in, grad_w_out = other_grads(meta, (g0, g1, g2, g3), w_in, w_out, *grads, chunk)
 
         y_all = {(d, k): v for k, side in enumerate((y_mine, y_twin)) for d, v in enumerate(side)}
         s_all = {(d, k): v for k, side in enumerate((s_mine, s_twin)) for d, v in enumerate(side)}
         s_late = {key: s_all.pop(key) for key in ((2, 1), (3, 1))}
-        moe_out, dlog, dwg = combine_y(meta, y_all, info, tokens, grad_out, n_tok // 4)
+        moe_out, dlog, dwg = combine_y(meta, y_all, info, tokens, grad_out, n_tok // 2)
         dwg = dwg + to_ep(dwg, 1)
         dwg = dwg + to_ep(dwg, 2)
         so_far = combine_s(meta, s_all, info, (), n_tok // 2)

time: 273 us -> 267 us (0.978)
  Pallas kernels: 162 us -> 157 us
    ppermute x13, waiting for transfers between devices: 33.1 us -> 37.9 us  [to_ep(): return lax.ppermute(v, 'ep', [(i, i ^ d) for i in range(ep_size)])]
    ppermute x10, waiting for transfers between devices: 42.7 us -> 38 us  [to_twin(): return lax.ppermute(v, 'tp', [(0, 1), (1, 0)])]
    pallas_call x2 -> x1, Pallas kernels: 16.3 us -> 11.7 us  [finished_grads(): pl.pallas_call(body, grid_spec=pltpu.PrefetchScalarGridSpec(num_scalar_pr...]
  transfers between devices with their start and end apart: 23 -> 23, of which waited for: 7 -> 7; matrix products, arithmetic and copies ran while one was open for 2% -> 2% of each run, Pallas kernels for 51% -> 50%
where the time goes in v4:
time: 267 us
  Pallas kernels  157 us (59%)
  waiting for transfers between devices  75.9 us (28%)
  starting transfers between devices  23.2 us (9%)
  local copies, waits for them, and re-layouts  8.27 us (3%)
    ppermute x10, waiting for transfers between devices, to_twin(): return lax.ppermute(v, 'tp', [(0, 1), (1, 0)])  38 us
    ppermute x13, waiting for transfers between devices, to_ep(): return lax.ppermute(v, 'ep', [(i, i ^ d) for i in range(ep_size)])  37.9 us
    pallas_call x3, Pallas kernels, far_half(): pl.pallas_call(body, grid=grid, in_specs=[full, full, pl.BlockSpec((d_mod...  29.2 us
    pallas_call x2, Pallas kernels, dispatch(): pl.pallas_call(body, grid_spec=pltpu.PrefetchScalarGridSpec(num_scalar_pr...  28.2 us
    pallas_call x2, Pallas kernels, own_half(): pl.pallas_call(body, grid_spec=pltpu.PrefetchScalarGridSpec(num_scalar_pr...  27.6 us
    pallas_call x2, Pallas kernels, combine_s(): pl.pallas_call(body, grid_spec=pltpu.PrefetchScalarGridSpec(num_scalar_pr...  20.2 us
    pallas_call x1, Pallas kernels, other_grads(): pl.pallas_call(body, grid_spec=pltpu.PrefetchScalarGridSpec(num_scalar_pr...  19 us
    pallas_call x1, Pallas kernels, combine_y(): pl.pallas_call(body, grid_spec=pltpu.PrefetchScalarGridSpec(num_scalar_pr...  17.4 us
  transfers between devices with their start and end apart: 23, of which 7 were waited for; matrix products, arithmetic and copies ran while one was open for 2% of the time, Pallas kernels for 50%

profile of v4, /device:TPU:0, one launch (start us, length us, event | category | flops | bytes accessed | tf_op | source)
XLA Modules:
  0.0 266.8 jit_solution(14455377563703155026)
XLA Ops:
  0.6 0.6 compare_select_fusion.meta_ref
  1.2 4.0 %route.1.info_ref.refs_8_.refs_6_.refs_2_ = f32[16,2048]{1,0:T(8,128)} custom-call(s32[1,2048]{1,0:T(1,128)} %bitcast.14, bf16[2048,768]{1,0:T(8,128)(2,1)} %refs_9_.1, bf16[8,768]{1,0:T(8,128)(2,1)} %bitcast.12), custom_call_target="tpu_custom_call" | custom-call | flops 2000000000 | bytes 3145728 | tf_op jit(solution)/shard_map/route/pallas_call | solution.py:87
  5.2 19.3 %dispatch.3 = (bf16[2,312,768]{2,1,0:T(8,128)(2,1)}, bf16[2,312,768]{2,1,0:T(8,128)(2,1)}, bf16[2,312,768]{2,1,0:T(8,128)(2,1)}, bf16[2,312,768]{2,1,0:T(8,128)(...) custom-call(s32[2]{0:T(128)} %compare_select_fusion.meta_ref, ...), custom_call_target="tpu_custom_call" | custom-call | flops 11777605632 | bytes 20971520 | tf_op jit(solution)/shard_map/dispatch/pallas_call | solution.py:129
  24.5 0.9 collective-permute-start.2
  25.4 1.5 dynamic-slice_bitcast_fusion.1
  26.9 2.5 collective-permute-start.5
  29.4 1.5 dynamic-slice_bitcast_fusion
  30.9 0.0 collective-permute-start.6
  30.9 8.9 %dispatch.2 = (bf16[2,312,768]{2,1,0:T(8,128)(2,1)}, bf16[2,312,768]{2,1,0:T(8,128)(2,1)}) custom-call(s32[2]{0:T(128)} %compare_select_fusion.meta_ref, f32[16,2048]{1,0:T(8,128)} %route.1.info_ref.refs_8_.refs_6_.refs_2_, bf16[2048,768]{1,0:T(8,128)(2,1)} %refs_9_.1, bf16[2048,768]{1,0:T(8,128)(2,1)} %refs_10_.1), custom_call_target="tpu_custom_call" | custom-call | flops 3925868544 | bytes 12582912 | tf_op jit(solution)/shard_map/dispatch/pallas_call | solution.py:129
  39.9 2.0 collective-permute-start
  41.9 1.2 dynamic-slice_bitcast_fusion.3
  43.1 1.2 dynamic-slice_bitcast_fusion.2
  44.3 1.5 collective-permute-start.3
  45.8 13.8 %own_half.2 = (bf16[1248,1536]{1,0:T(8,128)(2,1)}, bf16[1248,1536]{1,0:T(8,128)(2,1)}, f32[1248,768]{1,0:T(8,128)}, f32[1248,768]{1,0:T(8,128)}, bf16[1248,768]{1,0:T(8,128)(2,1)}, /*index=5*/bf16[1248,768]{1,0:T(8,128)(2,1)}) custom-call(s32[2]{0:T(128)} %compare_select_fusion.meta_ref, bf16[2,312,768]{2,1,0:T(8,128)(2,1)} %get-tuple-element.42.pa, ...), custom_call_target="tpu_custom_call" | custom-call | flops 5888802816 | bytes 20971520 | tf_op jit(solution)/shard_map/own_half/pallas_call | solution.py:178
  59.6 4.6 %collective-permute-done.pa = bf16[2,312,768]{2,1,0:T(8,128)(2,1)S(1)} collective-permute-done((bf16[2,312,768]{2,1,0:T(8,128)(2,1)}, bf16[2,312,768]{2,1,0:T(8,128)(2,1)S(1)}, u32[]{:S(2)}, u32[]{:S(2)}) %collective-permute-start) | collective-permute-done | bytes 958496 | tf_op jit(solution)/shard_map/ppermute | solution.py:449
  64.2 2.0 collective-permute-start.4
  66.2 17.1 %collective-permute-done.1.pb = bf16[2,312,768]{2,1,0:T(8,128)(2,1)S(1)} collective-permute-done((bf16[2,312,768]{2,1,0:T(8,128)(2,1)}, bf16[2,312,768]{2,1,0:T(8,128)(2,1)S(1)}, u32[]{:S(2)}, u32[]{:S(2)}) %collective-permute-start.1) | collective-permute-done | bytes 958496 | tf_op jit(solution)/shard_map/ppermute | solution.py:449
  83.3 0.9 collective-permute-start.18
  84.2 0.1 copy-done.3
  84.3 13.8 %own_half.3 = (bf16[1248,1536]{1,0:T(8,128)(2,1)}, bf16[1248,1536]{1,0:T(8,128)(2,1)}, f32[1248,768]{1,0:T(8,128)}, f32[1248,768]{1,0:T(8,128)}, bf16[1248,768]{1,0:T(8,128)(2,1)}, /*index=5*/bf16[1248,768]{1,0:T(8,128)(2,1)}) custom-call(s32[2]{0:T(128)} %compare_select_fusion.meta_ref, ...), custom_call_target="tpu_custom_call", output_to_operand_aliasing={{0}: (5, {}), {1}: (6, {}), {2}: (7, {}), {3}: (8, {}), {4}... | custom-call | flops 5888802816 | bytes 20971520 | tf_op jit(solution)/shard_map/own_half/pallas_call | solution.py:178
  98.1 0.0 collective-permute-done.5.wi_ref
  98.1 1.6 collective-permute-start.19
  99.7 0.6 collective-permute-start.20
  100.4 16.2 %far_half.3 = (f32[1248,768]{1,0:T(8,128)}, f32[1248,768]{1,0:T(8,128)}) custom-call(bf16[1248,768]{1,0:T(8,128)(2,1)} %get-tuple-element.50.x_ref, bf16[1248,768]{1,0:T(8,128)(2,1)} %get-tuple-element.51.dy_ref, bf16[768,1024]{1,0:T(8,128)(2,1)} %collective-permute-done.5.wi_ref, bf16[1024,768]{1,0:T(8,128)(2,1)} %collective-permute-done.6.wo_ref, ...), custom_call_target="tpu_custom_call" | custom-call | flops 7851737088 | bytes 10485760 | tf_op jit(solution)/shard_map/far_half/pallas_call | solution.py:241
  116.6 0.0 copy-start
  116.6 15.2 %collective-permute-done.4.wo_ref = bf16[512,768]{1,0:T(8,128)(2,1)S(1)} collective-permute-done((bf16[512,768]{1,0:T(8,128)(2,1)S(1)}, bf16[512,768]{1,0:T(8,128)(2,1)S(1)}, u32[]{:S(2)}, u32[]{:S(2)}) %collective-permute-start.4) | collective-permute-done | bytes 786464 | tf_op jit(solution)/shard_map/ppermute | solution.py:452
  131.9 0.9 copy-done.1
  132.8 6.6 %far_half.4 = (bf16[2,312,768]{2,1,0:T(8,128)(2,1)}, bf16[2,312,768]{2,1,0:T(8,128)(2,1)}) custom-call(bf16[1248,768]{1,0:T(8,128)(2,1)} %get-tuple-element.50.x_ref, bf16[1248,768]{1,0:T(8,128)(2,1)} %get-tuple-element.51.dy_ref, bf16[768,512]{1,0:T(8,128)(2,1)} %copy-done, bf16[512,768]{1,0:T(8,128)(2,1)} %copy-done.1, f32[1248,768]{1,0:T(8,128)} %get-tuple-element.54.y0, ...), custom_call_target="tpu_custom_call" | custom-call | flops 1962934272 | bytes 10485760 | tf_op jit(solution)/shard_map/far_half/pallas_call | solution.py:241
  139.4 0.0 collective-permute-start.7
  139.4 6.3 %far_half.5 = (bf16[312,768]{1,0:T(8,128)(2,1)}, bf16[312,768]{1,0:T(8,128)(2,1)}, bf16[312,768]{1,0:T(8,128)(2,1)}, bf16[312,768]{1,0:T(8,128)(2,1)}) custom-call(bf16[1248,768]{1,0:T(8,128)(2,1)} %get-tuple-element.50.x_ref, bf16[1248,768]{1,0:T(8,128)(2,1)} %get-tuple-element.51.dy_ref, bf16[768,512]{1,0:T(8,128)(2,1)} %copy-done, ...), custom_call_target="tpu_custom_call" | custom-call | flops 1962934272 | bytes 10485760 | tf_op jit(solution)/shard_map/far_half/pallas_call | solution.py:241
  145.7 1.7 collective-permute-start.8
  147.4 0.0 collective-permute-done.18.refs_1_
  147.4 0.2 collective-permute-start.9
  147.6 1.7 collective-permute-start.14
  149.3 11.7 %finished_grads.1 = (f32[2,768,1536]{2,1,0:T(8,128)}, f32[2,1536,768]{2,1,0:T(8,128)}) custom-call(s32[2]{0:T(128)} %compare_select_fusion.meta_ref, bf16[1248,768]{1,0:T(8,128)(2,1)} %get-tuple-element.50.x_ref, bf16[1248,768]{1,0:T(8,128)(2,1)} %get-tuple-element.51.dy_ref, bf16[1248,1536]{1,0:T(8,128)(2,1)} %get-tuple-element.68.h_ref, ...), custom_call_target="tpu_custom_call" | custom-call | flops 5888802816 | bytes 26214400 | tf_op jit(solution)/shard_map/finished_grads/pallas_call | solution.py:269
  161.0 0.0 collective-permute-done.20.refs_3_
  161.0 0.0 copy-start.10
  161.0 1.5 collective-permute-start.10
  162.6 0.0 collective-permute-start.16
  162.6 6.7 %collective-permute-done.9.refs_3_ = bf16[312,768]{1,0:T(8,128)(2,1)S(1)} collective-permute-done((bf16[312,768]{1,0:T(8,128)(2,1)}, bf16[312,768]{1,0:T(8,128)(2,1)S(1)}, u32[]{:S(2)}, u32[]{:S(2)}) %collective-permute-start.9) | collective-permute-done | bytes 479264 | tf_op jit(solution)/shard_map/ppermute | solution.py:449
  169.4 1.5 collective-permute-start.12
  170.9 9.4 %collective-permute-done.14.refs_2_ = bf16[312,768]{1,0:T(8,128)(2,1)S(1)} collective-permute-done((bf16[312,768]{1,0:T(8,128)(2,1)}, bf16[312,768]{1,0:T(8,128)(2,1)S(1)}, u32[]{:S(2)}, u32[]{:S(2)}) %collective-permute-start.14) | collective-permute-done | bytes 479264 | tf_op jit(solution)/shard_map/ppermute | solution.py:449
  180.3 1.7 collective-permute-start.13
  182.0 0.0 collective-permute-done.7.refs_1_
  182.0 0.3 collective-permute-start.11
  182.3 19.0 %other_grads.1 = (f32[2,768,1536]{2,1,0:T(8,128)}, f32[2,1536,768]{2,1,0:T(8,128)}) custom-call(s32[2]{0:T(128)} %compare_select_fusion.meta_ref, bf16[2,312,768]{2,1,0:T(8,128)(2,1)} %get-tuple-element.64.refs_0_, bf16[2,312,768]{2,1,0:T(8,128)(2,1)} %collective-permute-done.18.refs_1_, ...), custom_call_target="tpu_custom_call", output_to_operand_aliasing={{0}: (7, {}), {1}: (8, {})} | custom-call | flops 11777605632 | bytes 26214400 | tf_op jit(solution)/shard_map/other_grads/pallas_call | solution.py:312
  201.3 0.0 collective-permute-done.16.refs_3_
  201.4 1.8 collective-permute-start.15
  203.1 0.3 collective-permute-start.17
  203.4 0.0 collective-permute-done.12.refs_6_
  203.4 2.4 collective-permute-done.13.refs_7_
  205.8 20.4 %collective-permute-done.11.refs_5_ = bf16[2,312,768]{2,1,0:T(8,128)(2,1)S(1)} collective-permute-done((bf16[2,312,768]{2,1,0:T(8,128)(2,1)S(1)}, bf16[2,312,768]{2,1,0:T(8,128)(2,1)S(1)}, u32[]{:S(2)}, u32[]{:S(2)}) %collective-permute-start.11) | collective-permute-done | bytes 958496 | tf_op jit(solution)/shard_map/ppermute | solution.py:452
  226.2 0.9 copy-done.12
  227.2 17.4 %combine_y.1 = (bf16[2048,768]{1,0:T(8,128)(2,1)}, bf16[2048,8]{1,0:T(8,128)(2,1)}, f32[8,768]{1,0:T(8,128)}) custom-call(s32[2]{0:T(128)} %compare_select_fusion.meta_ref, bf16[2,312,768]{2,1,0:T(8,128)(2,1)} %get-tuple-element.56.refs_0_, bf16[2,312,768]{2,1,0:T(8,128)(2,1)} %copy-done.8, bf16[312,768]{1,0:T(8,128)(2,1)} %copy-done.14, ...), custom_call_target="tpu_custom_call" | custom-call | flops 7851737088 | bytes 16777216 | tf_op jit(solution)/shard_map/combine_y/pallas_call | solution.py:389
  244.6 0.0 copy-start.6
  244.6 0.0 collective-permute-start.21
  244.6 11.7 %combine_s.2.refs_3_ = bf16[2048,768]{1,0:T(8,128)(2,1)} custom-call(s32[2]{0:T(128)} %compare_select_fusion.meta_ref, bf16[2,312,768]{2,1,0:T(8,128)(2,1)} %get-tuple-element.56.refs_0_, bf16[2,312,768]{2,1,0:T(8,128)(2,1)} %copy-done.8, bf16[312,768]{1,0:T(8,128)(2,1)} %copy-done.13, bf16[312,768]{1,0:T(8,128)(2,1)} %copy-done.16, ...), custom_call_target="tpu_custom_call" | custom-call | flops 5888802816 | bytes 10485760 | tf_op jit(solution)/shard_map/combine_s/pallas_call | solution.py:426
  256.4 0.0 collective-permute-done.21
  256.4 0.3 collective-permute-start.22
  256.7 0.0 collective-permute-done.15.refs_0_
  256.8 0.8 copy-done.4
  257.5 0.2 copy-done.5
  257.7 8.5 %combine_s.3 = bf16[2048,768]{1,0:T(8,128)(2,1)} custom-call(s32[2]{0:T(128)} %compare_select_fusion.meta_ref, bf16[312,768]{1,0:T(8,128)(2,1)} %copy-done.4, bf16[312,768]{1,0:T(8,128)(2,1)} %copy-done.5, f32[16,2048]{1,0:T(8,128)} %route.1.info_ref.refs_8_.refs_6_.refs_2_, bf16[2048,768]{1,0:T(8,128)(2,1)} %combine_s.2.refs_3_, ...), custom_call_target="tpu_custom_call" | custom-call | flops 1962934272 | bytes 10485760 | tf_op jit(solution)/shard_map/combine_s/pallas_call | solution.py:426
  266.2 0.6 add_bitcast_fusion
  (40 shorter events, 0.1 us)
Async XLA Ops:
  24.5 19.8 %collective-permute-start.2 = (bf16[2,312,768]{2,1,0:T(8,128)(2,1)}, bf16[2,312,768]{2,1,0:T(8,128)(2,1)}, u32[]{:S(2)}, u32[]{:S(2)}) collective-permute-start(bf16[2,312,768]{2,1,0:T(8,128)(2,1)} %get-tuple-element.43), channel_id=1, source_target_pairs={{0,1},{1,0},{2,3},{3,2},{4,5},{5,4},{6,7},{7,6}} | collective-permute-start | bytes 2875400 | tf_op jit(solution)/shard_map/ppermute | solution.py:449
  26.9 71.2 %collective-permute-start.5 = (bf16[768,1024]{1,0:T(8,128)(2,1)S(1)}, bf16[768,1024]{1,0:T(8,128)(2,1)}, u32[]{:S(2)}, u32[]{:S(2)}) collective-permute-start(bf16[768,1024]{1,0:T(8,128)(2,1)S(1)} %dynamic-slice_bitcast_fusion.1), channel_id=1, source_target_pairs={{0,4},{4,0},{1,5},{5,1},{2,6},{6,2},{3,7},{7,3}} | collective-permute-start | bytes 4718600 | tf_op jit(solution)/shard_map/ppermute | solution.py:452
  30.9 68.8 %collective-permute-start.6 = (bf16[1024,768]{1,0:T(8,128)(2,1)S(1)}, bf16[1024,768]{1,0:T(8,128)(2,1)}, u32[]{:S(2)}, u32[]{:S(2)}) collective-permute-start(bf16[1024,768]{1,0:T(8,128)(2,1)S(1)} %dynamic-slice_bitcast_fusion), channel_id=1, source_target_pairs={{0,4},{4,0},{1,5},{5,1},{2,6},{6,2},{3,7},{7,3}} | collective-permute-start | bytes 4718600 | tf_op jit(solution)/shard_map/ppermute | solution.py:452
  39.9 24.3 %collective-permute-start = (bf16[2,312,768]{2,1,0:T(8,128)(2,1)}, bf16[2,312,768]{2,1,0:T(8,128)(2,1)S(1)}, u32[]{:S(2)}, u32[]{:S(2)}) collective-permute-start(bf16[2,312,768]{2,1,0:T(8,128)(2,1)} %get-tuple-element.40), channel_id=1, source_target_pairs={{0,2},{1,3},{2,0},{3,1},{4,6},{5,7},{6,4},{7,5}} | collective-permute-start | bytes 2875400 | tf_op jit(solution)/shard_map/ppermute | solution.py:449
  41.9 41.5 %collective-permute-start.1 = (bf16[2,312,768]{2,1,0:T(8,128)(2,1)}, bf16[2,312,768]{2,1,0:T(8,128)(2,1)S(1)}, u32[]{:S(2)}, u32[]{:S(2)}) collective-permute-start(bf16[2,312,768]{2,1,0:T(8,128)(2,1)} %get-tuple-element.41), channel_id=1, source_target_pairs={{0,3},{1,2},{2,1},{3,0},{4,7},{5,6},{6,5},{7,4}} | collective-permute-start | bytes 2875400 | tf_op jit(solution)/shard_map/ppermute | solution.py:449
  44.3 72.4 %collective-permute-start.3 = (bf16[768,512]{1,0:T(8,128)(2,1)S(1)}, bf16[768,512]{1,0:T(8,128)(2,1)S(1)}, u32[]{:S(2)}, u32[]{:S(2)}) collective-permute-start(bf16[768,512]{1,0:T(8,128)(2,1)S(1)} %dynamic-slice_bitcast_fusion.3), channel_id=1, source_target_pairs={{0,4},{4,0},{1,5},{5,1},{2,6},{6,2},{3,7},{7,3}} | collective-permute-start | bytes 2359304 | tf_op jit(solution)/shard_map/ppermute | solution.py:452
  64.2 20.0 %copy-start.2 = (bf16[2,312,768]{2,1,0:T(8,128)(2,1)}, bf16[2,312,768]{2,1,0:T(8,128)(2,1)S(1)}, u32[]{:S(2)}) copy-start(bf16[2,312,768]{2,1,0:T(8,128)(2,1)S(1)} %collective-permute-done.pa) | copy-start | bytes 2875396
  64.2 67.7 %collective-permute-start.4 = (bf16[512,768]{1,0:T(8,128)(2,1)S(1)}, bf16[512,768]{1,0:T(8,128)(2,1)S(1)}, u32[]{:S(2)}, u32[]{:S(2)}) collective-permute-start(bf16[512,768]{1,0:T(8,128)(2,1)S(1)} %dynamic-slice_bitcast_fusion.2), channel_id=1, source_target_pairs={{0,4},{4,0},{1,5},{5,1},{2,6},{6,2},{3,7},{7,3}} | collective-permute-start | bytes 2359304 | tf_op jit(solution)/shard_map/ppermute | solution.py:452
  83.3 1.0 copy-start.3
  83.3 64.1 %collective-permute-start.18 = (bf16[2,312,768]{2,1,0:T(8,128)(2,1)}, bf16[2,312,768]{2,1,0:T(8,128)(2,1)}, u32[]{:S(2)}, u32[]{:S(2)}) collective-permute-start(bf16[2,312,768]{2,1,0:T(8,128)(2,1)} %get-tuple-element.65), channel_id=1, source_target_pairs={{0,1},{1,0},{2,3},{3,2},{4,5},{5,4},{6,7},{7,6}} | collective-permute-start | bytes 2875400 | tf_op jit(solution)/shard_map/ppermute | solution.py:449
  98.1 49.5 %collective-permute-start.19 = (bf16[2,312,768]{2,1,0:T(8,128)(2,1)}, bf16[2,312,768]{2,1,0:T(8,128)(2,1)S(1)}, u32[]{:S(2)}, u32[]{:S(2)}) collective-permute-start(bf16[2,312,768]{2,1,0:T(8,128)(2,1)} %get-tuple-element.66), channel_id=1, source_target_pairs={{0,2},{1,3},{2,0},{3,1},{4,6},{5,7},{6,4},{7,5}} | collective-permute-start | bytes 2875400 | tf_op jit(solution)/shard_map/ppermute | solution.py:449
  99.7 61.3 %collective-permute-start.20 = (bf16[2,312,768]{2,1,0:T(8,128)(2,1)}, bf16[2,312,768]{2,1,0:T(8,128)(2,1)S(1)}, u32[]{:S(2)}, u32[]{:S(2)}) collective-permute-start(bf16[2,312,768]{2,1,0:T(8,128)(2,1)} %get-tuple-element.67), channel_id=1, source_target_pairs={{0,3},{1,2},{2,1},{3,0},{4,7},{5,6},{6,5},{7,4}} | collective-permute-start | bytes 2875400 | tf_op jit(solution)/shard_map/ppermute | solution.py:449
  116.6 15.2 %copy-start = (bf16[768,512]{1,0:T(8,128)(2,1)}, bf16[768,512]{1,0:T(8,128)(2,1)S(1)}, u32[]{:S(2)}) copy-start(bf16[768,512]{1,0:T(8,128)(2,1)S(1)} %collective-permute-done.3.wi_ref) | copy-start | bytes 2359300
  131.9 0.9 copy-start.1
  139.4 42.6 %collective-permute-start.7 = (bf16[2,312,768]{2,1,0:T(8,128)(2,1)}, bf16[2,312,768]{2,1,0:T(8,128)(2,1)S(1)}, u32[]{:S(2)}, u32[]{:S(2)}) collective-permute-start(bf16[2,312,768]{2,1,0:T(8,128)(2,1)} %get-tuple-element.57), channel_id=1, source_target_pairs={{0,1},{1,0},{2,3},{3,2},{4,5},{5,4},{6,7},{7,6}} | collective-permute-start | bytes 2875400 | tf_op jit(solution)/shard_map/ppermute | solution.py:449
  145.7 16.9 %collective-permute-start.8 = (bf16[312,768]{1,0:T(8,128)(2,1)}, bf16[312,768]{1,0:T(8,128)(2,1)S(1)}, u32[]{:S(2)}, u32[]{:S(2)}) collective-permute-start(bf16[312,768]{1,0:T(8,128)(2,1)} %get-tuple-element.58), channel_id=1, source_target_pairs={{0,2},{1,3},{2,0},{3,1},{4,6},{5,7},{6,4},{7,5}} | collective-permute-start | bytes 1437704 | tf_op jit(solution)/shard_map/ppermute | solution.py:449
  147.4 21.9 %collective-permute-start.9 = (bf16[312,768]{1,0:T(8,128)(2,1)}, bf16[312,768]{1,0:T(8,128)(2,1)S(1)}, u32[]{:S(2)}, u32[]{:S(2)}) collective-permute-start(bf16[312,768]{1,0:T(8,128)(2,1)} %get-tuple-element.59), channel_id=1, source_target_pairs={{0,3},{1,2},{2,1},{3,0},{4,7},{5,6},{6,5},{7,4}} | collective-permute-start | bytes 1437704 | tf_op jit(solution)/shard_map/ppermute | solution.py:449
  147.6 13.4 %copy-start.9 = (bf16[2,312,768]{2,1,0:T(8,128)(2,1)}, bf16[2,312,768]{2,1,0:T(8,128)(2,1)S(1)}, u32[]{:S(2)}) copy-start(bf16[2,312,768]{2,1,0:T(8,128)(2,1)S(1)} %collective-permute-done.19.refs_2_) | copy-start | bytes 2875396
  147.6 32.7 %collective-permute-start.14 = (bf16[312,768]{1,0:T(8,128)(2,1)}, bf16[312,768]{1,0:T(8,128)(2,1)S(1)}, u32[]{:S(2)}, u32[]{:S(2)}) collective-permute-start(bf16[312,768]{1,0:T(8,128)(2,1)} %get-tuple-element.61), channel_id=1, source_target_pairs={{0,2},{1,3},{2,0},{3,1},{4,6},{5,7},{6,4},{7,5}} | collective-permute-start | bytes 1437704 | tf_op jit(solution)/shard_map/ppermute | solution.py:449
  149.3 11.7 %copy-start.7 = (bf16[2,312,768]{2,1,0:T(8,128)(2,1)S(1)}, bf16[2,312,768]{2,1,0:T(8,128)(2,1)}, u32[]{:S(2)}) copy-start(bf16[2,312,768]{2,1,0:T(8,128)(2,1)} %get-tuple-element.56.refs_0_) | copy-start | bytes 2875396
  149.3 13.3 %copy-start.17 = (bf16[312,768]{1,0:T(8,128)(2,1)S(1)}, bf16[312,768]{1,0:T(8,128)(2,1)}, u32[]{:S(2)}) copy-start(bf16[312,768]{1,0:T(8,128)(2,1)} %get-tuple-element.62) | copy-start | bytes 1437700
  161.0 21.3 %copy-start.10 = (bf16[2,312,768]{2,1,0:T(8,128)(2,1)}, bf16[2,312,768]{2,1,0:T(8,128)(2,1)S(1)}, u32[]{:S(2)}) copy-start(bf16[2,312,768]{2,1,0:T(8,128)(2,1)S(1)} %collective-permute-done.20.refs_3_) | copy-start | bytes 2875396
  161.0 42.1 %collective-permute-start.10 = (bf16[2,312,768]{2,1,0:T(8,128)(2,1)S(1)}, bf16[2,312,768]{2,1,0:T(8,128)(2,1)S(1)}, u32[]{:S(2)}, u32[]{:S(2)}) collective-permute-start(bf16[2,312,768]{2,1,0:T(8,128)(2,1)S(1)} %copy-done.7), channel_id=1, source_target_pairs={{0,4},{4,0},{1,5},{5,1},{2,6},{6,2},{3,7},{7,3}} | collective-permute-start | bytes 2875400 | tf_op jit(solution)/shard_map/ppermute | solution.py:452
  162.6 38.8 %copy-start.14 = (bf16[312,768]{1,0:T(8,128)(2,1)}, bf16[312,768]{1,0:T(8,128)(2,1)S(1)}, u32[]{:S(2)}) copy-start(bf16[312,768]{1,0:T(8,128)(2,1)S(1)} %collective-permute-done.8.refs_2_) | copy-start | bytes 1437700
  162.6 38.8 %collective-permute-start.16 = (bf16[312,768]{1,0:T(8,128)(2,1)S(1)}, bf16[312,768]{1,0:T(8,128)(2,1)S(1)}, u32[]{:S(2)}, u32[]{:S(2)}) collective-permute-start(bf16[312,768]{1,0:T(8,128)(2,1)S(1)} %copy-done.17), channel_id=1, source_target_pairs={{0,3},{1,2},{2,1},{3,0},{4,7},{5,6},{6,5},{7,4}} | collective-permute-start | bytes 1437704 | tf_op jit(solution)/shard_map/ppermute | solution.py:449
  169.3 32.0 %copy-start.15 = (bf16[312,768]{1,0:T(8,128)(2,1)}, bf16[312,768]{1,0:T(8,128)(2,1)S(1)}, u32[]{:S(2)}) copy-start(bf16[312,768]{1,0:T(8,128)(2,1)S(1)} %collective-permute-done.9.refs_3_) | copy-start | bytes 1437700
  169.4 34.1 %collective-permute-start.12 = (bf16[312,768]{1,0:T(8,128)(2,1)S(1)}, bf16[312,768]{1,0:T(8,128)(2,1)S(1)}, u32[]{:S(2)}, u32[]{:S(2)}) collective-permute-start(bf16[312,768]{1,0:T(8,128)(2,1)S(1)} %collective-permute-done.8.refs_2_), channel_id=1, source_target_pairs={{0,4},{4,0},{1,5},{5,1},{2,6},{6,2},{3,7},{7,3}} | collective-permute-start | bytes 1437704 | tf_op jit(solution)/shard_map/ppermute | solution.py:452
  180.3 21.1 %copy-start.13 = (bf16[312,768]{1,0:T(8,128)(2,1)}, bf16[312,768]{1,0:T(8,128)(2,1)S(1)}, u32[]{:S(2)}) copy-start(bf16[312,768]{1,0:T(8,128)(2,1)S(1)} %collective-permute-done.14.refs_2_) | copy-start | bytes 1437700
  180.3 25.5 %collective-permute-start.13 = (bf16[312,768]{1,0:T(8,128)(2,1)S(1)}, bf16[312,768]{1,0:T(8,128)(2,1)}, u32[]{:S(2)}, u32[]{:S(2)}) collective-permute-start(bf16[312,768]{1,0:T(8,128)(2,1)S(1)} %collective-permute-done.9.refs_3_), channel_id=1, source_target_pairs={{0,4},{4,0},{1,5},{5,1},{2,6},{6,2},{3,7},{7,3}} | collective-permute-start | bytes 1437704 | tf_op jit(solution)/shard_map/ppermute | solution.py:452
  182.0 19.3 %copy-start.8 = (bf16[2,312,768]{2,1,0:T(8,128)(2,1)}, bf16[2,312,768]{2,1,0:T(8,128)(2,1)S(1)}, u32[]{:S(2)}) copy-start(bf16[2,312,768]{2,1,0:T(8,128)(2,1)S(1)} %collective-permute-done.7.refs_1_) | copy-start | bytes 2875396
  182.0 44.2 %collective-permute-start.11 = (bf16[2,312,768]{2,1,0:T(8,128)(2,1)S(1)}, bf16[2,312,768]{2,1,0:T(8,128)(2,1)S(1)}, u32[]{:S(2)}, u32[]{:S(2)}) collective-permute-start(bf16[2,312,768]{2,1,0:T(8,128)(2,1)S(1)} %collective-permute-done.7.refs_1_), channel_id=1, source_target_pairs={{0,4},{4,0},{1,5},{5,1},{2,6},{6,2},{3,7},{7,3}} | collective-permute-start | bytes 2875400 | tf_op jit(solution)/shard_map/ppermute | solution.py:452
  201.4 43.2 %copy-start.16 = (bf16[312,768]{1,0:T(8,128)(2,1)}, bf16[312,768]{1,0:T(8,128)(2,1)S(1)}, u32[]{:S(2)}) copy-start(bf16[312,768]{1,0:T(8,128)(2,1)S(1)} %collective-permute-done.16.refs_3_) | copy-start | bytes 1437700
  201.4 55.4 %collective-permute-start.15 = (bf16[312,768]{1,0:T(8,128)(2,1)S(1)}, bf16[312,768]{1,0:T(8,128)(2,1)S(1)}, u32[]{:S(2)}, u32[]{:S(2)}) collective-permute-start(bf16[312,768]{1,0:T(8,128)(2,1)S(1)} %collective-permute-done.14.refs_2_), channel_id=1, source_target_pairs={{0,4},{4,0},{1,5},{5,1},{2,6},{6,2},{3,7},{7,3}} | collective-permute-start | bytes 1437704 | tf_op jit(solution)/shard_map/ppermute | solution.py:452
  203.1 23.1 %copy-start.11 = (bf16[2,312,768]{2,1,0:T(8,128)(2,1)}, bf16[2,312,768]{2,1,0:T(8,128)(2,1)S(1)}, u32[]{:S(2)}) copy-start(bf16[2,312,768]{2,1,0:T(8,128)(2,1)S(1)} %collective-permute-done.10.refs_4_) | copy-start | bytes 2875396
  203.1 53.6 %collective-permute-start.17 = (bf16[312,768]{1,0:T(8,128)(2,1)S(1)}, bf16[312,768]{1,0:T(8,128)(2,1)S(1)}, u32[]{:S(2)}, u32[]{:S(2)}) collective-permute-start(bf16[312,768]{1,0:T(8,128)(2,1)S(1)} %collective-permute-done.16.refs_3_), channel_id=1, source_target_pairs={{0,4},{4,0},{1,5},{5,1},{2,6},{6,2},{3,7},{7,3}} | collective-permute-start | bytes 1437704 | tf_op jit(solution)/shard_map/ppermute | solution.py:452
  203.4 22.8 %copy-start.18 = (bf16[312,768]{1,0:T(8,128)(2,1)}, bf16[312,768]{1,0:T(8,128)(2,1)S(1)}, u32[]{:S(2)}) copy-start(bf16[312,768]{1,0:T(8,128)(2,1)S(1)} %collective-permute-done.12.refs_6_) | copy-start | bytes 1437700
  226.2 0.9 copy-start.12
  244.6 11.8 %copy-start.6 = (f32[8,768]{1,0:T(8,128)S(1)}, f32[8,768]{1,0:T(8,128)}, u32[]{:S(2)}) copy-start(f32[8,768]{1,0:T(8,128)} %get-tuple-element.74) | copy-start | bytes 73732
  244.6 11.8 %collective-permute-start.21 = (f32[8,768]{1,0:T(8,128)}, f32[8,768]{1,0:T(8,128)S(1)}, u32[]{:S(2)}, u32[]{:S(2)}) collective-permute-start(f32[8,768]{1,0:T(8,128)} %get-tuple-element.74), channel_id=1, source_target_pairs={{0,1},{1,0},{2,3},{3,2},{4,5},{5,4},{6,7},{7,6}} | collective-permute-start | bytes 73736 | tf_op jit(solution)/shard_map/ppermute | solution.py:449
  256.4 9.8 %collective-permute-start.22 = (f32[8,768]{1,0:T(8,128)S(1)}, f32[8,768]{1,0:T(8,128)S(1)}, u32[]{:S(2)}, u32[]{:S(2)}) collective-permute-start(f32[8,768]{1,0:T(8,128)S(1)} %add.14), channel_id=1, source_target_pairs={{0,2},{1,3},{2,0},{3,1},{4,6},{5,7},{6,4},{7,5}} | collective-permute-start | bytes 73736 | tf_op jit(solution)/shard_map/ppermute | solution.py:449
  256.7 0.8 copy-start.4
  256.8 0.9 copy-start.5

commit v5 on v4

--- a/solution.py
+++ b/solution.py
@@ -10,7 +10,7 @@
 GELU_K = 0.044715
 BF16 = jnp.bfloat16
 F32 = jnp.float32
-VMEM_LIMIT = 56 * 2**20
+VMEM_LIMIT = 67043328
 INFO_ROWS = 16
 
 
@@ -144,18 +144,17 @@
 def own_half(meta, pair_a, pair_b, w_in, w_out, chunk, group, so_far):
     _, d_model, width = w_in.shape
     cap = pair_a.shape[1]
-    rows = 2 * cap
 
     def body(meta_ref, pa, pb, wi, wo, *refs):
         h_ref, da_ref, y_ref, s_ref, x_ref, dy_ref = refs[-6:]
-        c = pl.program_id(0)
-
-        @pl.when(c == 0)
-        def _():
-            x_ref[:cap] = pa[0]
-            x_ref[cap:] = pb[0]
-            dy_ref[:cap] = pa[1]
-            dy_ref[cap:] = pb[1]
+        p, c = pl.program_id(0), pl.program_id(1)
+
+        for source, pair in enumerate((pa, pb)):
+
+            @pl.when(jnp.logical_and(c == 0, p == source))
+            def _():
+                x_ref[...] = pair[0]
+                dy_ref[...] = pair[1]
 
         h, da = hidden_grads(x_ref[...], dy_ref[...], wi[0], wo[0])
         h_ref[...] = h
@@ -173,36 +172,35 @@
             y_ref[...] += y
             s_ref[...] += s
 
-    hid = pl.BlockSpec((rows, chunk), lambda c, m: (group, c))
-    full = pl.BlockSpec((rows, d_model), lambda c, m: (group, 0))
+    hid = pl.BlockSpec((cap, chunk), lambda p, c, m: (2 * group + p, c))
+    full = pl.BlockSpec((cap, d_model), lambda p, c, m: (2 * group + p, 0))
     return pl.pallas_call(
         body,
         grid_spec=pltpu.PrefetchScalarGridSpec(
             num_scalar_prefetch=1,
-            grid=(width // chunk,),
+            grid=(2, width // chunk),
             in_specs=[
                 whole(pair_a.shape),
                 whole(pair_a.shape),
-                pl.BlockSpec((1, d_model, chunk), lambda c, m: (m[0], 0, c)),
-                pl.BlockSpec((1, chunk, d_model), lambda c, m: (m[0], c, 0)),
+                pl.BlockSpec((1, d_model, chunk), lambda p, c, m: (m[0], 0, c)),
+                pl.BlockSpec((1, chunk, d_model), lambda p, c, m: (m[0], c, 0)),
             ]
             + [pl.BlockSpec(memory_space=pl.ANY)] * len(so_far),
             out_specs=[hid, hid] + [full] * 4,
         ),
-        out_shape=[shape((2 * rows, width))] * 2
-        + [shape((2 * rows, d_model), F32)] * 2
-        + [shape((2 * rows, d_model))] * 2,
+        out_shape=[shape((4 * cap, width))] * 2
+        + [shape((4 * cap, d_model), F32)] * 2
+        + [shape((4 * cap, d_model))] * 2,
         input_output_aliases={5 + i: i for i in range(len(so_far))},
-        compiler_params=params(1),
-        cost_estimate=cost(8 * rows * width * d_model, 20),
+        compiler_params=params(2),
+        cost_estimate=cost(16 * cap * width * d_model, 20),
         name="own_half",
     )(meta, pair_a, pair_b, w_in, w_out, *so_far)
 
 
 def far_half(x, dy, wi, wo, y_in, s_in, chunk, group, joined):
     d_model = x.shape[1]
-    rows = x.shape[0] // 2
-    cap = rows // 2
+    cap = x.shape[0] // 4
     width = wi.shape[1]
     steps = width // chunk
 
@@ -210,14 +208,19 @@
         h, da = hidden_grads(x_ref[...], dy_ref[...], wi_ref[...], wo_ref[...])
         y = nn(h, wo_ref[...])
         s = nt(da, wi_ref[...])
+        c = pl.program_id(1)
         if group is not None:
+            y = (y0[...] + y).astype(BF16)
+            s = (s0[...] + s).astype(BF16)
             for p in range(2):
-                part = slice(p * cap, (p + 1) * cap)
-                y_out, s_out = (outs[p].at[0], outs[p].at[1]) if joined else (outs[p], outs[2 + p])
-                y_out[...] = (y0[part] + y[part]).astype(BF16)
-                s_out[...] = (s0[part] + s[part]).astype(BF16)
+
+                @pl.when(pl.program_id(0) == p)
+                def _():
+                    y_out, s_out = (outs[p].at[0], outs[p].at[1]) if joined else (outs[p], outs[2 + p])
+                    y_out[...] = y
+                    s_out[...] = s
+
             return
-        c = pl.program_id(1)
 
         @pl.when(c == 0)
         def _():
@@ -229,30 +232,28 @@
             outs[0][...] += y
             outs[1][...] += s
 
+    blocks, base = (4, 0) if group is None else (2, 2 * group)
+    full = pl.BlockSpec((cap, d_model), lambda p, c: (base + p, 0))
     if group is None:
-        grid = (2, steps)
-        full = pl.BlockSpec((rows, d_model), lambda g, c: (g, 0))
         out_specs, out_shape = [full] * 2, [shape(x.shape, F32)] * 2
     else:
-        grid = (1, steps)
-        full = pl.BlockSpec((rows, d_model), lambda g, c: (group, 0))
         dims, count = ((2, cap, d_model), 2) if joined else ((cap, d_model), 4)
         out_specs, out_shape = [whole(dims)] * count, [shape(dims)] * count
     return pl.pallas_call(
         body,
-        grid=grid,
+        grid=(blocks, steps),
         in_specs=[
             full,
             full,
-            pl.BlockSpec((d_model, chunk), lambda g, c: (0, c)),
-            pl.BlockSpec((chunk, d_model), lambda g, c: (c, 0)),
+            pl.BlockSpec((d_model, chunk), lambda p, c: (0, c)),
+            pl.BlockSpec((chunk, d_model), lambda p, c: (c, 0)),
             full,
             full,
         ],
         out_specs=out_specs,
         out_shape=out_shape,
         compiler_params=params(2),
-        cost_estimate=cost(8 * rows * grid[0] * width * d_model, 10),
+        cost_estimate=cost(8 * cap * blocks * width * d_model, 10),
         name="far_half",
     )(x, dy, wi, wo, y_in, s_in)
 
@@ -356,7 +357,7 @@
     return specs, arrays, arrays[0].shape[-2]
 
 
-def combine_y(meta, pieces, info, tokens, grad_out, block):
+def combine_y(meta, pieces, info, so_far, tokens, grad_out, block):
     n_tok, d_model = tokens.shape
     keys = list(pieces)
     specs, rows, cap = piece_specs(pieces.values())
@@ -364,10 +365,10 @@
 
     def body(meta_ref, *refs):
         parts = refs[: len(keys)]
-        info_ref, x_ref, gy_ref, out_ref, dlog_ref, dwg_ref, all_rows = refs[len(keys) :]
+        info_ref, so_ref, x_ref, gy_ref, out_ref, dlog_ref, dwg_ref, all_rows = refs[len(keys) :]
         stack_rows(parts, all_rows)
         info_v = info_ref[...].T
-        y = nn(piece_pick(meta_ref, info_v, keys, cap), all_rows[...])
+        y = nn(piece_pick(meta_ref, info_v, keys, cap), all_rows[...]) + so_ref[...].astype(F32)
         gate = info_v[:, 1:2]
         prob = info_v[:, 8:16]
         hot = info_v[:, 2:3] == lax.broadcasted_iota(jnp.int32, prob.shape, 1).astype(F32)
@@ -392,7 +393,7 @@
             num_scalar_prefetch=1,
             grid=(n_tok // block,),
             in_specs=specs
-            + [pl.BlockSpec((INFO_ROWS, block), lambda b, m: (0, b)), tok, tok],
+            + [pl.BlockSpec((INFO_ROWS, block), lambda b, m: (0, b)), tok, tok, tok],
             out_specs=[tok, pl.BlockSpec((block, n_experts), lambda b, m: (b, 0)), whole((n_experts, d_model))],
             scratch_shapes=[pltpu.VMEM((cap * len(keys), d_model), BF16)],
         ),
@@ -400,7 +401,7 @@
         compiler_params=params(1),
         cost_estimate=cost(2 * n_tok * cap * len(keys) * d_model, 16),
         name="combine_y",
-    )(meta, *rows, info, tokens, grad_out)
+    )(meta, *rows, info, so_far, tokens, grad_out)
 
 
 def combine_s(meta, pieces, info, extra, block):
@@ -497,7 +498,9 @@
         y_all = {(d, k): v for k, side in enumerate((y_mine, y_twin)) for d, v in enumerate(side)}
         s_all = {(d, k): v for k, side in enumerate((s_mine, s_twin)) for d, v in enumerate(side)}
         s_late = {key: s_all.pop(key) for key in ((2, 1), (3, 1))}
-        moe_out, dlog, dwg = combine_y(meta, y_all, info, tokens, grad_out, n_tok // 2)
+        y_late = {key: y_all.pop(key) for key in ((1, 1), (2, 1), (3, 1))}
+        y_first = combine_s(meta, y_all, info, (), n_tok // 2)
+        moe_out, dlog, dwg = combine_y(meta, y_late, info, y_first, tokens, grad_out, n_tok // 2)
         dwg = dwg + to_ep(dwg, 1)
         dwg = dwg + to_ep(dwg, 2)
         so_far = combine_s(meta, s_all, info, (), n_tok // 2)

time: 267 us -> 263 us (0.985)
  waiting for transfers between devices: 75.9 us -> 60.2 us
  Pallas kernels: 157 us -> 166 us
    ppermute x10, waiting for transfers between devices: 38 us -> 24.9 us  [to_twin(): return lax.ppermute(v, 'tp', [(0, 1), (1, 0)])]
    pallas_call x2 -> x3, Pallas kernels: 20.2 us -> 30.4 us  [combine_s(): pl.pallas_call(body, grid_spec=pltpu.PrefetchScalarGridSpec(num_scalar_pr...]
    pallas_call x1, Pallas kernels: 17.4 us -> 12.3 us  [combine_y(): pl.pallas_call(body, grid_spec=pltpu.PrefetchScalarGridSpec(num_scalar_pr...]
    unnamed x38 -> x0, local copies, waits for them, and re-layouts: 2.86 us -> none
  transfers between devices with their start and end apart: 23 -> 23, of which waited for: 7 -> 6; matrix products, arithmetic and copies ran while one was open for 2% -> 4% of each run, Pallas kernels for 50% -> 54%
where the time goes in v5:
time: 263 us; the launch traced here: 262 us
  Pallas kernels  166 us (63%)
  waiting for transfers between devices  60.2 us (23%)
  starting transfers between devices  22.6 us (9%)
  local copies, waits for them, and re-layouts  9.47 us (4%)
  other arithmetic  3.31 us (1%)
    ppermute x13, waiting for transfers between devices, to_ep(): return lax.ppermute(v, 'ep', [(i, i ^ d) for i in range(ep_size)])  35.4 us
    pallas_call x3, Pallas kernels, far_half(): pl.pallas_call(body, grid=(blocks, steps), in_specs=[full, full, pl.Block...  31 us
    pallas_call x3, Pallas kernels, combine_s(): pl.pallas_call(body, grid_spec=pltpu.PrefetchScalarGridSpec(num_scalar_pr...  30.4 us
    pallas_call x2, Pallas kernels, own_half(): pl.pallas_call(body, grid_spec=pltpu.PrefetchScalarGridSpec(num_scalar_pr...  29.8 us
    pallas_call x2, Pallas kernels, dispatch(): pl.pallas_call(body, grid_spec=pltpu.PrefetchScalarGridSpec(num_scalar_pr...  28.2 us
    ppermute x10, waiting for transfers between devices, to_twin(): return lax.ppermute(v, 'tp', [(0, 1), (1, 0)])  24.9 us
    pallas_call x1, Pallas kernels, other_grads(): pl.pallas_call(body, grid_spec=pltpu.PrefetchScalarGridSpec(num_scalar_pr...  18.8 us
    ppermute x10, starting transfers between devices, to_twin(): return lax.ppermute(v, 'tp', [(0, 1), (1, 0)])  13.3 us
  transfers between devices with their start and end apart: 23, of which 6 were waited for; matrix products, arithmetic and copies ran while one was open for 4% of the time, Pallas kernels for 54%

profile of v5, /device:TPU:0, one launch (start us, length us, event | category | flops | bytes accessed | tf_op | source)
XLA Modules:
  0.0 262.4 jit_solution(8966301763847740192)
XLA Ops:
  0.6 0.6 compare_select_fusion.meta_ref
  1.2 4.0 %route.1.info_ref.refs_5_.refs_3_.refs_6_.refs_2_ = f32[16,2048]{1,0:T(8,128)} custom-call(s32[1,2048]{1,0:T(1,128)} %bitcast.14, bf16[2048,768]{1,0:T(8,128)(2,1)} %refs_5_.2, bf16[8,768]{1,0:T(8,128)(2,1)} %bitcast.12), custom_call_target="tpu_custom_call" | custom-call | flops 2000000000 | bytes 3145728 | tf_op jit(solution)/shard_map/route/pallas_call | solution.py:87
  5.2 19.3 %dispatch.3 = (bf16[2,312,768]{2,1,0:T(8,128)(2,1)}, bf16[2,312,768]{2,1,0:T(8,128)(2,1)}, bf16[2,312,768]{2,1,0:T(8,128)(2,1)}, bf16[2,312,768]{2,1,0:T(8,128)(...) custom-call(s32[2]{0:T(128)} %compare_select_fusion.meta_ref, ...), custom_call_target="tpu_custom_call" | custom-call | flops 11777605632 | bytes 20971520 | tf_op jit(solution)/shard_map/dispatch/pallas_call | solution.py:129
  24.5 0.8 collective-permute-start.2
  25.3 2.7 %dynamic-slice_bitcast_fusion.1 = bf16[768,1024]{1,0:T(8,128)(2,1)} fusion(bf16[2,768,1536]{2,1,0:T(8,128)(2,1)} %refs_4_.1, s32[]{:T(128)S(6)} %select_n.11), kind=kLoop, calls=%fused_computation.1 | loop fusion | bytes 3145732 | tf_op jit(solution)/shard_map/squeeze | solution.py:468
  28.1 2.5 collective-permute-start.5
  30.6 2.7 %dynamic-slice_bitcast_fusion = bf16[1024,768]{1,0:T(8,128)(2,1)} fusion(bf16[2,1536,768]{2,1,0:T(8,128)(2,1)} %refs_5_.3, s32[]{:T(128)S(6)} %select_n.11), kind=kLoop, calls=%fused_computation | loop fusion | bytes 3145732 | tf_op jit(solution)/shard_map/squeeze | solution.py:469
  33.2 0.0 collective-permute-start.6
  33.2 8.9 %dispatch.2 = (bf16[2,312,768]{2,1,0:T(8,128)(2,1)}, bf16[2,312,768]{2,1,0:T(8,128)(2,1)}) custom-call(s32[2]{0:T(128)} %compare_select_fusion.meta_ref, f32[16,2048]{1,0:T(8,128)} %route.1.info_ref.refs_5_.refs_3_.refs_6_.refs_2_, bf16[2048,768]{1,0:T(8,128)(2,1)} %refs_5_.2, bf16[2048,768]{1,0:T(8,128)(2,1)} %refs_6_.1), custom_call_target="tpu_custom_call" | custom-call | flops 3925868544 | bytes 12582912 | tf_op jit(solution)/shard_map/dispatch/pallas_call | solution.py:129
  42.1 2.0 collective-permute-start
  44.1 0.0 collective-permute-start.1
  44.1 2.1 dynamic-slice_bitcast_fusion.3
  46.2 2.0 dynamic-slice_bitcast_fusion.2
  48.2 0.0 collective-permute-done.2.pb
  48.2 1.5 collective-permute-start.3
  49.8 14.9 %own_half.2 = (bf16[1248,1536]{1,0:T(8,128)(2,1)}, bf16[1248,1536]{1,0:T(8,128)(2,1)}, f32[1248,768]{1,0:T(8,128)}, f32[1248,768]{1,0:T(8,128)}, bf16[1248,768]{1,0:T(8,128)(2,1)}, /*index=5*/bf16[1248,768]{1,0:T(8,128)(2,1)}) custom-call(s32[2]{0:T(128)} %compare_select_fusion.meta_ref, bf16[2,312,768]{2,1,0:T(8,128)(2,1)} %get-tuple-element.42.pa, ...), custom_call_target="tpu_custom_call" | custom-call | flops 5888802816 | bytes 20971520 | tf_op jit(solution)/shard_map/own_half/pallas_call | solution.py:177
  64.7 1.9 collective-permute-done.pa
  66.5 2.0 collective-permute-start.4
  68.6 17.0 %collective-permute-done.1.pb = bf16[2,312,768]{2,1,0:T(8,128)(2,1)} collective-permute-done((bf16[2,312,768]{2,1,0:T(8,128)(2,1)}, bf16[2,312,768]{2,1,0:T(8,128)(2,1)}, u32[]{:S(2)}, u32[]{:S(2)}) %collective-permute-start.1) | collective-permute-done | bytes 958496 | tf_op jit(solution)/shard_map/ppermute | solution.py:450
  85.6 0.8 collective-permute-start.18
  86.5 14.9 %own_half.3 = (bf16[1248,1536]{1,0:T(8,128)(2,1)}, bf16[1248,1536]{1,0:T(8,128)(2,1)}, f32[1248,768]{1,0:T(8,128)}, f32[1248,768]{1,0:T(8,128)}, bf16[1248,768]{1,0:T(8,128)(2,1)}, /*index=5*/bf16[1248,768]{1,0:T(8,128)(2,1)}) custom-call(s32[2]{0:T(128)} %compare_select_fusion.meta_ref, ...), custom_call_target="tpu_custom_call", output_to_operand_aliasing={{0}: (5, {}), {1}: (6, {}), {2}: (7, {}), {3}: (8, {}), {4}... | custom-call | flops 5888802816 | bytes 20971520 | tf_op jit(solution)/shard_map/own_half/pallas_call | solution.py:177
  101.4 0.0 collective-permute-done.5.wi_ref
  101.4 1.7 collective-permute-start.19
  103.1 0.0 collective-permute-done.6.wo_ref
  103.1 0.0 collective-permute-start.20
  103.1 17.9 %far_half.3 = (f32[1248,768]{1,0:T(8,128)}, f32[1248,768]{1,0:T(8,128)}) custom-call(bf16[1248,768]{1,0:T(8,128)(2,1)} %get-tuple-element.50.x_ref, bf16[1248,768]{1,0:T(8,128)(2,1)} %get-tuple-element.51.dy_ref, bf16[768,1024]{1,0:T(8,128)(2,1)} %collective-permute-done.5.wi_ref, bf16[1024,768]{1,0:T(8,128)(2,1)} %collective-permute-done.6.wo_ref, ...), custom_call_target="tpu_custom_call" | custom-call | flops 7851737088 | bytes 10485760 | tf_op jit(solution)/shard_map/far_half/pallas_call | solution.py:242
  121.0 12.3 %collective-permute-done.4.wo_ref = bf16[512,768]{1,0:T(8,128)(2,1)} collective-permute-done((bf16[512,768]{1,0:T(8,128)(2,1)}, bf16[512,768]{1,0:T(8,128)(2,1)}, u32[]{:S(2)}, u32[]{:S(2)}) %collective-permute-start.4) | collective-permute-done | bytes 786464 | tf_op jit(solution)/shard_map/ppermute | solution.py:453
  133.4 6.6 %far_half.4 = (bf16[2,312,768]{2,1,0:T(8,128)(2,1)}, bf16[2,312,768]{2,1,0:T(8,128)(2,1)}) custom-call(bf16[1248,768]{1,0:T(8,128)(2,1)} %get-tuple-element.50.x_ref, bf16[1248,768]{1,0:T(8,128)(2,1)} %get-tuple-element.51.dy_ref, bf16[768,512]{1,0:T(8,128)(2,1)} %collective-permute-done.3.wi_ref, bf16[512,768]{1,0:T(8,128)(2,1)} %collective-permute-done.4.wo_ref, ...), custom_call_target="tpu_custom_call" | custom-call | flops 1962934272 | bytes 10485760 | tf_op jit(solution)/shard_map/far_half/pallas_call | solution.py:242
  139.9 0.0 collective-permute-start.7
  139.9 6.5 %far_half.5 = (bf16[312,768]{1,0:T(8,128)(2,1)}, bf16[312,768]{1,0:T(8,128)(2,1)}, bf16[312,768]{1,0:T(8,128)(2,1)}, bf16[312,768]{1,0:T(8,128)(2,1)}) custom-call(bf16[1248,768]{1,0:T(8,128)(2,1)} %get-tuple-element.50.x_ref, bf16[1248,768]{1,0:T(8,128)(2,1)} %get-tuple-element.51.dy_ref, bf16[768,512]{1,0:T(8,128)(2,1)} %collective-permute-done.3.wi_ref, ...), custom_call_target="tpu_custom_call" | custom-call | flops 1962934272 | bytes 10485760 | tf_op jit(solution)/shard_map/far_half/pallas_call | solution.py:242
  146.4 1.7 collective-permute-start.9
  148.1 0.0 collective-permute-done.18.refs_1_
  148.1 0.1 collective-permute-start.11
  148.3 0.0 collective-permute-done.19.refs_2_
  148.3 1.7 collective-permute-start.14
  150.0 11.6 %finished_grads.1 = (f32[2,768,1536]{2,1,0:T(8,128)}, f32[2,1536,768]{2,1,0:T(8,128)}) custom-call(s32[2]{0:T(128)} %compare_select_fusion.meta_ref, bf16[1248,768]{1,0:T(8,128)(2,1)} %get-tuple-element.50.x_ref, bf16[1248,768]{1,0:T(8,128)(2,1)} %get-tuple-element.51.dy_ref, bf16[1248,1536]{1,0:T(8,128)(2,1)} %get-tuple-element.68.h_ref, ...), custom_call_target="tpu_custom_call" | custom-call | flops 5888802816 | bytes 26214400 | tf_op jit(solution)/shard_map/finished_grads/pallas_call | solution.py:270
  161.5 0.0 collective-permute-done.20.refs_3_
  161.5 1.6 collective-permute-start.13
  163.1 0.0 collective-permute-done.9.refs_2_
  163.1 0.0 collective-permute-start.16
  163.1 6.9 %collective-permute-done.11.refs_3_ = bf16[312,768]{1,0:T(8,128)(2,1)} collective-permute-done((bf16[312,768]{1,0:T(8,128)(2,1)}, bf16[312,768]{1,0:T(8,128)(2,1)}, u32[]{:S(2)}, u32[]{:S(2)}) %collective-permute-start.11) | collective-permute-done | bytes 479264 | tf_op jit(solution)/shard_map/ppermute | solution.py:450
  170.1 1.6 collective-permute-start.10
  171.6 9.5 %collective-permute-done.14.refs_2_ = bf16[312,768]{1,0:T(8,128)(2,1)} collective-permute-done((bf16[312,768]{1,0:T(8,128)(2,1)}, bf16[312,768]{1,0:T(8,128)(2,1)}, u32[]{:S(2)}, u32[]{:S(2)}) %collective-permute-start.14) | collective-permute-done | bytes 479264 | tf_op jit(solution)/shard_map/ppermute | solution.py:450
  181.1 1.8 collective-permute-start.12
  182.9 0.0 collective-permute-done.7.refs_1_
  182.9 0.3 collective-permute-start.8
  183.1 18.8 %other_grads.1 = (f32[2,768,1536]{2,1,0:T(8,128)}, f32[2,1536,768]{2,1,0:T(8,128)}) custom-call(s32[2]{0:T(128)} %compare_select_fusion.meta_ref, bf16[2,312,768]{2,1,0:T(8,128)(2,1)} %get-tuple-element.64.refs_0_, bf16[2,312,768]{2,1,0:T(8,128)(2,1)} %collective-permute-done.18.refs_1_, ...), custom_call_target="tpu_custom_call", output_to_operand_aliasing={{0}: (7, {}), {1}: (8, {})} | custom-call | flops 11777605632 | bytes 26214400 | tf_op jit(solution)/shard_map/other_grads/pallas_call | solution.py:313
  201.9 0.0 collective-permute-done.16.refs_3_
  201.9 1.8 collective-permute-start.15
  203.7 0.3 collective-permute-start.17
  204.0 10.6 %combine_s.3.refs_4_ = bf16[2048,768]{1,0:T(8,128)(2,1)} custom-call(s32[2]{0:T(128)} %compare_select_fusion.meta_ref, bf16[2,312,768]{2,1,0:T(8,128)(2,1)} %get-tuple-element.59.refs_0_, bf16[2,312,768]{2,1,0:T(8,128)(2,1)} %collective-permute-done.7.refs_1_, bf16[312,768]{1,0:T(8,128)(2,1)} %collective-permute-done.9.refs_2_, ...), custom_call_target="tpu_custom_call" | custom-call | flops 4907335680 | bytes 10485760 | tf_op jit(solution)/shard_map/combine_s/pallas_call | solution.py:427
  214.5 0.0 collective-permute-done.10.refs_1_
  214.5 0.0 collective-permute-done.12.refs_2_
  214.6 12.5 %collective-permute-done.8.refs_0_.refs_5_ = bf16[2,312,768]{2,1,0:T(8,128)(2,1)} collective-permute-done((bf16[2,312,768]{2,1,0:T(8,128)(2,1)}, bf16[2,312,768]{2,1,0:T(8,128)(2,1)}, u32[]{:S(2)}, u32[]{:S(2)}) %collective-permute-start.8) | collective-permute-done | bytes 958496 | tf_op jit(solution)/shard_map/ppermute | solution.py:453
  227.1 12.3 %combine_y.1 = (bf16[2048,768]{1,0:T(8,128)(2,1)}, bf16[2048,8]{1,0:T(8,128)(2,1)}, f32[8,768]{1,0:T(8,128)}) custom-call(s32[2]{0:T(128)} %compare_select_fusion.meta_ref, bf16[2,312,768]{2,1,0:T(8,128)(2,1)} %collective-permute-done.8.refs_0_.refs_5_, bf16[312,768]{1,0:T(8,128)(2,1)} %collective-permute-done.10.refs_1_, ...), custom_call_target="tpu_custom_call" | custom-call | flops 2944401408 | bytes 16777216 | tf_op jit(solution)/shard_map/combine_y/pallas_call | solution.py:390
  239.4 0.0 collective-permute-start.21
  239.4 11.4 %combine_s.4.refs_3_ = bf16[2048,768]{1,0:T(8,128)(2,1)} custom-call(s32[2]{0:T(128)} %compare_select_fusion.meta_ref, bf16[2,312,768]{2,1,0:T(8,128)(2,1)} %get-tuple-element.59.refs_0_, bf16[2,312,768]{2,1,0:T(8,128)(2,1)} %collective-permute-done.7.refs_1_, bf16[312,768]{1,0:T(8,128)(2,1)} %collective-permute-done.14.refs_2_, ...), custom_call_target="tpu_custom_call" | custom-call | flops 5888802816 | bytes 10485760 | tf_op jit(solution)/shard_map/combine_s/pallas_call | solution.py:427
  250.8 0.0 collective-permute-done.21
  250.8 1.4 add.14
  252.2 0.3 collective-permute-start.22
  252.6 0.0 collective-permute-done.17.refs_1_
  252.6 8.5 %combine_s.5 = bf16[2048,768]{1,0:T(8,128)(2,1)} custom-call(s32[2]{0:T(128)} %compare_select_fusion.meta_ref, bf16[312,768]{1,0:T(8,128)(2,1)} %collective-permute-done.15.refs_0_, bf16[312,768]{1,0:T(8,128)(2,1)} %collective-permute-done.17.refs_1_, f32[16,2048]{1,0:T(8,128)} %route.1.info_ref.refs_5_.refs_3_.refs_6_.refs_2_, ...), custom_call_target="tpu_custom_call" | custom-call | flops 1962934272 | bytes 10485760 | tf_op jit(solution)/shard_map/combine_s/pallas_call | solution.py:427
  261.0 0.0 collective-permute-done.22
  261.0 1.4 add_bitcast_fusion
  (3 shorter events, 0.0 us)
Async XLA Ops:
  24.5 23.7 %collective-permute-start.2 = (bf16[2,312,768]{2,1,0:T(8,128)(2,1)}, bf16[2,312,768]{2,1,0:T(8,128)(2,1)}, u32[]{:S(2)}, u32[]{:S(2)}) collective-permute-start(bf16[2,312,768]{2,1,0:T(8,128)(2,1)} %get-tuple-element.43), channel_id=1, source_target_pairs={{0,1},{1,0},{2,3},{3,2},{4,5},{5,4},{6,7},{7,6}} | collective-permute-start | bytes 2875400 | tf_op jit(solution)/shard_map/ppermute | solution.py:450
  28.1 73.3 %collective-permute-start.5 = (bf16[768,1024]{1,0:T(8,128)(2,1)}, bf16[768,1024]{1,0:T(8,128)(2,1)}, u32[]{:S(2)}, u32[]{:S(2)}) collective-permute-start(bf16[768,1024]{1,0:T(8,128)(2,1)} %dynamic-slice_bitcast_fusion.1), channel_id=1, source_target_pairs={{0,4},{4,0},{1,5},{5,1},{2,6},{6,2},{3,7},{7,3}} | collective-permute-start | bytes 4718600 | tf_op jit(solution)/shard_map/ppermute | solution.py:453
  33.2 69.9 %collective-permute-start.6 = (bf16[1024,768]{1,0:T(8,128)(2,1)}, bf16[1024,768]{1,0:T(8,128)(2,1)}, u32[]{:S(2)}, u32[]{:S(2)}) collective-permute-start(bf16[1024,768]{1,0:T(8,128)(2,1)} %dynamic-slice_bitcast_fusion), channel_id=1, source_target_pairs={{0,4},{4,0},{1,5},{5,1},{2,6},{6,2},{3,7},{7,3}} | collective-permute-start | bytes 4718600 | tf_op jit(solution)/shard_map/ppermute | solution.py:453
  42.1 24.4 %collective-permute-start = (bf16[2,312,768]{2,1,0:T(8,128)(2,1)}, bf16[2,312,768]{2,1,0:T(8,128)(2,1)}, u32[]{:S(2)}, u32[]{:S(2)}) collective-permute-start(bf16[2,312,768]{2,1,0:T(8,128)(2,1)} %get-tuple-element.40), channel_id=1, source_target_pairs={{0,2},{1,3},{2,0},{3,1},{4,6},{5,7},{6,4},{7,5}} | collective-permute-start | bytes 2875400 | tf_op jit(solution)/shard_map/ppermute | solution.py:450
  44.1 41.5 %collective-permute-start.1 = (bf16[2,312,768]{2,1,0:T(8,128)(2,1)}, bf16[2,312,768]{2,1,0:T(8,128)(2,1)}, u32[]{:S(2)}, u32[]{:S(2)}) collective-permute-start(bf16[2,312,768]{2,1,0:T(8,128)(2,1)} %get-tuple-element.41), channel_id=1, source_target_pairs={{0,3},{1,2},{2,1},{3,0},{4,7},{5,6},{6,5},{7,4}} | collective-permute-start | bytes 2875400 | tf_op jit(solution)/shard_map/ppermute | solution.py:450
  48.2 72.8 %collective-permute-start.3 = (bf16[768,512]{1,0:T(8,128)(2,1)}, bf16[768,512]{1,0:T(8,128)(2,1)}, u32[]{:S(2)}, u32[]{:S(2)}) collective-permute-start(bf16[768,512]{1,0:T(8,128)(2,1)} %dynamic-slice_bitcast_fusion.3), channel_id=1, source_target_pairs={{0,4},{4,0},{1,5},{5,1},{2,6},{6,2},{3,7},{7,3}} | collective-permute-start | bytes 2359304 | tf_op jit(solution)/shard_map/ppermute | solution.py:453
  66.5 66.8 %collective-permute-start.4 = (bf16[512,768]{1,0:T(8,128)(2,1)}, bf16[512,768]{1,0:T(8,128)(2,1)}, u32[]{:S(2)}, u32[]{:S(2)}) collective-permute-start(bf16[512,768]{1,0:T(8,128)(2,1)} %dynamic-slice_bitcast_fusion.2), channel_id=1, source_target_pairs={{0,4},{4,0},{1,5},{5,1},{2,6},{6,2},{3,7},{7,3}} | collective-permute-start | bytes 2359304 | tf_op jit(solution)/shard_map/ppermute | solution.py:453
  85.6 62.5 %collective-permute-start.18 = (bf16[2,312,768]{2,1,0:T(8,128)(2,1)}, bf16[2,312,768]{2,1,0:T(8,128)(2,1)}, u32[]{:S(2)}, u32[]{:S(2)}) collective-permute-start(bf16[2,312,768]{2,1,0:T(8,128)(2,1)} %get-tuple-element.65), channel_id=1, source_target_pairs={{0,1},{1,0},{2,3},{3,2},{4,5},{5,4},{6,7},{7,6}} | collective-permute-start | bytes 2875400 | tf_op jit(solution)/shard_map/ppermute | solution.py:450
  101.4 46.9 %collective-permute-start.19 = (bf16[2,312,768]{2,1,0:T(8,128)(2,1)}, bf16[2,312,768]{2,1,0:T(8,128)(2,1)}, u32[]{:S(2)}, u32[]{:S(2)}) collective-permute-start(bf16[2,312,768]{2,1,0:T(8,128)(2,1)} %get-tuple-element.66), channel_id=1, source_target_pairs={{0,2},{1,3},{2,0},{3,1},{4,6},{5,7},{6,4},{7,5}} | collective-permute-start | bytes 2875400 | tf_op jit(solution)/shard_map/ppermute | solution.py:450
  103.1 58.4 %collective-permute-start.20 = (bf16[2,312,768]{2,1,0:T(8,128)(2,1)}, bf16[2,312,768]{2,1,0:T(8,128)(2,1)}, u32[]{:S(2)}, u32[]{:S(2)}) collective-permute-start(bf16[2,312,768]{2,1,0:T(8,128)(2,1)} %get-tuple-element.67), channel_id=1, source_target_pairs={{0,3},{1,2},{2,1},{3,0},{4,7},{5,6},{6,5},{7,4}} | collective-permute-start | bytes 2875400 | tf_op jit(solution)/shard_map/ppermute | solution.py:450
  139.9 43.0 %collective-permute-start.7 = (bf16[2,312,768]{2,1,0:T(8,128)(2,1)}, bf16[2,312,768]{2,1,0:T(8,128)(2,1)}, u32[]{:S(2)}, u32[]{:S(2)}) collective-permute-start(bf16[2,312,768]{2,1,0:T(8,128)(2,1)} %get-tuple-element.56), channel_id=1, source_target_pairs={{0,1},{1,0},{2,3},{3,2},{4,5},{5,4},{6,7},{7,6}} | collective-permute-start | bytes 2875400 | tf_op jit(solution)/shard_map/ppermute | solution.py:450
  146.4 16.7 %collective-permute-start.9 = (bf16[312,768]{1,0:T(8,128)(2,1)}, bf16[312,768]{1,0:T(8,128)(2,1)}, u32[]{:S(2)}, u32[]{:S(2)}) collective-permute-start(bf16[312,768]{1,0:T(8,128)(2,1)} %get-tuple-element.57), channel_id=1, source_target_pairs={{0,2},{1,3},{2,0},{3,1},{4,6},{5,7},{6,4},{7,5}} | collective-permute-start | bytes 1437704 | tf_op jit(solution)/shard_map/ppermute | solution.py:450
  148.1 21.9 %collective-permute-start.11 = (bf16[312,768]{1,0:T(8,128)(2,1)}, bf16[312,768]{1,0:T(8,128)(2,1)}, u32[]{:S(2)}, u32[]{:S(2)}) collective-permute-start(bf16[312,768]{1,0:T(8,128)(2,1)} %get-tuple-element.58), channel_id=1, source_target_pairs={{0,3},{1,2},{2,1},{3,0},{4,7},{5,6},{6,5},{7,4}} | collective-permute-start | bytes 1437704 | tf_op jit(solution)/shard_map/ppermute | solution.py:450
  148.3 32.8 %collective-permute-start.14 = (bf16[312,768]{1,0:T(8,128)(2,1)}, bf16[312,768]{1,0:T(8,128)(2,1)}, u32[]{:S(2)}, u32[]{:S(2)}) collective-permute-start(bf16[312,768]{1,0:T(8,128)(2,1)} %get-tuple-element.61), channel_id=1, source_target_pairs={{0,2},{1,3},{2,0},{3,1},{4,6},{5,7},{6,4},{7,5}} | collective-permute-start | bytes 1437704 | tf_op jit(solution)/shard_map/ppermute | solution.py:450
  161.5 42.1 %collective-permute-start.13 = (bf16[2,312,768]{2,1,0:T(8,128)(2,1)}, bf16[2,312,768]{2,1,0:T(8,128)(2,1)}, u32[]{:S(2)}, u32[]{:S(2)}) collective-permute-start(bf16[2,312,768]{2,1,0:T(8,128)(2,1)} %get-tuple-element.59.refs_0_), channel_id=1, source_target_pairs={{0,4},{4,0},{1,5},{5,1},{2,6},{6,2},{3,7},{7,3}} | collective-permute-start | bytes 2875400 | tf_op jit(solution)/shard_map/ppermute | solution.py:453
  163.1 38.8 %collective-permute-start.16 = (bf16[312,768]{1,0:T(8,128)(2,1)}, bf16[312,768]{1,0:T(8,128)(2,1)}, u32[]{:S(2)}, u32[]{:S(2)}) collective-permute-start(bf16[312,768]{1,0:T(8,128)(2,1)} %get-tuple-element.62), channel_id=1, source_target_pairs={{0,3},{1,2},{2,1},{3,0},{4,7},{5,6},{6,5},{7,4}} | collective-permute-start | bytes 1437704 | tf_op jit(solution)/shard_map/ppermute | solution.py:450
  170.1 44.5 %collective-permute-start.10 = (bf16[312,768]{1,0:T(8,128)(2,1)}, bf16[312,768]{1,0:T(8,128)(2,1)}, u32[]{:S(2)}, u32[]{:S(2)}) collective-permute-start(bf16[312,768]{1,0:T(8,128)(2,1)} %collective-permute-done.9.refs_2_), channel_id=1, source_target_pairs={{0,4},{4,0},{1,5},{5,1},{2,6},{6,2},{3,7},{7,3}} | collective-permute-start | bytes 1437704 | tf_op jit(solution)/shard_map/ppermute | solution.py:453
  181.1 33.4 %collective-permute-start.12 = (bf16[312,768]{1,0:T(8,128)(2,1)}, bf16[312,768]{1,0:T(8,128)(2,1)}, u32[]{:S(2)}, u32[]{:S(2)}) collective-permute-start(bf16[312,768]{1,0:T(8,128)(2,1)} %collective-permute-done.11.refs_3_), channel_id=1, source_target_pairs={{0,4},{4,0},{1,5},{5,1},{2,6},{6,2},{3,7},{7,3}} | collective-permute-start | bytes 1437704 | tf_op jit(solution)/shard_map/ppermute | solution.py:453
  182.9 44.2 %collective-permute-start.8 = (bf16[2,312,768]{2,1,0:T(8,128)(2,1)}, bf16[2,312,768]{2,1,0:T(8,128)(2,1)}, u32[]{:S(2)}, u32[]{:S(2)}) collective-permute-start(bf16[2,312,768]{2,1,0:T(8,128)(2,1)} %collective-permute-done.7.refs_1_), channel_id=1, source_target_pairs={{0,4},{4,0},{1,5},{5,1},{2,6},{6,2},{3,7},{7,3}} | collective-permute-start | bytes 2875400 | tf_op jit(solution)/shard_map/ppermute | solution.py:453
  201.9 50.6 %collective-permute-start.15 = (bf16[312,768]{1,0:T(8,128)(2,1)}, bf16[312,768]{1,0:T(8,128)(2,1)}, u32[]{:S(2)}, u32[]{:S(2)}) collective-permute-start(bf16[312,768]{1,0:T(8,128)(2,1)} %collective-permute-done.14.refs_2_), channel_id=1, source_target_pairs={{0,4},{4,0},{1,5},{5,1},{2,6},{6,2},{3,7},{7,3}} | collective-permute-start | bytes 1437704 | tf_op jit(solution)/shard_map/ppermute | solution.py:453
  203.7 48.9 %collective-permute-start.17 = (bf16[312,768]{1,0:T(8,128)(2,1)}, bf16[312,768]{1,0:T(8,128)(2,1)}, u32[]{:S(2)}, u32[]{:S(2)}) collective-permute-start(bf16[312,768]{1,0:T(8,128)(2,1)} %collective-permute-done.16.refs_3_), channel_id=1, source_target_pairs={{0,4},{4,0},{1,5},{5,1},{2,6},{6,2},{3,7},{7,3}} | collective-permute-start | bytes 1437704 | tf_op jit(solution)/shard_map/ppermute | solution.py:453
  239.4 11.4 %collective-permute-start.21 = (f32[8,768]{1,0:T(8,128)}, f32[8,768]{1,0:T(8,128)}, u32[]{:S(2)}, u32[]{:S(2)}) collective-permute-start(f32[8,768]{1,0:T(8,128)} %get-tuple-element.74), channel_id=1, source_target_pairs={{0,1},{1,0},{2,3},{3,2},{4,5},{5,4},{6,7},{7,6}} | collective-permute-start | bytes 73736 | tf_op jit(solution)/shard_map/ppermute | solution.py:450
  252.2 8.8 %collective-permute-start.22 = (f32[8,768]{1,0:T(8,128)}, f32[8,768]{1,0:T(8,128)}, u32[]{:S(2)}, u32[]{:S(2)}) collective-permute-start(f32[8,768]{1,0:T(8,128)} %add.14), channel_id=1, source_target_pairs={{0,2},{1,3},{2,0},{3,1},{4,6},{5,7},{6,4},{7,5}} | collective-permute-start | bytes 73736 | tf_op jit(solution)/shard_map/ppermute | solution.py:450

commit v6 on v5

--- a/solution.py
+++ b/solution.py
@@ -11,6 +11,7 @@
 BF16 = jnp.bfloat16
 F32 = jnp.float32
 VMEM_LIMIT = 67043328
+SMALL_VMEM = 56 * 2**20
 INFO_ROWS = 16
 
 
@@ -41,8 +42,8 @@
     return act.astype(BF16), (dh * slope).astype(BF16)
 
 
-def params(dims):
-    return pltpu.CompilerParams(dimension_semantics=("arbitrary",) * dims, vmem_limit_bytes=VMEM_LIMIT)
+def params(dims, vmem=VMEM_LIMIT):
+    return pltpu.CompilerParams(dimension_semantics=("arbitrary",) * dims, vmem_limit_bytes=vmem)
 
 
 def cost(flops, mib):
@@ -57,74 +58,101 @@
     return pl.BlockSpec(dims, lambda *_: (0,) * len(dims))
 
 
-def route(ids_row, tokens, wg_t, capacity, cap):
-    n_experts = wg_t.shape[0]
-    n_tok = tokens.shape[0]
+def route_tokens(ids, x, wg_t, info_ref, capacity, cap):
+    n_experts, n_tok = wg_t.shape[0], x.shape[0]
     step = 256
-
-    def body(ids_ref, x_ref, wg_ref, info_ref):
-        ids = ids_ref[...]
-        logits = nt(wg_ref[...], x_ref[...])
-        raised = jnp.exp(logits - jnp.max(logits, axis=0, keepdims=True))
-        prob = raised / jnp.sum(raised, axis=0, keepdims=True)
-        hot = ids == lax.broadcasted_iota(jnp.int32, (n_experts, n_tok), 0)
-        hot_f = jnp.where(hot, 1.0, 0.0)
-        upper = lax.broadcasted_iota(jnp.int32, (step, step), 0) <= lax.broadcasted_iota(jnp.int32, (step, step), 1)
-        upper = jnp.where(upper, 1.0, 0.0).astype(BF16)
-        carry = jnp.zeros((n_experts, 1), F32)
-        for b in range(n_tok // step):
-            cols = slice(b * step, (b + 1) * step)
-            seen = nn(hot_f[:, cols].astype(BF16), upper) + carry
-            carry = seen[:, step - 1 : step]
-            pos = jnp.sum(seen * hot_f[:, cols], axis=0, keepdims=True) - 1.0
-            slot = ids[:, cols].astype(F32) * cap + pos
-            info_ref[0:1, cols] = jnp.where(pos < capacity, slot, -1.0)
-        info_ref[1:2, :] = jnp.sum(hot_f * prob, axis=0, keepdims=True)
-        info_ref[2:3, :] = ids.astype(F32)
-        info_ref[3:8, :] = jnp.zeros((5, n_tok), F32)
-        info_ref[8:16, :] = prob
-
-    return pl.pallas_call(
-        body,
-        grid=(1,),
-        in_specs=[whole(ids_row.shape), whole(tokens.shape), whole(wg_t.shape)],
-        out_specs=whole((INFO_ROWS, n_tok)),
-        out_shape=shape((INFO_ROWS, n_tok), F32),
-        compiler_params=params(1),
-        cost_estimate=cost(2e9, 3),
+    logits = nt(wg_t, x)
+    raised = jnp.exp(logits - jnp.max(logits, axis=0, keepdims=True))
+    prob = raised / jnp.sum(raised, axis=0, keepdims=True)
+    hot = ids == lax.broadcasted_iota(jnp.int32, (n_experts, n_tok), 0)
+    hot_f = jnp.where(hot, 1.0, 0.0)
+    upper = lax.broadcasted_iota(jnp.int32, (step, step), 0) <= lax.broadcasted_iota(jnp.int32, (step, step), 1)
+    upper = jnp.where(upper, 1.0, 0.0).astype(BF16)
+    carry = jnp.zeros((n_experts, 1), F32)
+    for b in range(n_tok // step):
+        cols = slice(b * step, (b + 1) * step)
+        seen = nn(hot_f[:, cols].astype(BF16), upper) + carry
+        carry = seen[:, step - 1 : step]
+        pos = jnp.sum(seen * hot_f[:, cols], axis=0, keepdims=True) - 1.0
+        slot = ids[:, cols].astype(F32) * cap + pos
+        info_ref[0:1, cols] = jnp.where(pos < capacity, slot, -1.0)
+    info_ref[1:2, :] = jnp.sum(hot_f * prob, axis=0, keepdims=True)
+    info_ref[2:3, :] = ids.astype(F32)
+    info_ref[3:8, :] = jnp.zeros((5, n_tok), F32)
+    info_ref[8:16, :] = prob
+
+
+def pick_rows(meta_ref, info_ref, x_ref, gy_ref, first, flip, cap):
+    k = jnp.bitwise_xor(meta_ref[0], flip)
+    row = lax.broadcasted_iota(jnp.int32, (2 * cap, 1), 0)
+    base_a = (jnp.bitwise_xor(meta_ref[1], first) * 2 + k) * cap
+    base_b = (jnp.bitwise_xor(meta_ref[1], first + 1) * 2 + k) * cap - cap
+    codes = (row + jnp.where(row < cap, base_a, base_b)).astype(F32)
+    hit = info_ref[0:1, :] == codes
+    pick = jnp.where(hit, 1.0, 0.0).astype(BF16)
+    row_gate = jnp.sum(jnp.where(hit, info_ref[1:2, :], 0.0), axis=1, keepdims=True)
+    x = nn(pick, x_ref[...]).astype(BF16)
+    return x, (row_gate * nn(pick, gy_ref[...])).astype(BF16)
+
+
+def route_and_dispatch(meta, ids_row, tokens, grad_out, wg_t, first, flip, capacity, cap):
+    n_tok, d_model = tokens.shape
+
+    def body(meta_ref, ids_ref, x_ref, wg_ref, gy_hbm, info_ref, out_a, out_b, gy_ref, sem):
+        load = pltpu.make_async_copy(gy_hbm, gy_ref, sem)
+        load.start()
+        route_tokens(ids_ref[...], x_ref[...], wg_ref[...], info_ref, capacity, cap)
+        load.wait()
+        x, dy = pick_rows(meta_ref, info_ref, x_ref, gy_ref, first, flip, cap)
+        out_a[0], out_a[1], out_b[0], out_b[1] = x[:cap], dy[:cap], x[cap:], dy[cap:]
+
+    return pl.pallas_call(
+        body,
+        grid_spec=pltpu.PrefetchScalarGridSpec(
+            num_scalar_prefetch=1,
+            grid=(1,),
+            in_specs=[whole(ids_row.shape), whole(tokens.shape), whole(wg_t.shape), pl.BlockSpec(memory_space=pl.ANY)],
+            out_specs=[whole((INFO_ROWS, n_tok))] + [whole((2, cap, d_model))] * 2,
+            scratch_shapes=[pltpu.VMEM((n_tok, d_model), BF16), pltpu.SemaphoreType.DMA],
+        ),
+        out_shape=[shape((INFO_ROWS, n_tok), F32)] + [shape((2, cap, d_model))] * 2,
+        compiler_params=params(1, SMALL_VMEM),
+        cost_estimate=cost(8 * cap * n_tok * d_model, 10),
         name="route",
-    )(ids_row, tokens, wg_t)
+    )(meta, ids_row, tokens, wg_t, grad_out)
 
 
 def dispatch(meta, info, tokens, grad_out, groups, cap):
     n_tok, d_model = tokens.shape
     count = len(groups)
 
-    def body(meta_ref, info_ref, x_ref, gy_ref, *outs):
+    def body(meta_ref, info_ref, x_ref, gy_ref, *refs):
+        outs, (stage, sems) = refs[: 2 * count], refs[2 * count :]
         g = pl.program_id(0)
         first, flip = groups[0]
         for p in range(1, count):
             first = jnp.where(g == p, groups[p][0], first)
             flip = jnp.where(g == p, groups[p][1], flip)
-        k = jnp.bitwise_xor(meta_ref[0], flip)
-        row = lax.broadcasted_iota(jnp.int32, (2 * cap, 1), 0)
-        low = row < cap
-        base_a = (jnp.bitwise_xor(meta_ref[1], first) * 2 + k) * cap
-        base_b = (jnp.bitwise_xor(meta_ref[1], first + 1) * 2 + k) * cap - cap
-        codes = (row + jnp.where(low, base_a, base_b)).astype(F32)
-        hit = info_ref[0:1, :] == codes
-        pick = jnp.where(hit, 1.0, 0.0).astype(BF16)
-        row_gate = jnp.sum(jnp.where(hit, info_ref[1:2, :], 0.0), axis=1, keepdims=True)
-        x = nn(pick, x_ref[...]).astype(BF16)
-        dy = (row_gate * nn(pick, gy_ref[...])).astype(BF16)
+        x, dy = pick_rows(meta_ref, info_ref, x_ref, gy_ref, first, flip, cap)
+        for half in range(2):
+            part = slice(half * cap, (half + 1) * cap)
+            stage[2 * g + half, 0] = x[part]
+            stage[2 * g + half, 1] = dy[part]
+
+        def store(i):
+            return pltpu.make_async_copy(stage.at[i], outs[i], sems.at[i])
+
         for p in range(count):
 
             @pl.when(g == p)
             def _():
-                outs[2 * p][0] = x[:cap]
-                outs[2 * p][1] = dy[:cap]
-                outs[2 * p + 1][0] = x[cap:]
-                outs[2 * p + 1][1] = dy[cap:]
+                store(2 * p).start()
+                store(2 * p + 1).start()
+
+        @pl.when(g == count - 1)
+        def _():
+            for i in range(2 * count):
+                store(i).wait()
 
     return pl.pallas_call(
         body,
@@ -132,10 +160,14 @@
             num_scalar_prefetch=1,
             grid=(count,),
             in_specs=[whole(info.shape), whole(tokens.shape), whole(tokens.shape)],
-            out_specs=[whole((2, cap, d_model))] * (2 * count),
+            out_specs=[pl.BlockSpec(memory_space=pl.ANY)] * (2 * count),
+            scratch_shapes=[
+                pltpu.VMEM((2 * count, 2, cap, d_model), BF16),
+                pltpu.SemaphoreType.DMA((2 * count,)),
+            ],
         ),
         out_shape=[shape((2, cap, d_model))] * (2 * count),
-        compiler_params=params(1),
+        compiler_params=params(1, SMALL_VMEM),
         cost_estimate=cost(8 * count * cap * n_tok * d_model, 8 + 4 * count),
         name="dispatch",
     )(meta, info, tokens, grad_out)
@@ -144,17 +176,18 @@
 def own_half(meta, pair_a, pair_b, w_in, w_out, chunk, group, so_far):
     _, d_model, width = w_in.shape
     cap = pair_a.shape[1]
+    rows = 2 * cap
 
     def body(meta_ref, pa, pb, wi, wo, *refs):
         h_ref, da_ref, y_ref, s_ref, x_ref, dy_ref = refs[-6:]
-        p, c = pl.program_id(0), pl.program_id(1)
-
-        for source, pair in enumerate((pa, pb)):
-
-            @pl.when(jnp.logical_and(c == 0, p == source))
-            def _():
-                x_ref[...] = pair[0]
-                dy_ref[...] = pair[1]
+        c = pl.program_id(0)
+
+        @pl.when(c == 0)
+        def _():
+            x_ref[:cap] = pa[0]
+            x_ref[cap:] = pb[0]
+            dy_ref[:cap] = pa[1]
+            dy_ref[cap:] = pb[1]
 
         h, da = hidden_grads(x_ref[...], dy_ref[...], wi[0], wo[0])
         h_ref[...] = h
@@ -172,28 +205,28 @@
             y_ref[...] += y
             s_ref[...] += s
 
-    hid = pl.BlockSpec((cap, chunk), lambda p, c, m: (2 * group + p, c))
-    full = pl.BlockSpec((cap, d_model), lambda p, c, m: (2 * group + p, 0))
-    return pl.pallas_call(
-        body,
-        grid_spec=pltpu.PrefetchScalarGridSpec(
-            num_scalar_prefetch=1,
-            grid=(2, width // chunk),
+    hid = pl.BlockSpec((rows, chunk), lambda c, m: (group, c))
+    full = pl.BlockSpec((rows, d_model), lambda c, m: (group, 0))
+    return pl.pallas_call(
+        body,
+        grid_spec=pltpu.PrefetchScalarGridSpec(
+            num_scalar_prefetch=1,
+            grid=(width // chunk,),
             in_specs=[
                 whole(pair_a.shape),
                 whole(pair_a.shape),
-                pl.BlockSpec((1, d_model, chunk), lambda p, c, m: (m[0], 0, c)),
-                pl.BlockSpec((1, chunk, d_model), lambda p, c, m: (m[0], c, 0)),
+                pl.BlockSpec((1, d_model, chunk), lambda c, m: (m[0], 0, c)),
+                pl.BlockSpec((1, chunk, d_model), lambda c, m: (m[0], c, 0)),
             ]
             + [pl.BlockSpec(memory_space=pl.ANY)] * len(so_far),
             out_specs=[hid, hid] + [full] * 4,
         ),
-        out_shape=[shape((4 * cap, width))] * 2
-        + [shape((4 * cap, d_model), F32)] * 2
-        + [shape((4 * cap, d_model))] * 2,
+        out_shape=[shape((2 * rows, width))] * 2
+        + [shape((2 * rows, d_model), F32)] * 2
+        + [shape((2 * rows, d_model))] * 2,
         input_output_aliases={5 + i: i for i in range(len(so_far))},
-        compiler_params=params(2),
-        cost_estimate=cost(16 * cap * width * d_model, 20),
+        compiler_params=params(1, SMALL_VMEM),
+        cost_estimate=cost(8 * rows * width * d_model, 20),
         name="own_half",
     )(meta, pair_a, pair_b, w_in, w_out, *so_far)
 
@@ -232,8 +265,8 @@
             outs[0][...] += y
             outs[1][...] += s
 
-    blocks, base = (4, 0) if group is None else (2, 2 * group)
-    full = pl.BlockSpec((cap, d_model), lambda p, c: (base + p, 0))
+    blocks, base, rows = (2, 0, 2 * cap) if group is None else (2, 2 * group, cap)
+    full = pl.BlockSpec((rows, d_model), lambda p, c: (base + p, 0))
     if group is None:
         out_specs, out_shape = [full] * 2, [shape(x.shape, F32)] * 2
     else:
@@ -252,8 +285,8 @@
         ],
         out_specs=out_specs,
         out_shape=out_shape,
-        compiler_params=params(2),
-        cost_estimate=cost(8 * cap * blocks * width * d_model, 10),
+        compiler_params=params(2, SMALL_VMEM if group is None else VMEM_LIMIT),
+        cost_estimate=cost(8 * rows * blocks * width * d_model, 10),
         name="far_half",
     )(x, dy, wi, wo, y_in, s_in)
 
@@ -469,9 +502,10 @@
             part_out = lax.dynamic_slice(w_out, (1 - tp, lo, 0), (1, size, d_model))[0]
             far_w[stage] = to_twin(part_in), to_twin(part_out)
 
-        info = route(expert_ids[None, :], tokens, w_router.T, capacity, cap)
-
-        f2, f3 = dispatch(meta, info, tokens, grad_out, ((2, 0),), cap)
+        wg_t = w_router.T
+        info, f2, f3 = route_and_dispatch(
+            meta, expert_ids[None, :], tokens, grad_out, wg_t, 2, 0, capacity, cap
+        )
         f2, f3 = to_ep(f2, 2), to_ep(f3, 3)
         f0, f1, g2, g3, g0, g1 = dispatch(meta, info, tokens, grad_out, ((0, 0), (2, 1), (0, 1)), cap)
         f1 = to_ep(f1, 1)
@@ -500,12 +534,13 @@
         s_late = {key: s_all.pop(key) for key in ((2, 1), (3, 1))}
         y_late = {key: y_all.pop(key) for key in ((1, 1), (2, 1), (3, 1))}
         y_first = combine_s(meta, y_all, info, (), n_tok // 2)
-        moe_out, dlog, dwg = combine_y(meta, y_late, info, y_first, tokens, grad_out, n_tok // 2)
+        moe_out, dlog, dwg = combine_y(meta, y_late, info, y_first, tokens, grad_out, n_tok // 4)
         dwg = dwg + to_ep(dwg, 1)
-        dwg = dwg + to_ep(dwg, 2)
+        dwg_far = to_ep(dwg, 2)
+        dwg = (dwg + dwg_far).T
         so_far = combine_s(meta, s_all, info, (), n_tok // 2)
-        grad_tokens = combine_s(meta, s_late, info, (so_far, dlog, w_router.T), n_tok // 2)
-        return moe_out, grad_tokens, grad_w_in, grad_w_out, dwg.T
+        grad_tokens = combine_s(meta, s_late, info, (so_far, dlog, wg_t), n_tok // 2)
+        return moe_out, grad_tokens, grad_w_in, grad_w_out, dwg
 
     in_specs = (row_spec, row_spec, P(None, None), P("ep", None, "tp"), P("ep", "tp", None), P(("dp", "ep")))
     out_specs = (row_spec, row_spec, P(("dp", "ep"), None, "tp"), P(("dp", "ep"), "tp", None), P("dp", None))

time: 263 us -> 266 us (1.011)
  waiting for transfers between devices: 60.2 us -> 74.9 us
  Pallas kernels: 166 us -> 157 us
  local copies, waits for them, and re-layouts: 9.47 us -> 5.45 us
    ppermute x10, waiting for transfers between devices: 24.9 us -> 36.7 us  [to_twin(): return lax.ppermute(v, 'tp', [(0, 1), (1, 0)])]
    pallas_call x2 -> x1, Pallas kernels: 28.2 us -> 17.7 us  [dispatch(): pl.pallas_call(body, grid_spec=pltpu.PrefetchScalarGridSpec(num_scalar_pr...]
    pallas_call x1, Pallas kernels: 3.99 us -> 9.88 us  [route_and_dispatch(): pl.pallas_call(body, grid_spec=pltpu.PrefetchScalarGridSpec(num_scalar_pr...]
    ppermute x13, waiting for transfers between devices: 35.4 us -> 38.2 us  [to_ep(): return lax.ppermute(v, 'ep', [(i, i ^ d) for i in range(ep_size)])]
  transfers between devices with their start and end apart: 23 -> 23, of which waited for: 6 -> 7; matrix products, arithmetic and copies ran while one was open for 4% -> 3% of each run, Pallas kernels for 54% -> 49%
where the time goes in v6:
time: 266 us; the launch traced here: 265 us
  Pallas kernels  157 us (59%)
  waiting for transfers between devices  74.9 us (28%)
  starting transfers between devices  23.3 us (9%)
  local copies, waits for them, and re-layouts  5.45 us (2%)
  other arithmetic  3.26 us (1%)
    ppermute x13, waiting for transfers between devices, to_ep(): return lax.ppermute(v, 'ep', [(i, i ^ d) for i in range(ep_size)])  38.2 us
    ppermute x10, waiting for transfers between devices, to_twin(): return lax.ppermute(v, 'tp', [(0, 1), (1, 0)])  36.7 us
    pallas_call x3, Pallas kernels, combine_s(): pl.pallas_call(body, grid_spec=pltpu.PrefetchScalarGridSpec(num_scalar_pr...  30.5 us
    pallas_call x3, Pallas kernels, far_half(): pl.pallas_call(body, grid=(blocks, steps), in_specs=[full, full, pl.Block...  29.3 us
    pallas_call x2, Pallas kernels, own_half(): pl.pallas_call(body, grid_spec=pltpu.PrefetchScalarGridSpec(num_scalar_pr...  27.6 us
    pallas_call x1, Pallas kernels, other_grads(): pl.pallas_call(body, grid_spec=pltpu.PrefetchScalarGridSpec(num_scalar_pr...  18.8 us
    pallas_call x1, Pallas kernels, dispatch(): pl.pallas_call(body, grid_spec=pltpu.PrefetchScalarGridSpec(num_scalar_pr...  17.7 us
    ppermute x10, starting transfers between devices, to_twin(): return lax.ppermute(v, 'tp', [(0, 1), (1, 0)])  13.3 us
  transfers between devices with their start and end apart: 23, of which 7 were waited for; matrix products, arithmetic and copies ran while one was open for 3% of the time, Pallas kernels for 49%

profile of v6, /device:TPU:0, one launch (start us, length us, event | category | flops | bytes accessed | tf_op | source)
XLA Modules:
  0.0 265.0 jit_solution(1747536107159447782)
XLA Ops:
  0.6 0.5 compare_select_fusion.meta_ref
  1.2 9.9 %route.1 = (f32[16,2048]{1,0:T(8,128)}, bf16[2,312,768]{2,1,0:T(8,128)(2,1)}, bf16[2,312,768]{2,1,0:T(8,128)(2,1)}) custom-call(s32[2]{0:T(128)} %compare_select_fusion.meta_ref, s32[1,2048]{1,0:T(1,128)} %bitcast.14, bf16[2048,768]{1,0:T(8,128)(2,1)} %refs_5_.2, bf16[8,768]{1,0:T(8,128)(2,1)} %bitcast.12, bf16[2048,768]{1,0:T(8,128)(2,1)} %refs_6_.1), custom_call_target="tpu_custom_call" | custom-call | flops 3925868544 | bytes 10485760 | tf_op jit(solution)/shard_map/route/pallas_call | solution.py:109
  11.0 17.7 %dispatch.1 = (bf16[2,312,768]{2,1,0:T(8,128)(2,1)}, bf16[2,312,768]{2,1,0:T(8,128)(2,1)}, bf16[2,312,768]{2,1,0:T(8,128)(2,1)}, bf16[2,312,768]{2,1,0:T(8,128)(...) custom-call(s32[2]{0:T(128)} %compare_select_fusion.meta_ref, ...), custom_call_target="tpu_custom_call" | custom-call | flops 11777605632 | bytes 20971520 | tf_op jit(solution)/shard_map/dispatch/pallas_call | solution.py:157
  28.7 0.8 collective-permute-start.2
  29.6 1.5 dynamic-slice_bitcast_fusion.1
  31.1 2.6 collective-permute-start.5
  33.7 1.5 dynamic-slice_bitcast_fusion
  35.2 0.0 collective-permute-start.6
  35.2 2.0 collective-permute-start
  37.2 0.0 collective-permute-start.1
  37.2 1.2 dynamic-slice_bitcast_fusion.3
  38.4 1.2 dynamic-slice_bitcast_fusion.2
  39.6 0.0 collective-permute-done.2.pb
  39.6 1.5 collective-permute-start.3
  41.1 13.8 %own_half.2 = (bf16[1248,1536]{1,0:T(8,128)(2,1)}, bf16[1248,1536]{1,0:T(8,128)(2,1)}, f32[1248,768]{1,0:T(8,128)}, f32[1248,768]{1,0:T(8,128)}, bf16[1248,768]{1,0:T(8,128)(2,1)}, /*index=5*/bf16[1248,768]{1,0:T(8,128)(2,1)}) custom-call(s32[2]{0:T(128)} %compare_select_fusion.meta_ref, bf16[2,312,768]{2,1,0:T(8,128)(2,1)} %get-tuple-element.44.pa, ...), custom_call_target="tpu_custom_call" | custom-call | flops 5888802816 | bytes 20971520 | tf_op jit(solution)/shard_map/own_half/pallas_call | solution.py:210
  54.9 4.6 %collective-permute-done.pa = bf16[2,312,768]{2,1,0:T(8,128)(2,1)S(1)} collective-permute-done((bf16[2,312,768]{2,1,0:T(8,128)(2,1)}, bf16[2,312,768]{2,1,0:T(8,128)(2,1)S(1)}, u32[]{:S(2)}, u32[]{:S(2)}) %collective-permute-start) | collective-permute-done | bytes 958496 | tf_op jit(solution)/shard_map/ppermute | solution.py:483
  59.6 2.0 collective-permute-start.4
  61.5 17.1 %collective-permute-done.1.pb = bf16[2,312,768]{2,1,0:T(8,128)(2,1)S(1)} collective-permute-done((bf16[2,312,768]{2,1,0:T(8,128)(2,1)}, bf16[2,312,768]{2,1,0:T(8,128)(2,1)S(1)}, u32[]{:S(2)}, u32[]{:S(2)}) %collective-permute-start.1) | collective-permute-done | bytes 958496 | tf_op jit(solution)/shard_map/ppermute | solution.py:483
  78.6 0.9 collective-permute-start.18
  79.6 0.0 copy-done.1
  79.6 13.8 %own_half.3 = (bf16[1248,1536]{1,0:T(8,128)(2,1)}, bf16[1248,1536]{1,0:T(8,128)(2,1)}, f32[1248,768]{1,0:T(8,128)}, f32[1248,768]{1,0:T(8,128)}, bf16[1248,768]{1,0:T(8,128)(2,1)}, /*index=5*/bf16[1248,768]{1,0:T(8,128)(2,1)}) custom-call(s32[2]{0:T(128)} %compare_select_fusion.meta_ref, ...), custom_call_target="tpu_custom_call", output_to_operand_aliasing={{0}: (5, {}), {1}: (6, {}), {2}: (7, {}), {3}: (8, {}), {4}... | custom-call | flops 5888802816 | bytes 20971520 | tf_op jit(solution)/shard_map/own_half/pallas_call | solution.py:210
  93.4 0.0 collective-permute-done.5.wi_ref
  93.4 1.7 collective-permute-start.19
  95.1 7.6 %collective-permute-done.6.wo_ref = bf16[1024,768]{1,0:T(8,128)(2,1)} collective-permute-done((bf16[1024,768]{1,0:T(8,128)(2,1)S(1)}, bf16[1024,768]{1,0:T(8,128)(2,1)}, u32[]{:S(2)}, u32[]{:S(2)}) %collective-permute-start.6) | collective-permute-done | bytes 1572896 | tf_op jit(solution)/shard_map/ppermute | solution.py:486
  102.7 0.7 collective-permute-start.20
  103.5 16.2 %far_half.3 = (f32[1248,768]{1,0:T(8,128)}, f32[1248,768]{1,0:T(8,128)}) custom-call(bf16[1248,768]{1,0:T(8,128)(2,1)} %get-tuple-element.52.x_ref, bf16[1248,768]{1,0:T(8,128)(2,1)} %get-tuple-element.53.dy_ref, bf16[768,1024]{1,0:T(8,128)(2,1)} %copy-done.2, bf16[1024,768]{1,0:T(8,128)(2,1)} %collective-permute-done.6.wo_ref, ...), custom_call_target="tpu_custom_call" | custom-call | flops 7851737088 | bytes 10485760 | tf_op jit(solution)/shard_map/far_half/pallas_call | solution.py:275
  119.7 0.0 collective-permute-done.3.wi_ref
  119.7 16.5 %collective-permute-done.4.wo_ref = bf16[512,768]{1,0:T(8,128)(2,1)} collective-permute-done((bf16[512,768]{1,0:T(8,128)(2,1)S(1)}, bf16[512,768]{1,0:T(8,128)(2,1)}, u32[]{:S(2)}, u32[]{:S(2)}) %collective-permute-start.4) | collective-permute-done | bytes 786464 | tf_op jit(solution)/shard_map/ppermute | solution.py:486
  136.2 6.6 %far_half.4 = (bf16[2,312,768]{2,1,0:T(8,128)(2,1)}, bf16[2,312,768]{2,1,0:T(8,128)(2,1)}) custom-call(bf16[1248,768]{1,0:T(8,128)(2,1)} %get-tuple-element.52.x_ref, bf16[1248,768]{1,0:T(8,128)(2,1)} %get-tuple-element.53.dy_ref, bf16[768,512]{1,0:T(8,128)(2,1)} %collective-permute-done.3.wi_ref, bf16[512,768]{1,0:T(8,128)(2,1)} %collective-permute-done.4.wo_ref, ...), custom_call_target="tpu_custom_call" | custom-call | flops 1962934272 | bytes 10485760 | tf_op jit(solution)/shard_map/far_half/pallas_call | solution.py:275
  142.8 0.0 collective-permute-start.7
  142.8 6.5 %far_half.5 = (bf16[312,768]{1,0:T(8,128)(2,1)}, bf16[312,768]{1,0:T(8,128)(2,1)}, bf16[312,768]{1,0:T(8,128)(2,1)}, bf16[312,768]{1,0:T(8,128)(2,1)}) custom-call(bf16[1248,768]{1,0:T(8,128)(2,1)} %get-tuple-element.52.x_ref, bf16[1248,768]{1,0:T(8,128)(2,1)} %get-tuple-element.53.dy_ref, bf16[768,512]{1,0:T(8,128)(2,1)} %collective-permute-done.3.wi_ref, ...), custom_call_target="tpu_custom_call" | custom-call | flops 1962934272 | bytes 10485760 | tf_op jit(solution)/shard_map/far_half/pallas_call | solution.py:275
  149.3 1.7 collective-permute-start.9
  151.1 0.0 collective-permute-done.18.refs_1_
  151.1 0.1 collective-permute-start.11
  151.2 0.0 collective-permute-done.19.refs_2_
  151.2 1.7 collective-permute-start.14
  152.9 11.6 %finished_grads.1 = (f32[2,768,1536]{2,1,0:T(8,128)}, f32[2,1536,768]{2,1,0:T(8,128)}) custom-call(s32[2]{0:T(128)} %compare_select_fusion.meta_ref, bf16[1248,768]{1,0:T(8,128)(2,1)} %get-tuple-element.52.x_ref, bf16[1248,768]{1,0:T(8,128)(2,1)} %get-tuple-element.53.dy_ref, bf16[1248,1536]{1,0:T(8,128)(2,1)} %get-tuple-element.70.h_ref, ...), custom_call_target="tpu_custom_call" | custom-call | flops 5888802816 | bytes 26214400 | tf_op jit(solution)/shard_map/finished_grads/pallas_call | solution.py:303
  164.5 1.5 collective-permute-start.13
  166.0 0.0 collective-permute-done.9.refs_2_
  166.0 0.0 collective-permute-start.16
  166.0 7.0 %collective-permute-done.11.refs_3_ = bf16[312,768]{1,0:T(8,128)(2,1)} collective-permute-done((bf16[312,768]{1,0:T(8,128)(2,1)}, bf16[312,768]{1,0:T(8,128)(2,1)}, u32[]{:S(2)}, u32[]{:S(2)}) %collective-permute-start.11) | collective-permute-done | bytes 479264 | tf_op jit(solution)/shard_map/ppermute | solution.py:483
  173.0 1.6 collective-permute-start.10
  174.5 9.5 %collective-permute-done.14.refs_2_ = bf16[312,768]{1,0:T(8,128)(2,1)} collective-permute-done((bf16[312,768]{1,0:T(8,128)(2,1)}, bf16[312,768]{1,0:T(8,128)(2,1)}, u32[]{:S(2)}, u32[]{:S(2)}) %collective-permute-start.14) | collective-permute-done | bytes 479264 | tf_op jit(solution)/shard_map/ppermute | solution.py:483
  184.0 1.7 collective-permute-start.12
  185.8 0.3 collective-permute-start.8
  186.1 18.8 %other_grads.1 = (f32[2,768,1536]{2,1,0:T(8,128)}, f32[2,1536,768]{2,1,0:T(8,128)}) custom-call(s32[2]{0:T(128)} %compare_select_fusion.meta_ref, bf16[2,312,768]{2,1,0:T(8,128)(2,1)} %get-tuple-element.66.refs_0_, bf16[2,312,768]{2,1,0:T(8,128)(2,1)} %collective-permute-done.18.refs_1_, ...), custom_call_target="tpu_custom_call", output_to_operand_aliasing={{0}: (7, {}), {1}: (8, {})} | custom-call | flops 11777605632 | bytes 26214400 | tf_op jit(solution)/shard_map/other_grads/pallas_call | solution.py:346
  204.8 0.0 collective-permute-done.16.refs_3_
  204.8 1.8 collective-permute-start.15
  206.6 0.3 collective-permute-start.17
  206.9 10.6 %combine_s.3.refs_4_ = bf16[2048,768]{1,0:T(8,128)(2,1)} custom-call(s32[2]{0:T(128)} %compare_select_fusion.meta_ref, bf16[2,312,768]{2,1,0:T(8,128)(2,1)} %get-tuple-element.61.refs_0_, bf16[2,312,768]{2,1,0:T(8,128)(2,1)} %collective-permute-done.7.refs_1_, bf16[312,768]{1,0:T(8,128)(2,1)} %collective-permute-done.9.refs_2_, ...), custom_call_target="tpu_custom_call" | custom-call | flops 4907335680 | bytes 10485760 | tf_op jit(solution)/shard_map/combine_s/pallas_call | solution.py:460
  217.5 0.0 collective-permute-done.10.refs_1_
  217.5 0.0 collective-permute-done.12.refs_2_
  217.5 12.5 %collective-permute-done.8.refs_0_.refs_5_ = bf16[2,312,768]{2,1,0:T(8,128)(2,1)} collective-permute-done((bf16[2,312,768]{2,1,0:T(8,128)(2,1)}, bf16[2,312,768]{2,1,0:T(8,128)(2,1)}, u32[]{:S(2)}, u32[]{:S(2)}) %collective-permute-start.8) | collective-permute-done | bytes 958496 | tf_op jit(solution)/shard_map/ppermute | solution.py:486
  230.0 12.1 %combine_y.1 = (bf16[2048,768]{1,0:T(8,128)(2,1)}, bf16[2048,8]{1,0:T(8,128)(2,1)}, f32[8,768]{1,0:T(8,128)}) custom-call(s32[2]{0:T(128)} %compare_select_fusion.meta_ref, bf16[2,312,768]{2,1,0:T(8,128)(2,1)} %collective-permute-done.8.refs_0_.refs_5_, bf16[312,768]{1,0:T(8,128)(2,1)} %collective-permute-done.10.refs_1_, ...), custom_call_target="tpu_custom_call" | custom-call | flops 2944401408 | bytes 16777216 | tf_op jit(solution)/shard_map/combine_y/pallas_call | solution.py:423
  242.1 0.0 collective-permute-start.21
  242.1 11.4 %combine_s.4.refs_3_ = bf16[2048,768]{1,0:T(8,128)(2,1)} custom-call(s32[2]{0:T(128)} %compare_select_fusion.meta_ref, bf16[2,312,768]{2,1,0:T(8,128)(2,1)} %get-tuple-element.61.refs_0_, bf16[2,312,768]{2,1,0:T(8,128)(2,1)} %collective-permute-done.7.refs_1_, bf16[312,768]{1,0:T(8,128)(2,1)} %collective-permute-done.14.refs_2_, ...), custom_call_target="tpu_custom_call" | custom-call | flops 5888802816 | bytes 10485760 | tf_op jit(solution)/shard_map/combine_s/pallas_call | solution.py:460
  253.5 0.0 collective-permute-done.21
  253.5 1.4 add.14
  254.9 0.3 collective-permute-start.22
  255.2 0.0 collective-permute-done.15.refs_0_
  255.2 0.0 collective-permute-done.17.refs_1_
  255.2 8.5 %combine_s.5 = bf16[2048,768]{1,0:T(8,128)(2,1)} custom-call(s32[2]{0:T(128)} %compare_select_fusion.meta_ref, bf16[312,768]{1,0:T(8,128)(2,1)} %collective-permute-done.15.refs_0_, bf16[312,768]{1,0:T(8,128)(2,1)} %collective-permute-done.17.refs_1_, f32[16,2048]{1,0:T(8,128)} %get-tuple-element.43.info_ref.refs_5_.refs_3_.refs_6_.refs_2_, ...), custom_call_target="tpu_custom_call" | custom-call | flops 1962934272 | bytes 10485760 | tf_op jit(solution)/shard_map/combine_s/pallas_call | solution.py:460
  263.7 0.0 collective-permute-done.22
  263.7 1.4 add_bitcast_fusion
  (8 shorter events, 0.0 us)
Async XLA Ops:
  28.7 10.9 %collective-permute-start.2 = (bf16[2,312,768]{2,1,0:T(8,128)(2,1)}, bf16[2,312,768]{2,1,0:T(8,128)(2,1)}, u32[]{:S(2)}, u32[]{:S(2)}) collective-permute-start(bf16[2,312,768]{2,1,0:T(8,128)(2,1)} %get-tuple-element.45), channel_id=1, source_target_pairs={{0,1},{1,0},{2,3},{3,2},{4,5},{5,4},{6,7},{7,6}} | collective-permute-start | bytes 2875400 | tf_op jit(solution)/shard_map/ppermute | solution.py:483
  31.1 62.3 %collective-permute-start.5 = (bf16[768,1024]{1,0:T(8,128)(2,1)S(1)}, bf16[768,1024]{1,0:T(8,128)(2,1)S(1)}, u32[]{:S(2)}, u32[]{:S(2)}) collective-permute-start(bf16[768,1024]{1,0:T(8,128)(2,1)S(1)} %dynamic-slice_bitcast_fusion.1), channel_id=1, source_target_pairs={{0,4},{4,0},{1,5},{5,1},{2,6},{6,2},{3,7},{7,3}} | collective-permute-start | bytes 4718600 | tf_op jit(solution)/shard_map/ppermute | solution.py:486
  35.2 67.5 %collective-permute-start.6 = (bf16[1024,768]{1,0:T(8,128)(2,1)S(1)}, bf16[1024,768]{1,0:T(8,128)(2,1)}, u32[]{:S(2)}, u32[]{:S(2)}) collective-permute-start(bf16[1024,768]{1,0:T(8,128)(2,1)S(1)} %dynamic-slice_bitcast_fusion), channel_id=1, source_target_pairs={{0,4},{4,0},{1,5},{5,1},{2,6},{6,2},{3,7},{7,3}} | collective-permute-start | bytes 4718600 | tf_op jit(solution)/shard_map/ppermute | solution.py:486
  35.2 24.3 %collective-permute-start = (bf16[2,312,768]{2,1,0:T(8,128)(2,1)}, bf16[2,312,768]{2,1,0:T(8,128)(2,1)S(1)}, u32[]{:S(2)}, u32[]{:S(2)}) collective-permute-start(bf16[2,312,768]{2,1,0:T(8,128)(2,1)} %get-tuple-element.41), channel_id=1, source_target_pairs={{0,2},{1,3},{2,0},{3,1},{4,6},{5,7},{6,4},{7,5}} | collective-permute-start | bytes 2875400 | tf_op jit(solution)/shard_map/ppermute | solution.py:483
  37.2 41.4 %collective-permute-start.1 = (bf16[2,312,768]{2,1,0:T(8,128)(2,1)}, bf16[2,312,768]{2,1,0:T(8,128)(2,1)S(1)}, u32[]{:S(2)}, u32[]{:S(2)}) collective-permute-start(bf16[2,312,768]{2,1,0:T(8,128)(2,1)} %get-tuple-element.42), channel_id=1, source_target_pairs={{0,3},{1,2},{2,1},{3,0},{4,7},{5,6},{6,5},{7,4}} | collective-permute-start | bytes 2875400 | tf_op jit(solution)/shard_map/ppermute | solution.py:483
  39.6 80.1 %collective-permute-start.3 = (bf16[768,512]{1,0:T(8,128)(2,1)S(1)}, bf16[768,512]{1,0:T(8,128)(2,1)}, u32[]{:S(2)}, u32[]{:S(2)}) collective-permute-start(bf16[768,512]{1,0:T(8,128)(2,1)S(1)} %dynamic-slice_bitcast_fusion.3), channel_id=1, source_target_pairs={{0,4},{4,0},{1,5},{5,1},{2,6},{6,2},{3,7},{7,3}} | collective-permute-start | bytes 2359304 | tf_op jit(solution)/shard_map/ppermute | solution.py:486
  59.6 20.0 %copy-start = (bf16[2,312,768]{2,1,0:T(8,128)(2,1)}, bf16[2,312,768]{2,1,0:T(8,128)(2,1)S(1)}, u32[]{:S(2)}) copy-start(bf16[2,312,768]{2,1,0:T(8,128)(2,1)S(1)} %collective-permute-done.pa) | copy-start | bytes 2875396
  59.6 76.7 %collective-permute-start.4 = (bf16[512,768]{1,0:T(8,128)(2,1)S(1)}, bf16[512,768]{1,0:T(8,128)(2,1)}, u32[]{:S(2)}, u32[]{:S(2)}) collective-permute-start(bf16[512,768]{1,0:T(8,128)(2,1)S(1)} %dynamic-slice_bitcast_fusion.2), channel_id=1, source_target_pairs={{0,4},{4,0},{1,5},{5,1},{2,6},{6,2},{3,7},{7,3}} | collective-permute-start | bytes 2359304 | tf_op jit(solution)/shard_map/ppermute | solution.py:486
  78.6 0.9 copy-start.1
  78.6 72.4 %collective-permute-start.18 = (bf16[2,312,768]{2,1,0:T(8,128)(2,1)}, bf16[2,312,768]{2,1,0:T(8,128)(2,1)}, u32[]{:S(2)}, u32[]{:S(2)}) collective-permute-start(bf16[2,312,768]{2,1,0:T(8,128)(2,1)} %get-tuple-element.67), channel_id=1, source_target_pairs={{0,1},{1,0},{2,3},{3,2},{4,5},{5,4},{6,7},{7,6}} | collective-permute-start | bytes 2875400 | tf_op jit(solution)/shard_map/ppermute | solution.py:483
  93.4 10.1 %copy-start.2 = (bf16[768,1024]{1,0:T(8,128)(2,1)}, bf16[768,1024]{1,0:T(8,128)(2,1)S(1)}, u32[]{:S(2)}) copy-start(bf16[768,1024]{1,0:T(8,128)(2,1)S(1)} %collective-permute-done.5.wi_ref) | copy-start | bytes 4718596
  93.4 57.8 %collective-permute-start.19 = (bf16[2,312,768]{2,1,0:T(8,128)(2,1)}, bf16[2,312,768]{2,1,0:T(8,128)(2,1)}, u32[]{:S(2)}, u32[]{:S(2)}) collective-permute-start(bf16[2,312,768]{2,1,0:T(8,128)(2,1)} %get-tuple-element.68), channel_id=1, source_target_pairs={{0,2},{1,3},{2,0},{3,1},{4,6},{5,7},{6,4},{7,5}} | collective-permute-start | bytes 2875400 | tf_op jit(solution)/shard_map/ppermute | solution.py:483
  102.7 61.8 %collective-permute-start.20 = (bf16[2,312,768]{2,1,0:T(8,128)(2,1)}, bf16[2,312,768]{2,1,0:T(8,128)(2,1)}, u32[]{:S(2)}, u32[]{:S(2)}) collective-permute-start(bf16[2,312,768]{2,1,0:T(8,128)(2,1)} %get-tuple-element.69), channel_id=1, source_target_pairs={{0,3},{1,2},{2,1},{3,0},{4,7},{5,6},{6,5},{7,4}} | collective-permute-start | bytes 2875400 | tf_op jit(solution)/shard_map/ppermute | solution.py:483
  142.8 43.0 %collective-permute-start.7 = (bf16[2,312,768]{2,1,0:T(8,128)(2,1)}, bf16[2,312,768]{2,1,0:T(8,128)(2,1)}, u32[]{:S(2)}, u32[]{:S(2)}) collective-permute-start(bf16[2,312,768]{2,1,0:T(8,128)(2,1)} %get-tuple-element.58), channel_id=1, source_target_pairs={{0,1},{1,0},{2,3},{3,2},{4,5},{5,4},{6,7},{7,6}} | collective-permute-start | bytes 2875400 | tf_op jit(solution)/shard_map/ppermute | solution.py:483
  149.3 16.7 %collective-permute-start.9 = (bf16[312,768]{1,0:T(8,128)(2,1)}, bf16[312,768]{1,0:T(8,128)(2,1)}, u32[]{:S(2)}, u32[]{:S(2)}) collective-permute-start(bf16[312,768]{1,0:T(8,128)(2,1)} %get-tuple-element.59), channel_id=1, source_target_pairs={{0,2},{1,3},{2,0},{3,1},{4,6},{5,7},{6,4},{7,5}} | collective-permute-start | bytes 1437704 | tf_op jit(solution)/shard_map/ppermute | solution.py:483
  151.1 21.9 %collective-permute-start.11 = (bf16[312,768]{1,0:T(8,128)(2,1)}, bf16[312,768]{1,0:T(8,128)(2,1)}, u32[]{:S(2)}, u32[]{:S(2)}) collective-permute-start(bf16[312,768]{1,0:T(8,128)(2,1)} %get-tuple-element.60), channel_id=1, source_target_pairs={{0,3},{1,2},{2,1},{3,0},{4,7},{5,6},{6,5},{7,4}} | collective-permute-start | bytes 1437704 | tf_op jit(solution)/shard_map/ppermute | solution.py:483
  151.2 32.8 %collective-permute-start.14 = (bf16[312,768]{1,0:T(8,128)(2,1)}, bf16[312,768]{1,0:T(8,128)(2,1)}, u32[]{:S(2)}, u32[]{:S(2)}) collective-permute-start(bf16[312,768]{1,0:T(8,128)(2,1)} %get-tuple-element.63), channel_id=1, source_target_pairs={{0,2},{1,3},{2,0},{3,1},{4,6},{5,7},{6,4},{7,5}} | collective-permute-start | bytes 1437704 | tf_op jit(solution)/shard_map/ppermute | solution.py:483
  164.5 42.1 %collective-permute-start.13 = (bf16[2,312,768]{2,1,0:T(8,128)(2,1)}, bf16[2,312,768]{2,1,0:T(8,128)(2,1)}, u32[]{:S(2)}, u32[]{:S(2)}) collective-permute-start(bf16[2,312,768]{2,1,0:T(8,128)(2,1)} %get-tuple-element.61.refs_0_), channel_id=1, source_target_pairs={{0,4},{4,0},{1,5},{5,1},{2,6},{6,2},{3,7},{7,3}} | collective-permute-start | bytes 2875400 | tf_op jit(solution)/shard_map/ppermute | solution.py:486
  166.0 38.8 %collective-permute-start.16 = (bf16[312,768]{1,0:T(8,128)(2,1)}, bf16[312,768]{1,0:T(8,128)(2,1)}, u32[]{:S(2)}, u32[]{:S(2)}) collective-permute-start(bf16[312,768]{1,0:T(8,128)(2,1)} %get-tuple-element.64), channel_id=1, source_target_pairs={{0,3},{1,2},{2,1},{3,0},{4,7},{5,6},{6,5},{7,4}} | collective-permute-start | bytes 1437704 | tf_op jit(solution)/shard_map/ppermute | solution.py:483
  173.0 44.5 %collective-permute-start.10 = (bf16[312,768]{1,0:T(8,128)(2,1)}, bf16[312,768]{1,0:T(8,128)(2,1)}, u32[]{:S(2)}, u32[]{:S(2)}) collective-permute-start(bf16[312,768]{1,0:T(8,128)(2,1)} %collective-permute-done.9.refs_2_), channel_id=1, source_target_pairs={{0,4},{4,0},{1,5},{5,1},{2,6},{6,2},{3,7},{7,3}} | collective-permute-start | bytes 1437704 | tf_op jit(solution)/shard_map/ppermute | solution.py:486
  184.0 33.5 %collective-permute-start.12 = (bf16[312,768]{1,0:T(8,128)(2,1)}, bf16[312,768]{1,0:T(8,128)(2,1)}, u32[]{:S(2)}, u32[]{:S(2)}) collective-permute-start(bf16[312,768]{1,0:T(8,128)(2,1)} %collective-permute-done.11.refs_3_), channel_id=1, source_target_pairs={{0,4},{4,0},{1,5},{5,1},{2,6},{6,2},{3,7},{7,3}} | collective-permute-start | bytes 1437704 | tf_op jit(solution)/shard_map/ppermute | solution.py:486
  185.8 44.2 %collective-permute-start.8 = (bf16[2,312,768]{2,1,0:T(8,128)(2,1)}, bf16[2,312,768]{2,1,0:T(8,128)(2,1)}, u32[]{:S(2)}, u32[]{:S(2)}) collective-permute-start(bf16[2,312,768]{2,1,0:T(8,128)(2,1)} %collective-permute-done.7.refs_1_), channel_id=1, source_target_pairs={{0,4},{4,0},{1,5},{5,1},{2,6},{6,2},{3,7},{7,3}} | collective-permute-start | bytes 2875400 | tf_op jit(solution)/shard_map/ppermute | solution.py:486
  204.8 50.3 %collective-permute-start.15 = (bf16[312,768]{1,0:T(8,128)(2,1)}, bf16[312,768]{1,0:T(8,128)(2,1)}, u32[]{:S(2)}, u32[]{:S(2)}) collective-permute-start(bf16[312,768]{1,0:T(8,128)(2,1)} %collective-permute-done.14.refs_2_), channel_id=1, source_target_pairs={{0,4},{4,0},{1,5},{5,1},{2,6},{6,2},{3,7},{7,3}} | collective-permute-start | bytes 1437704 | tf_op jit(solution)/shard_map/ppermute | solution.py:486
  206.6 48.6 %collective-permute-start.17 = (bf16[312,768]{1,0:T(8,128)(2,1)}, bf16[312,768]{1,0:T(8,128)(2,1)}, u32[]{:S(2)}, u32[]{:S(2)}) collective-permute-start(bf16[312,768]{1,0:T(8,128)(2,1)} %collective-permute-done.16.refs_3_), channel_id=1, source_target_pairs={{0,4},{4,0},{1,5},{5,1},{2,6},{6,2},{3,7},{7,3}} | collective-permute-start | bytes 1437704 | tf_op jit(solution)/shard_map/ppermute | solution.py:486
  242.1 11.4 %collective-permute-start.21 = (f32[8,768]{1,0:T(8,128)}, f32[8,768]{1,0:T(8,128)}, u32[]{:S(2)}, u32[]{:S(2)}) collective-permute-start(f32[8,768]{1,0:T(8,128)} %get-tuple-element.76), channel_id=1, source_target_pairs={{0,1},{1,0},{2,3},{3,2},{4,5},{5,4},{6,7},{7,6}} | collective-permute-start | bytes 73736 | tf_op jit(solution)/shard_map/ppermute | solution.py:483
  254.9 8.8 %collective-permute-start.22 = (f32[8,768]{1,0:T(8,128)}, f32[8,768]{1,0:T(8,128)}, u32[]{:S(2)}, u32[]{:S(2)}) collective-permute-start(f32[8,768]{1,0:T(8,128)} %add.14), channel_id=1, source_target_pairs={{0,2},{1,3},{2,0},{3,1},{4,6},{5,7},{6,4},{7,5}} | collective-permute-start | bytes 73736 | tf_op jit(solution)/shard_map/ppermute | solution.py:483

commit v7 on v6

--- a/solution.py
+++ b/solution.py
@@ -437,7 +437,7 @@
     )(meta, *rows, info, so_far, tokens, grad_out)
 
 
-def combine_s(meta, pieces, info, extra, block):
+def combine_s(meta, pieces, info, block):
     n_tok = info.shape[1]
     keys = list(pieces)
     specs, rows, cap = piece_specs(pieces.values())
@@ -445,34 +445,24 @@
 
     def body(meta_ref, *refs):
         parts = refs[: len(keys)]
-        info_ref, *mid, out_ref, all_rows = refs[len(keys) :]
+        info_ref, out_ref, all_rows = refs[len(keys) :]
         stack_rows(parts, all_rows)
-        s = nn(piece_pick(meta_ref, info_ref[...].T, keys, cap), all_rows[...])
-        if extra:
-            so_far, dlog_ref, wg_ref = mid
-            s = s + so_far[...].astype(F32) + nn(dlog_ref[...], wg_ref[...])
-        out_ref[...] = s.astype(BF16)
-
-    tok = pl.BlockSpec((block, d_model), lambda b, m: (b, 0))
-    extra_specs = []
-    if extra:
-        extra_specs = [tok, pl.BlockSpec((block, extra[1].shape[1]), lambda b, m: (b, 0)), whole(extra[2].shape)]
+        out_ref[...] = nn(piece_pick(meta_ref, info_ref[...].T, keys, cap), all_rows[...]).astype(BF16)
+
     return pl.pallas_call(
         body,
         grid_spec=pltpu.PrefetchScalarGridSpec(
             num_scalar_prefetch=1,
             grid=(n_tok // block,),
-            in_specs=specs
-            + [pl.BlockSpec((INFO_ROWS, block), lambda b, m: (0, b))]
-            + extra_specs,
-            out_specs=tok,
+            in_specs=specs + [pl.BlockSpec((INFO_ROWS, block), lambda b, m: (0, b))],
+            out_specs=pl.BlockSpec((block, d_model), lambda b, m: (b, 0)),
             scratch_shapes=[pltpu.VMEM((cap * len(keys), d_model), BF16)],
         ),
         out_shape=shape((n_tok, d_model)),
         compiler_params=params(1),
         cost_estimate=cost(2 * n_tok * cap * len(keys) * d_model, 10),
         name="combine_s",
-    )(meta, *rows, info, *extra)
+    )(meta, *rows, info)
 
 
 def solution(mesh):
@@ -533,13 +523,18 @@
         s_all = {(d, k): v for k, side in enumerate((s_mine, s_twin)) for d, v in enumerate(side)}
         s_late = {key: s_all.pop(key) for key in ((2, 1), (3, 1))}
         y_late = {key: y_all.pop(key) for key in ((1, 1), (2, 1), (3, 1))}
-        y_first = combine_s(meta, y_all, info, (), n_tok // 2)
+        y_first = combine_s(meta, y_all, info, n_tok // 2)
         moe_out, dlog, dwg = combine_y(meta, y_late, info, y_first, tokens, grad_out, n_tok // 4)
-        dwg = dwg + to_ep(dwg, 1)
-        dwg_far = to_ep(dwg, 2)
-        dwg = (dwg + dwg_far).T
-        so_far = combine_s(meta, s_all, info, (), n_tok // 2)
-        grad_tokens = combine_s(meta, s_late, info, (so_far, dlog, wg_t), n_tok // 2)
+        dwg_of = [to_ep(dwg, d) for d in (1, 2, 3)]
+        dwg = ((dwg + dwg_of[0]) + (dwg_of[1] + dwg_of[2])).T
+        so_far = combine_s(meta, s_all, info, n_tok // 2)
+        slot = info[0].astype(jnp.int32)
+        dx = so_far.astype(F32) + nn(dlog, wg_t)
+        for key in ((2, 1), (3, 1)):
+            owner = jnp.bitwise_xor(ep, key[0]) * 2 + jnp.bitwise_xor(tp, key[1])
+            pick = slot[:, None] - owner * cap == jnp.arange(cap)[None, :]
+            dx = dx + nn(pick.astype(BF16), s_late[key])
+        grad_tokens = dx.astype(BF16)
         return moe_out, grad_tokens, grad_w_in, grad_w_out, dwg
 
     in_specs = (row_spec, row_spec, P(None, None), P("ep", None, "tp"), P("ep", "tp", None), P(("dp", "ep")))

time: 266 us -> 282 us (1.060)
  matrix products: 0 us -> 17.4 us
  Pallas kernels: 157 us -> 149 us
  waiting for transfers between devices: 74.9 us -> 79.7 us
    dot_general x0 -> x3, matrix products: none -> 17.4 us  [nn(): return jnp.dot(a, b, preferred_element_type=F32)]
    ppermute x10, waiting for transfers between devices: 36.7 us -> 50.3 us  [to_twin(): return lax.ppermute(v, 'tp', [(0, 1), (1, 0)])]
    ppermute x13 -> x14, waiting for transfers between devices: 38.2 us -> 29.4 us  [to_ep(): return lax.ppermute(v, 'ep', [(i, i ^ d) for i in range(ep_size)])]
    pallas_call x3 -> x2, Pallas kernels: 30.5 us -> 22 us  [combine_s(): pl.pallas_call(body, grid_spec=pltpu.PrefetchScalarGridSpec(num_scalar_pr...]
    ppermute x13 -> x14, starting transfers between devices: 10.1 us -> 12.1 us  [to_ep(): return lax.ppermute(v, 'ep', [(i, i ^ d) for i in range(ep_size)])]
  transfers between devices with their start and end apart: 23 -> 24, of which waited for: 7 -> 7; matrix products, arithmetic and copies ran while one was open for 3% -> 9% of each run, Pallas kernels for 49% -> 43%
where the time goes in v7:
time: 282 us; the launch traced here: 281 us
  Pallas kernels  149 us (53%)
  waiting for transfers between devices  79.7 us (28%)
  starting transfers between devices  25.5 us (9%)
  matrix products  17.4 us (6%)
  local copies, waits for them, and re-layouts  5.41 us (2%)
  other arithmetic  3.35 us (1%)
    ppermute x10, waiting for transfers between devices, to_twin(): return lax.ppermute(v, 'tp', [(0, 1), (1, 0)])  50.3 us
    ppermute x14, waiting for transfers between devices, to_ep(): return lax.ppermute(v, 'ep', [(i, i ^ d) for i in range(ep_size)])  29.4 us
    pallas_call x3, Pallas kernels, far_half(): pl.pallas_call(body, grid=(blocks, steps), in_specs=[full, full, pl.Block...  29.3 us
    pallas_call x2, Pallas kernels, own_half(): pl.pallas_call(body, grid_spec=pltpu.PrefetchScalarGridSpec(num_scalar_pr...  27.6 us
    pallas_call x2, Pallas kernels, combine_s(): pl.pallas_call(body, grid_spec=pltpu.PrefetchScalarGridSpec(num_scalar_pr...  22 us
    pallas_call x1, Pallas kernels, other_grads(): pl.pallas_call(body, grid_spec=pltpu.PrefetchScalarGridSpec(num_scalar_pr...  18.8 us
    pallas_call x1, Pallas kernels, dispatch(): pl.pallas_call(body, grid_spec=pltpu.PrefetchScalarGridSpec(num_scalar_pr...  17.7 us
    dot_general x3, matrix products, nn(): return jnp.dot(a, b, preferred_element_type=F32)  17.4 us
  transfers between devices with their start and end apart: 24, of which 7 were waited for; matrix products, arithmetic and copies ran while one was open for 9% of the time, Pallas kernels for 43%

profile of v7, /device:TPU:0, one launch (start us, length us, event | category | flops | bytes accessed | tf_op | source)
XLA Modules:
  0.0 281.0 jit_solution(1282702409468134235)
XLA Ops:
  0.6 0.5 compare_select_fusion.meta_ref
  1.1 9.9 %route.1 = (f32[16,2048]{1,0:T(8,128)}, bf16[2,312,768]{2,1,0:T(8,128)(2,1)}, bf16[2,312,768]{2,1,0:T(8,128)(2,1)}) custom-call(s32[2]{0:T(128)} %compare_select_fusion.meta_ref, s32[1,2048]{1,0:T(1,128)} %bitcast.21, bf16[2048,768]{1,0:T(8,128)(2,1)} %refs_5_.2, bf16[8,768]{1,0:T(8,128)(2,1)} %bitcast.20, bf16[2048,768]{1,0:T(8,128)(2,1)} %refs_6_.1), custom_call_target="tpu_custom_call" | custom-call | flops 3925868544 | bytes 10485760 | tf_op jit(solution)/shard_map/route/pallas_call | solution.py:109
  11.0 17.7 %dispatch.1 = (bf16[2,312,768]{2,1,0:T(8,128)(2,1)}, bf16[2,312,768]{2,1,0:T(8,128)(2,1)}, bf16[2,312,768]{2,1,0:T(8,128)(2,1)}, bf16[2,312,768]{2,1,0:T(8,128)(...) custom-call(s32[2]{0:T(128)} %compare_select_fusion.meta_ref, ...), custom_call_target="tpu_custom_call" | custom-call | flops 11777605632 | bytes 20971520 | tf_op jit(solution)/shard_map/dispatch/pallas_call | solution.py:157
  28.7 0.8 collective-permute-start.2
  29.6 1.5 dynamic-slice_bitcast_fusion.1
  31.1 2.6 collective-permute-start.5
  33.7 1.5 dynamic-slice_bitcast_fusion
  35.2 0.0 collective-permute-start.6
  35.2 2.0 collective-permute-start
  37.2 0.0 collective-permute-start.1
  37.2 1.2 dynamic-slice_bitcast_fusion.3
  38.4 1.2 dynamic-slice_bitcast_fusion.2
  39.6 0.0 collective-permute-done.2.pb
  39.6 1.5 collective-permute-start.3
  41.1 13.8 %own_half.2 = (bf16[1248,1536]{1,0:T(8,128)(2,1)}, bf16[1248,1536]{1,0:T(8,128)(2,1)}, f32[1248,768]{1,0:T(8,128)}, f32[1248,768]{1,0:T(8,128)}, bf16[1248,768]{1,0:T(8,128)(2,1)}, /*index=5*/bf16[1248,768]{1,0:T(8,128)(2,1)}) custom-call(s32[2]{0:T(128)} %compare_select_fusion.meta_ref, bf16[2,312,768]{2,1,0:T(8,128)(2,1)} %get-tuple-element.44.pa, ...), custom_call_target="tpu_custom_call" | custom-call | flops 5888802816 | bytes 20971520 | tf_op jit(solution)/shard_map/own_half/pallas_call | solution.py:210
  54.9 4.8 %collective-permute-done.pa = bf16[2,312,768]{2,1,0:T(8,128)(2,1)} collective-permute-done((bf16[2,312,768]{2,1,0:T(8,128)(2,1)}, bf16[2,312,768]{2,1,0:T(8,128)(2,1)}, u32[]{:S(2)}, u32[]{:S(2)}) %collective-permute-start) | collective-permute-done | bytes 958496 | tf_op jit(solution)/shard_map/ppermute | solution.py:473
  59.6 2.0 collective-permute-start.4
  61.6 17.0 %collective-permute-done.1.pb = bf16[2,312,768]{2,1,0:T(8,128)(2,1)} collective-permute-done((bf16[2,312,768]{2,1,0:T(8,128)(2,1)}, bf16[2,312,768]{2,1,0:T(8,128)(2,1)}, u32[]{:S(2)}, u32[]{:S(2)}) %collective-permute-start.1) | collective-permute-done | bytes 958496 | tf_op jit(solution)/shard_map/ppermute | solution.py:473
  78.7 0.9 collective-permute-start.18
  79.5 13.8 %own_half.3 = (bf16[1248,1536]{1,0:T(8,128)(2,1)}, bf16[1248,1536]{1,0:T(8,128)(2,1)}, f32[1248,768]{1,0:T(8,128)}, f32[1248,768]{1,0:T(8,128)}, bf16[1248,768]{1,0:T(8,128)(2,1)}, /*index=5*/bf16[1248,768]{1,0:T(8,128)(2,1)}) custom-call(s32[2]{0:T(128)} %compare_select_fusion.meta_ref, ...), custom_call_target="tpu_custom_call", output_to_operand_aliasing={{0}: (5, {}), {1}: (6, {}), {2}: (7, {}), {3}: (8, {}), {4}... | custom-call | flops 5888802816 | bytes 20971520 | tf_op jit(solution)/shard_map/own_half/pallas_call | solution.py:210
  93.3 0.0 collective-permute-done.5.wi_ref
  93.3 1.7 collective-permute-start.19
  95.0 7.7 %collective-permute-done.6.wo_ref = bf16[1024,768]{1,0:T(8,128)(2,1)} collective-permute-done((bf16[1024,768]{1,0:T(8,128)(2,1)S(1)}, bf16[1024,768]{1,0:T(8,128)(2,1)}, u32[]{:S(2)}, u32[]{:S(2)}) %collective-permute-start.6) | collective-permute-done | bytes 1572896 | tf_op jit(solution)/shard_map/ppermute | solution.py:476
  102.7 0.7 collective-permute-start.20
  103.5 16.3 %far_half.3 = (f32[1248,768]{1,0:T(8,128)}, f32[1248,768]{1,0:T(8,128)}) custom-call(bf16[1248,768]{1,0:T(8,128)(2,1)} %get-tuple-element.52.x_ref, bf16[1248,768]{1,0:T(8,128)(2,1)} %get-tuple-element.53.dy_ref, bf16[768,1024]{1,0:T(8,128)(2,1)} %collective-permute-done.5.wi_ref, bf16[1024,768]{1,0:T(8,128)(2,1)} %collective-permute-done.6.wo_ref, ...), custom_call_target="tpu_custom_call" | custom-call | flops 7851737088 | bytes 10485760 | tf_op jit(solution)/shard_map/far_half/pallas_call | solution.py:275
  119.7 0.0 collective-permute-done.3.wi_ref
  119.7 16.5 %collective-permute-done.4.wo_ref = bf16[512,768]{1,0:T(8,128)(2,1)} collective-permute-done((bf16[512,768]{1,0:T(8,128)(2,1)S(1)}, bf16[512,768]{1,0:T(8,128)(2,1)}, u32[]{:S(2)}, u32[]{:S(2)}) %collective-permute-start.4) | collective-permute-done | bytes 786464 | tf_op jit(solution)/shard_map/ppermute | solution.py:476
  136.2 6.5 %far_half.4 = (bf16[2,312,768]{2,1,0:T(8,128)(2,1)}, bf16[2,312,768]{2,1,0:T(8,128)(2,1)}) custom-call(bf16[1248,768]{1,0:T(8,128)(2,1)} %get-tuple-element.52.x_ref, bf16[1248,768]{1,0:T(8,128)(2,1)} %get-tuple-element.53.dy_ref, bf16[768,512]{1,0:T(8,128)(2,1)} %collective-permute-done.3.wi_ref, bf16[512,768]{1,0:T(8,128)(2,1)} %collective-permute-done.4.wo_ref, ...), custom_call_target="tpu_custom_call" | custom-call | flops 1962934272 | bytes 10485760 | tf_op jit(solution)/shard_map/far_half/pallas_call | solution.py:275
  142.8 0.0 collective-permute-start.7
  142.8 1.5 convert_subtract_fusion
  144.2 6.6 %far_half.5 = (bf16[312,768]{1,0:T(8,128)(2,1)}, bf16[312,768]{1,0:T(8,128)(2,1)}, bf16[312,768]{1,0:T(8,128)(2,1)}, bf16[312,768]{1,0:T(8,128)(2,1)}) custom-call(bf16[1248,768]{1,0:T(8,128)(2,1)} %get-tuple-element.52.x_ref, bf16[1248,768]{1,0:T(8,128)(2,1)} %get-tuple-element.53.dy_ref, bf16[768,512]{1,0:T(8,128)(2,1)} %collective-permute-done.3.wi_ref, ...), custom_call_target="tpu_custom_call" | custom-call | flops 1962934272 | bytes 10485760 | tf_op jit(solution)/shard_map/far_half/pallas_call | solution.py:275
  150.8 1.7 collective-permute-start.9
  152.5 0.0 collective-permute-done.18.refs_1_
  152.5 0.3 collective-permute-start.14
  152.8 11.6 %finished_grads.1 = (f32[2,768,1536]{2,1,0:T(8,128)}, f32[2,1536,768]{2,1,0:T(8,128)}) custom-call(s32[2]{0:T(128)} %compare_select_fusion.meta_ref, bf16[1248,768]{1,0:T(8,128)(2,1)} %get-tuple-element.52.x_ref, bf16[1248,768]{1,0:T(8,128)(2,1)} %get-tuple-element.53.dy_ref, bf16[1248,1536]{1,0:T(8,128)(2,1)} %get-tuple-element.70.h_ref, ...), custom_call_target="tpu_custom_call" | custom-call | flops 5888802816 | bytes 26214400 | tf_op jit(solution)/shard_map/finished_grads/pallas_call | solution.py:303
  164.4 0.0 collective-permute-done.19.refs_2_
  164.4 1.3 collective-permute-start.11
  165.7 1.5 collective-permute-start.13
  167.2 0.0 collective-permute-done.9.refs_2_
  167.2 0.4 collective-permute-start.15
  167.6 7.6 %collective-permute-done.14.refs_2_ = bf16[312,768]{1,0:T(8,128)(2,1)} collective-permute-done((bf16[312,768]{1,0:T(8,128)(2,1)}, bf16[312,768]{1,0:T(8,128)(2,1)}, u32[]{:S(2)}, u32[]{:S(2)}) %collective-permute-start.14) | collective-permute-done | bytes 479264 | tf_op jit(solution)/shard_map/ppermute | solution.py:473
  175.2 1.7 collective-permute-start.16
  176.9 0.3 collective-permute-start.8
  177.2 18.8 %other_grads.1 = (f32[2,768,1536]{2,1,0:T(8,128)}, f32[2,1536,768]{2,1,0:T(8,128)}) custom-call(s32[2]{0:T(128)} %compare_select_fusion.meta_ref, bf16[2,312,768]{2,1,0:T(8,128)(2,1)} %get-tuple-element.66.refs_0_, bf16[2,312,768]{2,1,0:T(8,128)(2,1)} %collective-permute-done.18.refs_1_, ...), custom_call_target="tpu_custom_call", output_to_operand_aliasing={{0}: (7, {}), {1}: (8, {})} | custom-call | flops 11777605632 | bytes 26214400 | tf_op jit(solution)/shard_map/other_grads/pallas_call | solution.py:346
  196.0 0.0 collective-permute-done.11.refs_3_
  196.0 1.8 collective-permute-start.10
  197.8 0.3 collective-permute-start.12
  198.0 0.0 collective-permute-done.13.refs_4_
  198.0 1.7 collective-permute-start.17
  199.8 10.6 %combine_s.2.refs_4_ = bf16[2048,768]{1,0:T(8,128)(2,1)} custom-call(s32[2]{0:T(128)} %compare_select_fusion.meta_ref, bf16[2,312,768]{2,1,0:T(8,128)(2,1)} %get-tuple-element.61.refs_0_, bf16[2,312,768]{2,1,0:T(8,128)(2,1)} %collective-permute-done.7.refs_1_, bf16[312,768]{1,0:T(8,128)(2,1)} %collective-permute-done.9.refs_2_, ...), custom_call_target="tpu_custom_call" | custom-call | flops 4907335680 | bytes 10485760 | tf_op jit(solution)/shard_map/combine_s/pallas_call | solution.py:452
  210.4 4.9 %fusion = f32[2048,768]{1,0:T(8,128)} fusion(bf16[312,768]{1,0:T(8,128)(2,1)} %collective-permute-done.16, s32[2048]{0:T(1024)} %bitcast.18), kind=kOutput, calls=%fused_computation.3 | convolution fusion | flops 982106112 | bytes 6778880 | tf_op jit(solution)/shard_map/dot_general | solution.py:19
  215.3 15.9 %collective-permute-done.10.refs_1_ = bf16[312,768]{1,0:T(8,128)(2,1)} collective-permute-done((bf16[312,768]{1,0:T(8,128)(2,1)}, bf16[312,768]{1,0:T(8,128)(2,1)}, u32[]{:S(2)}, u32[]{:S(2)}) %collective-permute-start.10) | collective-permute-done | bytes 479264 | tf_op jit(solution)/shard_map/ppermute | solution.py:476
  231.2 10.3 %collective-permute-done.12.refs_2_ = bf16[312,768]{1,0:T(8,128)(2,1)} collective-permute-done((bf16[312,768]{1,0:T(8,128)(2,1)}, bf16[312,768]{1,0:T(8,128)(2,1)}, u32[]{:S(2)}, u32[]{:S(2)}) %collective-permute-start.12) | collective-permute-done | bytes 479264 | tf_op jit(solution)/shard_map/ppermute | solution.py:476
  241.4 0.0 collective-permute-done.8.refs_0_.refs_5_
  241.4 12.1 %combine_y.1 = (bf16[2048,768]{1,0:T(8,128)(2,1)}, bf16[2048,8]{1,0:T(8,128)(2,1)}, f32[8,768]{1,0:T(8,128)}) custom-call(s32[2]{0:T(128)} %compare_select_fusion.meta_ref, bf16[2,312,768]{2,1,0:T(8,128)(2,1)} %collective-permute-done.8.refs_0_.refs_5_, bf16[312,768]{1,0:T(8,128)(2,1)} %collective-permute-done.10.refs_1_, ...), custom_call_target="tpu_custom_call" | custom-call | flops 2944401408 | bytes 16777216 | tf_op jit(solution)/shard_map/combine_y/pallas_call | solution.py:423
  253.5 0.5 collective-permute-start.22
  254.0 0.2 collective-permute-start.23
  254.2 1.5 collective-permute-start.21
  255.7 4.6 %fusion.4 = f32[2048,768]{1,0:T(8,128)} fusion(bf16[2048,8]{1,0:T(8,128)(2,1)} %get-tuple-element.65, bf16[768,8]{0,1:T(8,128)(2,1)} %param.8), kind=kOutput, calls=%fused_computation.15 | convolution fusion | flops 25165824 | bytes 6336512 | tf_op jit(solution)/shard_map/dot_general | solution.py:19
  260.2 11.4 %combine_s.3 = bf16[2048,768]{1,0:T(8,128)(2,1)} custom-call(s32[2]{0:T(128)} %compare_select_fusion.meta_ref, bf16[2,312,768]{2,1,0:T(8,128)(2,1)} %get-tuple-element.61.refs_0_, bf16[2,312,768]{2,1,0:T(8,128)(2,1)} %collective-permute-done.7.refs_1_, bf16[312,768]{1,0:T(8,128)(2,1)} %collective-permute-done.14.refs_2_, ...), custom_call_target="tpu_custom_call" | custom-call | flops 5888802816 | bytes 10485760 | tf_op jit(solution)/shard_map/combine_s/pallas_call | solution.py:452
  271.6 8.0 %add_convert_fusion = bf16[2048,768]{1,0:T(8,128)(2,1)} fusion(f32[2048,768]{1,0:T(8,128)} %fusion, f32[2048,768]{1,0:T(8,128)} %fusion.4, bf16[2048,768]{1,0:T(8,128)(2,1)} %combine_s.3, bf16[312,768]{1,0:T(8,128)(2,1)} %collective-permute-done.17, s32[2048]{0:T(1024)} %bitcast.19), kind=kOutput, calls=%fused_computation | convolution fusion | flops 989970432 | bytes 19361792 | tf_op jit(solution)/shard_map/dot_general | solution.py:19
  279.5 0.0 collective-permute-done.22
  279.6 0.0 collective-permute-done.23
  279.6 1.4 add_bitcast_fusion
  (8 shorter events, 0.0 us)
Async XLA Ops:
  28.7 10.9 %collective-permute-start.2 = (bf16[2,312,768]{2,1,0:T(8,128)(2,1)}, bf16[2,312,768]{2,1,0:T(8,128)(2,1)}, u32[]{:S(2)}, u32[]{:S(2)}) collective-permute-start(bf16[2,312,768]{2,1,0:T(8,128)(2,1)} %get-tuple-element.45), channel_id=1, source_target_pairs={{0,1},{1,0},{2,3},{3,2},{4,5},{5,4},{6,7},{7,6}} | collective-permute-start | bytes 2875400 | tf_op jit(solution)/shard_map/ppermute | solution.py:473
  31.1 62.2 %collective-permute-start.5 = (bf16[768,1024]{1,0:T(8,128)(2,1)S(1)}, bf16[768,1024]{1,0:T(8,128)(2,1)}, u32[]{:S(2)}, u32[]{:S(2)}) collective-permute-start(bf16[768,1024]{1,0:T(8,128)(2,1)S(1)} %dynamic-slice_bitcast_fusion.1), channel_id=1, source_target_pairs={{0,4},{4,0},{1,5},{5,1},{2,6},{6,2},{3,7},{7,3}} | collective-permute-start | bytes 4718600 | tf_op jit(solution)/shard_map/ppermute | solution.py:476
  35.2 67.5 %collective-permute-start.6 = (bf16[1024,768]{1,0:T(8,128)(2,1)S(1)}, bf16[1024,768]{1,0:T(8,128)(2,1)}, u32[]{:S(2)}, u32[]{:S(2)}) collective-permute-start(bf16[1024,768]{1,0:T(8,128)(2,1)S(1)} %dynamic-slice_bitcast_fusion), channel_id=1, source_target_pairs={{0,4},{4,0},{1,5},{5,1},{2,6},{6,2},{3,7},{7,3}} | collective-permute-start | bytes 4718600 | tf_op jit(solution)/shard_map/ppermute | solution.py:476
  35.2 24.4 %collective-permute-start = (bf16[2,312,768]{2,1,0:T(8,128)(2,1)}, bf16[2,312,768]{2,1,0:T(8,128)(2,1)}, u32[]{:S(2)}, u32[]{:S(2)}) collective-permute-start(bf16[2,312,768]{2,1,0:T(8,128)(2,1)} %get-tuple-element.41), channel_id=1, source_target_pairs={{0,2},{1,3},{2,0},{3,1},{4,6},{5,7},{6,4},{7,5}} | collective-permute-start | bytes 2875400 | tf_op jit(solution)/shard_map/ppermute | solution.py:473
  37.2 41.5 %collective-permute-start.1 = (bf16[2,312,768]{2,1,0:T(8,128)(2,1)}, bf16[2,312,768]{2,1,0:T(8,128)(2,1)}, u32[]{:S(2)}, u32[]{:S(2)}) collective-permute-start(bf16[2,312,768]{2,1,0:T(8,128)(2,1)} %get-tuple-element.42), channel_id=1, source_target_pairs={{0,3},{1,2},{2,1},{3,0},{4,7},{5,6},{6,5},{7,4}} | collective-permute-start | bytes 2875400 | tf_op jit(solution)/shard_map/ppermute | solution.py:473
  39.6 80.1 %collective-permute-start.3 = (bf16[768,512]{1,0:T(8,128)(2,1)S(1)}, bf16[768,512]{1,0:T(8,128)(2,1)}, u32[]{:S(2)}, u32[]{:S(2)}) collective-permute-start(bf16[768,512]{1,0:T(8,128)(2,1)S(1)} %dynamic-slice_bitcast_fusion.3), channel_id=1, source_target_pairs={{0,4},{4,0},{1,5},{5,1},{2,6},{6,2},{3,7},{7,3}} | collective-permute-start | bytes 2359304 | tf_op jit(solution)/shard_map/ppermute | solution.py:476
  59.6 76.6 %collective-permute-start.4 = (bf16[512,768]{1,0:T(8,128)(2,1)S(1)}, bf16[512,768]{1,0:T(8,128)(2,1)}, u32[]{:S(2)}, u32[]{:S(2)}) collective-permute-start(bf16[512,768]{1,0:T(8,128)(2,1)S(1)} %dynamic-slice_bitcast_fusion.2), channel_id=1, source_target_pairs={{0,4},{4,0},{1,5},{5,1},{2,6},{6,2},{3,7},{7,3}} | collective-permute-start | bytes 2359304 | tf_op jit(solution)/shard_map/ppermute | solution.py:476
  78.7 73.8 %collective-permute-start.18 = (bf16[2,312,768]{2,1,0:T(8,128)(2,1)}, bf16[2,312,768]{2,1,0:T(8,128)(2,1)}, u32[]{:S(2)}, u32[]{:S(2)}) collective-permute-start(bf16[2,312,768]{2,1,0:T(8,128)(2,1)} %get-tuple-element.67), channel_id=1, source_target_pairs={{0,1},{1,0},{2,3},{3,2},{4,5},{5,4},{6,7},{7,6}} | collective-permute-start | bytes 2875400 | tf_op jit(solution)/shard_map/ppermute | solution.py:473
  93.3 71.0 %collective-permute-start.19 = (bf16[2,312,768]{2,1,0:T(8,128)(2,1)}, bf16[2,312,768]{2,1,0:T(8,128)(2,1)}, u32[]{:S(2)}, u32[]{:S(2)}) collective-permute-start(bf16[2,312,768]{2,1,0:T(8,128)(2,1)} %get-tuple-element.68), channel_id=1, source_target_pairs={{0,2},{1,3},{2,0},{3,1},{4,6},{5,7},{6,4},{7,5}} | collective-permute-start | bytes 2875400 | tf_op jit(solution)/shard_map/ppermute | solution.py:473
  102.7 62.9 %collective-permute-start.20 = (bf16[2,312,768]{2,1,0:T(8,128)(2,1)}, bf16[2,312,768]{2,1,0:T(8,128)(2,1)}, u32[]{:S(2)}, u32[]{:S(2)}) collective-permute-start(bf16[2,312,768]{2,1,0:T(8,128)(2,1)} %get-tuple-element.69), channel_id=1, source_target_pairs={{0,3},{1,2},{2,1},{3,0},{4,7},{5,6},{6,5},{7,4}} | collective-permute-start | bytes 2875400 | tf_op jit(solution)/shard_map/ppermute | solution.py:473
  142.8 34.2 %collective-permute-start.7 = (bf16[2,312,768]{2,1,0:T(8,128)(2,1)}, bf16[2,312,768]{2,1,0:T(8,128)(2,1)}, u32[]{:S(2)}, u32[]{:S(2)}) collective-permute-start(bf16[2,312,768]{2,1,0:T(8,128)(2,1)} %get-tuple-element.58), channel_id=1, source_target_pairs={{0,1},{1,0},{2,3},{3,2},{4,5},{5,4},{6,7},{7,6}} | collective-permute-start | bytes 2875400 | tf_op jit(solution)/shard_map/ppermute | solution.py:473
  150.8 16.4 %collective-permute-start.9 = (bf16[312,768]{1,0:T(8,128)(2,1)}, bf16[312,768]{1,0:T(8,128)(2,1)}, u32[]{:S(2)}, u32[]{:S(2)}) collective-permute-start(bf16[312,768]{1,0:T(8,128)(2,1)} %get-tuple-element.59), channel_id=1, source_target_pairs={{0,2},{1,3},{2,0},{3,1},{4,6},{5,7},{6,4},{7,5}} | collective-permute-start | bytes 1437704 | tf_op jit(solution)/shard_map/ppermute | solution.py:473
  152.5 22.7 %collective-permute-start.14 = (bf16[312,768]{1,0:T(8,128)(2,1)}, bf16[312,768]{1,0:T(8,128)(2,1)}, u32[]{:S(2)}, u32[]{:S(2)}) collective-permute-start(bf16[312,768]{1,0:T(8,128)(2,1)} %get-tuple-element.63), channel_id=1, source_target_pairs={{0,2},{1,3},{2,0},{3,1},{4,6},{5,7},{6,4},{7,5}} | collective-permute-start | bytes 1437704 | tf_op jit(solution)/shard_map/ppermute | solution.py:473
  164.4 31.6 %collective-permute-start.11 = (bf16[312,768]{1,0:T(8,128)(2,1)}, bf16[312,768]{1,0:T(8,128)(2,1)}, u32[]{:S(2)}, u32[]{:S(2)}) collective-permute-start(bf16[312,768]{1,0:T(8,128)(2,1)} %get-tuple-element.60), channel_id=1, source_target_pairs={{0,3},{1,2},{2,1},{3,0},{4,7},{5,6},{6,5},{7,4}} | collective-permute-start | bytes 1437704 | tf_op jit(solution)/shard_map/ppermute | solution.py:473
  165.7 32.4 %collective-permute-start.13 = (bf16[2,312,768]{2,1,0:T(8,128)(2,1)}, bf16[2,312,768]{2,1,0:T(8,128)(2,1)}, u32[]{:S(2)}, u32[]{:S(2)}) collective-permute-start(bf16[2,312,768]{2,1,0:T(8,128)(2,1)} %get-tuple-element.61.refs_0_), channel_id=1, source_target_pairs={{0,4},{4,0},{1,5},{5,1},{2,6},{6,2},{3,7},{7,3}} | collective-permute-start | bytes 2875400 | tf_op jit(solution)/shard_map/ppermute | solution.py:476
  167.2 30.6 %collective-permute-start.15 = (bf16[312,768]{1,0:T(8,128)(2,1)}, bf16[312,768]{1,0:T(8,128)(2,1)}, u32[]{:S(2)}, u32[]{:S(2)}) collective-permute-start(bf16[312,768]{1,0:T(8,128)(2,1)} %get-tuple-element.64), channel_id=1, source_target_pairs={{0,3},{1,2},{2,1},{3,0},{4,7},{5,6},{6,5},{7,4}} | collective-permute-start | bytes 1437704 | tf_op jit(solution)/shard_map/ppermute | solution.py:473
  175.2 35.2 %collective-permute-start.16 = (bf16[312,768]{1,0:T(8,128)(2,1)}, bf16[312,768]{1,0:T(8,128)(2,1)}, u32[]{:S(2)}, u32[]{:S(2)}) collective-permute-start(bf16[312,768]{1,0:T(8,128)(2,1)} %collective-permute-done.14.refs_2_), channel_id=1, source_target_pairs={{0,4},{4,0},{1,5},{5,1},{2,6},{6,2},{3,7},{7,3}} | collective-permute-start | bytes 1437704 | tf_op jit(solution)/shard_map/ppermute | solution.py:476
  176.9 64.5 %collective-permute-start.8 = (bf16[2,312,768]{2,1,0:T(8,128)(2,1)}, bf16[2,312,768]{2,1,0:T(8,128)(2,1)}, u32[]{:S(2)}, u32[]{:S(2)}) collective-permute-start(bf16[2,312,768]{2,1,0:T(8,128)(2,1)} %collective-permute-done.7.refs_1_), channel_id=1, source_target_pairs={{0,4},{4,0},{1,5},{5,1},{2,6},{6,2},{3,7},{7,3}} | collective-permute-start | bytes 2875400 | tf_op jit(solution)/shard_map/ppermute | solution.py:476
  196.0 35.2 %collective-permute-start.10 = (bf16[312,768]{1,0:T(8,128)(2,1)}, bf16[312,768]{1,0:T(8,128)(2,1)}, u32[]{:S(2)}, u32[]{:S(2)}) collective-permute-start(bf16[312,768]{1,0:T(8,128)(2,1)} %collective-permute-done.9.refs_2_), channel_id=1, source_target_pairs={{0,4},{4,0},{1,5},{5,1},{2,6},{6,2},{3,7},{7,3}} | collective-permute-start | bytes 1437704 | tf_op jit(solution)/shard_map/ppermute | solution.py:476
  197.8 43.7 %collective-permute-start.12 = (bf16[312,768]{1,0:T(8,128)(2,1)}, bf16[312,768]{1,0:T(8,128)(2,1)}, u32[]{:S(2)}, u32[]{:S(2)}) collective-permute-start(bf16[312,768]{1,0:T(8,128)(2,1)} %collective-permute-done.11.refs_3_), channel_id=1, source_target_pairs={{0,4},{4,0},{1,5},{5,1},{2,6},{6,2},{3,7},{7,3}} | collective-permute-start | bytes 1437704 | tf_op jit(solution)/shard_map/ppermute | solution.py:476
  198.0 73.5 %collective-permute-start.17 = (bf16[312,768]{1,0:T(8,128)(2,1)}, bf16[312,768]{1,0:T(8,128)(2,1)}, u32[]{:S(2)}, u32[]{:S(2)}) collective-permute-start(bf16[312,768]{1,0:T(8,128)(2,1)} %collective-permute-done.15.refs_3_), channel_id=1, source_target_pairs={{0,4},{4,0},{1,5},{5,1},{2,6},{6,2},{3,7},{7,3}} | collective-permute-start | bytes 1437704 | tf_op jit(solution)/shard_map/ppermute | solution.py:476
  253.5 26.1 %collective-permute-start.22 = (f32[8,768]{1,0:T(8,128)}, f32[8,768]{1,0:T(8,128)}, u32[]{:S(2)}, u32[]{:S(2)}) collective-permute-start(f32[8,768]{1,0:T(8,128)} %get-tuple-element.76), channel_id=1, source_target_pairs={{0,2},{1,3},{2,0},{3,1},{4,6},{5,7},{6,4},{7,5}} | collective-permute-start | bytes 73736 | tf_op jit(solution)/shard_map/ppermute | solution.py:473
  254.0 25.5 %collective-permute-start.23 = (f32[8,768]{1,0:T(8,128)}, f32[8,768]{1,0:T(8,128)}, u32[]{:S(2)}, u32[]{:S(2)}) collective-permute-start(f32[8,768]{1,0:T(8,128)} %get-tuple-element.76), channel_id=1, source_target_pairs={{0,3},{1,2},{2,1},{3,0},{4,7},{5,6},{6,5},{7,4}} | collective-permute-start | bytes 73736 | tf_op jit(solution)/shard_map/ppermute | solution.py:473
  254.2 25.4 %collective-permute-start.21 = (f32[8,768]{1,0:T(8,128)}, f32[8,768]{1,0:T(8,128)}, u32[]{:S(2)}, u32[]{:S(2)}) collective-permute-start(f32[8,768]{1,0:T(8,128)} %get-tuple-element.76), channel_id=1, source_target_pairs={{0,1},{1,0},{2,3},{3,2},{4,5},{5,4},{6,7},{7,6}} | collective-permute-start | bytes 73736 | tf_op jit(solution)/shard_map/ppermute | solution.py:473
  271.6 8.0 %copy-start = (f32[8,768]{1,0:T(8,128)S(1)}, f32[8,768]{1,0:T(8,128)}, u32[]{:S(2)}) copy-start(f32[8,768]{1,0:T(8,128)} %get-tuple-element.76) | copy-start | bytes 73732

commit v8 on v7

--- a/solution.py
+++ b/solution.py
@@ -169,7 +169,7 @@
         out_shape=[shape((2, cap, d_model))] * (2 * count),
         compiler_params=params(1, SMALL_VMEM),
         cost_estimate=cost(8 * count * cap * n_tok * d_model, 8 + 4 * count),
-        name="dispatch",
+        name="disp",
     )(meta, info, tokens, grad_out)
 
 
@@ -227,7 +227,7 @@
         input_output_aliases={5 + i: i for i in range(len(so_far))},
         compiler_params=params(1, SMALL_VMEM),
         cost_estimate=cost(8 * rows * width * d_model, 20),
-        name="own_half",
+        name="own",
     )(meta, pair_a, pair_b, w_in, w_out, *so_far)
 
 
@@ -287,7 +287,7 @@
         out_shape=out_shape,
         compiler_params=params(2, SMALL_VMEM if group is None else VMEM_LIMIT),
         cost_estimate=cost(8 * rows * blocks * width * d_model, 10),
-        name="far_half",
+        name="far",
     )(x, dy, wi, wo, y_in, s_in)
 
 
@@ -314,7 +314,7 @@
         out_shape=[shape((n_local, d_model, width), F32), shape((n_local, width, d_model), F32)],
         compiler_params=params(1),
         cost_estimate=cost(4 * rows * width * d_model, 25),
-        name="finished_grads",
+        name="grads_a",
     )(meta, x, dy, h, da)
 
 
@@ -356,7 +356,7 @@
         input_output_aliases={len(pairs) + 3: 0, len(pairs) + 4: 1},
         compiler_params=params(1),
         cost_estimate=cost(8 * rows * width * d_model, 25),
-        name="other_grads",
+        name="grads_b",
     )(meta, *pairs, w_in, w_out, grad_w_in, grad_w_out)
 
 
@@ -433,7 +433,7 @@
         out_shape=[shape((n_tok, d_model)), shape((n_tok, n_experts)), shape((n_experts, d_model), F32)],
         compiler_params=params(1),
         cost_estimate=cost(2 * n_tok * cap * len(keys) * d_model, 16),
-        name="combine_y",
+        name="comb_y",
     )(meta, *rows, info, so_far, tokens, grad_out)
 
 
@@ -461,7 +461,7 @@
         out_shape=shape((n_tok, d_model)),
         compiler_params=params(1),
         cost_estimate=cost(2 * n_tok * cap * len(keys) * d_model, 10),
-        name="combine_s",
+        name="comb_s",
     )(meta, *rows, info)
 
 
@@ -504,7 +504,7 @@
 
         part = own_half(meta, f0, f1, w_in, w_out, chunk, 0, ())
         h, da, y, s, x, dy = own_half(meta, f2, f3, w_in, w_out, chunk, 1, part)
-        y, s = far_half(x, dy, *far_w["a"], y, s, chunk, None, False)
+        y, s = far_half(x, dy, *far_w["a"], y, s, 2 * chunk, None, False)
         grads = finished_grads(meta, x, dy, h, da, w_in.shape[0], chunk)
         ys0, ys1 = far_half(x, dy, *far_w["b"], y, s, chunk, 0, True)
         y2, y3, s2, s3 = far_half(x, dy, *far_w["b"], y, s, chunk, 1, False)

time: 282 us -> 282 us (level)
  transfers between devices with their start and end apart: 24 -> 24, of which waited for: 7 -> 8; matrix products, arithmetic and copies ran while one was open for 9% -> 9% of each run, Pallas kernels for 43% -> 43%
where the time goes in v8:
time: 282 us; the launch traced here: 281 us
  Pallas kernels  147 us (52%)
  waiting for transfers between devices  81.7 us (29%)
  starting transfers between devices  25.5 us (9%)
  matrix products  17.4 us (6%)
  local copies, waits for them, and re-layouts  5.41 us (2%)
  other arithmetic  3.35 us (1%)
    ppermute x10, waiting for transfers between devices, to_twin(): return lax.ppermute(v, 'tp', [(0, 1), (1, 0)])  52.3 us
    ppermute x14, waiting for transfers between devices, to_ep(): return lax.ppermute(v, 'ep', [(i, i ^ d) for i in range(ep_size)])  29.4 us
    pallas_call x2, Pallas kernels, own_half(): pl.pallas_call(body, grid_spec=pltpu.PrefetchScalarGridSpec(num_scalar_pr...  27.6 us
    pallas_call x3, Pallas kernels, far_half(): pl.pallas_call(body, grid=(blocks, steps), in_specs=[full, full, pl.Block...  27.4 us
    pallas_call x2, Pallas kernels, combine_s(): pl.pallas_call(body, grid_spec=pltpu.PrefetchScalarGridSpec(num_scalar_pr...  22 us
    pallas_call x1, Pallas kernels, other_grads(): pl.pallas_call(body, grid_spec=pltpu.PrefetchScalarGridSpec(num_scalar_pr...  19 us
    pallas_call x1, Pallas kernels, dispatch(): pl.pallas_call(body, grid_spec=pltpu.PrefetchScalarGridSpec(num_scalar_pr...  17.7 us
    dot_general x3, matrix products, nn(): return jnp.dot(a, b, preferred_element_type=F32)  17.4 us
  transfers between devices with their start and end apart: 24, of which 8 were waited for; matrix products, arithmetic and copies ran while one was open for 9% of the time, Pallas kernels for 43%

profile of v8, /device:TPU:0, one launch (start us, length us, event | category | flops | bytes accessed | tf_op | source)
XLA Modules:
  0.0 281.3 jit_solution(17471748243102956432)
XLA Ops:
  0.6 0.5 compare_select_fusion.meta_ref
  1.1 9.9 %route.1 = (f32[16,2048]{1,0:T(8,128)}, bf16[2,312,768]{2,1,0:T(8,128)(2,1)}, bf16[2,312,768]{2,1,0:T(8,128)(2,1)}) custom-call(s32[2]{0:T(128)} %compare_select_fusion.meta_ref, s32[1,2048]{1,0:T(1,128)} %bitcast.21, bf16[2048,768]{1,0:T(8,128)(2,1)} %refs_5_.2, bf16[8,768]{1,0:T(8,128)(2,1)} %bitcast.20, bf16[2048,768]{1,0:T(8,128)(2,1)} %refs_6_.1), custom_call_target="tpu_custom_call" | custom-call | flops 3925868544 | bytes 10485760 | tf_op jit(solution)/shard_map/route/pallas_call | solution.py:109
  11.0 17.7 %disp.1 = (bf16[2,312,768]{2,1,0:T(8,128)(2,1)}, bf16[2,312,768]{2,1,0:T(8,128)(2,1)}, bf16[2,312,768]{2,1,0:T(8,128)(2,1)}, bf16[2,312,768]{2,1,0:T(8,128)(2,1)...) custom-call(s32[2]{0:T(128)} %compare_select_fusion.meta_ref, ...), custom_call_target="tpu_custom_call" | custom-call | flops 11777605632 | bytes 20971520 | tf_op jit(solution)/shard_map/disp/pallas_call | solution.py:157
  28.7 0.8 collective-permute-start.2
  29.6 1.5 dynamic-slice_bitcast_fusion.1
  31.1 2.6 collective-permute-start.5
  33.7 1.5 dynamic-slice_bitcast_fusion
  35.2 0.0 collective-permute-start.6
  35.2 2.0 collective-permute-start
  37.2 0.0 collective-permute-start.1
  37.2 1.2 dynamic-slice_bitcast_fusion.3
  38.4 1.2 dynamic-slice_bitcast_fusion.2
  39.6 0.0 collective-permute-done.2.pb
  39.6 1.5 collective-permute-start.3
  41.1 13.8 %own.2 = (bf16[1248,1536]{1,0:T(8,128)(2,1)}, bf16[1248,1536]{1,0:T(8,128)(2,1)}, f32[1248,768]{1,0:T(8,128)}, f32[1248,768]{1,0:T(8,128)}, bf16[1248,768]{1,0:T(8,128)(2,1)}, /*index=5*/bf16[1248,768]{1,0:T(8,128)(2,1)}) custom-call(s32[2]{0:T(128)} %compare_select_fusion.meta_ref, bf16[2,312,768]{2,1,0:T(8,128)(2,1)} %get-tuple-element.44.pa, ...), custom_call_target="tpu_custom_call" | custom-call | flops 5888802816 | bytes 20971520 | tf_op jit(solution)/shard_map/own/pallas_call | solution.py:210
  54.9 4.8 %collective-permute-done.pa = bf16[2,312,768]{2,1,0:T(8,128)(2,1)} collective-permute-done((bf16[2,312,768]{2,1,0:T(8,128)(2,1)}, bf16[2,312,768]{2,1,0:T(8,128)(2,1)}, u32[]{:S(2)}, u32[]{:S(2)}) %collective-permute-start) | collective-permute-done | bytes 958496 | tf_op jit(solution)/shard_map/ppermute | solution.py:473
  59.6 2.0 collective-permute-start.4
  61.6 17.0 %collective-permute-done.1.pb = bf16[2,312,768]{2,1,0:T(8,128)(2,1)} collective-permute-done((bf16[2,312,768]{2,1,0:T(8,128)(2,1)}, bf16[2,312,768]{2,1,0:T(8,128)(2,1)}, u32[]{:S(2)}, u32[]{:S(2)}) %collective-permute-start.1) | collective-permute-done | bytes 958496 | tf_op jit(solution)/shard_map/ppermute | solution.py:473
  78.7 0.9 collective-permute-start.18
  79.5 13.8 %own.3 = (bf16[1248,1536]{1,0:T(8,128)(2,1)}, bf16[1248,1536]{1,0:T(8,128)(2,1)}, f32[1248,768]{1,0:T(8,128)}, f32[1248,768]{1,0:T(8,128)}, bf16[1248,768]{1,0:T(8,128)(2,1)}, /*index=5*/bf16[1248,768]{1,0:T(8,128)(2,1)}) custom-call(s32[2]{0:T(128)} %compare_select_fusion.meta_ref, ...), custom_call_target="tpu_custom_call", output_to_operand_aliasing={{0}: (5, {}), {1}: (6, {}), {2}: (7, {}), {3}: (8, {}), {4}... | custom-call | flops 5888802816 | bytes 20971520 | tf_op jit(solution)/shard_map/own/pallas_call | solution.py:210
  93.3 0.0 collective-permute-done.5.wi_ref
  93.3 1.7 collective-permute-start.19
  95.0 7.7 %collective-permute-done.6.wo_ref = bf16[1024,768]{1,0:T(8,128)(2,1)} collective-permute-done((bf16[1024,768]{1,0:T(8,128)(2,1)S(1)}, bf16[1024,768]{1,0:T(8,128)(2,1)}, u32[]{:S(2)}, u32[]{:S(2)}) %collective-permute-start.6) | collective-permute-done | bytes 1572896 | tf_op jit(solution)/shard_map/ppermute | solution.py:476
  102.7 0.7 collective-permute-start.20
  103.5 14.3 %far.3 = (f32[1248,768]{1,0:T(8,128)}, f32[1248,768]{1,0:T(8,128)}) custom-call(bf16[1248,768]{1,0:T(8,128)(2,1)} %get-tuple-element.52.x_ref, bf16[1248,768]{1,0:T(8,128)(2,1)} %get-tuple-element.53.dy_ref, bf16[768,1024]{1,0:T(8,128)(2,1)} %collective-permute-done.5.wi_ref, bf16[1024,768]{1,0:T(8,128)(2,1)} %collective-permute-done.6.wo_ref, ...), custom_call_target="tpu_custom_call" | custom-call | flops 7851737088 | bytes 10485760 | tf_op jit(solution)/shard_map/far/pallas_call | solution.py:275
  117.7 1.8 collective-permute-done.3.wi_ref
  119.6 16.6 %collective-permute-done.4.wo_ref = bf16[512,768]{1,0:T(8,128)(2,1)} collective-permute-done((bf16[512,768]{1,0:T(8,128)(2,1)S(1)}, bf16[512,768]{1,0:T(8,128)(2,1)}, u32[]{:S(2)}, u32[]{:S(2)}) %collective-permute-start.4) | collective-permute-done | bytes 786464 | tf_op jit(solution)/shard_map/ppermute | solution.py:476
  136.2 6.5 %far.4 = (bf16[2,312,768]{2,1,0:T(8,128)(2,1)}, bf16[2,312,768]{2,1,0:T(8,128)(2,1)}) custom-call(bf16[1248,768]{1,0:T(8,128)(2,1)} %get-tuple-element.52.x_ref, bf16[1248,768]{1,0:T(8,128)(2,1)} %get-tuple-element.53.dy_ref, bf16[768,512]{1,0:T(8,128)(2,1)} %collective-permute-done.3.wi_ref, bf16[512,768]{1,0:T(8,128)(2,1)} %collective-permute-done.4.wo_ref, ...), custom_call_target="tpu_custom_call" | custom-call | flops 1962934272 | bytes 10485760 | tf_op jit(solution)/shard_map/far/pallas_call | solution.py:275
  142.7 0.0 collective-permute-start.7
  142.7 1.5 convert_subtract_fusion
  144.2 6.6 %far.5 = (bf16[312,768]{1,0:T(8,128)(2,1)}, bf16[312,768]{1,0:T(8,128)(2,1)}, bf16[312,768]{1,0:T(8,128)(2,1)}, bf16[312,768]{1,0:T(8,128)(2,1)}) custom-call(bf16[1248,768]{1,0:T(8,128)(2,1)} %get-tuple-element.52.x_ref, bf16[1248,768]{1,0:T(8,128)(2,1)} %get-tuple-element.53.dy_ref, bf16[768,512]{1,0:T(8,128)(2,1)} %collective-permute-done.3.wi_ref, ...), custom_call_target="tpu_custom_call" | custom-call | flops 1962934272 | bytes 10485760 | tf_op jit(solution)/shard_map/far/pallas_call | solution.py:275
  150.8 1.7 collective-permute-start.9
  152.5 0.0 collective-permute-done.18.refs_1_
  152.5 0.3 collective-permute-start.14
  152.8 11.6 %grads_a.1 = (f32[2,768,1536]{2,1,0:T(8,128)}, f32[2,1536,768]{2,1,0:T(8,128)}) custom-call(s32[2]{0:T(128)} %compare_select_fusion.meta_ref, bf16[1248,768]{1,0:T(8,128)(2,1)} %get-tuple-element.52.x_ref, bf16[1248,768]{1,0:T(8,128)(2,1)} %get-tuple-element.53.dy_ref, bf16[1248,1536]{1,0:T(8,128)(2,1)} %get-tuple-element.70.h_ref, ...), custom_call_target="tpu_custom_call" | custom-call | flops 5888802816 | bytes 26214400 | tf_op jit(solution)/shard_map/grads_a/pallas_call | solution.py:303
  164.4 0.0 collective-permute-done.19.refs_2_
  164.4 1.3 collective-permute-start.11
  165.7 0.0 collective-permute-done.20.refs_3_
  165.7 1.5 collective-permute-start.13
  167.2 0.0 collective-permute-done.9.refs_2_
  167.2 0.4 collective-permute-start.15
  167.6 7.6 %collective-permute-done.14.refs_2_ = bf16[312,768]{1,0:T(8,128)(2,1)} collective-permute-done((bf16[312,768]{1,0:T(8,128)(2,1)}, bf16[312,768]{1,0:T(8,128)(2,1)}, u32[]{:S(2)}, u32[]{:S(2)}) %collective-permute-start.14) | collective-permute-done | bytes 479264 | tf_op jit(solution)/shard_map/ppermute | solution.py:473
  175.2 1.7 collective-permute-start.16
  176.9 0.3 collective-permute-start.8
  177.2 19.0 %grads_b.1 = (f32[2,768,1536]{2,1,0:T(8,128)}, f32[2,1536,768]{2,1,0:T(8,128)}) custom-call(s32[2]{0:T(128)} %compare_select_fusion.meta_ref, bf16[2,312,768]{2,1,0:T(8,128)(2,1)} %get-tuple-element.66.refs_0_, bf16[2,312,768]{2,1,0:T(8,128)(2,1)} %collective-permute-done.18.refs_1_, ...), custom_call_target="tpu_custom_call", output_to_operand_aliasing={{0}: (7, {}), {1}: (8, {})} | custom-call | flops 11777605632 | bytes 26214400 | tf_op jit(solution)/shard_map/grads_b/pallas_call | solution.py:346
  196.3 1.8 collective-permute-start.10
  198.0 0.0 collective-permute-done.15.refs_3_
  198.0 0.3 collective-permute-start.12
  198.3 1.7 collective-permute-start.17
  200.0 10.4 %comb_s.2.refs_4_ = bf16[2048,768]{1,0:T(8,128)(2,1)} custom-call(s32[2]{0:T(128)} %compare_select_fusion.meta_ref, bf16[2,312,768]{2,1,0:T(8,128)(2,1)} %get-tuple-element.61.refs_0_, bf16[2,312,768]{2,1,0:T(8,128)(2,1)} %collective-permute-done.7.refs_1_, bf16[312,768]{1,0:T(8,128)(2,1)} %collective-permute-done.9.refs_2_, ...), custom_call_target="tpu_custom_call" | custom-call | flops 4907335680 | bytes 10485760 | tf_op jit(solution)/shard_map/comb_s/pallas_call | solution.py:452
  210.4 4.9 %fusion = f32[2048,768]{1,0:T(8,128)} fusion(bf16[312,768]{1,0:T(8,128)(2,1)} %collective-permute-done.16, s32[2048]{0:T(1024)} %bitcast.18), kind=kOutput, calls=%fused_computation.3 | convolution fusion | flops 982106112 | bytes 6778880 | tf_op jit(solution)/shard_map/dot_general | solution.py:19
  215.3 15.9 %collective-permute-done.10.refs_1_ = bf16[312,768]{1,0:T(8,128)(2,1)} collective-permute-done((bf16[312,768]{1,0:T(8,128)(2,1)}, bf16[312,768]{1,0:T(8,128)(2,1)}, u32[]{:S(2)}, u32[]{:S(2)}) %collective-permute-start.10) | collective-permute-done | bytes 479264 | tf_op jit(solution)/shard_map/ppermute | solution.py:476
  231.1 10.3 %collective-permute-done.12.refs_2_ = bf16[312,768]{1,0:T(8,128)(2,1)} collective-permute-done((bf16[312,768]{1,0:T(8,128)(2,1)}, bf16[312,768]{1,0:T(8,128)(2,1)}, u32[]{:S(2)}, u32[]{:S(2)}) %collective-permute-start.12) | collective-permute-done | bytes 479264 | tf_op jit(solution)/shard_map/ppermute | solution.py:476
  241.4 12.1 %comb_y.1 = (bf16[2048,768]{1,0:T(8,128)(2,1)}, bf16[2048,8]{1,0:T(8,128)(2,1)}, f32[8,768]{1,0:T(8,128)}) custom-call(s32[2]{0:T(128)} %compare_select_fusion.meta_ref, bf16[2,312,768]{2,1,0:T(8,128)(2,1)} %collective-permute-done.8.refs_0_.refs_5_, bf16[312,768]{1,0:T(8,128)(2,1)} %collective-permute-done.10.refs_1_, ...), custom_call_target="tpu_custom_call" | custom-call | flops 2944401408 | bytes 16777216 | tf_op jit(solution)/shard_map/comb_y/pallas_call | solution.py:423
  253.5 0.5 collective-permute-start.22
  254.0 0.2 collective-permute-start.23
  254.2 1.5 collective-permute-start.21
  255.6 4.6 %fusion.4 = f32[2048,768]{1,0:T(8,128)} fusion(bf16[2048,8]{1,0:T(8,128)(2,1)} %get-tuple-element.65, bf16[768,8]{0,1:T(8,128)(2,1)} %param.8), kind=kOutput, calls=%fused_computation.15 | convolution fusion | flops 25165824 | bytes 6336512 | tf_op jit(solution)/shard_map/dot_general | solution.py:19
  260.2 11.7 %comb_s.3 = bf16[2048,768]{1,0:T(8,128)(2,1)} custom-call(s32[2]{0:T(128)} %compare_select_fusion.meta_ref, bf16[2,312,768]{2,1,0:T(8,128)(2,1)} %get-tuple-element.61.refs_0_, bf16[2,312,768]{2,1,0:T(8,128)(2,1)} %collective-permute-done.7.refs_1_, bf16[312,768]{1,0:T(8,128)(2,1)} %collective-permute-done.14.refs_2_, ...), custom_call_target="tpu_custom_call" | custom-call | flops 5888802816 | bytes 10485760 | tf_op jit(solution)/shard_map/comb_s/pallas_call | solution.py:452
  271.9 0.0 collective-permute-done.17
  271.9 8.0 %add_convert_fusion = bf16[2048,768]{1,0:T(8,128)(2,1)} fusion(f32[2048,768]{1,0:T(8,128)} %fusion, f32[2048,768]{1,0:T(8,128)} %fusion.4, bf16[2048,768]{1,0:T(8,128)(2,1)} %comb_s.3, bf16[312,768]{1,0:T(8,128)(2,1)} %collective-permute-done.17, s32[2048]{0:T(1024)} %bitcast.19), kind=kOutput, calls=%fused_computation | convolution fusion | flops 989970432 | bytes 19361792 | tf_op jit(solution)/shard_map/dot_general | solution.py:19
  279.8 0.0 collective-permute-done.22
  279.8 0.0 collective-permute-done.21
  279.9 1.4 add_bitcast_fusion
  (8 shorter events, 0.0 us)
Async XLA Ops:
  28.7 10.9 %collective-permute-start.2 = (bf16[2,312,768]{2,1,0:T(8,128)(2,1)}, bf16[2,312,768]{2,1,0:T(8,128)(2,1)}, u32[]{:S(2)}, u32[]{:S(2)}) collective-permute-start(bf16[2,312,768]{2,1,0:T(8,128)(2,1)} %get-tuple-element.45), channel_id=1, source_target_pairs={{0,1},{1,0},{2,3},{3,2},{4,5},{5,4},{6,7},{7,6}} | collective-permute-start | bytes 2875400 | tf_op jit(solution)/shard_map/ppermute | solution.py:473
  31.1 62.2 %collective-permute-start.5 = (bf16[768,1024]{1,0:T(8,128)(2,1)S(1)}, bf16[768,1024]{1,0:T(8,128)(2,1)}, u32[]{:S(2)}, u32[]{:S(2)}) collective-permute-start(bf16[768,1024]{1,0:T(8,128)(2,1)S(1)} %dynamic-slice_bitcast_fusion.1), channel_id=1, source_target_pairs={{0,4},{4,0},{1,5},{5,1},{2,6},{6,2},{3,7},{7,3}} | collective-permute-start | bytes 4718600 | tf_op jit(solution)/shard_map/ppermute | solution.py:476
  35.2 67.5 %collective-permute-start.6 = (bf16[1024,768]{1,0:T(8,128)(2,1)S(1)}, bf16[1024,768]{1,0:T(8,128)(2,1)}, u32[]{:S(2)}, u32[]{:S(2)}) collective-permute-start(bf16[1024,768]{1,0:T(8,128)(2,1)S(1)} %dynamic-slice_bitcast_fusion), channel_id=1, source_target_pairs={{0,4},{4,0},{1,5},{5,1},{2,6},{6,2},{3,7},{7,3}} | collective-permute-start | bytes 4718600 | tf_op jit(solution)/shard_map/ppermute | solution.py:476
  35.2 24.4 %collective-permute-start = (bf16[2,312,768]{2,1,0:T(8,128)(2,1)}, bf16[2,312,768]{2,1,0:T(8,128)(2,1)}, u32[]{:S(2)}, u32[]{:S(2)}) collective-permute-start(bf16[2,312,768]{2,1,0:T(8,128)(2,1)} %get-tuple-element.41), channel_id=1, source_target_pairs={{0,2},{1,3},{2,0},{3,1},{4,6},{5,7},{6,4},{7,5}} | collective-permute-start | bytes 2875400 | tf_op jit(solution)/shard_map/ppermute | solution.py:473
  37.2 41.5 %collective-permute-start.1 = (bf16[2,312,768]{2,1,0:T(8,128)(2,1)}, bf16[2,312,768]{2,1,0:T(8,128)(2,1)}, u32[]{:S(2)}, u32[]{:S(2)}) collective-permute-start(bf16[2,312,768]{2,1,0:T(8,128)(2,1)} %get-tuple-element.42), channel_id=1, source_target_pairs={{0,3},{1,2},{2,1},{3,0},{4,7},{5,6},{6,5},{7,4}} | collective-permute-start | bytes 2875400 | tf_op jit(solution)/shard_map/ppermute | solution.py:473
  39.6 80.0 %collective-permute-start.3 = (bf16[768,512]{1,0:T(8,128)(2,1)S(1)}, bf16[768,512]{1,0:T(8,128)(2,1)}, u32[]{:S(2)}, u32[]{:S(2)}) collective-permute-start(bf16[768,512]{1,0:T(8,128)(2,1)S(1)} %dynamic-slice_bitcast_fusion.3), channel_id=1, source_target_pairs={{0,4},{4,0},{1,5},{5,1},{2,6},{6,2},{3,7},{7,3}} | collective-permute-start | bytes 2359304 | tf_op jit(solution)/shard_map/ppermute | solution.py:476
  59.6 76.6 %collective-permute-start.4 = (bf16[512,768]{1,0:T(8,128)(2,1)S(1)}, bf16[512,768]{1,0:T(8,128)(2,1)}, u32[]{:S(2)}, u32[]{:S(2)}) collective-permute-start(bf16[512,768]{1,0:T(8,128)(2,1)S(1)} %dynamic-slice_bitcast_fusion.2), channel_id=1, source_target_pairs={{0,4},{4,0},{1,5},{5,1},{2,6},{6,2},{3,7},{7,3}} | collective-permute-start | bytes 2359304 | tf_op jit(solution)/shard_map/ppermute | solution.py:476
  78.7 73.8 %collective-permute-start.18 = (bf16[2,312,768]{2,1,0:T(8,128)(2,1)}, bf16[2,312,768]{2,1,0:T(8,128)(2,1)}, u32[]{:S(2)}, u32[]{:S(2)}) collective-permute-start(bf16[2,312,768]{2,1,0:T(8,128)(2,1)} %get-tuple-element.67), channel_id=1, source_target_pairs={{0,1},{1,0},{2,3},{3,2},{4,5},{5,4},{6,7},{7,6}} | collective-permute-start | bytes 2875400 | tf_op jit(solution)/shard_map/ppermute | solution.py:473
  93.3 71.0 %collective-permute-start.19 = (bf16[2,312,768]{2,1,0:T(8,128)(2,1)}, bf16[2,312,768]{2,1,0:T(8,128)(2,1)}, u32[]{:S(2)}, u32[]{:S(2)}) collective-permute-start(bf16[2,312,768]{2,1,0:T(8,128)(2,1)} %get-tuple-element.68), channel_id=1, source_target_pairs={{0,2},{1,3},{2,0},{3,1},{4,6},{5,7},{6,4},{7,5}} | collective-permute-start | bytes 2875400 | tf_op jit(solution)/shard_map/ppermute | solution.py:473
  102.7 62.9 %collective-permute-start.20 = (bf16[2,312,768]{2,1,0:T(8,128)(2,1)}, bf16[2,312,768]{2,1,0:T(8,128)(2,1)}, u32[]{:S(2)}, u32[]{:S(2)}) collective-permute-start(bf16[2,312,768]{2,1,0:T(8,128)(2,1)} %get-tuple-element.69), channel_id=1, source_target_pairs={{0,3},{1,2},{2,1},{3,0},{4,7},{5,6},{6,5},{7,4}} | collective-permute-start | bytes 2875400 | tf_op jit(solution)/shard_map/ppermute | solution.py:473
  142.7 34.2 %collective-permute-start.7 = (bf16[2,312,768]{2,1,0:T(8,128)(2,1)}, bf16[2,312,768]{2,1,0:T(8,128)(2,1)}, u32[]{:S(2)}, u32[]{:S(2)}) collective-permute-start(bf16[2,312,768]{2,1,0:T(8,128)(2,1)} %get-tuple-element.58), channel_id=1, source_target_pairs={{0,1},{1,0},{2,3},{3,2},{4,5},{5,4},{6,7},{7,6}} | collective-permute-start | bytes 2875400 | tf_op jit(solution)/shard_map/ppermute | solution.py:473
  150.8 16.4 %collective-permute-start.9 = (bf16[312,768]{1,0:T(8,128)(2,1)}, bf16[312,768]{1,0:T(8,128)(2,1)}, u32[]{:S(2)}, u32[]{:S(2)}) collective-permute-start(bf16[312,768]{1,0:T(8,128)(2,1)} %get-tuple-element.59), channel_id=1, source_target_pairs={{0,2},{1,3},{2,0},{3,1},{4,6},{5,7},{6,4},{7,5}} | collective-permute-start | bytes 1437704 | tf_op jit(solution)/shard_map/ppermute | solution.py:473
  152.5 22.7 %collective-permute-start.14 = (bf16[312,768]{1,0:T(8,128)(2,1)}, bf16[312,768]{1,0:T(8,128)(2,1)}, u32[]{:S(2)}, u32[]{:S(2)}) collective-permute-start(bf16[312,768]{1,0:T(8,128)(2,1)} %get-tuple-element.63), channel_id=1, source_target_pairs={{0,2},{1,3},{2,0},{3,1},{4,6},{5,7},{6,4},{7,5}} | collective-permute-start | bytes 1437704 | tf_op jit(solution)/shard_map/ppermute | solution.py:473
  164.4 31.9 %collective-permute-start.11 = (bf16[312,768]{1,0:T(8,128)(2,1)}, bf16[312,768]{1,0:T(8,128)(2,1)}, u32[]{:S(2)}, u32[]{:S(2)}) collective-permute-start(bf16[312,768]{1,0:T(8,128)(2,1)} %get-tuple-element.60), channel_id=1, source_target_pairs={{0,3},{1,2},{2,1},{3,0},{4,7},{5,6},{6,5},{7,4}} | collective-permute-start | bytes 1437704 | tf_op jit(solution)/shard_map/ppermute | solution.py:473
  165.7 32.7 %collective-permute-start.13 = (bf16[2,312,768]{2,1,0:T(8,128)(2,1)}, bf16[2,312,768]{2,1,0:T(8,128)(2,1)}, u32[]{:S(2)}, u32[]{:S(2)}) collective-permute-start(bf16[2,312,768]{2,1,0:T(8,128)(2,1)} %get-tuple-element.61.refs_0_), channel_id=1, source_target_pairs={{0,4},{4,0},{1,5},{5,1},{2,6},{6,2},{3,7},{7,3}} | collective-permute-start | bytes 2875400 | tf_op jit(solution)/shard_map/ppermute | solution.py:476
  167.2 30.8 %collective-permute-start.15 = (bf16[312,768]{1,0:T(8,128)(2,1)}, bf16[312,768]{1,0:T(8,128)(2,1)}, u32[]{:S(2)}, u32[]{:S(2)}) collective-permute-start(bf16[312,768]{1,0:T(8,128)(2,1)} %get-tuple-element.64), channel_id=1, source_target_pairs={{0,3},{1,2},{2,1},{3,0},{4,7},{5,6},{6,5},{7,4}} | collective-permute-start | bytes 1437704 | tf_op jit(solution)/shard_map/ppermute | solution.py:473
  175.2 35.2 %collective-permute-start.16 = (bf16[312,768]{1,0:T(8,128)(2,1)}, bf16[312,768]{1,0:T(8,128)(2,1)}, u32[]{:S(2)}, u32[]{:S(2)}) collective-permute-start(bf16[312,768]{1,0:T(8,128)(2,1)} %collective-permute-done.14.refs_2_), channel_id=1, source_target_pairs={{0,4},{4,0},{1,5},{5,1},{2,6},{6,2},{3,7},{7,3}} | collective-permute-start | bytes 1437704 | tf_op jit(solution)/shard_map/ppermute | solution.py:476
  176.9 64.5 %collective-permute-start.8 = (bf16[2,312,768]{2,1,0:T(8,128)(2,1)}, bf16[2,312,768]{2,1,0:T(8,128)(2,1)}, u32[]{:S(2)}, u32[]{:S(2)}) collective-permute-start(bf16[2,312,768]{2,1,0:T(8,128)(2,1)} %collective-permute-done.7.refs_1_), channel_id=1, source_target_pairs={{0,4},{4,0},{1,5},{5,1},{2,6},{6,2},{3,7},{7,3}} | collective-permute-start | bytes 2875400 | tf_op jit(solution)/shard_map/ppermute | solution.py:476
  196.3 34.9 %collective-permute-start.10 = (bf16[312,768]{1,0:T(8,128)(2,1)}, bf16[312,768]{1,0:T(8,128)(2,1)}, u32[]{:S(2)}, u32[]{:S(2)}) collective-permute-start(bf16[312,768]{1,0:T(8,128)(2,1)} %collective-permute-done.9.refs_2_), channel_id=1, source_target_pairs={{0,4},{4,0},{1,5},{5,1},{2,6},{6,2},{3,7},{7,3}} | collective-permute-start | bytes 1437704 | tf_op jit(solution)/shard_map/ppermute | solution.py:476
  198.0 43.4 %collective-permute-start.12 = (bf16[312,768]{1,0:T(8,128)(2,1)}, bf16[312,768]{1,0:T(8,128)(2,1)}, u32[]{:S(2)}, u32[]{:S(2)}) collective-permute-start(bf16[312,768]{1,0:T(8,128)(2,1)} %collective-permute-done.11.refs_3_), channel_id=1, source_target_pairs={{0,4},{4,0},{1,5},{5,1},{2,6},{6,2},{3,7},{7,3}} | collective-permute-start | bytes 1437704 | tf_op jit(solution)/shard_map/ppermute | solution.py:476
  198.3 73.6 %collective-permute-start.17 = (bf16[312,768]{1,0:T(8,128)(2,1)}, bf16[312,768]{1,0:T(8,128)(2,1)}, u32[]{:S(2)}, u32[]{:S(2)}) collective-permute-start(bf16[312,768]{1,0:T(8,128)(2,1)} %collective-permute-done.15.refs_3_), channel_id=1, source_target_pairs={{0,4},{4,0},{1,5},{5,1},{2,6},{6,2},{3,7},{7,3}} | collective-permute-start | bytes 1437704 | tf_op jit(solution)/shard_map/ppermute | solution.py:476
  253.5 26.4 %collective-permute-start.22 = (f32[8,768]{1,0:T(8,128)}, f32[8,768]{1,0:T(8,128)}, u32[]{:S(2)}, u32[]{:S(2)}) collective-permute-start(f32[8,768]{1,0:T(8,128)} %get-tuple-element.76), channel_id=1, source_target_pairs={{0,2},{1,3},{2,0},{3,1},{4,6},{5,7},{6,4},{7,5}} | collective-permute-start | bytes 73736 | tf_op jit(solution)/shard_map/ppermute | solution.py:473
  254.0 25.8 %collective-permute-start.23 = (f32[8,768]{1,0:T(8,128)}, f32[8,768]{1,0:T(8,128)}, u32[]{:S(2)}, u32[]{:S(2)}) collective-permute-start(f32[8,768]{1,0:T(8,128)} %get-tuple-element.76), channel_id=1, source_target_pairs={{0,3},{1,2},{2,1},{3,0},{4,7},{5,6},{6,5},{7,4}} | collective-permute-start | bytes 73736 | tf_op jit(solution)/shard_map/ppermute | solution.py:473
  254.2 25.7 %collective-permute-start.21 = (f32[8,768]{1,0:T(8,128)}, f32[8,768]{1,0:T(8,128)}, u32[]{:S(2)}, u32[]{:S(2)}) collective-permute-start(f32[8,768]{1,0:T(8,128)} %get-tuple-element.76), channel_id=1, source_target_pairs={{0,1},{1,0},{2,3},{3,2},{4,5},{5,4},{6,7},{7,6}} | collective-permute-start | bytes 73736 | tf_op jit(solution)/shard_map/ppermute | solution.py:473
  271.9 8.0 %copy-start = (f32[8,768]{1,0:T(8,128)S(1)}, f32[8,768]{1,0:T(8,128)}, u32[]{:S(2)}) copy-start(f32[8,768]{1,0:T(8,128)} %get-tuple-element.76) | copy-start | bytes 73732
